TPU v7x, 8 devices: a whole 2x2x1 slice. The times are simulated.
8 devices in a mesh: exam: 1 (over z), cols: 2 (over y), rows: 4 (over x, core).
Axes of the slice: x: 2, y: 2, z: 1, core: 2. Of those that a mesh axis runs over, the one named last changes fastest.
Arguments:
- kspace: float32 [2, 8, 32768], P(None, None, ('exam', 'rows', 'cols'))
- wts_y: float32 [6, 32768], P(None, ('exam', 'rows', 'cols'))
- wts_x: float32 [6, 32768], P(None, ('exam', 'rows', 'cols'))
- idx_y: int32 [32768], P(('exam', 'rows', 'cols'))
- idx_x: int32 [32768], P(('exam', 'rows', 'cols'))
- coil_maps: float32 [2, 8, 320, 320], P(None, ('exam', 'cols'), None, 'rows')
- deapod: float32 [320], replicated
Outputs:
- output: float32 [2, 320, 320], P(None, ('exam', 'cols'), 'rows')
All inputs are finite; a program needn't handle non-finite values.
Results may differ from a plain program's by a relative error of at most 0.001.
Values are sent between devices in bfloat16 or wider.
A program may use at most 1 GiB of HBM per device.

v0:
```python
import math
import jax
import jax.numpy as jnp
from jax import lax
from jax.sharding import PartitionSpec as P


def dft_matrix(n_img, n_grid):
    freq_idx = jnp.arange(n_grid) - n_grid // 2
    pos_idx = jnp.arange(n_img) - n_img // 2
    phase_int = (freq_idx[:, None] * pos_idx[None, :]) % n_grid
    phase_ang = phase_int.astype(jnp.float32) * (2.0 * math.pi / n_grid)
    dft_norm = 1.0 / math.sqrt(n_grid)
    cos_t = jnp.cos(phase_ang) * dft_norm
    sin_t = jnp.sin(phase_ang) * dft_norm
    upper_half = jnp.stack([cos_t, sin_t], axis=1)
    lower_half = jnp.stack([-sin_t, cos_t], axis=1)
    return jnp.stack([upper_half, lower_half], axis=0).astype(jnp.bfloat16)


def tap_matrix(tap_off, weights):
    tap_ids = jnp.arange(weights.shape[0]).reshape((-1,) + (1,) * tap_off.ndim)
    return jnp.sum(jnp.where(tap_off[None] == tap_ids, weights[..., None, :], 0.0), axis=0)


def spread_block(kspace, wts_y, wts_x, row_loc, col_loc, row_len, col_len):
    n_coils = kspace.shape[1]
    kern_width = wts_y.shape[0]
    n_slots = kspace.shape[2]
    tile_len = math.gcd(n_slots, 256)
    n_steps = n_slots // tile_len
    tile_data = (
        jnp.moveaxis(kspace.reshape(2, n_coils, n_steps, tile_len), 2, 0),
        jnp.moveaxis(wts_y.reshape(kern_width, n_steps, tile_len), 1, 0),
        jnp.moveaxis(wts_x.reshape(kern_width, n_steps, tile_len), 1, 0),
        row_loc.reshape(n_steps, tile_len),
        col_loc.reshape(n_steps, tile_len),
    )
    row_pos = jnp.arange(row_len)[:, None]
    col_pos = jnp.arange(col_len)[:, None]

    def add_tile(acc_buf, tile_in):
        samp_t, wy_t, wx_t, ry_t, rx_t = tile_in
        row_mat = tap_matrix(row_pos - ry_t[None, :], wy_t)
        col_mat = tap_matrix(col_pos - rx_t[None, :], wx_t)
        scaled = samp_t[:, :, None, :] * row_mat
        return acc_buf + jnp.einsum('sclm,km->sclk', scaled, col_mat, precision=lax.Precision.HIGHEST, preferred_element_type=jnp.float32), None

    start_buf = jnp.zeros((2, n_coils, row_len, col_len), jnp.float32)
    spread_buf, _ = lax.scan(add_tile, start_buf, tile_data)
    return spread_buf


def fold_ghosts(spread_buf, axis, axis_name, n_dev, half_w, core_len):
    lead_band, head_band, body_band, tail_band, trail_band = jnp.split(spread_buf, [half_w, 2 * half_w, core_len, core_len + half_w], axis=axis)
    to_prev = [(k, (k - 1) % n_dev) for k in range(n_dev)]
    to_next = [(k, (k + 1) % n_dev) for k in range(n_dev)]
    from_next = lax.ppermute(lead_band, axis_name, to_prev)
    from_prev = lax.ppermute(trail_band, axis_name, to_next)
    return jnp.concatenate([head_band + from_prev, body_band, tail_band + from_next], axis=axis)


def solution(mesh):
    n_rows = mesh.shape['rows']
    n_cols = mesh.shape['cols']
    sample_spec = ('exam', 'rows', 'cols')

    def local_fn(kspace, wts_y, wts_x, idx_y, idx_x, coil_maps, deapod):
        kern_width = wts_y.shape[0]
        half_w = kern_width // 2
        n_img = deapod.shape[0]
        n_grid = 2 * n_img
        row_blk = n_grid // n_rows
        col_blk = n_grid // n_cols
        row_id = lax.axis_index('rows')
        col_id = lax.axis_index('cols')
        spread_buf = spread_block(kspace, wts_y, wts_x, idx_y - row_id * row_blk, idx_x - col_id * col_blk, row_blk + kern_width, col_blk + kern_width)
        spread_buf = fold_ghosts(spread_buf, 2, 'rows', n_rows, half_w, row_blk)
        spread_buf = fold_ghosts(spread_buf, 3, 'cols', n_cols, half_w, col_blk)
        k_grid = lax.all_to_all(spread_buf.astype(jnp.bfloat16), 'cols', 1, 3, tiled=True)
        dft_mat = dft_matrix(n_img, n_grid)
        half_img = jnp.einsum('scuv,svtq->tcuq', k_grid, dft_mat, preferred_element_type=jnp.float32).astype(jnp.bfloat16)
        half_img = lax.all_to_all(half_img, 'rows', 3, 2, tiled=True)
        coil_img = jnp.einsum('tcuq,tuop->ocpq', half_img, dft_mat, preferred_element_type=jnp.float32)
        part_re = jnp.sum(coil_maps[0] * coil_img[0] + coil_maps[1] * coil_img[1], axis=0)
        part_im = jnp.sum(coil_maps[0] * coil_img[1] - coil_maps[1] * coil_img[0], axis=0)
        combined = lax.psum_scatter(jnp.stack([part_re, part_im]), 'cols', scatter_dimension=1, tiled=True)
        d_rows = deapod.reshape(n_cols, n_img // n_cols)[col_id]
        d_cols = deapod.reshape(n_rows, n_img // n_rows)[row_id]
        return combined * (d_rows[:, None] * d_cols[None, :])

    return jax.shard_map(
        local_fn,
        mesh=mesh,
        in_specs=(P(None, None, sample_spec), P(None, sample_spec), P(None, sample_spec), P(sample_spec), P(sample_spec), P(None, ('exam', 'cols'), None, 'rows'), P()),
        out_specs=P(None, ('exam', 'cols'), 'rows'),
        check_vma=False,
    )
```

profile of v0, /device:TPU:0, one launch (start us, length us, event | category | flops | bytes accessed | tf_op | source)
XLA Modules:
  0.0 271.9 jit_solution(6150010934374759468)
XLA Ops:
  9.0 138.0 %while.11 = (s32[]{:T(128)}, f32[2,8,166,326]{3,2,1,0:T(8,128)}, f32[16,2,8,256]{3,0,2,1:T(8,128)S(1)}, s32[16,256]{1,0:T(8,128)S(1)}, f32[16,6,256]{2,1,0:T(8,1...) while((s32[]{:T(128)}, f32[2,8,166,326]{3,2,1,0:T(8,128)}, ...), condition=%wide.region_3.4_spmd.clone, body=%wide.region_0.3_spmd.clone.sunk | while | flops 2664588288 | bytes 9067131 | solution.py:50
  10.2 6.0 %select_add_fusion.2 = f32[2,8,166,326]{3,2,1,0:T(8,128)} fusion(f32[2,8,166,326]{3,2,1,0:T(8,128)} %get-tuple-element.197, pred[]{:T(512)S(6)} %compare.3, f32[166,256]{1,0:T(8,128)S(1)} %select_reduce_fusion.4, f32[2,8,256]{2,1,0:T(8,128)S(1)} %bitcast.91, f32[326,256]{1,0:T(8,128)S(1)} %select_reduce_fusion.5), kind=kOutput, calls=%fused_computation.2.clone.1 | convolution fusion | flops 2662321152 | bytes 7447041 | tf_op jit(solution)/shard_map/while/body/eval_jaxpr/sclm,km->sclk/dot_general | solution.py:47
  17.4 7.6 %select_add_fusion.2 = f32[2,8,166,326]{3,2,1,0:T(8,128)} fusion(f32[2,8,166,326]{3,2,1,0:T(8,128)} %get-tuple-element.197, pred[]{:T(512)S(6)} %compare.3, f32[166,256]{1,0:T(8,128)S(1)} %select_reduce_fusion.4, f32[2,8,256]{2,1,0:T(8,128)S(1)} %bitcast.91, f32[326,256]{1,0:T(8,128)S(1)} %select_reduce_fusion.5), kind=kOutput, calls=%fused_computation.2.clone.1 | convolution fusion | flops 2662321152 | bytes 7447041 | tf_op jit(solution)/shard_map/while/body/eval_jaxpr/sclm,km->sclk/dot_general | solution.py:47
  26.1 7.6 %select_add_fusion.2 = f32[2,8,166,326]{3,2,1,0:T(8,128)} fusion(f32[2,8,166,326]{3,2,1,0:T(8,128)} %get-tuple-element.197, pred[]{:T(512)S(6)} %compare.3, f32[166,256]{1,0:T(8,128)S(1)} %select_reduce_fusion.4, f32[2,8,256]{2,1,0:T(8,128)S(1)} %bitcast.91, f32[326,256]{1,0:T(8,128)S(1)} %select_reduce_fusion.5), kind=kOutput, calls=%fused_computation.2.clone.1 | convolution fusion | flops 2662321152 | bytes 7447041 | tf_op jit(solution)/shard_map/while/body/eval_jaxpr/sclm,km->sclk/dot_general | solution.py:47
  34.8 7.6 %select_add_fusion.2 = f32[2,8,166,326]{3,2,1,0:T(8,128)} fusion(f32[2,8,166,326]{3,2,1,0:T(8,128)} %get-tuple-element.197, pred[]{:T(512)S(6)} %compare.3, f32[166,256]{1,0:T(8,128)S(1)} %select_reduce_fusion.4, f32[2,8,256]{2,1,0:T(8,128)S(1)} %bitcast.91, f32[326,256]{1,0:T(8,128)S(1)} %select_reduce_fusion.5), kind=kOutput, calls=%fused_computation.2.clone.1 | convolution fusion | flops 2662321152 | bytes 7447041 | tf_op jit(solution)/shard_map/while/body/eval_jaxpr/sclm,km->sclk/dot_general | solution.py:47
  43.5 7.6 %select_add_fusion.2 = f32[2,8,166,326]{3,2,1,0:T(8,128)} fusion(f32[2,8,166,326]{3,2,1,0:T(8,128)} %get-tuple-element.197, pred[]{:T(512)S(6)} %compare.3, f32[166,256]{1,0:T(8,128)S(1)} %select_reduce_fusion.4, f32[2,8,256]{2,1,0:T(8,128)S(1)} %bitcast.91, f32[326,256]{1,0:T(8,128)S(1)} %select_reduce_fusion.5), kind=kOutput, calls=%fused_computation.2.clone.1 | convolution fusion | flops 2662321152 | bytes 7447041 | tf_op jit(solution)/shard_map/while/body/eval_jaxpr/sclm,km->sclk/dot_general | solution.py:47
  52.2 7.6 %select_add_fusion.2 = f32[2,8,166,326]{3,2,1,0:T(8,128)} fusion(f32[2,8,166,326]{3,2,1,0:T(8,128)} %get-tuple-element.197, pred[]{:T(512)S(6)} %compare.3, f32[166,256]{1,0:T(8,128)S(1)} %select_reduce_fusion.4, f32[2,8,256]{2,1,0:T(8,128)S(1)} %bitcast.91, f32[326,256]{1,0:T(8,128)S(1)} %select_reduce_fusion.5), kind=kOutput, calls=%fused_computation.2.clone.1 | convolution fusion | flops 2662321152 | bytes 7447041 | tf_op jit(solution)/shard_map/while/body/eval_jaxpr/sclm,km->sclk/dot_general | solution.py:47
  61.0 7.6 %select_add_fusion.2 = f32[2,8,166,326]{3,2,1,0:T(8,128)} fusion(f32[2,8,166,326]{3,2,1,0:T(8,128)} %get-tuple-element.197, pred[]{:T(512)S(6)} %compare.3, f32[166,256]{1,0:T(8,128)S(1)} %select_reduce_fusion.4, f32[2,8,256]{2,1,0:T(8,128)S(1)} %bitcast.91, f32[326,256]{1,0:T(8,128)S(1)} %select_reduce_fusion.5), kind=kOutput, calls=%fused_computation.2.clone.1 | convolution fusion | flops 2662321152 | bytes 7447041 | tf_op jit(solution)/shard_map/while/body/eval_jaxpr/sclm,km->sclk/dot_general | solution.py:47
  69.7 7.6 %select_add_fusion.2 = f32[2,8,166,326]{3,2,1,0:T(8,128)} fusion(f32[2,8,166,326]{3,2,1,0:T(8,128)} %get-tuple-element.197, pred[]{:T(512)S(6)} %compare.3, f32[166,256]{1,0:T(8,128)S(1)} %select_reduce_fusion.4, f32[2,8,256]{2,1,0:T(8,128)S(1)} %bitcast.91, f32[326,256]{1,0:T(8,128)S(1)} %select_reduce_fusion.5), kind=kOutput, calls=%fused_computation.2.clone.1 | convolution fusion | flops 2662321152 | bytes 7447041 | tf_op jit(solution)/shard_map/while/body/eval_jaxpr/sclm,km->sclk/dot_general | solution.py:47
  78.4 7.6 %select_add_fusion.2 = f32[2,8,166,326]{3,2,1,0:T(8,128)} fusion(f32[2,8,166,326]{3,2,1,0:T(8,128)} %get-tuple-element.197, pred[]{:T(512)S(6)} %compare.3, f32[166,256]{1,0:T(8,128)S(1)} %select_reduce_fusion.4, f32[2,8,256]{2,1,0:T(8,128)S(1)} %bitcast.91, f32[326,256]{1,0:T(8,128)S(1)} %select_reduce_fusion.5), kind=kOutput, calls=%fused_computation.2.clone.1 | convolution fusion | flops 2662321152 | bytes 7447041 | tf_op jit(solution)/shard_map/while/body/eval_jaxpr/sclm,km->sclk/dot_general | solution.py:47
  87.1 7.6 %select_add_fusion.2 = f32[2,8,166,326]{3,2,1,0:T(8,128)} fusion(f32[2,8,166,326]{3,2,1,0:T(8,128)} %get-tuple-element.197, pred[]{:T(512)S(6)} %compare.3, f32[166,256]{1,0:T(8,128)S(1)} %select_reduce_fusion.4, f32[2,8,256]{2,1,0:T(8,128)S(1)} %bitcast.91, f32[326,256]{1,0:T(8,128)S(1)} %select_reduce_fusion.5), kind=kOutput, calls=%fused_computation.2.clone.1 | convolution fusion | flops 2662321152 | bytes 7447041 | tf_op jit(solution)/shard_map/while/body/eval_jaxpr/sclm,km->sclk/dot_general | solution.py:47
  95.9 7.6 %select_add_fusion.2 = f32[2,8,166,326]{3,2,1,0:T(8,128)} fusion(f32[2,8,166,326]{3,2,1,0:T(8,128)} %get-tuple-element.197, pred[]{:T(512)S(6)} %compare.3, f32[166,256]{1,0:T(8,128)S(1)} %select_reduce_fusion.4, f32[2,8,256]{2,1,0:T(8,128)S(1)} %bitcast.91, f32[326,256]{1,0:T(8,128)S(1)} %select_reduce_fusion.5), kind=kOutput, calls=%fused_computation.2.clone.1 | convolution fusion | flops 2662321152 | bytes 7447041 | tf_op jit(solution)/shard_map/while/body/eval_jaxpr/sclm,km->sclk/dot_general | solution.py:47
  104.6 7.6 %select_add_fusion.2 = f32[2,8,166,326]{3,2,1,0:T(8,128)} fusion(f32[2,8,166,326]{3,2,1,0:T(8,128)} %get-tuple-element.197, pred[]{:T(512)S(6)} %compare.3, f32[166,256]{1,0:T(8,128)S(1)} %select_reduce_fusion.4, f32[2,8,256]{2,1,0:T(8,128)S(1)} %bitcast.91, f32[326,256]{1,0:T(8,128)S(1)} %select_reduce_fusion.5), kind=kOutput, calls=%fused_computation.2.clone.1 | convolution fusion | flops 2662321152 | bytes 7447041 | tf_op jit(solution)/shard_map/while/body/eval_jaxpr/sclm,km->sclk/dot_general | solution.py:47
  113.3 7.6 %select_add_fusion.2 = f32[2,8,166,326]{3,2,1,0:T(8,128)} fusion(f32[2,8,166,326]{3,2,1,0:T(8,128)} %get-tuple-element.197, pred[]{:T(512)S(6)} %compare.3, f32[166,256]{1,0:T(8,128)S(1)} %select_reduce_fusion.4, f32[2,8,256]{2,1,0:T(8,128)S(1)} %bitcast.91, f32[326,256]{1,0:T(8,128)S(1)} %select_reduce_fusion.5), kind=kOutput, calls=%fused_computation.2.clone.1 | convolution fusion | flops 2662321152 | bytes 7447041 | tf_op jit(solution)/shard_map/while/body/eval_jaxpr/sclm,km->sclk/dot_general | solution.py:47
  122.0 7.6 %select_add_fusion.2 = f32[2,8,166,326]{3,2,1,0:T(8,128)} fusion(f32[2,8,166,326]{3,2,1,0:T(8,128)} %get-tuple-element.197, pred[]{:T(512)S(6)} %compare.3, f32[166,256]{1,0:T(8,128)S(1)} %select_reduce_fusion.4, f32[2,8,256]{2,1,0:T(8,128)S(1)} %bitcast.91, f32[326,256]{1,0:T(8,128)S(1)} %select_reduce_fusion.5), kind=kOutput, calls=%fused_computation.2.clone.1 | convolution fusion | flops 2662321152 | bytes 7447041 | tf_op jit(solution)/shard_map/while/body/eval_jaxpr/sclm,km->sclk/dot_general | solution.py:47
  130.7 7.6 %select_add_fusion.2 = f32[2,8,166,326]{3,2,1,0:T(8,128)} fusion(f32[2,8,166,326]{3,2,1,0:T(8,128)} %get-tuple-element.197, pred[]{:T(512)S(6)} %compare.3, f32[166,256]{1,0:T(8,128)S(1)} %select_reduce_fusion.4, f32[2,8,256]{2,1,0:T(8,128)S(1)} %bitcast.91, f32[326,256]{1,0:T(8,128)S(1)} %select_reduce_fusion.5), kind=kOutput, calls=%fused_computation.2.clone.1 | convolution fusion | flops 2662321152 | bytes 7447041 | tf_op jit(solution)/shard_map/while/body/eval_jaxpr/sclm,km->sclk/dot_general | solution.py:47
  139.5 7.6 %select_add_fusion.2 = f32[2,8,166,326]{3,2,1,0:T(8,128)} fusion(f32[2,8,166,326]{3,2,1,0:T(8,128)} %get-tuple-element.197, pred[]{:T(512)S(6)} %compare.3, f32[166,256]{1,0:T(8,128)S(1)} %select_reduce_fusion.4, f32[2,8,256]{2,1,0:T(8,128)S(1)} %bitcast.91, f32[326,256]{1,0:T(8,128)S(1)} %select_reduce_fusion.5), kind=kOutput, calls=%fused_computation.2.clone.1 | convolution fusion | flops 2662321152 | bytes 7447041 | tf_op jit(solution)/shard_map/while/body/eval_jaxpr/sclm,km->sclk/dot_general | solution.py:47
  150.9 4.0 %collective-permute-done = f32[2,8,3,326]{3,1,2,0:T(8,128)S(1)} collective-permute-done((f32[2,8,3,326]{3,1,2,0:T(8,128)S(1)}, f32[2,8,3,326]{3,1,2,0:T(8,128)S(1)}, u32[]{:S(2)}, u32[]{:S(2)}) %collective-permute-start) | collective-permute-done | bytes 62624 | tf_op jit(solution)/shard_map/ppermute | solution.py:59
  154.9 6.5 %copy.45 = f32[2,8,166,326]{2,1,3,0:T(8,128)} copy(f32[2,8,166,326]{3,2,1,0:T(8,128)} %get-tuple-element.52) | data formatting | bytes 6926848 | tf_op jit(solution)/shard_map/while | solution.py:50
  161.4 6.3 %split.43 = f32[2,8,154,326]{2,1,3,0:T(8,128)} slice(f32[2,8,166,326]{2,1,3,0:T(8,128)} %copy.45), slice={[0:2], [0:8], [6:160], [0:326]} | slice | bytes 6426112 | tf_op jit(solution)/shard_map/split | solution.py:55
  188.3 3.9 %all-to-all-start = ((bf16[2,8,160,320]{3,2,0,1:T(8,128)(2,1)}), bf16[2,8,160,320]{3,2,0,1:T(8,128)(2,1)S(1)}, u32[]{:S(2)}, u32[]{:S(2)}) async-start(bf16[2,8,160,320]{3,2,0,1:T(8,128)(2,1)} %copy.50), calls=%async_computation | async-start | bytes 3932160 | tf_op jit(solution)/shard_map/all_to_all | solution.py:80
  197.2 18.4 %all-to-all-done = bf16[2,8,160,320]{3,2,0,1:T(8,128)(2,1)S(1)} async-done(((bf16[2,8,160,320]{3,2,0,1:T(8,128)(2,1)}), bf16[2,8,160,320]{3,2,0,1:T(8,128)(2,1)S(1)}, u32[]{:S(2)}, u32[]{:S(2)}) %all-to-all-start) | async-done | bytes 1638432 | tf_op jit(solution)/shard_map/all_to_all | solution.py:80
  232.2 16.8 %all-to-all-done.1 = bf16[2,4,160,320]{2,1,0,3:T(4,128)(2,1)S(1)} async-done(((bf16[2,4,160,320]{2,1,0,3:T(4,128)(2,1)}), bf16[2,4,160,320]{2,1,0,3:T(4,128)(2,1)S(1)}, u32[]{:S(2)}, u32[]{:S(2)}) %all-to-all-start.1) | async-done | bytes 819232 | tf_op jit(solution)/shard_map/all_to_all | solution.py:83
  254.3 8.7 %reduce-scatter.4.cloned.1.call-done = f32[160,160]{1,0:T(8,128)} async-done(((f32[320,160]{1,0:T(8,128)}), f32[160,160]{1,0:T(8,128)}) %reduce-scatter.4.cloned.1.call-update) | async-done | bytes 102416
  (199 shorter events, 73.4 us)
Async XLA Ops:
  150.0 4.9 %copy-start.3 = (f32[2,8,166,326]{3,1,2,0:T(8,128)}, f32[2,8,166,326]{3,1,2,0:T(8,128)S(1)}, u32[]{:S(2)}) copy-start(f32[2,8,166,326]{3,1,2,0:T(8,128)S(1)} %copy.43) | copy-start | bytes 10390276
  150.0 4.8 %collective-permute-start = (f32[2,8,3,326]{3,1,2,0:T(8,128)S(1)}, f32[2,8,3,326]{3,1,2,0:T(8,128)S(1)}, u32[]{:S(2)}, u32[]{:S(2)}) collective-permute-start(f32[2,8,3,326]{3,1,2,0:T(8,128)S(1)} %split.42), channel_id=1, source_target_pairs={{0,1},{1,2},{2,3},{3,0},{4,5},{5,6},{6,7},{7,4}} | collective-permute-start | bytes 187784 | tf_op jit(solution)/shard_map/ppermute | solution.py:59
  154.9 15.3 %collective-permute-start.1 = (f32[2,8,3,326]{3,1,2,0:T(8,128)S(1)}, f32[2,8,3,326]{3,1,2,0:T(8,128)S(1)}, u32[]{:S(2)}, u32[]{:S(2)}) collective-permute-start(f32[2,8,3,326]{3,1,2,0:T(8,128)S(1)} %get-tuple-element.130), channel_id=1, source_target_pairs={{0,3},{1,0},{2,1},{3,2},{4,7},{5,4},{6,5},{7,6}} | collective-permute-start | bytes 187784 | tf_op jit(solution)/shard_map/ppermute | solution.py:58
  171.1 6.0 %slice-start = ((s8[5341184]{0:T(1024)(128)(4,1)}), s8[1146880]{0:T(1024)(128)(4,1)S(1)}, s32[]{:S(2)}) async-start(s8[5341184]{0:T(1024)(128)(4,1)} %bitcast.85), calls=%async_computation.4 | async-start | bytes 2293760
  173.7 3.4 %slice-start.1 = ((s8[5341184]{0:T(1024)(128)(4,1)}), s8[4194304]{0:T(1024)(128)(4,1)S(1)}, s32[]{:S(2)}) async-start(s8[5341184]{0:T(1024)(128)(4,1)} %bitcast.85), calls=%async_computation.5 | async-start | bytes 8388608
  173.7 3.4 %copy-start = (f32[2,8,3,326]{2,1,3,0:T(8,128)S(1)}, f32[2,8,3,326]{2,1,3,0:T(8,128)}, u32[]{:S(2)}) copy-start(f32[2,8,3,326]{2,1,3,0:T(8,128)} %copy.48) | copy-start | bytes 187780
  173.7 3.8 %copy-start.1 = (f32[2,8,3,326]{2,1,3,0:T(8,128)S(1)}, f32[2,8,3,326]{2,1,3,0:T(8,128)}, u32[]{:S(2)}) copy-start(f32[2,8,3,326]{2,1,3,0:T(8,128)} %copy.49) | copy-start | bytes 187780
  174.7 7.6 %collective-permute-start.3 = (f32[2,8,160,3]{2,1,3,0:T(8,128)S(1)}, f32[2,8,160,3]{2,1,3,0:T(8,128)S(1)}, u32[]{:S(2)}, u32[]{:S(2)}) collective-permute-start(f32[2,8,160,3]{2,1,3,0:T(8,128)S(1)} %pad_maximum_fusion.3), channel_id=1, source_target_pairs={{0,4},{4,0},{1,5},{5,1},{2,6},{6,2},{3,7},{7,3}} | collective-permute-start | bytes 92168 | tf_op jit(solution)/shard_map/ppermute | solution.py:58
  179.9 4.7 %collective-permute-start.2 = (f32[2,8,160,3]{2,1,3,0:T(8,128)S(1)}, f32[2,8,160,3]{2,1,3,0:T(8,128)S(1)}, u32[]{:S(2)}, u32[]{:S(2)}) collective-permute-start(f32[2,8,160,3]{2,1,3,0:T(8,128)S(1)} %split.47), channel_id=1, source_target_pairs={{0,4},{4,0},{1,5},{5,1},{2,6},{6,2},{3,7},{7,3}} | collective-permute-start | bytes 92168 | tf_op jit(solution)/shard_map/ppermute | solution.py:59
  188.3 27.3 %all-to-all-start = ((bf16[2,8,160,320]{3,2,0,1:T(8,128)(2,1)}), bf16[2,8,160,320]{3,2,0,1:T(8,128)(2,1)S(1)}, u32[]{:S(2)}, u32[]{:S(2)}) async-start(bf16[2,8,160,320]{3,2,0,1:T(8,128)(2,1)} %copy.50), calls=%async_computation | async-start | bytes 3932160 | tf_op jit(solution)/shard_map/all_to_all | solution.py:80
  215.6 1.3 copy-start.2
  226.0 6.0 %copy-start.5 = (f32[320]{0:T(512)S(1)}, f32[320]{0:T(512)}, u32[]{:S(2)}) copy-start(f32[320]{0:T(512)} %param.15) | copy-start | bytes 3844
  228.4 20.5 %all-to-all-start.1 = ((bf16[2,4,160,320]{2,1,0,3:T(4,128)(2,1)}), bf16[2,4,160,320]{2,1,0,3:T(4,128)(2,1)S(1)}, u32[]{:S(2)}, u32[]{:S(2)}) async-start(bf16[2,4,160,320]{2,1,0,3:T(4,128)(2,1)} %copy.52), calls=%async_computation.1 | async-start | bytes 2621440 | tf_op jit(solution)/shard_map/all_to_all | solution.py:83
  232.0 31.0 %reduce-scatter.4.cloned.1.call-start = ((), (), s32[]{:S(2)}) async-start(), calls=%async_computation.3 | async-start | bytes 491520
  250.8 2.1 copy-start.4
Sparse Core Ops, SparseCore 0:
  254.3 8.5 reduce-scatter.3
where the time goes:
time: 274 us; the launch traced here: 272 us
  matrix products  125 us (46%)
  local copies, waits for them, and re-layouts  52.4 us (19%)
  waiting for transfers between devices  50.1 us (18%)
  other arithmetic  17.1 us (6%)
  between operations  13.7 us (5%)
  starting transfers between devices  13.1 us (5%)
    dot_general x16, matrix products, add_tile(): jnp.einsum('sclm,km->sclk', scaled, col_mat, precision=lax.Precision.HIGH...  120 us
    all_to_all x1, waiting for transfers between devices, local_fn(): lax.all_to_all(spread_buf.astype(jnp.bfloat16), 'cols', 1, 3, tiled=True)  18.4 us
    all_to_all x1, waiting for transfers between devices, local_fn(): half_img = lax.all_to_all(half_img, 'rows', 3, 2, tiled=True)  16.8 us
    broadcast_in_dim x16, local copies, waits for them, and re-layouts, tap_matrix(): jnp.where(tap_off[None] == tap_ids, weights[..., None, :], 0.0)  11.5 us
    while x2, local copies, waits for them, and re-layouts, spread_block(): spread_buf, _ = lax.scan(add_tile, start_buf, tile_data)  9.45 us
    unnamed x2, waiting for transfers between devices  8.67 us
    split x4, local copies, waits for them, and re-layouts, fold_ghosts(): jnp.split(spread_buf, [half_w, 2 * half_w, core_len, core_len + half_w],...  6.55 us
    ppermute x2, waiting for transfers between devices, fold_ghosts(): from_prev = lax.ppermute(trail_band, axis_name, to_next)  6.25 us
  transfers between devices with their start and end apart: 7, of which 5 were waited for; matrix products, arithmetic and copies ran while one was open for 8% of the time, Pallas kernels for 0%

commit v1 on v0

v1 whole, which is shorter than its diff:
```python
import functools
import math

import jax
import jax.numpy as jnp
import numpy as np
from jax import lax
from jax.experimental import pallas as pl
from jax.experimental.pallas import tpu as pltpu
from jax.sharding import PartitionSpec as P

BF = jnp.bfloat16
F32 = jnp.float32
VMEM = pltpu.VMEM
LANES = 128
SUB, WIN, QTR, HALF = 8, 16, 32, 64
N_GRID, N_IMG, N_COILS, KW = 640, 320, 8, 6
ROWS, COLS = 4, 2
RB, CB, QB = N_GRID // ROWS, N_GRID // COLS, N_IMG // ROWS
PB = N_IMG // COLS
NS = 4096
NB = NS // LANES
NG = 21
CW = CB + WIN
T = 6
PS = 9
ORDER = (1, 2, 3, 0, 4)
GROUPS = ((0, 96), (96, 64))
MESH_ID = pl.DeviceIdType.MESH


def dft_parts():
    freq = np.arange(N_GRID) - N_GRID // 2
    pos = np.arange(N_IMG) - N_IMG // 2
    ang = ((freq[:, None] * pos[None, :]) % N_GRID).astype(np.float32) * np.float32(2.0 * math.pi / N_GRID)
    norm = np.float32(1.0 / math.sqrt(N_GRID))
    c, s = np.cos(ang) * norm, np.sin(ang) * norm
    return np.stack([np.stack([c, s], 1), np.stack([-s, c], 1)], 0)


def col_dft():
    e = dft_parts()
    out = np.zeros((2 * N_GRID, N_GRID), np.float32)
    for dp in range(2):
        for t in range(2):
            for h in range(2):
                q0 = QB * (2 * dp + h)
                l0 = LANES * (2 * dp + t) + HALF * h
                out[:, l0:l0 + HALF] = e[:, :, t, q0:q0 + HALF].reshape(2 * N_GRID, HALF)
    for t in range(2):
        for d in range(4):
            l0 = 4 * LANES + HALF * t + WIN * d
            out[:, l0:l0 + WIN] = e[:, :, t, QB * d + HALF:QB * d + 80].reshape(2 * N_GRID, WIN)
    return jnp.asarray(out, BF)


def row_dft():
    e = dft_parts()
    rows = np.concatenate([np.arange(QTR * l, QTR * l + QTR) for l in ORDER])
    parts = []
    for start, n in GROUPS:
        for t in range(2):
            for b in range(ROWS):
                u = b * RB + rows[start:start + n]
                parts.append(e[t, u].reshape(n, 2 * N_IMG))
    return jnp.asarray(np.concatenate(parts, 0).T, BF)


def unmix():
    m = np.zeros((256, 256), np.float32)
    for ch in range(SUB):
        for pp in range(2):
            for i in range(WIN):
                m[ch * QTR + WIN * pp + (i + SUB) % WIN, pp * 128 + i * SUB + ch] = 1.0
    return jnp.asarray(m, BF)


def prep_kernel(ks_ref, wy_ref, wx_ref, iy_ref, ix_ref, own_ref, far_ref, base_ref):
    k = lax.axis_index('cols')
    r = lax.axis_index('rows')
    iy = iy_ref[...]
    base_ref[...] = ((iy - r * RB + 5) >> 3) * CW + (ix_ref[...] - k * CB + 5)
    sh = ((iy + 5) & 15).astype(F32)
    lo = jnp.concatenate([ks_ref[0, 0:4, :], ks_ref[1, 0:4, :]], axis=0)
    hi = jnp.concatenate([ks_ref[0, 4:SUB, :], ks_ref[1, 4:SUB, :]], axis=0)
    own_ref[0:SUB, :] = jnp.where(k == 0, lo, hi)
    far_ref[0:SUB, :] = jnp.where(k == 0, hi, lo)
    zero2 = jnp.zeros((2, NS), F32)
    for ref in (own_ref, far_ref):
        ref[SUB:WIN, :] = jnp.concatenate([wx_ref[...], zero2], axis=0)
        ref[WIN:24, :] = jnp.concatenate([wy_ref[...], zero2], axis=0)
        for b in range(NB):
            ref[22:23, LANES * b:LANES * (b + 1)] = sh[b:b + 1, :]


def split3(x):
    hi = x.astype(BF).astype(F32)
    r = x - hi
    mid = r.astype(BF).astype(F32)
    return hi, mid, r - mid


def accumulate(base_ref, pay_ref, accs, us, xs, vs, r_ref):
    row_i = lax.broadcasted_iota(jnp.int32, (WIN, LANES), 0)

    def make_u(blk, k):
        off = pl.multiple_of(jnp.minimum(blk, NB - 1) * LANES, LANES)
        y8 = pay_ref[0:SUB, pl.ds(off, LANES)]
        wyp = pay_ref[WIN:24, pl.ds(off, LANES)]
        d = (row_i - wyp[6:7, :].astype(jnp.int32)) & 15
        p = jnp.zeros((WIN, LANES), F32)
        for a in range(KW):
            p = jnp.where(d == a, wyp[a:a + 1, :], p)
        us[k][...] = jnp.concatenate([y8 * p[i:i + 1, :] for i in range(WIN)], axis=0).T
        x3 = list(split3(pay_ref[SUB:WIN, pl.ds(off, LANES)])) + [jnp.zeros((104, LANES), F32)]
        xs[k][...] = jnp.concatenate(x3, axis=0).T

    def make_v(k):
        lhs = xs[k][...].astype(BF)
        u = us[k][...]
        for bp in range(3):
            w = jnp.dot(lhs, r_ref[:, 256 * bp:256 * bp + 256], preferred_element_type=F32)
            for c in range(2):
                v = w[:, LANES * c:LANES * (c + 1)] * u
                for g in range(WIN):
                    vs[k][pl.ds(SUB * PS * g + 2 * bp + c, SUB, stride=PS), :] = v[SUB * g:SUB * g + SUB, :]

    def add_tiles(blk, k):
        for j in range(LANES):
            acc = accs[j % T]
            b = base_ref[blk, j]
            acc[pl.ds(b, SUB), :] = acc[pl.ds(b, SUB), :] + vs[k][PS * j:PS * j + SUB, :]

    def clear(n, _):
        for a in accs:
            a[pl.ds(pl.multiple_of(n * CW, SUB), CW), :] = jnp.zeros((CW, LANES), F32)
        return 0

    lax.fori_loop(0, NG, clear, 0)
    kk = lax.broadcasted_iota(jnp.int32, (LANES, 768), 0)
    ll = lax.broadcasted_iota(jnp.int32, (LANES, 768), 1)
    r_ref[...] = jnp.where((kk < 24) & ((kk & 7) == (ll >> 7)), 1.0, 0.0).astype(BF)
    for v in vs:
        v[...] = jnp.zeros_like(v)
    make_u(0, 0)
    make_u(1, 1)
    make_v(0)

    def body(n, _):
        k = 2 * n
        make_v(1)
        add_tiles(k, 0)
        make_u(k + 2, 0)
        make_v(0)
        add_tiles(k + 1, 1)
        make_u(k + 3, 1)
        return 0

    lax.fori_loop(0, NB // 2, body, 0)


def folded(accs, off, n):
    def total(g):
        o = pl.multiple_of(g * CW + off, SUB)
        s = accs[0][pl.ds(o, n), :]
        for a in accs[1:]:
            s = s + a[pl.ds(o, n), :]
        return s

    high = lax.broadcasted_iota(jnp.int32, (n, LANES), 1) >= HALF
    even = [total(2 * p) for p in range(11)]
    tiles = [total(2 * p + 1) + jnp.where(high, even[p], even[p + 1]) for p in range(10)]
    return tiles + [jnp.where(high, even[10], even[0])]


def own_kernel(base_ref, pay_ref, out_ref, *scr):
    accs, us, xs, vs, r_ref = scr[:T], scr[T:T + 2], scr[T + 2:T + 4], scr[T + 4:T + 6], scr[T + 6]
    accumulate(base_ref, pay_ref, accs, us, xs, vs, r_ref)

    def fold(q, _):
        off = pl.multiple_of(q * SUB, SUB)
        for p, t in enumerate(folded(accs, off, SUB)):
            out_ref[p, pl.ds(off, SUB), :] = t
        return 0

    lax.fori_loop(0, CW // SUB, fold, 0)


def far_kernel(base_ref, pay_ref, a_ref, tb_ref, edge_ref, pack_ref, *scr):
    accs, us, xs, vs, r_ref, gh_ref = scr[:T], scr[T:T + 2], scr[T + 2:T + 4], scr[T + 4:T + 6], scr[T + 6], scr[T + 7]
    accumulate(base_ref, pay_ref, accs, us, xs, vs, r_ref)
    k = lax.axis_index('cols')
    own0 = k * CB
    far0 = CB - own0
    high = lax.broadcasted_iota(jnp.int32, (SUB, LANES), 1) >= HALF

    left = folded(accs, 0, SUB)
    right = folded(accs, CW - SUB, SUB)
    for src, dst in ((CW - SUB, SUB), (0, CB)):
        for p in range(10):
            rows = pl.ds((2 * p + 1) * CW + dst, SUB)
            accs[0][rows, :] = accs[0][rows, :] + a_ref[p, src:src + SUB, :]
        ghost = a_ref[10, src:src + SUB, :]
        accs[0][dst:dst + SUB, :] = accs[0][dst:dst + SUB, :] + jnp.where(high, 0.0, ghost)
        rows = pl.ds(20 * CW + dst, SUB)
        accs[0][rows, :] = accs[0][rows, :] + jnp.where(high, ghost, 0.0)

    high16 = lax.broadcasted_iota(jnp.int32, (WIN, LANES), 1) >= HALF

    def put(v, tiles):
        v = pl.multiple_of(v, WIN)
        for p in range(10):
            tb_ref[p, pl.ds(v, WIN), :] = tiles[p].astype(BF)
        edge_ref[pl.ds(v, WIN), :] = jnp.where(high16, tiles[0], tiles[9])
        gh_ref[pl.ds(v, WIN), :] = tiles[10]

    def far_part(s, _):
        put(far0 + WIN * s, folded(accs, pl.multiple_of(SUB + WIN * s, SUB), WIN))
        return 0

    lax.fori_loop(0, CB // WIN, far_part, 0)

    def own_part(s, _):
        put(own0 + WIN * s, [a_ref[p, pl.ds(pl.multiple_of(SUB + WIN * s, SUB), WIN), :] for p in range(11)])
        return 0

    lax.fori_loop(1, CB // WIN - 1, own_part, 0)
    put(own0, [jnp.concatenate([a_ref[p, SUB:WIN, :] + right[p], a_ref[p, WIN:24, :]], axis=0) for p in range(11)])
    put(own0 + CB - WIN, [jnp.concatenate([a_ref[p, CB - SUB:CB, :], a_ref[p, CB:CB + SUB, :] + left[p]], axis=0) for p in range(11)])

    slot = lax.broadcasted_iota(jnp.int32, (RB, LANES), 1) >> 5
    for side, lane0 in ((0, QTR), (1, HALF)):
        out = jnp.zeros((RB, LANES), F32)
        for j in range(4):
            piece = pltpu.roll(gh_ref[RB * j:RB * (j + 1), :], (QTR * j - lane0) % LANES, axis=1)
            out = jnp.where(slot == j, piece, out)
        pack_ref[side] = out


def image_kernel(tb_ref, edge_ref, pack_ref, s_ref, dd_ref, ev_hbm, eu_hbm, pm_ref, out_ref,
                 ev_ref, eu_ref, g_ref, halo, send_m, send_r, hm1, hm2, hr1, hr2, acc_m, acc_r, s_main, s_rem,
                 img_m, img_r, red_m, red_r,
                 load_sem, halo_ss, halo_rs, main_ss, main_rs, rem_ss, rem_rs, red_ss, red_rs):
    k = lax.axis_index('cols')
    r = lax.axis_index('rows')
    core = r % 2
    peers = (r + 1 - 2 * core, (r + 2) % 4, 3 - r)
    prev, nxt = (r + 3) % 4, (r + 1) % 4
    load_ev = pltpu.make_async_copy(ev_hbm, ev_ref, load_sem.at[0])
    load_eu = pltpu.make_async_copy(eu_hbm, eu_ref, load_sem.at[1])
    load_ev.start()
    load_eu.start()

    barrier = pltpu.get_barrier_semaphore()
    for d in peers:
        pl.semaphore_signal(barrier, inc=1, device_id={'rows': d}, device_id_type=MESH_ID)
    pl.semaphore_signal(barrier, inc=1, device_id={'cols': 1 - k}, device_id_type=MESH_ID)
    pl.semaphore_wait(barrier, 4)

    halos = []
    for side, dev in ((0, prev), (1, nxt)):
        cp = pltpu.make_async_remote_copy(src_ref=pack_ref.at[side], dst_ref=halo.at[side], send_sem=halo_ss.at[side],
                                          recv_sem=halo_rs.at[side], device_id={'rows': dev}, device_id_type=MESH_ID)
        cp.start()
        halos.append(cp)

    def to_rows(pos, t0, t1):
        a = jnp.concatenate([t0, t1], axis=1)
        g = lax.dot_general(pm_ref[...], a, (((1,), (1,)), ((), ())), preferred_element_type=F32).astype(BF)
        for ch in range(SUB):
            s, c = ch // 4, ch % 4
            g_ref[RB * c + QTR * pos:RB * c + QTR * pos + QTR, N_GRID * s:N_GRID * (s + 1)] = g[QTR * ch:QTR * ch + QTR, :]

    for pos in range(3):
        l = ORDER[pos]
        to_rows(pos, tb_ref[2 * l], tb_ref[2 * l + 1])
    load_ev.wait()

    hms, hrs = (hm1, hm2), (hr1, hr2)
    copies = {}

    def columns(grp):
        start, n = GROUPS[grp]
        lane = lax.broadcasted_iota(jnp.int32, (n, LANES), 1)
        low = lane < HALF
        block = (lane & 63) >> 4
        rems = []
        for cp in range(2):
            hs = []
            for c in (2 * cp, 2 * cp + 1):
                h = jnp.dot(g_ref[RB * c + start:RB * c + start + n, :], ev_ref[...], preferred_element_type=F32)
                hs.append([h[:, LANES * i:LANES * (i + 1)] for i in range(4)])
                rems.append(h[:, 4 * LANES:])
            for i in range(4):
                dp, t = i // 2, i % 2
                odd = pltpu.roll(hs[1][i], HALF, axis=1)
                send_m[2 * dp, cp, t, start:start + n, :] = jnp.where(low, hs[0][i], odd).astype(BF)
                send_m[2 * dp + 1, cp, t, start:start + n, :] = jnp.where(low, odd, hs[0][i]).astype(BF)
            for x in (1, 2, 0):
                i = 3 * (2 * grp + cp) + x
                rc = pltpu.make_async_remote_copy(
                    src_ref=send_m.at[peers[x], cp, :, pl.ds(start, n), :], dst_ref=hms[grp].at[cp, :, r],
                    send_sem=main_ss.at[i], recv_sem=main_rs.at[i], device_id={'rows': peers[x]}, device_id_type=MESH_ID)
                rc.start()
                copies['m', grp, cp, x] = rc
            hms[grp][cp, :, r] = send_m[r, cp, :, start:start + n, :]
        for d in range(4):
            out = jnp.zeros((n, LANES), F32)
            for c in range(4):
                piece = rems[c] if c == d else pltpu.roll(rems[c], (WIN * (c - d)) % LANES, axis=1)
                out = jnp.where(block == c, piece, out)
            send_r[d, start:start + n, :] = out.astype(BF)
        for x in (1, 2, 0):
            i = 3 * grp + x
            rc = pltpu.make_async_remote_copy(
                src_ref=send_r.at[peers[x], pl.ds(start, n), :], dst_ref=hrs[grp].at[r],
                send_sem=rem_ss.at[i], recv_sem=rem_rs.at[i], device_id={'rows': peers[x]}, device_id_type=MESH_ID)
            rc.start()
            copies['r', grp, x] = rc
        hrs[grp][r] = send_r[r, start:start + n, :]

    columns(0)

    for h in halos:
        h.wait()
    lane = lax.broadcasted_iota(jnp.int32, (RB, LANES), 1)
    high = lane >= HALF
    slot = lane >> 5
    t0s, t9s = [], []
    for j in range(4):
        rows = slice(RB * j, RB * (j + 1))
        add_first = pltpu.roll(halo[1], (HALF - QTR * j) % LANES, axis=1)
        add_last = pltpu.roll(halo[0], (QTR - QTR * j) % LANES, axis=1)
        e = edge_ref[rows, :] + jnp.where(slot == 2, add_first, jnp.where(slot == 1, add_last, 0.0))
        t0s.append(jnp.where(high, e, tb_ref[0, rows, :].astype(F32)).astype(BF))
        t9s.append(jnp.where(high, tb_ref[9, rows, :].astype(F32), e).astype(BF))
    to_rows(3, jnp.concatenate(t0s, axis=0), tb_ref[1])
    to_rows(4, tb_ref[SUB], jnp.concatenate(t9s, axis=0))
    columns(1)

    lane = lax.broadcasted_iota(jnp.int32, (N_IMG, LANES), 1)
    pad = jnp.zeros((N_IMG, LANES - QB), F32)
    for s in range(2):
        wide = [jnp.concatenate([s_ref[s, c], pad], axis=1) for c in range(4)]
        for cp in range(2):
            first = jnp.where(core == 0, wide[2 * cp], wide[2 * cp + 1])
            second = jnp.where(core == 0, wide[2 * cp + 1], wide[2 * cp])
            s_main[s, cp] = jnp.where(lane < HALF, first, pltpu.roll(second, HALF, axis=1))
        out = jnp.zeros((N_IMG, LANES), F32)
        for c in range(4):
            out = jnp.where((lane >> 4) == c, pltpu.roll(wide[c], (WIN * c - HALF) % LANES, axis=1), out)
        s_rem[s] = out
    load_eu.wait()

    k0 = (0, 2 * ROWS * 96)

    def rows_main(grp):
        n = GROUPS[grp][1]
        for cp in range(2):
            for x in range(3):
                copies['m', grp, cp, x].wait_recv()
        kk = 2 * ROWS * n
        rhs = jnp.concatenate([hms[grp][cp].reshape(kk, LANES) for cp in range(2)], axis=1)
        res = jnp.dot(eu_ref[:, k0[grp]:k0[grp] + kk], rhs, preferred_element_type=F32)
        return res

    def rows_rem(grp):
        n = GROUPS[grp][1]
        for x in range(3):
            copies['r', grp, x].wait_recv()
        kk = ROWS * n
        rhs = hrs[grp][...].reshape(kk, LANES)
        return [jnp.dot(eu_ref[:, k0[grp] + kk * t:k0[grp] + kk * (t + 1)], rhs, preferred_element_type=F32) for t in range(2)]

    acc_m[...] = rows_main(0)
    for t, v in enumerate(rows_rem(0)):
        acc_r[t] = v
    acc_m[...] = acc_m[...] + rows_main(1)

    low = lax.broadcasted_iota(jnp.int32, (PB, LANES), 1) < HALF

    def combine_main(p0):
        rows = pl.ds(pl.multiple_of(p0, SUB), PB)
        rows_im = pl.ds(pl.multiple_of(N_IMG + p0, SUB), PB)
        re = jnp.zeros((PB, LANES), F32)
        im = jnp.zeros((PB, LANES), F32)
        for cp in range(2):
            cols = slice(LANES * cp, LANES * (cp + 1))
            i_re, i_im = acc_m[rows, cols], acc_m[rows_im, cols]
            s_re, s_im = s_main[0, cp, rows, :], s_main[1, cp, rows, :]
            re = re + (s_re * i_re + s_im * i_im)
            im = im + (s_re * i_im - s_im * i_re)
        return jnp.where(low, re + pltpu.roll(re, HALF, axis=1), im + pltpu.roll(im, HALF, axis=1))

    lane = lax.broadcasted_iota(jnp.int32, (PB, LANES), 1)
    slot40 = lax.broadcasted_iota(jnp.int32, (PB // 4, LANES), 1) >> 5

    def combine_rem(p0):
        rows = pl.ds(pl.multiple_of(p0, SUB), PB)
        rows_im = pl.ds(pl.multiple_of(N_IMG + p0, SUB), PB)
        i_re = acc_r[0, rows, :] + pltpu.roll(acc_r[1, rows, :], HALF, axis=1)
        i_im = acc_r[0, rows_im, :] + pltpu.roll(acc_r[1, rows_im, :], HALF, axis=1)
        s_re, s_im = s_rem[0, rows, :], s_rem[1, rows, :]
        re = jnp.where(low, s_re * i_re + s_im * i_im, 0.0)
        im = jnp.where(low, s_re * i_im - s_im * i_re, 0.0)
        w = re + pltpu.roll(im, HALF, axis=1)
        w = w + pltpu.roll(w, LANES - QTR, axis=1)
        w = w + pltpu.roll(w, LANES - WIN, axis=1)
        w = jnp.where(lane < WIN, w, pltpu.roll(w, LANES - 48, axis=1))
        out = jnp.zeros((PB // 4, LANES), F32)
        for j in range(4):
            piece = w[PB // 4 * j:PB // 4 * (j + 1), :]
            out = jnp.where(slot40 == j, pltpu.roll(piece, QTR * j, axis=1) if j else piece, out)
        return out

    far_p, own_p = PB - k * PB, k * PB

    def reduce_copy(src, dst, i):
        return pltpu.make_async_remote_copy(src_ref=src, dst_ref=dst, send_sem=red_ss.at[i], recv_sem=red_rs.at[i],
                                            device_id={'cols': 1 - k}, device_id_type=MESH_ID)

    img_m[...] = combine_main(far_p)
    red_main = reduce_copy(img_m, red_m, 0)
    red_main.start()
    for t, v in enumerate(rows_rem(1)):
        acc_r[t] = acc_r[t] + v
    img_r[...] = combine_rem(far_p)
    red_rem = reduce_copy(img_r, red_r, 1)
    red_rem.start()
    own_main = combine_main(own_p)
    own_rem = combine_rem(own_p)
    red_main.wait_recv()
    main = own_main + red_m[...]
    red_rem.wait_recv()
    rem = own_rem + red_r[...]
    for o in range(2):
        m = main if o == 0 else pltpu.roll(main, HALF, axis=1)
        for j in range(4):
            rows = slice(PB // 4 * j, PB // 4 * (j + 1))
            piece = pltpu.roll(rem, (HALF - QTR * j - WIN * o) % LANES, axis=1)
            full = jnp.where(low[rows], m[rows], piece)
            out_ref[o, rows, :] = full[:, :QB] * dd_ref[rows, :]

    red_main.wait_send()
    red_rem.wait_send()
    for key in copies:
        copies[key].wait_send()


def solution(mesh):
    sample_spec = ('exam', 'rows', 'cols')
    vm = pl.BlockSpec(memory_space=pltpu.VMEM)
    sm = pl.BlockSpec(memory_space=pltpu.SMEM)
    anyspec = pl.BlockSpec(memory_space=pl.ANY)
    spread_scratch = ([VMEM((NG * CW, LANES), F32)] * T + [VMEM((LANES, LANES), F32)] * 4 + [VMEM((LANES * PS, LANES), F32)] * 2
                      + [VMEM((LANES, 768), BF)])
    big = 60 * 1024 * 1024

    def local_fn(kspace, wts_y, wts_x, idx_y, idx_x, coil_maps, deapod):
        k = lax.axis_index('cols')
        r = lax.axis_index('rows')
        own, far, base = pl.pallas_call(
            prep_kernel,
            out_shape=(jax.ShapeDtypeStruct((24, NS), F32), jax.ShapeDtypeStruct((24, NS), F32), jax.ShapeDtypeStruct((NB, LANES), jnp.int32)),
            in_specs=[vm] * 5, out_specs=(vm, vm, vm), name='prep',
        )(kspace, wts_y, wts_x, idx_y.reshape(NB, LANES), idx_x.reshape(NB, LANES))
        swap = [(0, 1), (1, 0)]
        far_in = lax.ppermute(far, 'cols', swap)
        base_in = lax.ppermute(base, 'cols', swap)
        half = pl.pallas_call(
            own_kernel, out_shape=jax.ShapeDtypeStruct((11, CW, LANES), F32), in_specs=[sm, vm], out_specs=vm,
            scratch_shapes=spread_scratch, compiler_params=pltpu.CompilerParams(vmem_limit_bytes=big), name='spread_own',
            cost_estimate=pl.CostEstimate(flops=4 * 10 ** 9, bytes_accessed=2 * 10 ** 6, transcendentals=0),
        )(base, own)
        tb, edge, pack = pl.pallas_call(
            far_kernel,
            out_shape=(jax.ShapeDtypeStruct((10, N_GRID, LANES), BF), jax.ShapeDtypeStruct((N_GRID, LANES), F32), jax.ShapeDtypeStruct((2, RB, LANES), F32)),
            in_specs=[sm, vm, vm], out_specs=(vm, vm, vm), scratch_shapes=spread_scratch + [VMEM((N_GRID, LANES), F32)],
            compiler_params=pltpu.CompilerParams(vmem_limit_bytes=big), name='spread_far',
            cost_estimate=pl.CostEstimate(flops=4 * 10 ** 9, bytes_accessed=4 * 10 ** 6, transcendentals=0),
        )(base_in, far_in, half)
        dd = lax.dynamic_slice(deapod, (k * PB,), (PB,))[:, None] * lax.dynamic_slice(deapod, (r * QB,), (QB,))[None, :]
        dma = pltpu.SemaphoreType.DMA
        return pl.pallas_call(
            image_kernel,
            out_shape=jax.ShapeDtypeStruct((2, PB, QB), F32),
            in_specs=[vm] * 5 + [anyspec] * 2 + [vm], out_specs=vm,
            scratch_shapes=[
                VMEM((2 * N_GRID, N_GRID), BF), VMEM((2 * N_IMG, 2 * N_GRID), BF), VMEM((4 * RB, 2 * N_GRID), BF), VMEM((2, RB, LANES), F32),
                VMEM((4, 2, 2, RB, LANES), BF), VMEM((4, RB, LANES), BF),
                VMEM((2, 2, ROWS, 96, LANES), BF), VMEM((2, 2, ROWS, HALF, LANES), BF), VMEM((ROWS, 96, LANES), BF), VMEM((ROWS, HALF, LANES), BF),
                VMEM((2 * N_IMG, 2 * LANES), F32), VMEM((2, 2 * N_IMG, LANES), F32), VMEM((2, 2, N_IMG, LANES), F32), VMEM((2, N_IMG, LANES), F32),
                VMEM((PB, LANES), F32), VMEM((PB // 4, LANES), F32), VMEM((PB, LANES), F32), VMEM((PB // 4, LANES), F32),
                dma((2,)), dma((2,)), dma((2,)), dma((12,)), dma((12,)), dma((6,)), dma((6,)), dma((2,)), dma((2,)),
            ],
            compiler_params=pltpu.CompilerParams(vmem_limit_bytes=40 * 1024 * 1024, collective_id=0, has_side_effects=True), name='image',
        )(tb, edge, pack, coil_maps, dd, col_dft(), row_dft(), unmix())

    return jax.shard_map(
        local_fn,
        mesh=mesh,
        in_specs=(P(None, None, sample_spec), P(None, sample_spec), P(None, sample_spec), P(sample_spec), P(sample_spec), P(None, ('exam', 'cols'), None, 'rows'), P()),
        out_specs=P(None, ('exam', 'cols'), 'rows'),
        check_vma=False,
    )
```

time: 274 us -> 56.6 us (0.21)
  matrix products: 125 us -> 0 us
  waiting for transfers between devices: 50.1 us -> 0.01 us
  Pallas kernels: 0 us -> 45.4 us
  local copies, waits for them, and re-layouts: 52.4 us -> 7.34 us
  other arithmetic: 17.1 us -> 0.09 us
  between operations: 13.7 us -> 0.09 us
  starting transfers between devices: 13.1 us -> 3.39 us
    dot_general x18 -> x0, matrix products: 125 us -> none  [the longest x16 120 us: add_tile(): jnp.einsum('sclm,km->sclk', scaled, col_mat, precision=lax.Precision.HIGH...]
    pallas_call x0 -> x4, Pallas kernels: none -> 45.4 us  [the longest x1 19.8 us: local_fn(): pl.pallas_call(image_kernel, out_shape=jax.ShapeDtypeStruct((2, PB, QB),...]
    all_to_all x2 -> x0, waiting for transfers between devices: 35.2 us -> none  [the longest x1 18.4 us: local_fn(): lax.all_to_all(spread_buf.astype(jnp.bfloat16), 'cols', 1, 3, tiled=True)]
    broadcast_in_dim x16 -> x0, local copies, waits for them, and re-layouts: 11.5 us -> none  [tap_matrix(): jnp.where(tap_off[None] == tap_ids, weights[..., None, :], 0.0)]
    while x2 -> x0, local copies, waits for them, and re-layouts: 9.45 us -> none  [spread_block(): spread_buf, _ = lax.scan(add_tile, start_buf, tile_data)]
    unnamed x2 -> x0, waiting for transfers between devices: 8.67 us -> none
    all_to_all x4 -> x0, local copies, waits for them, and re-layouts: 7.76 us -> none  [the longest x2 5.92 us: local_fn(): lax.all_to_all(spread_buf.astype(jnp.bfloat16), 'cols', 1, 3, tiled=True)]
    all_to_all x2 -> x0, starting transfers between devices: 7.46 us -> none  [the longest x1 3.92 us: local_fn(): lax.all_to_all(spread_buf.astype(jnp.bfloat16), 'cols', 1, 3, tiled=True)]
  transfers between devices with their start and end apart: 7 -> 2, of which waited for: 5 -> 0; matrix products, arithmetic and copies ran while one was open for 8% -> 1% of each run, Pallas kernels for 0% -> 21%
where the time goes in v1:
time: 56.6 us; the launch traced here: 56.3 us
  Pallas kernels  45.4 us (80%)
  local copies, waits for them, and re-layouts  7.34 us (13%)
  starting transfers between devices  3.39 us (6%)
    pallas_call x1, Pallas kernels, local_fn(): pl.pallas_call(image_kernel, out_shape=jax.ShapeDtypeStruct((2, PB, QB),...  19.8 us
    pallas_call x1, Pallas kernels, local_fn(): pl.pallas_call(far_kernel, out_shape=(jax.ShapeDtypeStruct((10, N_GRID, L...  11.9 us
    pallas_call x1, Pallas kernels, local_fn(): pl.pallas_call(own_kernel, out_shape=jax.ShapeDtypeStruct((11, CW, LANES)...  11.6 us
    unnamed x22, local copies, waits for them, and re-layouts  7.19 us
    ppermute x1, starting transfers between devices, local_fn(): base_in = lax.ppermute(base, 'cols', swap)  3.37 us
    pallas_call x1, Pallas kernels, local_fn(): pl.pallas_call(prep_kernel, out_shape=(jax.ShapeDtypeStruct((24, NS), F32...  2.06 us
  transfers between devices with their start and end apart: 2, of which 0 were waited for; matrix products, arithmetic and copies ran while one was open for 1% of the time, Pallas kernels for 21%

profile of v1, /device:TPU:0, one launch (start us, length us, event | category | flops | bytes accessed | tf_op | source)
XLA Modules:
  0.0 56.3 jit_solution(7523571090929959458)
XLA Ops:
  0.0 2.1 %prep.1 = (f32[24,4096]{1,0:T(8,128)}, f32[24,4096]{1,0:T(8,128)}, s32[32,128]{1,0:T(8,128)}) custom-call(f32[2,8,4096]{2,1,0:T(8,128)} %ks_ref.1, f32[6,4096]{1,0:T(8,128)} %wy_ref.1, f32[6,4096]{1,0:T(8,128)} %wx_ref.1, s32[32,128]{1,0:T(8,128)} %bitcast.2, s32[32,128]{1,0:T(8,128)} %bitcast.3), custom_call_target="tpu_custom_call" | custom-call | tf_op jit(solution)/shard_map/prep/pallas_call | solution.py:462
  2.1 3.4 %collective-permute-start = (s32[32,128]{1,0:T(8,128)}, s32[32,128]{1,0:T(8,128)S(1)}, u32[]{:S(2)}, u32[]{:S(2)}) collective-permute-start(s32[32,128]{1,0:T(8,128)} %get-tuple-element.11.base_ref), channel_id=1, source_target_pairs={{0,4},{4,0},{1,5},{5,1},{2,6},{6,2},{3,7},{7,3}} | collective-permute-start | bytes 49160 | tf_op jit(solution)/shard_map/ppermute | solution.py:469
  5.4 0.0 collective-permute-start.1
  5.5 11.6 %spread_own.1.a_ref = f32[11,336,128]{2,1,0:T(8,128)} custom-call(s32[32,128]{1,0:T(8,128)} %get-tuple-element.11.base_ref, f32[24,4096]{1,0:T(8,128)} %get-tuple-element.13.pay_ref), custom_call_target="tpu_custom_call" | custom-call | flops 4000000000 | bytes 2000000 | tf_op jit(solution)/shard_map/spread_own/pallas_call | solution.py:470
  17.1 0.0 copy-done.7
  17.1 0.1 dynamic_slice.7
  17.2 0.1 dynamic_slice.6
  17.3 0.1 broadcast_multiply_fusion.dd_ref
  17.3 0.0 copy-done.6
  17.4 0.4 copy.11.s_ref
  17.8 0.0 copy-start
  17.8 0.0 copy-start.5
  17.8 0.0 collective-permute-done.base_ref
  17.8 0.0 collective-permute-done.1.pay_ref
  17.8 0.6 %copy-done.9 = s32[32,128]{1,0:T(8,128)} copy-done((s32[32,128]{1,0:T(8,128)}, s32[32,128]{1,0:T(8,128)S(1)}, u32[]{:S(2)}) %copy-start.9) | copy-done | bytes 16408
  18.4 0.8 %copy-done.8 = f32[24,4096]{1,0:T(8,128)} copy-done((f32[24,4096]{1,0:T(8,128)}, f32[24,4096]{1,0:T(8,128)S(1)}, u32[]{:S(2)}) %copy-start.8) | copy-done | bytes 393240
  19.2 11.9 %spread_far.1 = (bf16[10,640,128]{2,1,0:T(8,128)(2,1)}, f32[640,128]{1,0:T(8,128)}, f32[2,160,128]{2,1,0:T(8,128)}) custom-call(s32[32,128]{1,0:T(8,128)} %copy-done.9, f32[24,4096]{1,0:T(8,128)} %copy-done.8, f32[11,336,128]{2,1,0:T(8,128)} %spread_own.1.a_ref), custom_call_target="tpu_custom_call" | custom-call | flops 4000000000 | bytes 4000000 | tf_op jit(solution)/shard_map/spread_far/pallas_call | solution.py:475
  31.1 0.0 copy-done.5
  31.1 1.4 %copy-done.1 = bf16[640,1280]{1,0:T(8,128)(2,1)S(1)} copy-done((bf16[640,1280]{1,0:T(8,128)(2,1)S(1)}, bf16[640,1280]{1,0:T(8,128)(2,1)}, u32[]{:S(2)}) %copy-start.1) | copy-done | bytes 1638424
  32.5 1.4 %copy-done.2 = bf16[10,640,128]{2,1,0:T(8,128)(2,1)S(1)} copy-done((bf16[10,640,128]{2,1,0:T(8,128)(2,1)S(1)}, bf16[10,640,128]{2,1,0:T(8,128)(2,1)}, u32[]{:S(2)}) %copy-start.2) | copy-done | bytes 1638424
  34.0 1.0 %copy-done.3 = f32[640,128]{1,0:T(8,128)S(1)} copy-done((f32[640,128]{1,0:T(8,128)S(1)}, f32[640,128]{1,0:T(8,128)}, u32[]{:S(2)}) %copy-start.3) | copy-done | bytes 327704
  34.9 0.9 %copy-done.4 = f32[2,160,128]{2,1,0:T(8,128)S(1)} copy-done((f32[2,160,128]{2,1,0:T(8,128)S(1)}, f32[2,160,128]{2,1,0:T(8,128)}, u32[]{:S(2)}) %copy-start.4) | copy-done | bytes 163864
  35.8 19.8 %image.1 = f32[2,160,80]{2,1,0:T(8,128)S(1)} custom-call(bf16[10,640,128]{2,1,0:T(8,128)(2,1)S(1)} %copy-done.2, f32[640,128]{1,0:T(8,128)S(1)} %copy-done.3, f32[2,160,128]{2,1,0:T(8,128)S(1)} %copy-done.4, f32[2,4,320,80]{3,2,1,0:T(8,128)S(1)} %copy.11.s_ref, f32[160,80]{1,0:T(8,128)S(1)} %broadcast_multiply_fusion.dd_ref, bf16[1280,640]{1,0:T(8,128)(2,1)S(1)} %copy-done, ...), custom_call_target="tpu_custom_call" | custom-call | tf_op jit(solution)/shard_map/image/pallas_call | solution.py:484
  55.6 0.7 %copy.13 = f32[2,160,80]{2,1,0:T(8,128)} copy(f32[2,160,80]{2,1,0:T(8,128)S(1)} %image.1) | data formatting | bytes 204800
  (9 shorter events, 0.0 us)
Async XLA Ops:
  2.1 15.8 %collective-permute-start = (s32[32,128]{1,0:T(8,128)}, s32[32,128]{1,0:T(8,128)S(1)}, u32[]{:S(2)}, u32[]{:S(2)}) collective-permute-start(s32[32,128]{1,0:T(8,128)} %get-tuple-element.11.base_ref), channel_id=1, source_target_pairs={{0,4},{4,0},{1,5},{5,1},{2,6},{6,2},{3,7},{7,3}} | collective-permute-start | bytes 49160 | tf_op jit(solution)/shard_map/ppermute | solution.py:469
  5.4 12.4 %collective-permute-start.1 = (f32[24,4096]{1,0:T(8,128)}, f32[24,4096]{1,0:T(8,128)S(1)}, u32[]{:S(2)}, u32[]{:S(2)}) collective-permute-start(f32[24,4096]{1,0:T(8,128)} %get-tuple-element.12), channel_id=1, source_target_pairs={{0,4},{4,0},{1,5},{5,1},{2,6},{6,2},{3,7},{7,3}} | collective-permute-start | bytes 1179656 | tf_op jit(solution)/shard_map/ppermute | solution.py:468
  5.5 11.6 %copy-start.7 = (f32[320]{0:T(512)S(1)}, f32[320]{0:T(512)}, u32[]{:S(2)}) copy-start(f32[320]{0:T(512)} %param.16) | copy-start | bytes 3844
  5.5 11.9 %copy-start.6 = (f32[2,4,320,80]{2,3,1,0:T(8,128)S(1)}, f32[2,4,320,80]{2,3,1,0:T(8,128)}, u32[]{:S(2)}) copy-start(f32[2,4,320,80]{2,3,1,0:T(8,128)} %param.15) | copy-start | bytes 2457604
  17.8 13.3 %copy-start = (bf16[1280,640]{1,0:T(8,128)(2,1)S(1)}, bf16[1280,640]{1,0:T(8,128)(2,1)}, u32[]{:S(2)}) copy-start(bf16[1280,640]{1,0:T(8,128)(2,1)} %constant.23.clone.ev_hbm) | copy-start | bytes 4915204
  17.8 13.3 %copy-start.5 = (bf16[256,256]{1,0:T(8,128)(2,1)S(1)}, bf16[256,256]{1,0:T(8,128)(2,1)}, u32[]{:S(2)}) copy-start(bf16[256,256]{1,0:T(8,128)(2,1)} %constant.25.clone.pm_ref) | copy-start | bytes 393220
  17.8 0.6 %copy-start.9 = (s32[32,128]{1,0:T(8,128)}, s32[32,128]{1,0:T(8,128)S(1)}, u32[]{:S(2)}) copy-start(s32[32,128]{1,0:T(8,128)S(1)} %collective-permute-done.base_ref) | copy-start | bytes 49156
  18.4 0.8 %copy-start.8 = (f32[24,4096]{1,0:T(8,128)}, f32[24,4096]{1,0:T(8,128)S(1)}, u32[]{:S(2)}) copy-start(f32[24,4096]{1,0:T(8,128)S(1)} %collective-permute-done.1.pay_ref) | copy-start | bytes 1179652
  31.1 1.4 %copy-start.1 = (bf16[640,1280]{1,0:T(8,128)(2,1)S(1)}, bf16[640,1280]{1,0:T(8,128)(2,1)}, u32[]{:S(2)}) copy-start(bf16[640,1280]{1,0:T(8,128)(2,1)} %constant.24.clone.eu_hbm) | copy-start | bytes 4915204
  32.5 1.4 %copy-start.2 = (bf16[10,640,128]{2,1,0:T(8,128)(2,1)S(1)}, bf16[10,640,128]{2,1,0:T(8,128)(2,1)}, u32[]{:S(2)}) copy-start(bf16[10,640,128]{2,1,0:T(8,128)(2,1)} %get-tuple-element.14.tb_ref) | copy-start | bytes 4915204
  34.0 1.0 %copy-start.3 = (f32[640,128]{1,0:T(8,128)S(1)}, f32[640,128]{1,0:T(8,128)}, u32[]{:S(2)}) copy-start(f32[640,128]{1,0:T(8,128)} %get-tuple-element.15.edge_ref) | copy-start | bytes 983044
  34.9 0.9 %copy-start.4 = (f32[2,160,128]{2,1,0:T(8,128)S(1)}, f32[2,160,128]{2,1,0:T(8,128)}, u32[]{:S(2)}) copy-start(f32[2,160,128]{2,1,0:T(8,128)} %get-tuple-element.16.pack_ref) | copy-start | bytes 491524

commit v2 on v1

--- a/solution.py
+++ b/solution.py
@@ -75,22 +75,32 @@
     return jnp.asarray(m, BF)
 
 
-def prep_kernel(ks_ref, wy_ref, wx_ref, iy_ref, ix_ref, own_ref, far_ref, base_ref):
+def prep_kernel(ks_hbm, wy_hbm, wx_hbm, iy_hbm, ix_hbm, own_ref, far_ref, base_ref, ks_ref, wy_ref, wx_ref, iy_ref, ix_ref, sem):
     k = lax.axis_index('cols')
     r = lax.axis_index('rows')
+    loads = []
+    for src, dst in ((iy_hbm, iy_ref), (ix_hbm, ix_ref), (wx_hbm, wx_ref), (wy_hbm, wy_ref), (ks_hbm, ks_ref)):
+        cp = pltpu.make_async_copy(src, dst, sem.at[len(loads)])
+        cp.start()
+        loads.append(cp)
+    loads[0].wait()
+    loads[1].wait()
     iy = iy_ref[...]
     base_ref[...] = ((iy - r * RB + 5) >> 3) * CW + (ix_ref[...] - k * CB + 5)
     sh = ((iy + 5) & 15).astype(F32)
-    lo = jnp.concatenate([ks_ref[0, 0:4, :], ks_ref[1, 0:4, :]], axis=0)
-    hi = jnp.concatenate([ks_ref[0, 4:SUB, :], ks_ref[1, 4:SUB, :]], axis=0)
-    own_ref[0:SUB, :] = jnp.where(k == 0, lo, hi)
-    far_ref[0:SUB, :] = jnp.where(k == 0, hi, lo)
+    loads[2].wait()
+    loads[3].wait()
     zero2 = jnp.zeros((2, NS), F32)
     for ref in (own_ref, far_ref):
         ref[SUB:WIN, :] = jnp.concatenate([wx_ref[...], zero2], axis=0)
         ref[WIN:24, :] = jnp.concatenate([wy_ref[...], zero2], axis=0)
         for b in range(NB):
             ref[22:23, LANES * b:LANES * (b + 1)] = sh[b:b + 1, :]
+    loads[4].wait()
+    lo = jnp.concatenate([ks_ref[0, 0:4, :], ks_ref[1, 0:4, :]], axis=0)
+    hi = jnp.concatenate([ks_ref[0, 4:SUB, :], ks_ref[1, 4:SUB, :]], axis=0)
+    own_ref[0:SUB, :] = jnp.where(k == 0, lo, hi)
+    far_ref[0:SUB, :] = jnp.where(k == 0, hi, lo)
 
 
 def split3(x):
@@ -237,19 +247,15 @@
         pack_ref[side] = out
 
 
-def image_kernel(tb_ref, edge_ref, pack_ref, s_ref, dd_ref, ev_hbm, eu_hbm, pm_ref, out_ref,
-                 ev_ref, eu_ref, g_ref, halo, send_m, send_r, hm1, hm2, hr1, hr2, acc_m, acc_r, s_main, s_rem,
+def image_kernel(tb_ref, edge_ref, pack_ref, s_ref, d_ref, ev_ref, eu_ref, pm_ref, out_ref,
+                 g_ref, halo, send_m, send_r, hm1, hm2, hr1, hr2, acc_m, acc_r, s_main, s_rem,
                  img_m, img_r, red_m, red_r,
-                 load_sem, halo_ss, halo_rs, main_ss, main_rs, rem_ss, rem_rs, red_ss, red_rs):
+                 halo_ss, halo_rs, main_ss, main_rs, rem_ss, rem_rs, red_ss, red_rs):
     k = lax.axis_index('cols')
     r = lax.axis_index('rows')
     core = r % 2
     peers = (r + 1 - 2 * core, (r + 2) % 4, 3 - r)
     prev, nxt = (r + 3) % 4, (r + 1) % 4
-    load_ev = pltpu.make_async_copy(ev_hbm, ev_ref, load_sem.at[0])
-    load_eu = pltpu.make_async_copy(eu_hbm, eu_ref, load_sem.at[1])
-    load_ev.start()
-    load_eu.start()
 
     barrier = pltpu.get_barrier_semaphore()
     for d in peers:
@@ -274,7 +280,6 @@
     for pos in range(3):
         l = ORDER[pos]
         to_rows(pos, tb_ref[2 * l], tb_ref[2 * l + 1])
-    load_ev.wait()
 
     hms, hrs = (hm1, hm2), (hr1, hr2)
     copies = {}
@@ -339,9 +344,9 @@
     columns(1)
 
     lane = lax.broadcasted_iota(jnp.int32, (N_IMG, LANES), 1)
-    pad = jnp.zeros((N_IMG, LANES - QB), F32)
+    pad = jnp.zeros((LANES - QB, N_IMG), F32)
     for s in range(2):
-        wide = [jnp.concatenate([s_ref[s, c], pad], axis=1) for c in range(4)]
+        wide = [jnp.concatenate([s_ref[s, c], pad], axis=0).T for c in range(4)]
         for cp in range(2):
             first = jnp.where(core == 0, wide[2 * cp], wide[2 * cp + 1])
             second = jnp.where(core == 0, wide[2 * cp + 1], wide[2 * cp])
@@ -350,7 +355,12 @@
         for c in range(4):
             out = jnp.where((lane >> 4) == c, pltpu.roll(wide[c], (WIN * c - HALF) % LANES, axis=1), out)
         s_rem[s] = out
-    load_eu.wait()
+    d8 = jnp.broadcast_to(jnp.concatenate([d_ref[...], jnp.zeros((1, HALF), F32)], axis=1), (SUB, N_IMG + HALF))
+    dq = d8
+    for j in range(1, ROWS):
+        dq = jnp.where(r == j, pltpu.roll(d8, N_IMG + HALF - QB * j, axis=1), dq)
+    dp = jnp.where(k == 0, d8, pltpu.roll(d8, N_IMG + HALF - PB, axis=1))[:, :2 * LANES]
+    dd = jnp.concatenate([dp] * WIN, axis=0).T[:PB] * dq[:1, :LANES]
 
     k0 = (0, 2 * ROWS * 96)
 
@@ -439,7 +449,7 @@
             rows = slice(PB // 4 * j, PB // 4 * (j + 1))
             piece = pltpu.roll(rem, (HALF - QTR * j - WIN * o) % LANES, axis=1)
             full = jnp.where(low[rows], m[rows], piece)
-            out_ref[o, rows, :] = full[:, :QB] * dd_ref[rows, :]
+            out_ref[o, rows, :] = (full * dd[rows])[:, :QB]
 
     red_main.wait_send()
     red_rem.wait_send()
@@ -451,18 +461,18 @@
     sample_spec = ('exam', 'rows', 'cols')
     vm = pl.BlockSpec(memory_space=pltpu.VMEM)
     sm = pl.BlockSpec(memory_space=pltpu.SMEM)
-    anyspec = pl.BlockSpec(memory_space=pl.ANY)
+    hbm = pl.BlockSpec(memory_space=pltpu.HBM)
     spread_scratch = ([VMEM((NG * CW, LANES), F32)] * T + [VMEM((LANES, LANES), F32)] * 4 + [VMEM((LANES * PS, LANES), F32)] * 2
                       + [VMEM((LANES, 768), BF)])
-    big = 60 * 1024 * 1024
+    big = 28 * 1024 * 1024
 
     def local_fn(kspace, wts_y, wts_x, idx_y, idx_x, coil_maps, deapod):
-        k = lax.axis_index('cols')
-        r = lax.axis_index('rows')
         own, far, base = pl.pallas_call(
             prep_kernel,
             out_shape=(jax.ShapeDtypeStruct((24, NS), F32), jax.ShapeDtypeStruct((24, NS), F32), jax.ShapeDtypeStruct((NB, LANES), jnp.int32)),
-            in_specs=[vm] * 5, out_specs=(vm, vm, vm), name='prep',
+            in_specs=[hbm] * 5, out_specs=(vm, vm, vm), name='prep',
+            scratch_shapes=[VMEM((2, SUB, NS), F32), VMEM((KW, NS), F32), VMEM((KW, NS), F32), VMEM((NB, LANES), jnp.int32), VMEM((NB, LANES), jnp.int32), pltpu.SemaphoreType.DMA((5,))],
+            compiler_params=pltpu.CompilerParams(vmem_limit_bytes=SUB * 1024 * 1024),
         )(kspace, wts_y, wts_x, idx_y.reshape(NB, LANES), idx_x.reshape(NB, LANES))
         swap = [(0, 1), (1, 0)]
         far_in = lax.ppermute(far, 'cols', swap)
@@ -479,22 +489,21 @@
             compiler_params=pltpu.CompilerParams(vmem_limit_bytes=big), name='spread_far',
             cost_estimate=pl.CostEstimate(flops=4 * 10 ** 9, bytes_accessed=4 * 10 ** 6, transcendentals=0),
         )(base_in, far_in, half)
-        dd = lax.dynamic_slice(deapod, (k * PB,), (PB,))[:, None] * lax.dynamic_slice(deapod, (r * QB,), (QB,))[None, :]
         dma = pltpu.SemaphoreType.DMA
         return pl.pallas_call(
             image_kernel,
             out_shape=jax.ShapeDtypeStruct((2, PB, QB), F32),
-            in_specs=[vm] * 5 + [anyspec] * 2 + [vm], out_specs=vm,
+            in_specs=[vm] * 8, out_specs=vm,
             scratch_shapes=[
-                VMEM((2 * N_GRID, N_GRID), BF), VMEM((2 * N_IMG, 2 * N_GRID), BF), VMEM((4 * RB, 2 * N_GRID), BF), VMEM((2, RB, LANES), F32),
+                VMEM((4 * RB, 2 * N_GRID), BF), VMEM((2, RB, LANES), F32),
                 VMEM((4, 2, 2, RB, LANES), BF), VMEM((4, RB, LANES), BF),
                 VMEM((2, 2, ROWS, 96, LANES), BF), VMEM((2, 2, ROWS, HALF, LANES), BF), VMEM((ROWS, 96, LANES), BF), VMEM((ROWS, HALF, LANES), BF),
                 VMEM((2 * N_IMG, 2 * LANES), F32), VMEM((2, 2 * N_IMG, LANES), F32), VMEM((2, 2, N_IMG, LANES), F32), VMEM((2, N_IMG, LANES), F32),
                 VMEM((PB, LANES), F32), VMEM((PB // 4, LANES), F32), VMEM((PB, LANES), F32), VMEM((PB // 4, LANES), F32),
-                dma((2,)), dma((2,)), dma((2,)), dma((12,)), dma((12,)), dma((6,)), dma((6,)), dma((2,)), dma((2,)),
+                dma((2,)), dma((2,)), dma((12,)), dma((12,)), dma((6,)), dma((6,)), dma((2,)), dma((2,)),
             ],
-            compiler_params=pltpu.CompilerParams(vmem_limit_bytes=40 * 1024 * 1024, collective_id=0, has_side_effects=True), name='image',
-        )(tb, edge, pack, coil_maps, dd, col_dft(), row_dft(), unmix())
+            compiler_params=pltpu.CompilerParams(vmem_limit_bytes=20 * 1024 * 1024, collective_id=0, has_side_effects=True), name='image',
+        )(tb, edge, pack, jnp.swapaxes(coil_maps, 2, 3), deapod.reshape(1, N_IMG), col_dft(), row_dft(), unmix())
 
     return jax.shard_map(
         local_fn,

time: 56.6 us -> 48.4 us (0.86)
  Pallas kernels: 45.4 us -> 39.7 us
  local copies, waits for them, and re-layouts: 7.34 us -> 4.89 us
    ppermute x1, starting transfers between devices: 0.02 us -> 3.39 us  [local_fn(): far_in = lax.ppermute(far, 'cols', swap)]
    ppermute x1, starting transfers between devices: 3.37 us -> 0.03 us  [local_fn(): base_in = lax.ppermute(base, 'cols', swap)]
    unnamed x22 -> x21, local copies, waits for them, and re-layouts: 7.19 us -> 4.89 us
    pallas_call x1, Pallas kernels: 11.9 us -> 9.8 us  [local_fn(): pl.pallas_call(far_kernel, out_shape=(jax.ShapeDtypeStruct((10, N_GRID, L...]
    pallas_call x1, Pallas kernels: 11.6 us -> 10.1 us  [local_fn(): pl.pallas_call(own_kernel, out_shape=jax.ShapeDtypeStruct((11, CW, LANES)...]
    pallas_call x1, Pallas kernels: 2.06 us -> 0.52 us  [local_fn(): pl.pallas_call(prep_kernel, out_shape=(jax.ShapeDtypeStruct((24, NS), F32...]
  transfers between devices with their start and end apart: 2 -> 2, of which waited for: 0 -> 0; matrix products, arithmetic and copies ran while one was open for 1% -> 0% of each run, Pallas kernels for 21% -> 21%
where the time goes in v2:
time: 48.4 us; the launch traced here: 48.2 us
  Pallas kernels  39.7 us (82%)
  local copies, waits for them, and re-layouts  4.89 us (10%)
  starting transfers between devices  3.42 us (7%)
    pallas_call x1, Pallas kernels, local_fn(): pl.pallas_call(image_kernel, out_shape=jax.ShapeDtypeStruct((2, PB, QB),...  19.3 us
    pallas_call x1, Pallas kernels, local_fn(): pl.pallas_call(own_kernel, out_shape=jax.ShapeDtypeStruct((11, CW, LANES)...  10.1 us
    pallas_call x1, Pallas kernels, local_fn(): pl.pallas_call(far_kernel, out_shape=(jax.ShapeDtypeStruct((10, N_GRID, L...  9.8 us
    unnamed x21, local copies, waits for them, and re-layouts  4.89 us
    ppermute x1, starting transfers between devices, local_fn(): far_in = lax.ppermute(far, 'cols', swap)  3.39 us
  transfers between devices with their start and end apart: 2, of which 0 were waited for; matrix products, arithmetic and copies ran while one was open for 0% of the time, Pallas kernels for 21%

profile of v2, /device:TPU:0, one launch (start us, length us, event | category | flops | bytes accessed | tf_op | source)
XLA Modules:
  0.0 48.2 jit_solution(11683240912658578448)
XLA Ops:
  0.0 0.0 copy-start.3
  0.0 0.9 %copy-done.3 = f32[2,8,4096]{2,1,0:T(8,128)S(1)} copy-done((f32[2,8,4096]{2,1,0:T(8,128)S(1)}, f32[2,8,4096]{2,1,0:T(8,128)}, u32[]{:S(2)}) %copy-start.3) | copy-done | bytes 262168
  1.0 0.9 %copy-done.4 = f32[6,4096]{1,0:T(8,128)S(1)} copy-done((f32[6,4096]{1,0:T(8,128)S(1)}, f32[6,4096]{1,0:T(8,128)}, u32[]{:S(2)}) %copy-start.4) | copy-done | bytes 98328
  1.9 0.9 %copy-done.5 = f32[6,4096]{1,0:T(8,128)S(1)} copy-done((f32[6,4096]{1,0:T(8,128)S(1)}, f32[6,4096]{1,0:T(8,128)}, u32[]{:S(2)}) %copy-start.5) | copy-done | bytes 98328
  2.8 0.7 %copy-done.7 = s32[4096]{0:T(1024)S(1)} copy-done((s32[4096]{0:T(1024)S(1)}, s32[4096]{0:T(1024)}, u32[]{:S(2)}) %copy-start.7) | copy-done | bytes 16408
  3.5 0.7 %copy-done.8 = s32[4096]{0:T(1024)S(1)} copy-done((s32[4096]{0:T(1024)S(1)}, s32[4096]{0:T(1024)}, u32[]{:S(2)}) %copy-start.8) | copy-done | bytes 16408
  4.2 0.5 %prep.1 = (f32[24,4096]{1,0:T(8,128)S(1)}, f32[24,4096]{1,0:T(8,128)S(1)}, s32[32,128]{1,0:T(8,128)S(1)}) custom-call(f32[2,8,4096]{2,1,0:T(8,128)S(1)} %copy-done.3, f32[6,4096]{1,0:T(8,128)S(1)} %copy-done.4, f32[6,4096]{1,0:T(8,128)S(1)} %copy-done.5, s32[32,128]{1,0:T(8,128)S(1)} %bitcast.4, s32[32,128]{1,0:T(8,128)S(1)} %bitcast.5), custom_call_target="tpu_custom_call" | custom-call | tf_op jit(solution)/shard_map/prep/pallas_call | solution.py:470
  4.7 3.4 %collective-permute-start.1 = (f32[24,4096]{1,0:T(8,128)S(1)}, f32[24,4096]{1,0:T(8,128)S(1)}, u32[]{:S(2)}, u32[]{:S(2)}) collective-permute-start(f32[24,4096]{1,0:T(8,128)S(1)} %get-tuple-element.12), channel_id=1, source_target_pairs={{0,4},{4,0},{1,5},{5,1},{2,6},{6,2},{3,7},{7,3}} | collective-permute-start | bytes 1179656 | tf_op jit(solution)/shard_map/ppermute | solution.py:478
  8.1 0.0 collective-permute-start
  8.1 10.1 %spread_own.1.a_ref = f32[11,336,128]{2,1,0:T(8,128)S(1)} custom-call(s32[32,128]{1,0:T(8,128)S(1)} %get-tuple-element.11.base_ref, f32[24,4096]{1,0:T(8,128)S(1)} %get-tuple-element.13.pay_ref), custom_call_target="tpu_custom_call" | custom-call | flops 4000000000 | bytes 2000000 | tf_op jit(solution)/shard_map/spread_own/pallas_call | solution.py:480
  18.2 0.0 copy-done.9
  18.2 0.0 copy-start
  18.3 0.0 copy-start.1
  18.3 0.0 copy-start.2
  18.3 0.0 copy-start.6
  18.3 0.0 collective-permute-done.base_ref
  18.3 0.0 collective-permute-done.1.pay_ref
  18.3 9.8 %spread_far.1 = (bf16[10,640,128]{2,1,0:T(8,128)(2,1)S(1)}, f32[640,128]{1,0:T(8,128)S(1)}, f32[2,160,128]{2,1,0:T(8,128)S(1)}) custom-call(s32[32,128]{1,0:T(8,128)S(1)} %collective-permute-done.base_ref, f32[24,4096]{1,0:T(8,128)S(1)} %collective-permute-done.1.pay_ref, f32[11,336,128]{2,1,0:T(8,128)S(1)} %spread_own.1.a_ref), custom_call_target="tpu_custom_call" | custom-call | flops 4000000000 | bytes 4000000 | tf_op jit(solution)/shard_map/spread_far/pallas_call | solution.py:485
  28.1 0.0 copy-done
  28.1 0.0 copy-done.1
  28.1 0.0 copy-done.2
  28.2 0.0 copy-done.6
  28.2 19.3 %image.1 = f32[2,160,80]{2,1,0:T(8,128)S(1)} custom-call(bf16[10,640,128]{2,1,0:T(8,128)(2,1)S(1)} %get-tuple-element.14.tb_ref, f32[640,128]{1,0:T(8,128)S(1)} %get-tuple-element.15.edge_ref, f32[2,160,128]{2,1,0:T(8,128)S(1)} %get-tuple-element.16.pack_ref, f32[2,4,80,320]{3,2,1,0:T(8,128)S(1)} %bitcast.3, f32[1,320]{1,0:T(1,128)S(1)} %reshape.11.d_ref, ...), custom_call_target="tpu_custom_call" | custom-call | tf_op jit(solution)/shard_map/image/pallas_call | solution.py:493
  47.5 0.7 %copy.12 = f32[2,160,80]{2,1,0:T(8,128)} copy(f32[2,160,80]{2,1,0:T(8,128)S(1)} %image.1) | data formatting | bytes 204800
  (6 shorter events, 0.0 us)
Async XLA Ops:
  0.0 0.9 %copy-start.3 = (f32[2,8,4096]{2,1,0:T(8,128)S(1)}, f32[2,8,4096]{2,1,0:T(8,128)}, u32[]{:S(2)}) copy-start(f32[2,8,4096]{2,1,0:T(8,128)} %ks_hbm.1) | copy-start | bytes 786436
  1.0 0.9 %copy-start.4 = (f32[6,4096]{1,0:T(8,128)S(1)}, f32[6,4096]{1,0:T(8,128)}, u32[]{:S(2)}) copy-start(f32[6,4096]{1,0:T(8,128)} %wy_hbm.1) | copy-start | bytes 294916
  1.9 0.9 %copy-start.5 = (f32[6,4096]{1,0:T(8,128)S(1)}, f32[6,4096]{1,0:T(8,128)}, u32[]{:S(2)}) copy-start(f32[6,4096]{1,0:T(8,128)} %wx_hbm.1) | copy-start | bytes 294916
  2.8 0.7 %copy-start.7 = (s32[4096]{0:T(1024)S(1)}, s32[4096]{0:T(1024)}, u32[]{:S(2)}) copy-start(s32[4096]{0:T(1024)} %param.13) | copy-start | bytes 49156
  3.5 0.7 %copy-start.8 = (s32[4096]{0:T(1024)S(1)}, s32[4096]{0:T(1024)}, u32[]{:S(2)}) copy-start(s32[4096]{0:T(1024)} %param.14) | copy-start | bytes 49156
  4.7 13.6 %collective-permute-start.1 = (f32[24,4096]{1,0:T(8,128)S(1)}, f32[24,4096]{1,0:T(8,128)S(1)}, u32[]{:S(2)}, u32[]{:S(2)}) collective-permute-start(f32[24,4096]{1,0:T(8,128)S(1)} %get-tuple-element.12), channel_id=1, source_target_pairs={{0,4},{4,0},{1,5},{5,1},{2,6},{6,2},{3,7},{7,3}} | collective-permute-start | bytes 1179656 | tf_op jit(solution)/shard_map/ppermute | solution.py:478
  8.1 10.2 %collective-permute-start = (s32[32,128]{1,0:T(8,128)S(1)}, s32[32,128]{1,0:T(8,128)S(1)}, u32[]{:S(2)}, u32[]{:S(2)}) collective-permute-start(s32[32,128]{1,0:T(8,128)S(1)} %get-tuple-element.11.base_ref), channel_id=1, source_target_pairs={{0,4},{4,0},{1,5},{5,1},{2,6},{6,2},{3,7},{7,3}} | collective-permute-start | bytes 49160 | tf_op jit(solution)/shard_map/ppermute | solution.py:479
  8.1 10.1 %copy-start.9 = (f32[320]{0:T(512)S(1)}, f32[320]{0:T(512)}, u32[]{:S(2)}) copy-start(f32[320]{0:T(512)} %param.16) | copy-start | bytes 3844
  18.2 9.9 %copy-start = (bf16[1280,640]{1,0:T(8,128)(2,1)S(1)}, bf16[1280,640]{1,0:T(8,128)(2,1)}, u32[]{:S(2)}) copy-start(bf16[1280,640]{1,0:T(8,128)(2,1)} %constant.6.clone.ev_ref) | copy-start | bytes 4915204
  18.3 9.9 %copy-start.1 = (bf16[640,1280]{1,0:T(8,128)(2,1)S(1)}, bf16[640,1280]{1,0:T(8,128)(2,1)}, u32[]{:S(2)}) copy-start(bf16[640,1280]{1,0:T(8,128)(2,1)} %constant.7.clone.eu_ref) | copy-start | bytes 4915204
  18.3 9.9 %copy-start.2 = (f32[2,4,320,80]{2,3,1,0:T(8,128)S(1)}, f32[2,4,320,80]{2,3,1,0:T(8,128)}, u32[]{:S(2)}) copy-start(f32[2,4,320,80]{2,3,1,0:T(8,128)} %param.15) | copy-start | bytes 2457604
  18.3 9.9 %copy-start.6 = (bf16[256,256]{1,0:T(8,128)(2,1)S(1)}, bf16[256,256]{1,0:T(8,128)(2,1)}, u32[]{:S(2)}) copy-start(bf16[256,256]{1,0:T(8,128)(2,1)} %constant.8.clone.pm_ref) | copy-start | bytes 393220

commit v3 on v2

--- a/solution.py
+++ b/solution.py
@@ -49,21 +49,24 @@
                 out[:, l0:l0 + HALF] = e[:, :, t, q0:q0 + HALF].reshape(2 * N_GRID, HALF)
     for t in range(2):
         for d in range(4):
-            l0 = 4 * LANES + HALF * t + WIN * d
-            out[:, l0:l0 + WIN] = e[:, :, t, QB * d + HALF:QB * d + 80].reshape(2 * N_GRID, WIN)
+            l0 = 4 * LANES + HALF * (d // 2) + WIN * (2 * t + d % 2)
+            out[:, l0:l0 + WIN] = e[:, :, t, QB * d + HALF:QB * (d + 1)].reshape(2 * N_GRID, WIN)
     return jnp.asarray(out, BF)
 
 
 def row_dft():
     e = dft_parts()
-    rows = np.concatenate([np.arange(QTR * l, QTR * l + QTR) for l in ORDER])
-    parts = []
-    for start, n in GROUPS:
-        for t in range(2):
-            for b in range(ROWS):
-                u = b * RB + rows[start:start + n]
-                parts.append(e[t, u].reshape(n, 2 * N_IMG))
-    return jnp.asarray(np.concatenate(parts, 0).T, BF)
+    rows = np.concatenate([np.arange(QTR * l, QTR * (l + 1)) for l in ORDER])
+    chips = []
+    for x in range(2):
+        parts = []
+        for start, n in GROUPS:
+            for t in range(2):
+                for b in range(2):
+                    parts.append(e[t, (2 * x + b) * RB + rows[start:start + n]])
+        m = np.concatenate(parts, 0)
+        chips.append([m[:, :, PB * h:PB * (h + 1)].reshape(N_GRID, N_IMG).T for h in range(2)])
+    return jnp.asarray(np.array(chips), BF)
 
 
 def unmix():
@@ -247,48 +250,49 @@
         pack_ref[side] = out
 
 
-def image_kernel(tb_ref, edge_ref, pack_ref, s_ref, d_ref, ev_ref, eu_ref, pm_ref, out_ref,
-                 g_ref, halo, send_m, send_r, hm1, hm2, hr1, hr2, acc_m, acc_r, s_main, s_rem,
-                 img_m, img_r, red_m, red_r,
-                 halo_ss, halo_rs, main_ss, main_rs, rem_ss, rem_rs, red_ss, red_rs):
+def image_kernel(tb_ref, edge_ref, pack_ref, so_ref, sx_ref, d_ref, ev_ref, eu_ref, pm_ref, out_ref,
+                 g_ref, halo, sm1, sm2, sr1, sr2, hm1, hm2, hr1, hr2, s_main, s_rem, pieces, recvs,
+                 halo_ss, halo_rs, swap_ss, swap_rs, red_ss, red_rs):
     k = lax.axis_index('cols')
     r = lax.axis_index('rows')
-    core = r % 2
-    peers = (r + 1 - 2 * core, (r + 2) % 4, 3 - r)
+    core, x = r % 2, r // 2
+    near = r + 1 - 2 * core
+    across = (r + 2) % 4
     prev, nxt = (r + 3) % 4, (r + 1) % 4
+    homes = ({'rows': across, 'cols': 1 - k}, {'cols': 1 - k}, {'rows': across})
 
     barrier = pltpu.get_barrier_semaphore()
-    for d in peers:
-        pl.semaphore_signal(barrier, inc=1, device_id={'rows': d}, device_id_type=MESH_ID)
-    pl.semaphore_signal(barrier, inc=1, device_id={'cols': 1 - k}, device_id_type=MESH_ID)
-    pl.semaphore_wait(barrier, 4)
-
-    halos = []
-    for side, dev in ((0, prev), (1, nxt)):
-        cp = pltpu.make_async_remote_copy(src_ref=pack_ref.at[side], dst_ref=halo.at[side], send_sem=halo_ss.at[side],
-                                          recv_sem=halo_rs.at[side], device_id={'rows': dev}, device_id_type=MESH_ID)
+    for dev in ({'rows': prev}, {'rows': nxt}) + homes:
+        pl.semaphore_signal(barrier, inc=1, device_id=dev, device_id_type=MESH_ID)
+    pl.semaphore_wait(barrier, 5)
+
+    def remote(src, dst, ss, rs, i, dev):
+        cp = pltpu.make_async_remote_copy(src_ref=src, dst_ref=dst, send_sem=ss.at[i], recv_sem=rs.at[i], device_id=dev, device_id_type=MESH_ID)
         cp.start()
-        halos.append(cp)
+        return cp
+
+    halos = [remote(pack_ref.at[i], halo.at[i], halo_ss, halo_rs, i, {'rows': dev}) for i, dev in ((0, prev), (1, nxt))]
 
     def to_rows(pos, t0, t1):
         a = jnp.concatenate([t0, t1], axis=1)
         g = lax.dot_general(pm_ref[...], a, (((1,), (1,)), ((), ())), preferred_element_type=F32).astype(BF)
         for ch in range(SUB):
             s, c = ch // 4, ch % 4
-            g_ref[RB * c + QTR * pos:RB * c + QTR * pos + QTR, N_GRID * s:N_GRID * (s + 1)] = g[QTR * ch:QTR * ch + QTR, :]
+            g_ref[RB * c + QTR * pos:RB * c + QTR * (pos + 1), N_GRID * s:N_GRID * (s + 1)] = g[QTR * ch:QTR * (ch + 1), :]
 
     for pos in range(3):
         l = ORDER[pos]
         to_rows(pos, tb_ref[2 * l], tb_ref[2 * l + 1])
 
-    hms, hrs = (hm1, hm2), (hr1, hr2)
-    copies = {}
+    sms, srs, hms, hrs = (sm1, sm2), (sr1, sr2), (hm1, hm2), (hr1, hr2)
+    swaps = []
 
     def columns(grp):
         start, n = GROUPS[grp]
         lane = lax.broadcasted_iota(jnp.int32, (n, LANES), 1)
-        low = lane < HALF
-        block = (lane & 63) >> 4
+        side = lane >> 6
+        own_even, far_even = side == core, side != core
+        block = (lane & (HALF - 1)) >> 4
         rems = []
         for cp in range(2):
             hs = []
@@ -299,37 +303,51 @@
             for i in range(4):
                 dp, t = i // 2, i % 2
                 odd = pltpu.roll(hs[1][i], HALF, axis=1)
-                send_m[2 * dp, cp, t, start:start + n, :] = jnp.where(low, hs[0][i], odd).astype(BF)
-                send_m[2 * dp + 1, cp, t, start:start + n, :] = jnp.where(low, odd, hs[0][i]).astype(BF)
-            for x in (1, 2, 0):
-                i = 3 * (2 * grp + cp) + x
-                rc = pltpu.make_async_remote_copy(
-                    src_ref=send_m.at[peers[x], cp, :, pl.ds(start, n), :], dst_ref=hms[grp].at[cp, :, r],
-                    send_sem=main_ss.at[i], recv_sem=main_rs.at[i], device_id={'rows': peers[x]}, device_id_type=MESH_ID)
-                rc.start()
-                copies['m', grp, cp, x] = rc
-            hms[grp][cp, :, r] = send_m[r, cp, :, start:start + n, :]
-        for d in range(4):
-            out = jnp.zeros((n, LANES), F32)
+                sms[grp][dp, cp, t] = jnp.where(far_even, hs[0][i], odd).astype(BF)
+                hms[grp][dp, cp, t, core] = jnp.where(own_even, hs[0][i], odd).astype(BF)
+        for t in range(2):
+            both = []
+            for h in range(2):
+                i = 2 * t + h
+                out = rems[i]
+                for c in range(4):
+                    if c != i:
+                        out = jnp.where(block == c, pltpu.roll(rems[c], (WIN * (c - i)) % LANES, axis=1), out)
+                both.append(out)
+            srs[grp][t] = jnp.where(core == 0, both[1], both[0]).astype(BF)
+            hrs[grp][t, core] = jnp.where(core == 0, both[0], both[1]).astype(BF)
+        swaps.append(remote(sms[grp], hms[grp].at[:, :, :, core], swap_ss, swap_rs, 2 * grp, {'rows': near}))
+        swaps.append(remote(srs[grp], hrs[grp].at[:, core], swap_ss, swap_rs, 2 * grp + 1, {'rows': near}))
+
+    columns(0)
+
+    lane = lax.broadcasted_iota(jnp.int32, (N_IMG, LANES), 1)
+    pad = jnp.zeros((LANES - QB, N_IMG), F32)
+    for s in range(2):
+        rem = []
+        for j, ref in ((0, so_ref), (1, sx_ref)):
+            wide = [jnp.concatenate([ref[s, c], pad], axis=0).T for c in range(4)]
+            for cp in range(2):
+                first = jnp.where(core == 0, wide[2 * cp], wide[2 * cp + 1])
+                second = jnp.where(core == 0, wide[2 * cp + 1], wide[2 * cp])
+                s_main[j, s, cp] = jnp.where(lane < HALF, first, pltpu.roll(second, HALF, axis=1))
+            out = wide[0]
             for c in range(4):
-                piece = rems[c] if c == d else pltpu.roll(rems[c], (WIN * (c - d)) % LANES, axis=1)
-                out = jnp.where(block == c, piece, out)
-            send_r[d, start:start + n, :] = out.astype(BF)
-        for x in (1, 2, 0):
-            i = 3 * grp + x
-            rc = pltpu.make_async_remote_copy(
-                src_ref=send_r.at[peers[x], pl.ds(start, n), :], dst_ref=hrs[grp].at[r],
-                send_sem=rem_ss.at[i], recv_sem=rem_rs.at[i], device_id={'rows': peers[x]}, device_id_type=MESH_ID)
-            rc.start()
-            copies['r', grp, x] = rc
-        hrs[grp][r] = send_r[r, start:start + n, :]
-
-    columns(0)
+                out = jnp.where((lane & (HALF - 1)) >> 4 == c, pltpu.roll(wide[c], (WIN * c + HALF) % LANES, axis=1), out)
+            rem.append(out)
+        flip = [pltpu.roll(v, HALF, axis=1) for v in rem]
+        s_rem[s] = jnp.where(x == 0, jnp.where(lane < HALF, rem[0], flip[1]), jnp.where(lane < HALF, rem[1], flip[0]))
+    d8 = jnp.broadcast_to(jnp.concatenate([d_ref[...], jnp.zeros((1, HALF), F32)], axis=1), (SUB, N_IMG + HALF))
+    dq = d8
+    for j in range(1, ROWS):
+        dq = jnp.where(r == j, pltpu.roll(d8, N_IMG + HALF - QB * j, axis=1), dq)
+    dp = jnp.where(k == 0, d8, pltpu.roll(d8, N_IMG + HALF - PB, axis=1))[:, :2 * LANES]
+    dd = jnp.concatenate([dp] * WIN, axis=0).T[:PB] * dq[:1, :LANES]
 
     for h in halos:
         h.wait()
     lane = lax.broadcasted_iota(jnp.int32, (RB, LANES), 1)
-    high = lane >= HALF
+    low = lane < HALF
     slot = lane >> 5
     t0s, t9s = [], []
     for j in range(4):
@@ -337,124 +355,77 @@
         add_first = pltpu.roll(halo[1], (HALF - QTR * j) % LANES, axis=1)
         add_last = pltpu.roll(halo[0], (QTR - QTR * j) % LANES, axis=1)
         e = edge_ref[rows, :] + jnp.where(slot == 2, add_first, jnp.where(slot == 1, add_last, 0.0))
-        t0s.append(jnp.where(high, e, tb_ref[0, rows, :].astype(F32)).astype(BF))
-        t9s.append(jnp.where(high, tb_ref[9, rows, :].astype(F32), e).astype(BF))
+        t0s.append(jnp.where(low, tb_ref[0, rows, :].astype(F32), e).astype(BF))
+        t9s.append(jnp.where(low, e, tb_ref[9, rows, :].astype(F32)).astype(BF))
     to_rows(3, jnp.concatenate(t0s, axis=0), tb_ref[1])
     to_rows(4, tb_ref[SUB], jnp.concatenate(t9s, axis=0))
     columns(1)
 
-    lane = lax.broadcasted_iota(jnp.int32, (N_IMG, LANES), 1)
-    pad = jnp.zeros((LANES - QB, N_IMG), F32)
-    for s in range(2):
-        wide = [jnp.concatenate([s_ref[s, c], pad], axis=0).T for c in range(4)]
-        for cp in range(2):
-            first = jnp.where(core == 0, wide[2 * cp], wide[2 * cp + 1])
-            second = jnp.where(core == 0, wide[2 * cp + 1], wide[2 * cp])
-            s_main[s, cp] = jnp.where(lane < HALF, first, pltpu.roll(second, HALF, axis=1))
-        out = jnp.zeros((N_IMG, LANES), F32)
-        for c in range(4):
-            out = jnp.where((lane >> 4) == c, pltpu.roll(wide[c], (WIN * c - HALF) % LANES, axis=1), out)
-        s_rem[s] = out
-    d8 = jnp.broadcast_to(jnp.concatenate([d_ref[...], jnp.zeros((1, HALF), F32)], axis=1), (SUB, N_IMG + HALF))
-    dq = d8
-    for j in range(1, ROWS):
-        dq = jnp.where(r == j, pltpu.roll(d8, N_IMG + HALF - QB * j, axis=1), dq)
-    dp = jnp.where(k == 0, d8, pltpu.roll(d8, N_IMG + HALF - PB, axis=1))[:, :2 * LANES]
-    dd = jnp.concatenate([dp] * WIN, axis=0).T[:PB] * dq[:1, :LANES]
-
-    k0 = (0, 2 * ROWS * 96)
-
-    def rows_main(grp):
-        n = GROUPS[grp][1]
-        for cp in range(2):
-            for x in range(3):
-                copies['m', grp, cp, x].wait_recv()
-        kk = 2 * ROWS * n
-        rhs = jnp.concatenate([hms[grp][cp].reshape(kk, LANES) for cp in range(2)], axis=1)
-        res = jnp.dot(eu_ref[:, k0[grp]:k0[grp] + kk], rhs, preferred_element_type=F32)
-        return res
-
-    def rows_rem(grp):
-        n = GROUPS[grp][1]
-        for x in range(3):
-            copies['r', grp, x].wait_recv()
-        kk = ROWS * n
-        rhs = hrs[grp][...].reshape(kk, LANES)
-        return [jnp.dot(eu_ref[:, k0[grp] + kk * t:k0[grp] + kk * (t + 1)], rhs, preferred_element_type=F32) for t in range(2)]
-
-    acc_m[...] = rows_main(0)
-    for t, v in enumerate(rows_rem(0)):
-        acc_r[t] = v
-    acc_m[...] = acc_m[...] + rows_main(1)
-
-    low = lax.broadcasted_iota(jnp.int32, (PB, LANES), 1) < HALF
-
-    def combine_main(p0):
-        rows = pl.ds(pl.multiple_of(p0, SUB), PB)
-        rows_im = pl.ds(pl.multiple_of(N_IMG + p0, SUB), PB)
-        re = jnp.zeros((PB, LANES), F32)
-        im = jnp.zeros((PB, LANES), F32)
+    for cp in swaps:
+        cp.wait_recv()
+
+    def rows_dft(half, rhs):
+        total, k0 = None, 0
+        for grp in range(2):
+            kk = 4 * GROUPS[grp][1]
+            part = jnp.dot(eu_ref[x, half, :, k0:k0 + kk], rhs(grp), preferred_element_type=F32)
+            total = part if total is None else total + part
+            k0 += kk
+        return total[:PB], total[PB:]
+
+    quarter = lax.broadcasted_iota(jnp.int32, (PB // 4, LANES), 1) >> 5
+
+    def rest(half):
+        i_re, i_im = rows_dft(half, lambda g: hrs[g][...].reshape(4 * GROUPS[g][1], LANES))
+        rows = pl.ds(pl.multiple_of(half * PB, SUB), PB)
+        s_re, s_im = s_rem[0, rows, :], s_rem[1, rows, :]
+
+        def fold(v):
+            v = v + pltpu.roll(v, LANES - QTR, axis=1)
+            return v + pltpu.roll(v, LANES - WIN, axis=1)
+
+        re, im = fold(s_re * i_re + s_im * i_im), fold(s_re * i_im - s_im * i_re)
+        return jnp.where(lane & (HALF - 1) < WIN, re, pltpu.roll(im, WIN, axis=1))
+
+    def piece(half, j, tail):
+        dp = (x + j) % 2
+        i_re, i_im = rows_dft(half, lambda g: jnp.concatenate([hms[g][dp, cp].reshape(4 * GROUPS[g][1], LANES) for cp in range(2)], axis=1))
+        rows = pl.ds(pl.multiple_of(half * PB, SUB), PB)
+        re, im = None, None
         for cp in range(2):
             cols = slice(LANES * cp, LANES * (cp + 1))
-            i_re, i_im = acc_m[rows, cols], acc_m[rows_im, cols]
-            s_re, s_im = s_main[0, cp, rows, :], s_main[1, cp, rows, :]
-            re = re + (s_re * i_re + s_im * i_im)
-            im = im + (s_re * i_im - s_im * i_re)
-        return jnp.where(low, re + pltpu.roll(re, HALF, axis=1), im + pltpu.roll(im, HALF, axis=1))
-
-    lane = lax.broadcasted_iota(jnp.int32, (PB, LANES), 1)
-    slot40 = lax.broadcasted_iota(jnp.int32, (PB // 4, LANES), 1) >> 5
-
-    def combine_rem(p0):
-        rows = pl.ds(pl.multiple_of(p0, SUB), PB)
-        rows_im = pl.ds(pl.multiple_of(N_IMG + p0, SUB), PB)
-        i_re = acc_r[0, rows, :] + pltpu.roll(acc_r[1, rows, :], HALF, axis=1)
-        i_im = acc_r[0, rows_im, :] + pltpu.roll(acc_r[1, rows_im, :], HALF, axis=1)
-        s_re, s_im = s_rem[0, rows, :], s_rem[1, rows, :]
-        re = jnp.where(low, s_re * i_re + s_im * i_im, 0.0)
-        im = jnp.where(low, s_re * i_im - s_im * i_re, 0.0)
-        w = re + pltpu.roll(im, HALF, axis=1)
-        w = w + pltpu.roll(w, LANES - QTR, axis=1)
-        w = w + pltpu.roll(w, LANES - WIN, axis=1)
-        w = jnp.where(lane < WIN, w, pltpu.roll(w, LANES - 48, axis=1))
-        out = jnp.zeros((PB // 4, LANES), F32)
-        for j in range(4):
-            piece = w[PB // 4 * j:PB // 4 * (j + 1), :]
-            out = jnp.where(slot40 == j, pltpu.roll(piece, QTR * j, axis=1) if j else piece, out)
-        return out
-
-    far_p, own_p = PB - k * PB, k * PB
-
-    def reduce_copy(src, dst, i):
-        return pltpu.make_async_remote_copy(src_ref=src, dst_ref=dst, send_sem=red_ss.at[i], recv_sem=red_rs.at[i],
-                                            device_id={'cols': 1 - k}, device_id_type=MESH_ID)
-
-    img_m[...] = combine_main(far_p)
-    red_main = reduce_copy(img_m, red_m, 0)
-    red_main.start()
-    for t, v in enumerate(rows_rem(1)):
-        acc_r[t] = acc_r[t] + v
-    img_r[...] = combine_rem(far_p)
-    red_rem = reduce_copy(img_r, red_r, 1)
-    red_rem.start()
-    own_main = combine_main(own_p)
-    own_rem = combine_rem(own_p)
-    red_main.wait_recv()
-    main = own_main + red_m[...]
-    red_rem.wait_recv()
-    rem = own_rem + red_r[...]
+            s_re, s_im = s_main[j, 0, cp, rows, :], s_main[j, 1, cp, rows, :]
+            a = s_re * i_re[:, cols] + s_im * i_im[:, cols]
+            b = s_re * i_im[:, cols] - s_im * i_re[:, cols]
+            re, im = (a, b) if re is None else (re + a, im + b)
+        main = jnp.where(low, re + pltpu.roll(re, HALF, axis=1), im + pltpu.roll(im, HALF, axis=1))
+        y = jnp.where(dp == 0, tail, pltpu.roll(tail, HALF, axis=1))
+        out = y[:PB // 4]
+        for g in range(1, 4):
+            out = jnp.where(quarter == g, pltpu.roll(y[PB // 4 * g:PB // 4 * (g + 1)], QTR * g, axis=1), out)
+        return main, out
+
+    sends = []
+    far_tail = rest(1 - k)
+    for i, (half, j) in enumerate(((1 - k, 1), (1 - k, 0), (k, 1))):
+        if i == 2:
+            own_tail = rest(k)
+        pieces[i, :PB], pieces[i, PB:] = piece(half, j, own_tail if i == 2 else far_tail)
+        sends.append(remote(pieces.at[i], recvs.at[i], red_ss, red_rs, i, homes[i]))
+    main, rem = piece(k, 0, own_tail)
+    for i in (2, 1, 0):
+        sends[i].wait_recv()
+        main = main + recvs[i, :PB]
+        rem = rem + recvs[i, PB:]
     for o in range(2):
-        m = main if o == 0 else pltpu.roll(main, HALF, axis=1)
+        m = pltpu.roll(main, HALF, axis=1) if o else main
         for j in range(4):
             rows = slice(PB // 4 * j, PB // 4 * (j + 1))
-            piece = pltpu.roll(rem, (HALF - QTR * j - WIN * o) % LANES, axis=1)
-            full = jnp.where(low[rows], m[rows], piece)
-            out_ref[o, rows, :] = (full * dd[rows])[:, :QB]
-
-    red_main.wait_send()
-    red_rem.wait_send()
-    for key in copies:
-        copies[key].wait_send()
+            tail = pltpu.roll(rem, (HALF - QTR * j - WIN * o) % LANES, axis=1)
+            out_ref[o, rows, :] = (jnp.where(low[rows], m[rows], tail) * dd[rows])[:, :QB]
+
+    for cp in sends + swaps:
+        cp.wait_send()
 
 
 def solution(mesh):
@@ -489,21 +460,20 @@
             compiler_params=pltpu.CompilerParams(vmem_limit_bytes=big), name='spread_far',
             cost_estimate=pl.CostEstimate(flops=4 * 10 ** 9, bytes_accessed=4 * 10 ** 6, transcendentals=0),
         )(base_in, far_in, half)
+        maps = jnp.swapaxes(coil_maps, 2, 3)
+        maps_x = lax.ppermute(maps, 'rows', [(i, (i + 2) % ROWS) for i in range(ROWS)])
         dma = pltpu.SemaphoreType.DMA
+        half_bufs = [VMEM((2, 2, 2, n, LANES), BF) for _, n in GROUPS] + [VMEM((2, n, LANES), BF) for _, n in GROUPS]
+        full_bufs = [VMEM((2, 2, 2, 2, n, LANES), BF) for _, n in GROUPS] + [VMEM((2, 2, n, LANES), BF) for _, n in GROUPS]
         return pl.pallas_call(
             image_kernel,
-            out_shape=jax.ShapeDtypeStruct((2, PB, QB), F32),
-            in_specs=[vm] * 8, out_specs=vm,
-            scratch_shapes=[
-                VMEM((4 * RB, 2 * N_GRID), BF), VMEM((2, RB, LANES), F32),
-                VMEM((4, 2, 2, RB, LANES), BF), VMEM((4, RB, LANES), BF),
-                VMEM((2, 2, ROWS, 96, LANES), BF), VMEM((2, 2, ROWS, HALF, LANES), BF), VMEM((ROWS, 96, LANES), BF), VMEM((ROWS, HALF, LANES), BF),
-                VMEM((2 * N_IMG, 2 * LANES), F32), VMEM((2, 2 * N_IMG, LANES), F32), VMEM((2, 2, N_IMG, LANES), F32), VMEM((2, N_IMG, LANES), F32),
-                VMEM((PB, LANES), F32), VMEM((PB // 4, LANES), F32), VMEM((PB, LANES), F32), VMEM((PB // 4, LANES), F32),
-                dma((2,)), dma((2,)), dma((12,)), dma((12,)), dma((6,)), dma((6,)), dma((2,)), dma((2,)),
+            out_shape=jax.ShapeDtypeStruct((2, PB, QB), F32), in_specs=[vm] * 9, out_specs=vm,
+            scratch_shapes=[VMEM((4 * RB, 2 * N_GRID), BF), VMEM((2, RB, LANES), F32)] + half_bufs + full_bufs + [
+                VMEM((2, 2, 2, N_IMG, LANES), F32), VMEM((2, N_IMG, LANES), F32), VMEM((3, PB + PB // 4, LANES), F32), VMEM((3, PB + PB // 4, LANES), F32),
+                dma((2,)), dma((2,)), dma((4,)), dma((4,)), dma((3,)), dma((3,)),
             ],
             compiler_params=pltpu.CompilerParams(vmem_limit_bytes=20 * 1024 * 1024, collective_id=0, has_side_effects=True), name='image',
-        )(tb, edge, pack, jnp.swapaxes(coil_maps, 2, 3), deapod.reshape(1, N_IMG), col_dft(), row_dft(), unmix())
+        )(tb, edge, pack, maps, maps_x, deapod.reshape(1, N_IMG), col_dft(), row_dft(), unmix())
 
     return jax.shard_map(
         local_fn,

time: 48.4 us -> 46.6 us (0.963)
  Pallas kernels: 39.7 us -> 35.9 us
  starting transfers between devices: 3.42 us -> 5.39 us
    pallas_call x1, Pallas kernels: 19.3 us -> 15.5 us  [local_fn(): pl.pallas_call(image_kernel, out_shape=jax.ShapeDtypeStruct((2, PB, QB),...]
    ppermute x0 -> x1, starting transfers between devices: none -> 3.34 us  [local_fn(): lax.ppermute(maps, 'rows', [(i, (i + 2) % ROWS) for i in range(ROWS)])]
    ppermute x1, starting transfers between devices: 3.39 us -> 1.54 us  [local_fn(): far_in = lax.ppermute(far, 'cols', swap)]
  transfers between devices with their start and end apart: 2 -> 3, of which waited for: 0 -> 0; matrix products, arithmetic and copies ran while one was open for 0% -> 0% of each run, Pallas kernels for 21% -> 44%
where the time goes in v3:
time: 46.6 us; the launch traced here: 46.4 us
  Pallas kernels  35.9 us (77%)
  starting transfers between devices  5.39 us (12%)
  local copies, waits for them, and re-layouts  4.89 us (10%)
    pallas_call x1, Pallas kernels, local_fn(): pl.pallas_call(image_kernel, out_shape=jax.ShapeDtypeStruct((2, PB, QB),...  15.5 us
    pallas_call x1, Pallas kernels, local_fn(): pl.pallas_call(own_kernel, out_shape=jax.ShapeDtypeStruct((11, CW, LANES)...  10.1 us
    pallas_call x1, Pallas kernels, local_fn(): pl.pallas_call(far_kernel, out_shape=(jax.ShapeDtypeStruct((10, N_GRID, L...  9.8 us
    unnamed x21, local copies, waits for them, and re-layouts  4.89 us
    ppermute x1, starting transfers between devices, local_fn(): lax.ppermute(maps, 'rows', [(i, (i + 2) % ROWS) for i in range(ROWS)])  3.34 us
    ppermute x1, starting transfers between devices, local_fn(): far_in = lax.ppermute(far, 'cols', swap)  1.54 us
  transfers between devices with their start and end apart: 3, of which 0 were waited for; matrix products, arithmetic and copies ran while one was open for 0% of the time, Pallas kernels for 44%

profile of v3, /device:TPU:0, one launch (start us, length us, event | category | flops | bytes accessed | tf_op | source)
XLA Modules:
  0.0 46.4 jit_solution(10206103847129913799)
XLA Ops:
  0.0 3.3 %collective-permute-start.2 = (f32[2,4,80,320]{3,2,1,0:T(8,128)}, f32[2,4,80,320]{3,2,1,0:T(8,128)S(1)}, u32[]{:S(2)}, u32[]{:S(2)}) collective-permute-start(f32[2,4,80,320]{3,2,1,0:T(8,128)} %bitcast.3), channel_id=1, source_target_pairs={{0,2},{1,3},{2,0},{3,1},{4,6},{5,7},{6,4},{7,5}} | collective-permute-start | bytes 2457608 | tf_op jit(solution)/shard_map/ppermute | solution.py:464
  3.3 0.9 %copy-done.3 = f32[2,8,4096]{2,1,0:T(8,128)S(1)} copy-done((f32[2,8,4096]{2,1,0:T(8,128)S(1)}, f32[2,8,4096]{2,1,0:T(8,128)}, u32[]{:S(2)}) %copy-start.3) | copy-done | bytes 262168
  4.3 0.9 %copy-done.5 = f32[6,4096]{1,0:T(8,128)S(1)} copy-done((f32[6,4096]{1,0:T(8,128)S(1)}, f32[6,4096]{1,0:T(8,128)}, u32[]{:S(2)}) %copy-start.5) | copy-done | bytes 98328
  5.2 0.9 %copy-done.6 = f32[6,4096]{1,0:T(8,128)S(1)} copy-done((f32[6,4096]{1,0:T(8,128)S(1)}, f32[6,4096]{1,0:T(8,128)}, u32[]{:S(2)}) %copy-start.6) | copy-done | bytes 98328
  6.1 0.7 %copy-done.7 = s32[4096]{0:T(1024)S(1)} copy-done((s32[4096]{0:T(1024)S(1)}, s32[4096]{0:T(1024)}, u32[]{:S(2)}) %copy-start.7) | copy-done | bytes 16408
  6.8 0.7 %copy-done.8 = s32[4096]{0:T(1024)S(1)} copy-done((s32[4096]{0:T(1024)S(1)}, s32[4096]{0:T(1024)}, u32[]{:S(2)}) %copy-start.8) | copy-done | bytes 16408
  7.5 0.5 %prep.1 = (f32[24,4096]{1,0:T(8,128)S(1)}, f32[24,4096]{1,0:T(8,128)S(1)}, s32[32,128]{1,0:T(8,128)S(1)}) custom-call(f32[2,8,4096]{2,1,0:T(8,128)S(1)} %copy-done.3, f32[6,4096]{1,0:T(8,128)S(1)} %copy-done.5, f32[6,4096]{1,0:T(8,128)S(1)} %copy-done.6, s32[32,128]{1,0:T(8,128)S(1)} %bitcast.5, s32[32,128]{1,0:T(8,128)S(1)} %bitcast.6), custom_call_target="tpu_custom_call" | custom-call | tf_op jit(solution)/shard_map/prep/pallas_call | solution.py:441
  8.1 1.5 %collective-permute-start.1 = (f32[24,4096]{1,0:T(8,128)S(1)}, f32[24,4096]{1,0:T(8,128)S(1)}, u32[]{:S(2)}, u32[]{:S(2)}) collective-permute-start(f32[24,4096]{1,0:T(8,128)S(1)} %get-tuple-element.12), channel_id=1, source_target_pairs={{0,4},{4,0},{1,5},{5,1},{2,6},{6,2},{3,7},{7,3}} | collective-permute-start | bytes 1179656 | tf_op jit(solution)/shard_map/ppermute | solution.py:449
  9.6 0.5 %collective-permute-start = (s32[32,128]{1,0:T(8,128)S(1)}, s32[32,128]{1,0:T(8,128)S(1)}, u32[]{:S(2)}, u32[]{:S(2)}) collective-permute-start(s32[32,128]{1,0:T(8,128)S(1)} %get-tuple-element.11.base_ref), channel_id=1, source_target_pairs={{0,4},{4,0},{1,5},{5,1},{2,6},{6,2},{3,7},{7,3}} | collective-permute-start | bytes 49160 | tf_op jit(solution)/shard_map/ppermute | solution.py:450
  10.1 10.1 %spread_own.1.a_ref = f32[11,336,128]{2,1,0:T(8,128)S(1)} custom-call(s32[32,128]{1,0:T(8,128)S(1)} %get-tuple-element.11.base_ref, f32[24,4096]{1,0:T(8,128)S(1)} %get-tuple-element.13.pay_ref), custom_call_target="tpu_custom_call" | custom-call | flops 4000000000 | bytes 2000000 | tf_op jit(solution)/shard_map/spread_own/pallas_call | solution.py:451
  20.2 0.0 copy-done.9
  20.2 0.0 copy-start
  20.2 0.0 copy-start.1
  20.2 0.0 copy-start.2
  20.2 0.0 copy-start.4
  20.2 0.0 collective-permute-done.base_ref
  20.3 0.0 collective-permute-done.1.pay_ref
  20.3 9.8 %spread_far.1 = (bf16[10,640,128]{2,1,0:T(8,128)(2,1)S(1)}, f32[640,128]{1,0:T(8,128)S(1)}, f32[2,160,128]{2,1,0:T(8,128)S(1)}) custom-call(s32[32,128]{1,0:T(8,128)S(1)} %collective-permute-done.base_ref, f32[24,4096]{1,0:T(8,128)S(1)} %collective-permute-done.1.pay_ref, f32[11,336,128]{2,1,0:T(8,128)S(1)} %spread_own.1.a_ref), custom_call_target="tpu_custom_call" | custom-call | flops 4000000000 | bytes 4000000 | tf_op jit(solution)/shard_map/spread_far/pallas_call | solution.py:456
  30.1 0.0 collective-permute-done.2.sx_ref
  30.1 0.0 copy-done
  30.1 0.0 copy-done.1
  30.1 0.0 copy-done.2
  30.1 15.5 %image.1 = f32[2,160,80]{2,1,0:T(8,128)S(1)} custom-call(bf16[10,640,128]{2,1,0:T(8,128)(2,1)S(1)} %get-tuple-element.14.tb_ref, f32[640,128]{1,0:T(8,128)S(1)} %get-tuple-element.15.edge_ref, f32[2,160,128]{2,1,0:T(8,128)S(1)} %get-tuple-element.16.pack_ref, f32[2,4,80,320]{3,2,1,0:T(8,128)S(1)} %bitcast.4, ...), custom_call_target="tpu_custom_call" | custom-call | tf_op jit(solution)/shard_map/image/pallas_call | solution.py:468
  45.7 0.7 %copy.12 = f32[2,160,80]{2,1,0:T(8,128)} copy(f32[2,160,80]{2,1,0:T(8,128)S(1)} %image.1) | data formatting | bytes 204800
  (8 shorter events, 0.0 us)
Async XLA Ops:
  0.0 30.1 %collective-permute-start.2 = (f32[2,4,80,320]{3,2,1,0:T(8,128)}, f32[2,4,80,320]{3,2,1,0:T(8,128)S(1)}, u32[]{:S(2)}, u32[]{:S(2)}) collective-permute-start(f32[2,4,80,320]{3,2,1,0:T(8,128)} %bitcast.3), channel_id=1, source_target_pairs={{0,2},{1,3},{2,0},{3,1},{4,6},{5,7},{6,4},{7,5}} | collective-permute-start | bytes 2457608 | tf_op jit(solution)/shard_map/ppermute | solution.py:464
  3.3 0.9 %copy-start.3 = (f32[2,8,4096]{2,1,0:T(8,128)S(1)}, f32[2,8,4096]{2,1,0:T(8,128)}, u32[]{:S(2)}) copy-start(f32[2,8,4096]{2,1,0:T(8,128)} %ks_hbm.1) | copy-start | bytes 786436
  4.3 0.9 %copy-start.5 = (f32[6,4096]{1,0:T(8,128)S(1)}, f32[6,4096]{1,0:T(8,128)}, u32[]{:S(2)}) copy-start(f32[6,4096]{1,0:T(8,128)} %wy_hbm.1) | copy-start | bytes 294916
  5.2 0.9 %copy-start.6 = (f32[6,4096]{1,0:T(8,128)S(1)}, f32[6,4096]{1,0:T(8,128)}, u32[]{:S(2)}) copy-start(f32[6,4096]{1,0:T(8,128)} %wx_hbm.1) | copy-start | bytes 294916
  6.1 0.7 %copy-start.7 = (s32[4096]{0:T(1024)S(1)}, s32[4096]{0:T(1024)}, u32[]{:S(2)}) copy-start(s32[4096]{0:T(1024)} %param.13) | copy-start | bytes 49156
  6.8 0.7 %copy-start.8 = (s32[4096]{0:T(1024)S(1)}, s32[4096]{0:T(1024)}, u32[]{:S(2)}) copy-start(s32[4096]{0:T(1024)} %param.14) | copy-start | bytes 49156
  8.1 12.2 %collective-permute-start.1 = (f32[24,4096]{1,0:T(8,128)S(1)}, f32[24,4096]{1,0:T(8,128)S(1)}, u32[]{:S(2)}, u32[]{:S(2)}) collective-permute-start(f32[24,4096]{1,0:T(8,128)S(1)} %get-tuple-element.12), channel_id=1, source_target_pairs={{0,4},{4,0},{1,5},{5,1},{2,6},{6,2},{3,7},{7,3}} | collective-permute-start | bytes 1179656 | tf_op jit(solution)/shard_map/ppermute | solution.py:449
  9.6 10.6 %collective-permute-start = (s32[32,128]{1,0:T(8,128)S(1)}, s32[32,128]{1,0:T(8,128)S(1)}, u32[]{:S(2)}, u32[]{:S(2)}) collective-permute-start(s32[32,128]{1,0:T(8,128)S(1)} %get-tuple-element.11.base_ref), channel_id=1, source_target_pairs={{0,4},{4,0},{1,5},{5,1},{2,6},{6,2},{3,7},{7,3}} | collective-permute-start | bytes 49160 | tf_op jit(solution)/shard_map/ppermute | solution.py:450
  10.1 10.1 %copy-start.9 = (f32[320]{0:T(512)S(1)}, f32[320]{0:T(512)}, u32[]{:S(2)}) copy-start(f32[320]{0:T(512)} %param.16) | copy-start | bytes 3844
  20.2 9.9 %copy-start = (bf16[1280,640]{1,0:T(8,128)(2,1)S(1)}, bf16[1280,640]{1,0:T(8,128)(2,1)}, u32[]{:S(2)}) copy-start(bf16[1280,640]{1,0:T(8,128)(2,1)} %constant.6.clone.ev_ref) | copy-start | bytes 4915204
  20.2 9.9 %copy-start.1 = (bf16[2,2,320,640]{3,2,1,0:T(8,128)(2,1)S(1)}, bf16[2,2,320,640]{3,2,1,0:T(8,128)(2,1)}, u32[]{:S(2)}) copy-start(bf16[2,2,320,640]{3,2,1,0:T(8,128)(2,1)} %constant.7.clone.eu_ref) | copy-start | bytes 4915204
  20.2 9.9 %copy-start.2 = (f32[2,4,320,80]{2,3,1,0:T(8,128)S(1)}, f32[2,4,320,80]{2,3,1,0:T(8,128)}, u32[]{:S(2)}) copy-start(f32[2,4,320,80]{2,3,1,0:T(8,128)} %param.15) | copy-start | bytes 2457604
  20.2 9.9 %copy-start.4 = (bf16[256,256]{1,0:T(8,128)(2,1)S(1)}, bf16[256,256]{1,0:T(8,128)(2,1)}, u32[]{:S(2)}) copy-start(bf16[256,256]{1,0:T(8,128)(2,1)} %constant.8.clone.pm_ref) | copy-start | bytes 393220

commit v4 on v3

--- a/solution.py
+++ b/solution.py
@@ -78,7 +78,7 @@
     return jnp.asarray(m, BF)
 
 
-def prep_kernel(ks_hbm, wy_hbm, wx_hbm, iy_hbm, ix_hbm, own_ref, far_ref, base_ref, ks_ref, wy_ref, wx_ref, iy_ref, ix_ref, sem):
+def prep_kernel(ks_hbm, wy_hbm, wx_hbm, iy_hbm, ix_hbm, own_ref, far_ref, ks_ref, wy_ref, wx_ref, iy_ref, ix_ref, sem):
     k = lax.axis_index('cols')
     r = lax.axis_index('rows')
     loads = []
@@ -89,7 +89,7 @@
     loads[0].wait()
     loads[1].wait()
     iy = iy_ref[...]
-    base_ref[...] = ((iy - r * RB + 5) >> 3) * CW + (ix_ref[...] - k * CB + 5)
+    base = (((iy - r * RB + 5) >> 3) * CW + (ix_ref[...] - k * CB + 5)).astype(F32)
     sh = ((iy + 5) & 15).astype(F32)
     loads[2].wait()
     loads[3].wait()
@@ -98,7 +98,7 @@
         ref[SUB:WIN, :] = jnp.concatenate([wx_ref[...], zero2], axis=0)
         ref[WIN:24, :] = jnp.concatenate([wy_ref[...], zero2], axis=0)
         for b in range(NB):
-            ref[22:23, LANES * b:LANES * (b + 1)] = sh[b:b + 1, :]
+            ref[22:24, LANES * b:LANES * (b + 1)] = jnp.concatenate([sh[b:b + 1, :], base[b:b + 1, :]], axis=0)
     loads[4].wait()
     lo = jnp.concatenate([ks_ref[0, 0:4, :], ks_ref[1, 0:4, :]], axis=0)
     hi = jnp.concatenate([ks_ref[0, 4:SUB, :], ks_ref[1, 4:SUB, :]], axis=0)
@@ -113,7 +113,7 @@
     return hi, mid, r - mid
 
 
-def accumulate(base_ref, pay_ref, accs, us, xs, vs, r_ref):
+def accumulate(pay_ref, accs, us, xs, vs, r_ref, int_ref, base_ref, sem):
     row_i = lax.broadcasted_iota(jnp.int32, (WIN, LANES), 0)
 
     def make_u(blk, k):
@@ -149,7 +149,11 @@
             a[pl.ds(pl.multiple_of(n * CW, SUB), CW), :] = jnp.zeros((CW, LANES), F32)
         return 0
 
+    for b in range(NB):
+        int_ref[b:b + 1, :] = pay_ref[23:24, LANES * b:LANES * (b + 1)].astype(jnp.int32)
     lax.fori_loop(0, NG, clear, 0)
+    load = pltpu.make_async_copy(int_ref, base_ref, sem)
+    load.start()
     kk = lax.broadcasted_iota(jnp.int32, (LANES, 768), 0)
     ll = lax.broadcasted_iota(jnp.int32, (LANES, 768), 1)
     r_ref[...] = jnp.where((kk < 24) & ((kk & 7) == (ll >> 7)), 1.0, 0.0).astype(BF)
@@ -158,6 +162,7 @@
     make_u(0, 0)
     make_u(1, 1)
     make_v(0)
+    load.wait()
 
     def body(n, _):
         k = 2 * n
@@ -186,9 +191,9 @@
     return tiles + [jnp.where(high, even[10], even[0])]
 
 
-def own_kernel(base_ref, pay_ref, out_ref, *scr):
-    accs, us, xs, vs, r_ref = scr[:T], scr[T:T + 2], scr[T + 2:T + 4], scr[T + 4:T + 6], scr[T + 6]
-    accumulate(base_ref, pay_ref, accs, us, xs, vs, r_ref)
+def own_kernel(pay_ref, out_ref, *scr):
+    accs = scr[:T]
+    accumulate(pay_ref, accs, scr[T:T + 2], scr[T + 2:T + 4], scr[T + 4:T + 6], *scr[T + 6:])
 
     def fold(q, _):
         off = pl.multiple_of(q * SUB, SUB)
@@ -199,9 +204,9 @@
     lax.fori_loop(0, CW // SUB, fold, 0)
 
 
-def far_kernel(base_ref, pay_ref, a_ref, tb_ref, edge_ref, pack_ref, *scr):
-    accs, us, xs, vs, r_ref, gh_ref = scr[:T], scr[T:T + 2], scr[T + 2:T + 4], scr[T + 4:T + 6], scr[T + 6], scr[T + 7]
-    accumulate(base_ref, pay_ref, accs, us, xs, vs, r_ref)
+def far_kernel(pay_ref, a_ref, tb_ref, edge_ref, pack_ref, gh_ref, *scr):
+    accs = scr[:T]
+    accumulate(pay_ref, accs, scr[T:T + 2], scr[T + 2:T + 4], scr[T + 4:T + 6], *scr[T + 6:])
     k = lax.axis_index('cols')
     own0 = k * CB
     far0 = CB - own0
@@ -431,36 +436,33 @@
 def solution(mesh):
     sample_spec = ('exam', 'rows', 'cols')
     vm = pl.BlockSpec(memory_space=pltpu.VMEM)
-    sm = pl.BlockSpec(memory_space=pltpu.SMEM)
     hbm = pl.BlockSpec(memory_space=pltpu.HBM)
     spread_scratch = ([VMEM((NG * CW, LANES), F32)] * T + [VMEM((LANES, LANES), F32)] * 4 + [VMEM((LANES * PS, LANES), F32)] * 2
-                      + [VMEM((LANES, 768), BF)])
+                      + [VMEM((LANES, 768), BF), VMEM((NB, LANES), jnp.int32), pltpu.SMEM((NB, LANES), jnp.int32), pltpu.SemaphoreType.DMA])
     big = 28 * 1024 * 1024
 
     def local_fn(kspace, wts_y, wts_x, idx_y, idx_x, coil_maps, deapod):
-        own, far, base = pl.pallas_call(
+        own, far = pl.pallas_call(
             prep_kernel,
-            out_shape=(jax.ShapeDtypeStruct((24, NS), F32), jax.ShapeDtypeStruct((24, NS), F32), jax.ShapeDtypeStruct((NB, LANES), jnp.int32)),
-            in_specs=[hbm] * 5, out_specs=(vm, vm, vm), name='prep',
+            out_shape=[jax.ShapeDtypeStruct((24, NS), F32)] * 2,
+            in_specs=[hbm] * 5, out_specs=[vm] * 2, name='prep',
             scratch_shapes=[VMEM((2, SUB, NS), F32), VMEM((KW, NS), F32), VMEM((KW, NS), F32), VMEM((NB, LANES), jnp.int32), VMEM((NB, LANES), jnp.int32), pltpu.SemaphoreType.DMA((5,))],
             compiler_params=pltpu.CompilerParams(vmem_limit_bytes=SUB * 1024 * 1024),
-        )(kspace, wts_y, wts_x, idx_y.reshape(NB, LANES), idx_x.reshape(NB, LANES))
-        swap = [(0, 1), (1, 0)]
-        far_in = lax.ppermute(far, 'cols', swap)
-        base_in = lax.ppermute(base, 'cols', swap)
+        )(*[pltpu.with_memory_space_constraint(v, pltpu.HBM) for v in (kspace, wts_y, wts_x, idx_y.reshape(NB, LANES), idx_x.reshape(NB, LANES))])
+        far_in = lax.ppermute(far, 'cols', [(0, 1), (1, 0)])
+        maps, _ = lax.optimization_barrier((jnp.swapaxes(coil_maps, 2, 3), far))
         half = pl.pallas_call(
-            own_kernel, out_shape=jax.ShapeDtypeStruct((11, CW, LANES), F32), in_specs=[sm, vm], out_specs=vm,
+            own_kernel, out_shape=jax.ShapeDtypeStruct((11, CW, LANES), F32), in_specs=[vm], out_specs=vm,
             scratch_shapes=spread_scratch, compiler_params=pltpu.CompilerParams(vmem_limit_bytes=big), name='spread_own',
             cost_estimate=pl.CostEstimate(flops=4 * 10 ** 9, bytes_accessed=2 * 10 ** 6, transcendentals=0),
-        )(base, own)
+        )(own)
         tb, edge, pack = pl.pallas_call(
             far_kernel,
             out_shape=(jax.ShapeDtypeStruct((10, N_GRID, LANES), BF), jax.ShapeDtypeStruct((N_GRID, LANES), F32), jax.ShapeDtypeStruct((2, RB, LANES), F32)),
-            in_specs=[sm, vm, vm], out_specs=(vm, vm, vm), scratch_shapes=spread_scratch + [VMEM((N_GRID, LANES), F32)],
+            in_specs=[vm, vm], out_specs=(vm, vm, vm), scratch_shapes=[VMEM((N_GRID, LANES), F32)] + spread_scratch,
             compiler_params=pltpu.CompilerParams(vmem_limit_bytes=big), name='spread_far',
             cost_estimate=pl.CostEstimate(flops=4 * 10 ** 9, bytes_accessed=4 * 10 ** 6, transcendentals=0),
-        )(base_in, far_in, half)
-        maps = jnp.swapaxes(coil_maps, 2, 3)
+        )(far_in, half)
         maps_x = lax.ppermute(maps, 'rows', [(i, (i + 2) % ROWS) for i in range(ROWS)])
         dma = pltpu.SemaphoreType.DMA
         half_bufs = [VMEM((2, 2, 2, n, LANES), BF) for _, n in GROUPS] + [VMEM((2, n, LANES), BF) for _, n in GROUPS]

time: 46.6 us -> 43.6 us (0.936)
  local copies, waits for them, and re-layouts: 4.89 us -> 1.38 us
  Pallas kernels: 35.9 us -> 36.8 us
  starting transfers between devices: 5.39 us -> 4.88 us
    unnamed x21 -> x9, local copies, waits for them, and re-layouts: 4.89 us -> 0.7 us
    pallas_call x1, Pallas kernels: 15.5 us -> 16.4 us  [local_fn(): pl.pallas_call(image_kernel, out_shape=jax.ShapeDtypeStruct((2, PB, QB),...]
    reshape x1, local copies, waits for them, and re-layouts: 0.01 us -> 0.68 us  [local_fn(): deapod.reshape(1, N_IMG)]
    pallas_call x1, Pallas kernels: 0.52 us -> 1.19 us  [local_fn(): pl.pallas_call(prep_kernel, out_shape=[jax.ShapeDtypeStruct((24, NS), F32...]
    ppermute x2 -> x1, starting transfers between devices: 2.05 us -> 1.52 us  [local_fn(): far_in = lax.ppermute(far, 'cols', [(0, 1), (1, 0)])]
  transfers between devices with their start and end apart: 3 -> 2, of which waited for: 0 -> 1; matrix products, arithmetic and copies ran while one was open for 0% -> 2% of each run, Pallas kernels for 44% -> 44%
where the time goes in v4:
time: 43.6 us; the launch traced here: 43.4 us
  Pallas kernels  36.8 us (84%)
  starting transfers between devices  4.88 us (11%)
  local copies, waits for them, and re-layouts  1.38 us (3%)
    pallas_call x1, Pallas kernels, local_fn(): pl.pallas_call(image_kernel, out_shape=jax.ShapeDtypeStruct((2, PB, QB),...  16.4 us
    pallas_call x1, Pallas kernels, local_fn(): pl.pallas_call(own_kernel, out_shape=jax.ShapeDtypeStruct((11, CW, LANES)...  9.71 us
    pallas_call x1, Pallas kernels, local_fn(): pl.pallas_call(far_kernel, out_shape=(jax.ShapeDtypeStruct((10, N_GRID, L...  9.48 us
    ppermute x1, starting transfers between devices, local_fn(): lax.ppermute(maps, 'rows', [(i, (i + 2) % ROWS) for i in range(ROWS)])  3.36 us
    ppermute x1, starting transfers between devices, local_fn(): far_in = lax.ppermute(far, 'cols', [(0, 1), (1, 0)])  1.52 us
    pallas_call x1, Pallas kernels, local_fn(): pl.pallas_call(prep_kernel, out_shape=[jax.ShapeDtypeStruct((24, NS), F32...  1.19 us
  transfers between devices with their start and end apart: 2, of which 1 were waited for; matrix products, arithmetic and copies ran while one was open for 2% of the time, Pallas kernels for 44%

profile of v4, /device:TPU:0, one launch (start us, length us, event | category | flops | bytes accessed | tf_op | source)
XLA Modules:
  0.0 43.4 jit_solution(11738933440072577991)
XLA Ops:
  0.0 1.2 %prep.1 = (f32[24,4096]{1,0:T(8,128)S(1)}, f32[24,4096]{1,0:T(8,128)S(1)}) custom-call(f32[2,8,4096]{2,1,0:T(8,128)} %ks_hbm.1, f32[6,4096]{1,0:T(8,128)} %wy_hbm.1, f32[6,4096]{1,0:T(8,128)} %wx_hbm.1, s32[32,128]{1,0:T(8,128)} %bitcast.5, s32[32,128]{1,0:T(8,128)} %bitcast.6), custom_call_target="tpu_custom_call" | custom-call | tf_op jit(solution)/shard_map/prep/pallas_call | solution.py:445
  1.2 3.4 %collective-permute-start.1 = (f32[2,4,80,320]{3,2,1,0:T(8,128)}, f32[2,4,80,320]{3,2,1,0:T(8,128)S(1)}, u32[]{:S(2)}, u32[]{:S(2)}) collective-permute-start(f32[2,4,80,320]{3,2,1,0:T(8,128)} %bitcast.3), channel_id=1, source_target_pairs={{0,2},{1,3},{2,0},{3,1},{4,6},{5,7},{6,4},{7,5}} | collective-permute-start | bytes 2457608 | tf_op jit(solution)/shard_map/ppermute | solution.py:466
  4.6 1.5 %collective-permute-start = (f32[24,4096]{1,0:T(8,128)S(1)}, f32[24,4096]{1,0:T(8,128)S(1)}, u32[]{:S(2)}, u32[]{:S(2)}) collective-permute-start(f32[24,4096]{1,0:T(8,128)S(1)} %get-tuple-element.11), channel_id=1, source_target_pairs={{0,4},{4,0},{1,5},{5,1},{2,6},{6,2},{3,7},{7,3}} | collective-permute-start | bytes 1179656 | tf_op jit(solution)/shard_map/ppermute | solution.py:452
  6.1 0.7 %reshape.11.d_ref = f32[1,320]{1,0:T(1,128)S(1)} reshape(f32[320]{0:T(512)} %param.16) | data formatting | bytes 2560 | tf_op jit(solution)/shard_map/reshape | solution.py:478
  6.8 9.7 %spread_own.1.a_ref = f32[11,336,128]{2,1,0:T(8,128)S(1)} custom-call(f32[24,4096]{1,0:T(8,128)S(1)} %get-tuple-element.12.pay_ref), custom_call_target="tpu_custom_call" | custom-call | flops 4000000000 | bytes 2000000 | tf_op jit(solution)/shard_map/spread_own/pallas_call | solution.py:454
  16.5 0.0 copy-start
  16.5 0.0 copy-start.1
  16.5 0.0 copy-start.2
  16.5 0.0 copy-start.3
  16.5 0.0 collective-permute-done.pay_ref
  16.5 9.5 %spread_far.1 = (bf16[10,640,128]{2,1,0:T(8,128)(2,1)S(1)}, f32[640,128]{1,0:T(8,128)S(1)}, f32[2,160,128]{2,1,0:T(8,128)S(1)}) custom-call(f32[24,4096]{1,0:T(8,128)S(1)} %collective-permute-done.pay_ref, f32[11,336,128]{2,1,0:T(8,128)S(1)} %spread_own.1.a_ref), custom_call_target="tpu_custom_call" | custom-call | flops 4000000000 | bytes 4000000 | tf_op jit(solution)/shard_map/spread_far/pallas_call | solution.py:459
  26.0 0.3 collective-permute-done.1.sx_ref
  26.3 0.0 copy-done
  26.3 0.0 copy-done.1
  26.3 0.0 copy-done.2
  26.3 0.0 copy-done.3
  26.3 16.4 %image.1 = f32[2,160,80]{2,1,0:T(8,128)S(1)} custom-call(bf16[10,640,128]{2,1,0:T(8,128)(2,1)S(1)} %get-tuple-element.13.tb_ref, f32[640,128]{1,0:T(8,128)S(1)} %get-tuple-element.14.edge_ref, f32[2,160,128]{2,1,0:T(8,128)S(1)} %get-tuple-element.15.pack_ref, f32[2,4,80,320]{3,2,1,0:T(8,128)S(1)} %bitcast.4, ...), custom_call_target="tpu_custom_call" | custom-call | tf_op jit(solution)/shard_map/image/pallas_call | solution.py:470
  42.7 0.7 %copy.12 = f32[2,160,80]{2,1,0:T(8,128)} copy(f32[2,160,80]{2,1,0:T(8,128)S(1)} %image.1) | data formatting | bytes 204800
Async XLA Ops:
  1.2 25.1 %collective-permute-start.1 = (f32[2,4,80,320]{3,2,1,0:T(8,128)}, f32[2,4,80,320]{3,2,1,0:T(8,128)S(1)}, u32[]{:S(2)}, u32[]{:S(2)}) collective-permute-start(f32[2,4,80,320]{3,2,1,0:T(8,128)} %bitcast.3), channel_id=1, source_target_pairs={{0,2},{1,3},{2,0},{3,1},{4,6},{5,7},{6,4},{7,5}} | collective-permute-start | bytes 2457608 | tf_op jit(solution)/shard_map/ppermute | solution.py:466
  4.6 12.0 %collective-permute-start = (f32[24,4096]{1,0:T(8,128)S(1)}, f32[24,4096]{1,0:T(8,128)S(1)}, u32[]{:S(2)}, u32[]{:S(2)}) collective-permute-start(f32[24,4096]{1,0:T(8,128)S(1)} %get-tuple-element.11), channel_id=1, source_target_pairs={{0,4},{4,0},{1,5},{5,1},{2,6},{6,2},{3,7},{7,3}} | collective-permute-start | bytes 1179656 | tf_op jit(solution)/shard_map/ppermute | solution.py:452
  16.5 9.8 %copy-start = (bf16[1280,640]{1,0:T(8,128)(2,1)S(1)}, bf16[1280,640]{1,0:T(8,128)(2,1)}, u32[]{:S(2)}) copy-start(bf16[1280,640]{1,0:T(8,128)(2,1)} %constant.6.clone.ev_ref) | copy-start | bytes 4915204
  16.5 9.8 %copy-start.1 = (bf16[2,2,320,640]{3,2,1,0:T(8,128)(2,1)S(1)}, bf16[2,2,320,640]{3,2,1,0:T(8,128)(2,1)}, u32[]{:S(2)}) copy-start(bf16[2,2,320,640]{3,2,1,0:T(8,128)(2,1)} %constant.7.clone.eu_ref) | copy-start | bytes 4915204
  16.5 9.8 %copy-start.2 = (f32[2,4,320,80]{2,3,1,0:T(8,128)S(1)}, f32[2,4,320,80]{2,3,1,0:T(8,128)}, u32[]{:S(2)}) copy-start(f32[2,4,320,80]{2,3,1,0:T(8,128)} %param.15) | copy-start | bytes 2457604
  16.5 9.8 %copy-start.3 = (bf16[256,256]{1,0:T(8,128)(2,1)S(1)}, bf16[256,256]{1,0:T(8,128)(2,1)}, u32[]{:S(2)}) copy-start(bf16[256,256]{1,0:T(8,128)(2,1)} %constant.8.clone.pm_ref) | copy-start | bytes 393220

commit v5 on v4

--- a/solution.py
+++ b/solution.py
@@ -13,7 +13,8 @@
 F32 = jnp.float32
 VMEM = pltpu.VMEM
 LANES = 128
-SUB, WIN, QTR, HALF = 8, 16, 32, 64
+MIB = 1 << 20
+SUB, WIN, QTR, HALF, WIDE = 8, 16, 32, 64, 256
 N_GRID, N_IMG, N_COILS, KW = 640, 320, 8, 6
 ROWS, COLS = 4, 2
 RB, CB, QB = N_GRID // ROWS, N_GRID // COLS, N_IMG // ROWS
@@ -24,8 +25,8 @@
 CW = CB + WIN
 T = 6
 PS = 9
-ORDER = (1, 2, 3, 0, 4)
-GROUPS = ((0, 96), (96, 64))
+ORDER = tuple(range(1, 9)) + (0, 9)
+GROUPS = ((0, 128), (128, 32))
 MESH_ID = pl.DeviceIdType.MESH
 
 
@@ -56,7 +57,7 @@
 
 def row_dft():
     e = dft_parts()
-    rows = np.concatenate([np.arange(QTR * l, QTR * (l + 1)) for l in ORDER])
+    rows = np.concatenate([np.arange(WIN * l, WIN * (l + 1)) for l in ORDER])
     chips = []
     for x in range(2):
         parts = []
@@ -65,12 +66,12 @@
                 for b in range(2):
                     parts.append(e[t, (2 * x + b) * RB + rows[start:start + n]])
         m = np.concatenate(parts, 0)
-        chips.append([m[:, :, PB * h:PB * (h + 1)].reshape(N_GRID, N_IMG).T for h in range(2)])
+        chips.append(np.concatenate([m[:, :, PB * h:PB * (h + 1)].reshape(N_GRID, N_IMG).T for h in range(2)], 0))
     return jnp.asarray(np.array(chips), BF)
 
 
 def unmix():
-    m = np.zeros((256, 256), np.float32)
+    m = np.zeros((WIDE, WIDE), np.float32)
     for ch in range(SUB):
         for pp in range(2):
             for i in range(WIN):
@@ -78,11 +79,11 @@
     return jnp.asarray(m, BF)
 
 
-def prep_kernel(ks_hbm, wy_hbm, wx_hbm, iy_hbm, ix_hbm, own_ref, far_ref, ks_ref, wy_ref, wx_ref, iy_ref, ix_ref, sem):
+def prep_kernel(ks_hbm, wy_hbm, wx_hbm, iy_hbm, ix_hbm, maps_hbm, own_ref, far_ref, sp_ref, ks_ref, wy_ref, wx_ref, iy_ref, ix_ref, maps_ref, sem):
     k = lax.axis_index('cols')
     r = lax.axis_index('rows')
     loads = []
-    for src, dst in ((iy_hbm, iy_ref), (ix_hbm, ix_ref), (wx_hbm, wx_ref), (wy_hbm, wy_ref), (ks_hbm, ks_ref)):
+    for src, dst in ((iy_hbm, iy_ref), (ix_hbm, ix_ref), (wx_hbm, wx_ref), (wy_hbm, wy_ref), (ks_hbm, ks_ref), (maps_hbm, maps_ref)):
         cp = pltpu.make_async_copy(src, dst, sem.at[len(loads)])
         cp.start()
         loads.append(cp)
@@ -104,6 +105,11 @@
     hi = jnp.concatenate([ks_ref[0, 4:SUB, :], ks_ref[1, 4:SUB, :]], axis=0)
     own_ref[0:SUB, :] = jnp.where(k == 0, lo, hi)
     far_ref[0:SUB, :] = jnp.where(k == 0, hi, lo)
+    loads[5].wait()
+    for c in range(4):
+        for i in range(2):
+            sp_ref[c, :, WIDE * i:WIDE * (i + 1)] = maps_ref[i, c, :, :WIDE]
+        sp_ref[c, :, 512:] = jnp.concatenate([maps_ref[i, c, :, WIDE:] for i in range(2)], axis=1)
 
 
 def split3(x):
@@ -132,7 +138,7 @@
         lhs = xs[k][...].astype(BF)
         u = us[k][...]
         for bp in range(3):
-            w = jnp.dot(lhs, r_ref[:, 256 * bp:256 * bp + 256], preferred_element_type=F32)
+            w = jnp.dot(lhs, r_ref[:, WIDE * bp:WIDE * bp + WIDE], preferred_element_type=F32)
             for c in range(2):
                 v = w[:, LANES * c:LANES * (c + 1)] * u
                 for g in range(WIN):
@@ -256,7 +262,7 @@
 
 
 def image_kernel(tb_ref, edge_ref, pack_ref, so_ref, sx_ref, d_ref, ev_ref, eu_ref, pm_ref, out_ref,
-                 g_ref, halo, sm1, sm2, sr1, sr2, hm1, hm2, hr1, hr2, s_main, s_rem, pieces, recvs,
+                 g_ref, halo, sm1, sm2, sr1, sr2, hm1, hm2, hr1, hr2, s_main, s_rem, acc_m, acc_r, pieces, recvs,
                  halo_ss, halo_rs, swap_ss, swap_rs, red_ss, red_rs):
     k = lax.axis_index('cols')
     r = lax.axis_index('rows')
@@ -278,16 +284,15 @@
 
     halos = [remote(pack_ref.at[i], halo.at[i], halo_ss, halo_rs, i, {'rows': dev}) for i, dev in ((0, prev), (1, nxt))]
 
-    def to_rows(pos, t0, t1):
+    def to_rows(row0, n, t0, t1):
         a = jnp.concatenate([t0, t1], axis=1)
         g = lax.dot_general(pm_ref[...], a, (((1,), (1,)), ((), ())), preferred_element_type=F32).astype(BF)
         for ch in range(SUB):
-            s, c = ch // 4, ch % 4
-            g_ref[RB * c + QTR * pos:RB * c + QTR * (pos + 1), N_GRID * s:N_GRID * (s + 1)] = g[QTR * ch:QTR * (ch + 1), :]
-
-    for pos in range(3):
-        l = ORDER[pos]
-        to_rows(pos, tb_ref[2 * l], tb_ref[2 * l + 1])
+            i, c = ch // 4, ch % 4
+            g_ref[row0 + n * c:row0 + n * c + QTR, N_GRID * i:N_GRID * (i + 1)] = g[QTR * ch:QTR * (ch + 1), :]
+
+    for m in range(4):
+        to_rows(QTR * m, LANES, tb_ref[2 * m + 1], tb_ref[2 * m + 2])
 
     sms, srs, hms, hrs = (sm1, sm2), (sr1, sr2), (hm1, hm2), (hr1, hr2)
     swaps = []
@@ -298,13 +303,11 @@
         side = lane >> 6
         own_even, far_even = side == core, side != core
         block = (lane & (HALF - 1)) >> 4
-        rems = []
+        h = jnp.dot(g_ref[4 * start:4 * (start + n), :], ev_ref[...], preferred_element_type=F32)
+        hc = [h[n * c:n * (c + 1)] for c in range(4)]
+        rems = [v[:, 4 * LANES:] for v in hc]
         for cp in range(2):
-            hs = []
-            for c in (2 * cp, 2 * cp + 1):
-                h = jnp.dot(g_ref[RB * c + start:RB * c + start + n, :], ev_ref[...], preferred_element_type=F32)
-                hs.append([h[:, LANES * i:LANES * (i + 1)] for i in range(4)])
-                rems.append(h[:, 4 * LANES:])
+            hs = [[v[:, LANES * i:LANES * (i + 1)] for i in range(4)] for v in hc[2 * cp:2 * cp + 2]]
             for i in range(4):
                 dp, t = i // 2, i % 2
                 odd = pltpu.roll(hs[1][i], HALF, axis=1)
@@ -326,28 +329,32 @@
 
     columns(0)
 
-    lane = lax.broadcasted_iota(jnp.int32, (N_IMG, LANES), 1)
-    pad = jnp.zeros((LANES - QB, N_IMG), F32)
-    for s in range(2):
-        rem = []
-        for j, ref in ((0, so_ref), (1, sx_ref)):
-            wide = [jnp.concatenate([ref[s, c], pad], axis=0).T for c in range(4)]
-            for cp in range(2):
-                first = jnp.where(core == 0, wide[2 * cp], wide[2 * cp + 1])
-                second = jnp.where(core == 0, wide[2 * cp + 1], wide[2 * cp])
-                s_main[j, s, cp] = jnp.where(lane < HALF, first, pltpu.roll(second, HALF, axis=1))
-            out = wide[0]
-            for c in range(4):
-                out = jnp.where((lane & (HALF - 1)) >> 4 == c, pltpu.roll(wide[c], (WIN * c + HALF) % LANES, axis=1), out)
-            rem.append(out)
-        flip = [pltpu.roll(v, HALF, axis=1) for v in rem]
-        s_rem[s] = jnp.where(x == 0, jnp.where(lane < HALF, rem[0], flip[1]), jnp.where(lane < HALF, rem[1], flip[0]))
+    def turn(rows):
+        t = [rows[:, LANES * i:LANES * (i + 1)].T for i in range(5)]
+        return [jnp.concatenate([t[2 * i], t[2 * i + 1], t[4][HALF * i:HALF * (i + 1)]], axis=0) for i in range(2)]
+
+    for j, ref in enumerate((so_ref, sx_ref)):
+        for cp in range(2):
+            s_main[j, 0, cp], s_main[j, 1, cp] = turn(jnp.concatenate([ref[2 * cp + core, :HALF, :], ref[2 * cp + 1 - core, :HALF, :]], axis=0))
+    last = [[ref[c, HALF:, :] for c in range(4)] for ref in (so_ref, sx_ref)]
+    s_rem[0], s_rem[1] = turn(jnp.concatenate([jnp.where(x == j, last[0][c], last[1][c]) for j in range(2) for c in range(4)], axis=0))
     d8 = jnp.broadcast_to(jnp.concatenate([d_ref[...], jnp.zeros((1, HALF), F32)], axis=1), (SUB, N_IMG + HALF))
     dq = d8
     for j in range(1, ROWS):
         dq = jnp.where(r == j, pltpu.roll(d8, N_IMG + HALF - QB * j, axis=1), dq)
     dp = jnp.where(k == 0, d8, pltpu.roll(d8, N_IMG + HALF - PB, axis=1))[:, :2 * LANES]
     dd = jnp.concatenate([dp] * WIN, axis=0).T[:PB] * dq[:1, :LANES]
+
+    for cp in swaps:
+        cp.wait_recv()
+    n0 = 4 * GROUPS[0][1]
+
+    def block_of(grp, j):
+        return jnp.concatenate([hms[grp][(x + j) % 2, cp].reshape(4 * GROUPS[grp][1], LANES) for cp in range(2)], axis=1)
+
+    for j in range(2):
+        acc_m[j] = jnp.dot(eu_ref[x, :, :n0], block_of(0, j), preferred_element_type=F32)
+    acc_r[...] = jnp.dot(eu_ref[x, :, :n0], hrs[0][...].reshape(n0, LANES), preferred_element_type=F32)
 
     for h in halos:
         h.wait()
@@ -362,26 +369,20 @@
         e = edge_ref[rows, :] + jnp.where(slot == 2, add_first, jnp.where(slot == 1, add_last, 0.0))
         t0s.append(jnp.where(low, tb_ref[0, rows, :].astype(F32), e).astype(BF))
         t9s.append(jnp.where(low, e, tb_ref[9, rows, :].astype(F32)).astype(BF))
-    to_rows(3, jnp.concatenate(t0s, axis=0), tb_ref[1])
-    to_rows(4, tb_ref[SUB], jnp.concatenate(t9s, axis=0))
+    to_rows(4 * LANES, QTR, jnp.concatenate(t0s, axis=0), jnp.concatenate(t9s, axis=0))
     columns(1)
-
-    for cp in swaps:
+    for cp in swaps[2:]:
         cp.wait_recv()
 
-    def rows_dft(half, rhs):
-        total, k0 = None, 0
-        for grp in range(2):
-            kk = 4 * GROUPS[grp][1]
-            part = jnp.dot(eu_ref[x, half, :, k0:k0 + kk], rhs(grp), preferred_element_type=F32)
-            total = part if total is None else total + part
-            k0 += kk
+    def rows_dft(half, acc, rhs):
+        rows = pl.ds(pl.multiple_of(half * N_IMG, WIN), N_IMG)
+        total = acc[rows, :] + jnp.dot(eu_ref[x, rows, n0:], rhs, preferred_element_type=F32)
         return total[:PB], total[PB:]
 
     quarter = lax.broadcasted_iota(jnp.int32, (PB // 4, LANES), 1) >> 5
 
     def rest(half):
-        i_re, i_im = rows_dft(half, lambda g: hrs[g][...].reshape(4 * GROUPS[g][1], LANES))
+        i_re, i_im = rows_dft(half, acc_r, hrs[1][...].reshape(4 * GROUPS[1][1], LANES))
         rows = pl.ds(pl.multiple_of(half * PB, SUB), PB)
         s_re, s_im = s_rem[0, rows, :], s_rem[1, rows, :]
 
@@ -394,7 +395,7 @@
 
     def piece(half, j, tail):
         dp = (x + j) % 2
-        i_re, i_im = rows_dft(half, lambda g: jnp.concatenate([hms[g][dp, cp].reshape(4 * GROUPS[g][1], LANES) for cp in range(2)], axis=1))
+        i_re, i_im = rows_dft(half, acc_m.at[j], block_of(1, j))
         rows = pl.ds(pl.multiple_of(half * PB, SUB), PB)
         re, im = None, None
         for cp in range(2):
@@ -439,18 +440,17 @@
     hbm = pl.BlockSpec(memory_space=pltpu.HBM)
     spread_scratch = ([VMEM((NG * CW, LANES), F32)] * T + [VMEM((LANES, LANES), F32)] * 4 + [VMEM((LANES * PS, LANES), F32)] * 2
                       + [VMEM((LANES, 768), BF), VMEM((NB, LANES), jnp.int32), pltpu.SMEM((NB, LANES), jnp.int32), pltpu.SemaphoreType.DMA])
-    big = 28 * 1024 * 1024
+    big = 28 * MIB
 
     def local_fn(kspace, wts_y, wts_x, idx_y, idx_x, coil_maps, deapod):
-        own, far = pl.pallas_call(
+        own, far, maps = pl.pallas_call(
             prep_kernel,
-            out_shape=[jax.ShapeDtypeStruct((24, NS), F32)] * 2,
-            in_specs=[hbm] * 5, out_specs=[vm] * 2, name='prep',
-            scratch_shapes=[VMEM((2, SUB, NS), F32), VMEM((KW, NS), F32), VMEM((KW, NS), F32), VMEM((NB, LANES), jnp.int32), VMEM((NB, LANES), jnp.int32), pltpu.SemaphoreType.DMA((5,))],
-            compiler_params=pltpu.CompilerParams(vmem_limit_bytes=SUB * 1024 * 1024),
-        )(*[pltpu.with_memory_space_constraint(v, pltpu.HBM) for v in (kspace, wts_y, wts_x, idx_y.reshape(NB, LANES), idx_x.reshape(NB, LANES))])
+            out_shape=[jax.ShapeDtypeStruct((24, NS), F32)] * 2 + [jax.ShapeDtypeStruct((4, QB, N_GRID), F32)],
+            in_specs=[hbm] * 6, out_specs=[vm] * 3, name='prep',
+            scratch_shapes=[VMEM((2, SUB, NS), F32), VMEM((KW, NS), F32), VMEM((KW, NS), F32), VMEM((NB, LANES), jnp.int32), VMEM((NB, LANES), jnp.int32), VMEM((2, 4, QB, N_IMG), F32), pltpu.SemaphoreType.DMA((6,))],
+            compiler_params=pltpu.CompilerParams(vmem_limit_bytes=SUB * MIB),
+        )(*[pltpu.with_memory_space_constraint(v, pltpu.HBM) for v in (kspace, wts_y, wts_x, idx_y.reshape(NB, LANES), idx_x.reshape(NB, LANES), jnp.swapaxes(coil_maps, 2, 3))])
         far_in = lax.ppermute(far, 'cols', [(0, 1), (1, 0)])
-        maps, _ = lax.optimization_barrier((jnp.swapaxes(coil_maps, 2, 3), far))
         half = pl.pallas_call(
             own_kernel, out_shape=jax.ShapeDtypeStruct((11, CW, LANES), F32), in_specs=[vm], out_specs=vm,
             scratch_shapes=spread_scratch, compiler_params=pltpu.CompilerParams(vmem_limit_bytes=big), name='spread_own',
@@ -471,10 +471,11 @@
             image_kernel,
             out_shape=jax.ShapeDtypeStruct((2, PB, QB), F32), in_specs=[vm] * 9, out_specs=vm,
             scratch_shapes=[VMEM((4 * RB, 2 * N_GRID), BF), VMEM((2, RB, LANES), F32)] + half_bufs + full_bufs + [
-                VMEM((2, 2, 2, N_IMG, LANES), F32), VMEM((2, N_IMG, LANES), F32), VMEM((3, PB + PB // 4, LANES), F32), VMEM((3, PB + PB // 4, LANES), F32),
+                VMEM((2, 2, 2, N_IMG, LANES), F32), VMEM((2, N_IMG, LANES), F32),
+                VMEM((2, 2 * N_IMG, 2 * LANES), F32), VMEM((2 * N_IMG, LANES), F32), VMEM((3, PB + PB // 4, LANES), F32), VMEM((3, PB + PB // 4, LANES), F32),
                 dma((2,)), dma((2,)), dma((4,)), dma((4,)), dma((3,)), dma((3,)),
             ],
-            compiler_params=pltpu.CompilerParams(vmem_limit_bytes=20 * 1024 * 1024, collective_id=0, has_side_effects=True), name='image',
+            compiler_params=pltpu.CompilerParams(vmem_limit_bytes=20 * MIB, collective_id=0, has_side_effects=True), name='image',
         )(tb, edge, pack, maps, maps_x, deapod.reshape(1, N_IMG), col_dft(), row_dft(), unmix())
 
     return jax.shard_map(

time: 43.6 us -> 41.9 us (0.961)
  Pallas kernels: 36.8 us -> 35.3 us
    pallas_call x1, Pallas kernels: 16.4 us -> 14.5 us  [local_fn(): pl.pallas_call(image_kernel, out_shape=jax.ShapeDtypeStruct((2, PB, QB),...]
    pallas_call x1, Pallas kernels: 1.19 us -> 1.65 us  [local_fn(): pl.pallas_call(prep_kernel, out_shape=[jax.ShapeDtypeStruct((24, NS), F32...]
  transfers between devices with their start and end apart: 2 -> 2, of which waited for: 1 -> 0; matrix products, arithmetic and copies ran while one was open for 2% -> 2% of each run, Pallas kernels for 44% -> 46%
where the time goes in v5:
time: 41.9 us; the launch traced here: 41.7 us
  Pallas kernels  35.3 us (84%)
  starting transfers between devices  4.88 us (12%)
  local copies, waits for them, and re-layouts  1.37 us (3%)
    pallas_call x1, Pallas kernels, local_fn(): pl.pallas_call(image_kernel, out_shape=jax.ShapeDtypeStruct((2, PB, QB),...  14.5 us
    pallas_call x1, Pallas kernels, local_fn(): pl.pallas_call(own_kernel, out_shape=jax.ShapeDtypeStruct((11, CW, LANES)...  9.74 us
    pallas_call x1, Pallas kernels, local_fn(): pl.pallas_call(far_kernel, out_shape=(jax.ShapeDtypeStruct((10, N_GRID, L...  9.47 us
    ppermute x1, starting transfers between devices, local_fn(): lax.ppermute(maps, 'rows', [(i, (i + 2) % ROWS) for i in range(ROWS)])  3.36 us
    pallas_call x1, Pallas kernels, local_fn(): pl.pallas_call(prep_kernel, out_shape=[jax.ShapeDtypeStruct((24, NS), F32...  1.65 us
    ppermute x1, starting transfers between devices, local_fn(): far_in = lax.ppermute(far, 'cols', [(0, 1), (1, 0)])  1.52 us
  transfers between devices with their start and end apart: 2, of which 0 were waited for; matrix products, arithmetic and copies ran while one was open for 2% of the time, Pallas kernels for 46%

profile of v5, /device:TPU:0, one launch (start us, length us, event | category | flops | bytes accessed | tf_op | source)
XLA Modules:
  0.0 41.7 jit_solution(6746497582279959016)
XLA Ops:
  0.0 1.6 %prep.1 = (f32[24,4096]{1,0:T(8,128)S(1)}, f32[24,4096]{1,0:T(8,128)S(1)}, f32[4,80,640]{2,1,0:T(8,128)S(1)}) custom-call(f32[2,8,4096]{2,1,0:T(8,128)} %ks_hbm.1, f32[6,4096]{1,0:T(8,128)} %wy_hbm.1, f32[6,4096]{1,0:T(8,128)} %wx_hbm.1, s32[32,128]{1,0:T(8,128)} %bitcast.4, s32[32,128]{1,0:T(8,128)} %bitcast.5, f32[2,4,80,320]{3,2,1,0:T(8,128)} %bitcast.3), custom_call_target="tpu_custom_call" | custom-call | tf_op jit(solution)/shard_map/prep/pallas_call | solution.py:446
  1.7 3.4 %collective-permute-start.1 = (f32[4,80,640]{2,1,0:T(8,128)S(1)}, f32[4,80,640]{2,1,0:T(8,128)S(1)}, u32[]{:S(2)}, u32[]{:S(2)}) collective-permute-start(f32[4,80,640]{2,1,0:T(8,128)S(1)} %get-tuple-element.16.so_ref), channel_id=1, source_target_pairs={{0,2},{1,3},{2,0},{3,1},{4,6},{5,7},{6,4},{7,5}} | collective-permute-start | bytes 2457608 | tf_op jit(solution)/shard_map/ppermute | solution.py:466
  5.0 1.5 %collective-permute-start = (f32[24,4096]{1,0:T(8,128)S(1)}, f32[24,4096]{1,0:T(8,128)S(1)}, u32[]{:S(2)}, u32[]{:S(2)}) collective-permute-start(f32[24,4096]{1,0:T(8,128)S(1)} %get-tuple-element.11), channel_id=1, source_target_pairs={{0,4},{4,0},{1,5},{5,1},{2,6},{6,2},{3,7},{7,3}} | collective-permute-start | bytes 1179656 | tf_op jit(solution)/shard_map/ppermute | solution.py:453
  6.5 0.7 %reshape.11.d_ref = f32[1,320]{1,0:T(1,128)S(1)} reshape(f32[320]{0:T(512)} %param.16) | data formatting | bytes 2560 | tf_op jit(solution)/shard_map/reshape | solution.py:479
  7.2 9.7 %spread_own.1.a_ref = f32[11,336,128]{2,1,0:T(8,128)S(1)} custom-call(f32[24,4096]{1,0:T(8,128)S(1)} %get-tuple-element.12.pay_ref), custom_call_target="tpu_custom_call" | custom-call | flops 4000000000 | bytes 2000000 | tf_op jit(solution)/shard_map/spread_own/pallas_call | solution.py:454
  17.0 0.0 copy-start
  17.0 0.0 copy-start.1
  17.0 0.0 copy-start.2
  17.0 0.0 collective-permute-done.pay_ref
  17.0 9.5 %spread_far.1 = (bf16[10,640,128]{2,1,0:T(8,128)(2,1)S(1)}, f32[640,128]{1,0:T(8,128)S(1)}, f32[2,160,128]{2,1,0:T(8,128)S(1)}) custom-call(f32[24,4096]{1,0:T(8,128)S(1)} %collective-permute-done.pay_ref, f32[11,336,128]{2,1,0:T(8,128)S(1)} %spread_own.1.a_ref), custom_call_target="tpu_custom_call" | custom-call | flops 4000000000 | bytes 4000000 | tf_op jit(solution)/shard_map/spread_far/pallas_call | solution.py:459
  26.5 0.0 collective-permute-done.1.sx_ref
  26.5 0.0 copy-done
  26.5 0.0 copy-done.1
  26.5 0.0 copy-done.2
  26.5 14.5 %image.1 = f32[2,160,80]{2,1,0:T(8,128)S(1)} custom-call(bf16[10,640,128]{2,1,0:T(8,128)(2,1)S(1)} %get-tuple-element.13.tb_ref, f32[640,128]{1,0:T(8,128)S(1)} %get-tuple-element.14.edge_ref, f32[2,160,128]{2,1,0:T(8,128)S(1)} %get-tuple-element.15.pack_ref, f32[4,80,640]{2,1,0:T(8,128)S(1)} %get-tuple-element.16.so_ref, ...), custom_call_target="tpu_custom_call" | custom-call | tf_op jit(solution)/shard_map/image/pallas_call | solution.py:470
  41.0 0.7 %copy.12 = f32[2,160,80]{2,1,0:T(8,128)} copy(f32[2,160,80]{2,1,0:T(8,128)S(1)} %image.1) | data formatting | bytes 204800
Async XLA Ops:
  1.7 24.8 %collective-permute-start.1 = (f32[4,80,640]{2,1,0:T(8,128)S(1)}, f32[4,80,640]{2,1,0:T(8,128)S(1)}, u32[]{:S(2)}, u32[]{:S(2)}) collective-permute-start(f32[4,80,640]{2,1,0:T(8,128)S(1)} %get-tuple-element.16.so_ref), channel_id=1, source_target_pairs={{0,2},{1,3},{2,0},{3,1},{4,6},{5,7},{6,4},{7,5}} | collective-permute-start | bytes 2457608 | tf_op jit(solution)/shard_map/ppermute | solution.py:466
  5.0 12.0 %collective-permute-start = (f32[24,4096]{1,0:T(8,128)S(1)}, f32[24,4096]{1,0:T(8,128)S(1)}, u32[]{:S(2)}, u32[]{:S(2)}) collective-permute-start(f32[24,4096]{1,0:T(8,128)S(1)} %get-tuple-element.11), channel_id=1, source_target_pairs={{0,4},{4,0},{1,5},{5,1},{2,6},{6,2},{3,7},{7,3}} | collective-permute-start | bytes 1179656 | tf_op jit(solution)/shard_map/ppermute | solution.py:453
  17.0 9.5 %copy-start = (bf16[1280,640]{1,0:T(8,128)(2,1)S(1)}, bf16[1280,640]{1,0:T(8,128)(2,1)}, u32[]{:S(2)}) copy-start(bf16[1280,640]{1,0:T(8,128)(2,1)} %constant.6.clone.ev_ref) | copy-start | bytes 4915204
  17.0 9.5 %copy-start.1 = (bf16[2,640,640]{2,1,0:T(8,128)(2,1)S(1)}, bf16[2,640,640]{2,1,0:T(8,128)(2,1)}, u32[]{:S(2)}) copy-start(bf16[2,640,640]{2,1,0:T(8,128)(2,1)} %constant.7.clone.eu_ref) | copy-start | bytes 4915204
  17.0 9.5 %copy-start.2 = (bf16[256,256]{1,0:T(8,128)(2,1)S(1)}, bf16[256,256]{1,0:T(8,128)(2,1)}, u32[]{:S(2)}) copy-start(bf16[256,256]{1,0:T(8,128)(2,1)} %constant.8.clone.pm_ref) | copy-start | bytes 393220

commit v6 on v5

--- a/solution.py
+++ b/solution.py
@@ -25,6 +25,9 @@
 CW = CB + WIN
 T = 6
 PS = 9
+PAY = 21
+CODE = 512
+HW = 24
 ORDER = tuple(range(1, 9)) + (0, 9)
 GROUPS = ((0, 128), (128, 32))
 MESH_ID = pl.DeviceIdType.MESH
@@ -90,21 +93,19 @@
     loads[0].wait()
     loads[1].wait()
     iy = iy_ref[...]
-    base = (((iy - r * RB + 5) >> 3) * CW + (ix_ref[...] - k * CB + 5)).astype(F32)
-    sh = ((iy + 5) & 15).astype(F32)
-    loads[2].wait()
-    loads[3].wait()
-    zero2 = jnp.zeros((2, NS), F32)
-    for ref in (own_ref, far_ref):
-        ref[SUB:WIN, :] = jnp.concatenate([wx_ref[...], zero2], axis=0)
-        ref[WIN:24, :] = jnp.concatenate([wy_ref[...], zero2], axis=0)
-        for b in range(NB):
-            ref[22:24, LANES * b:LANES * (b + 1)] = jnp.concatenate([sh[b:b + 1, :], base[b:b + 1, :]], axis=0)
-    loads[4].wait()
+    code = ((iy - r * RB + 5) * CODE + ix_ref[...] - k * CB + 5).astype(F32)
+    for i in range(2, 5):
+        loads[i].wait()
     lo = jnp.concatenate([ks_ref[0, 0:4, :], ks_ref[1, 0:4, :]], axis=0)
     hi = jnp.concatenate([ks_ref[0, 4:SUB, :], ks_ref[1, 4:SUB, :]], axis=0)
-    own_ref[0:SUB, :] = jnp.where(k == 0, lo, hi)
-    far_ref[0:SUB, :] = jnp.where(k == 0, hi, lo)
+    first = k == 0
+    for ref, y in ((own_ref, jnp.where(first, lo, hi)), (far_ref, jnp.where(first, hi, lo))):
+        for b in range(NB):
+            cols = slice(LANES * b, LANES * (b + 1))
+            ref[PAY * b:PAY * b + SUB, :] = y[:, cols]
+            ref[PAY * b + SUB:PAY * b + SUB + KW, :] = wx_ref[:, cols]
+            ref[PAY * (b + 1) - KW - 1:PAY * (b + 1) - 1, :] = wy_ref[:, cols]
+            ref[PAY * (b + 1) - 1:PAY * (b + 1), :] = code[b:b + 1, :]
     loads[5].wait()
     for c in range(4):
         for i in range(2):
@@ -123,15 +124,16 @@
     row_i = lax.broadcasted_iota(jnp.int32, (WIN, LANES), 0)
 
     def make_u(blk, k):
-        off = pl.multiple_of(jnp.minimum(blk, NB - 1) * LANES, LANES)
-        y8 = pay_ref[0:SUB, pl.ds(off, LANES)]
-        wyp = pay_ref[WIN:24, pl.ds(off, LANES)]
-        d = (row_i - wyp[6:7, :].astype(jnp.int32)) & 15
+        off = jnp.minimum(blk, NB - 1) * PAY
+        y8 = pay_ref[pl.ds(off, SUB), :]
+        wx = pay_ref[pl.ds(off + SUB, SUB), :]
+        wyp = pay_ref[pl.ds(off + PAY - SUB, SUB), :]
+        d = (row_i - (wyp[7:, :].astype(jnp.int32) // CODE)) & (WIN - 1)
         p = jnp.zeros((WIN, LANES), F32)
         for a in range(KW):
-            p = jnp.where(d == a, wyp[a:a + 1, :], p)
+            p = jnp.where(d == a, wyp[a + 1:a + 2, :], p)
         us[k][...] = jnp.concatenate([y8 * p[i:i + 1, :] for i in range(WIN)], axis=0).T
-        x3 = list(split3(pay_ref[SUB:WIN, pl.ds(off, LANES)])) + [jnp.zeros((104, LANES), F32)]
+        x3 = list(split3(wx)) + [jnp.zeros((LANES - HW, LANES), F32)]
         xs[k][...] = jnp.concatenate(x3, axis=0).T
 
     def make_v(k):
@@ -150,21 +152,15 @@
             b = base_ref[blk, j]
             acc[pl.ds(b, SUB), :] = acc[pl.ds(b, SUB), :] + vs[k][PS * j:PS * j + SUB, :]
 
-    def clear(n, _):
-        for a in accs:
-            a[pl.ds(pl.multiple_of(n * CW, SUB), CW), :] = jnp.zeros((CW, LANES), F32)
-        return 0
-
-    for b in range(NB):
-        int_ref[b:b + 1, :] = pay_ref[23:24, LANES * b:LANES * (b + 1)].astype(jnp.int32)
-    lax.fori_loop(0, NG, clear, 0)
+    code = jnp.concatenate([pay_ref[PAY * (b + 1) - 1:PAY * (b + 1), :] for b in range(NB)], axis=0).astype(jnp.int32)
+    int_ref[...] = (code // (CODE * SUB)) * CW + (code & (CODE - 1))
+    kk = lax.broadcasted_iota(jnp.int32, (LANES, WIDE * 3), 0)
+    ll = lax.broadcasted_iota(jnp.int32, (LANES, WIDE * 3), 1)
+    r_ref[...] = jnp.where((kk < HW) & ((kk & 7) == (ll >> 7)), 1.0, 0.0).astype(BF)
+    for v in vs:
+        v[...] = jnp.zeros_like(v)
     load = pltpu.make_async_copy(int_ref, base_ref, sem)
     load.start()
-    kk = lax.broadcasted_iota(jnp.int32, (LANES, 768), 0)
-    ll = lax.broadcasted_iota(jnp.int32, (LANES, 768), 1)
-    r_ref[...] = jnp.where((kk < 24) & ((kk & 7) == (ll >> 7)), 1.0, 0.0).astype(BF)
-    for v in vs:
-        v[...] = jnp.zeros_like(v)
     make_u(0, 0)
     make_u(1, 1)
     make_v(0)
@@ -183,13 +179,16 @@
     lax.fori_loop(0, NB // 2, body, 0)
 
 
-def folded(accs, off, n):
+def folded(accs, off, n, clear=False):
     def total(g):
-        o = pl.multiple_of(g * CW + off, SUB)
-        s = accs[0][pl.ds(o, n), :]
+        rows = pl.ds(pl.multiple_of(g * CW + off, SUB), n)
+        v = accs[0][rows, :]
         for a in accs[1:]:
-            s = s + a[pl.ds(o, n), :]
-        return s
+            v = v + a[rows, :]
+        if clear:
+            for a in accs:
+                a[rows, :] = jnp.zeros((n, LANES), F32)
+        return v
 
     high = lax.broadcasted_iota(jnp.int32, (n, LANES), 1) >= HALF
     even = [total(2 * p) for p in range(11)]
@@ -197,73 +196,68 @@
     return tiles + [jnp.where(high, even[10], even[0])]
 
 
-def own_kernel(pay_ref, out_ref, *scr):
-    accs = scr[:T]
-    accumulate(pay_ref, accs, scr[T:T + 2], scr[T + 2:T + 4], scr[T + 4:T + 6], *scr[T + 6:])
+def own_kernel(pay_ref, out_ref, *refs):
+    accs, scr = refs[:T], refs[T:]
+
+    def clear(n, _):
+        for a in accs:
+            a[pl.ds(pl.multiple_of(n * CW, SUB), CW), :] = jnp.zeros((CW, LANES), F32)
+        return 0
+
+    lax.fori_loop(0, NG, clear, 0)
+    accumulate(pay_ref, accs, scr[:2], scr[2:4], scr[4:6], *scr[6:])
 
     def fold(q, _):
-        off = pl.multiple_of(q * SUB, SUB)
-        for p, t in enumerate(folded(accs, off, SUB)):
-            out_ref[p, pl.ds(off, SUB), :] = t
+        off = pl.multiple_of(q * WIN, WIN)
+        for p, t in enumerate(folded(accs, off, WIN, clear=True)):
+            out_ref[p, pl.ds(off, WIN), :] = t
         return 0
 
-    lax.fori_loop(0, CW // SUB, fold, 0)
-
-
-def far_kernel(pay_ref, a_ref, tb_ref, edge_ref, pack_ref, gh_ref, *scr):
-    accs = scr[:T]
-    accumulate(pay_ref, accs, scr[T:T + 2], scr[T + 2:T + 4], scr[T + 4:T + 6], *scr[T + 6:])
-    k = lax.axis_index('cols')
-    own0 = k * CB
+    lax.fori_loop(0, CW // WIN, fold, 0)
+
+
+def far_kernel(pay_ref, a_ref, *refs):
+    accs, pack_ref, gh_ref, scr = refs[T:2 * T], refs[2 * T], refs[2 * T + 1], refs[2 * T + 2:]
+    accumulate(pay_ref, accs, scr[:2], scr[2:4], scr[4:6], *scr[6:])
+    own0 = lax.axis_index('cols') * CB
     far0 = CB - own0
-    high = lax.broadcasted_iota(jnp.int32, (SUB, LANES), 1) >= HALF
-
-    left = folded(accs, 0, SUB)
-    right = folded(accs, CW - SUB, SUB)
-    for src, dst in ((CW - SUB, SUB), (0, CB)):
-        for p in range(10):
-            rows = pl.ds((2 * p + 1) * CW + dst, SUB)
-            accs[0][rows, :] = accs[0][rows, :] + a_ref[p, src:src + SUB, :]
-        ghost = a_ref[10, src:src + SUB, :]
-        accs[0][dst:dst + SUB, :] = accs[0][dst:dst + SUB, :] + jnp.where(high, 0.0, ghost)
-        rows = pl.ds(20 * CW + dst, SUB)
-        accs[0][rows, :] = accs[0][rows, :] + jnp.where(high, ghost, 0.0)
-
-    high16 = lax.broadcasted_iota(jnp.int32, (WIN, LANES), 1) >= HALF
-
-    def put(v, tiles):
-        v = pl.multiple_of(v, WIN)
-        for p in range(10):
-            tb_ref[p, pl.ds(v, WIN), :] = tiles[p].astype(BF)
-        edge_ref[pl.ds(v, WIN), :] = jnp.where(high16, tiles[0], tiles[9])
-        gh_ref[pl.ds(v, WIN), :] = tiles[10]
-
-    def far_part(s, _):
-        put(far0 + WIN * s, folded(accs, pl.multiple_of(SUB + WIN * s, SUB), WIN))
+
+    def ghost(off, n):
+        high = lax.broadcasted_iota(jnp.int32, (n, LANES), 1) >= HALF
+        ends = []
+        for g in (0, NG - 1):
+            rows = pl.ds(pl.multiple_of(g * CW + off, SUB), n)
+            v = accs[0][rows, :]
+            for a in accs[1:]:
+                v = v + a[rows, :]
+            ends.append(v)
+        return jnp.where(high, ends[1], ends[0])
+
+    def copy(n, _):
+        o = pl.multiple_of(n * QTR, SUB)
+        gh_ref[pl.ds(pl.multiple_of(far0 + o, SUB), QTR), :] = ghost(SUB + o, QTR)
+        gh_ref[pl.ds(pl.multiple_of(own0 + o, SUB), QTR), :] = a_ref[10, pl.ds(pl.multiple_of(SUB + o, SUB), QTR), :]
         return 0
 
-    lax.fori_loop(0, CB // WIN, far_part, 0)
-
-    def own_part(s, _):
-        put(own0 + WIN * s, [a_ref[p, pl.ds(pl.multiple_of(SUB + WIN * s, SUB), WIN), :] for p in range(11)])
-        return 0
-
-    lax.fori_loop(1, CB // WIN - 1, own_part, 0)
-    put(own0, [jnp.concatenate([a_ref[p, SUB:WIN, :] + right[p], a_ref[p, WIN:24, :]], axis=0) for p in range(11)])
-    put(own0 + CB - WIN, [jnp.concatenate([a_ref[p, CB - SUB:CB, :], a_ref[p, CB:CB + SUB, :] + left[p]], axis=0) for p in range(11)])
-
-    slot = lax.broadcasted_iota(jnp.int32, (RB, LANES), 1) >> 5
-    for side, lane0 in ((0, QTR), (1, HALF)):
-        out = jnp.zeros((RB, LANES), F32)
-        for j in range(4):
-            piece = pltpu.roll(gh_ref[RB * j:RB * (j + 1), :], (QTR * j - lane0) % LANES, axis=1)
-            out = jnp.where(slot == j, piece, out)
+    lax.fori_loop(0, CB // QTR, copy, 0)
+    for dst, add in ((own0, ghost(CW - SUB, SUB)), (own0 + CB - SUB, ghost(0, SUB)), (far0, a_ref[10, CW - SUB:, :]), (far0 + CB - SUB, a_ref[10, :SUB, :])):
+        rows = pl.ds(pl.multiple_of(dst, SUB), SUB)
+        gh_ref[rows, :] = gh_ref[rows, :] + add
+
+    lane = lax.broadcasted_iota(jnp.int32, (LANES, LANES), 1)
+    for side, lane0 in ((0, HALF - HW), (1, HALF)):
+        out = jnp.zeros((LANES, LANES), F32)
+        for j in range(5):
+            piece = pltpu.roll(gh_ref[LANES * j:LANES * (j + 1), :], (HW * j - lane0) % LANES, axis=1)
+            out = jnp.where(lane >= HW * j, piece, out)
         pack_ref[side] = out
 
 
-def image_kernel(tb_ref, edge_ref, pack_ref, so_ref, sx_ref, d_ref, ev_ref, eu_ref, pm_ref, out_ref,
-                 g_ref, halo, sm1, sm2, sr1, sr2, hm1, hm2, hr1, hr2, s_main, s_rem, acc_m, acc_r, pieces, recvs,
-                 halo_ss, halo_rs, swap_ss, swap_rs, red_ss, red_rs):
+def image_kernel(*refs):
+    accs = refs[:T]
+    (a_ref, pack_ref, so_ref, sx_ref, d_ref, ev_ref, eu_ref, pm_ref, out_ref,
+     tb_ref, edge_ref, g_ref, halo, sm1, sm2, sr1, sr2, hm1, hm2, hr1, hr2, s_main, s_rem, acc_m, acc_r, pieces, recvs,
+     halo_ss, halo_rs, swap_ss, swap_rs, red_ss, red_rs) = refs[T:]
     k = lax.axis_index('cols')
     r = lax.axis_index('rows')
     core, x = r % 2, r // 2
@@ -275,6 +269,27 @@
     barrier = pltpu.get_barrier_semaphore()
     for dev in ({'rows': prev}, {'rows': nxt}) + homes:
         pl.semaphore_signal(barrier, inc=1, device_id=dev, device_id_type=MESH_ID)
+
+    own0 = k * CB
+    far0 = CB - own0
+    high16 = lax.broadcasted_iota(jnp.int32, (WIN, LANES), 1) >= HALF
+
+    def put(v, tiles):
+        rows = pl.ds(pl.multiple_of(v, WIN), WIN)
+        for p in range(10):
+            tb_ref[p, rows, :] = tiles[p].astype(BF)
+        edge_ref[rows, :] = jnp.where(high16, tiles[0], tiles[9])
+
+    def far_part(n, _):
+        put(far0 + WIN * n, folded(accs, pl.multiple_of(SUB + WIN * n, SUB), WIN))
+        return 0
+
+    def own_part(n, _):
+        put(own0 + WIN * n, [a_ref[p, pl.ds(pl.multiple_of(SUB + WIN * n, SUB), WIN), :] for p in range(10)])
+        return 0
+
+    last = CB // WIN - 1
+    lax.fori_loop(1, last, far_part, 0)
     pl.semaphore_wait(barrier, 5)
 
     def remote(src, dst, ss, rs, i, dev):
@@ -283,6 +298,16 @@
         return cp
 
     halos = [remote(pack_ref.at[i], halo.at[i], halo_ss, halo_rs, i, {'rows': dev}) for i, dev in ((0, prev), (1, nxt))]
+
+    lax.fori_loop(1, last, own_part, 0)
+    none = jnp.zeros((SUB, LANES), F32)
+    for n, side in ((0, CW - SUB), (last, 0)):
+        off = SUB + WIN * n
+        near_tiles = folded(accs, off, WIN)
+        far_ends = folded(accs, side, SUB)
+        order = (lambda v: [v, none]) if n == 0 else (lambda v: [none, v])
+        put(far0 + WIN * n, [near_tiles[p] + jnp.concatenate(order(a_ref[p, side:side + SUB, :]), axis=0) for p in range(10)])
+        put(own0 + WIN * n, [a_ref[p, off:off + WIN, :] + jnp.concatenate(order(far_ends[p]), axis=0) for p in range(10)])
 
     def to_rows(row0, n, t0, t1):
         a = jnp.concatenate([t0, t1], axis=1)
@@ -336,9 +361,9 @@
     for j, ref in enumerate((so_ref, sx_ref)):
         for cp in range(2):
             s_main[j, 0, cp], s_main[j, 1, cp] = turn(jnp.concatenate([ref[2 * cp + core, :HALF, :], ref[2 * cp + 1 - core, :HALF, :]], axis=0))
-    last = [[ref[c, HALF:, :] for c in range(4)] for ref in (so_ref, sx_ref)]
-    s_rem[0], s_rem[1] = turn(jnp.concatenate([jnp.where(x == j, last[0][c], last[1][c]) for j in range(2) for c in range(4)], axis=0))
-    d8 = jnp.broadcast_to(jnp.concatenate([d_ref[...], jnp.zeros((1, HALF), F32)], axis=1), (SUB, N_IMG + HALF))
+    tails = [[ref[c, HALF:, :] for c in range(4)] for ref in (so_ref, sx_ref)]
+    s_rem[0], s_rem[1] = turn(jnp.concatenate([jnp.where(x == j, tails[0][c], tails[1][c]) for j in range(2) for c in range(4)], axis=0))
+    d8 = jnp.broadcast_to(jnp.concatenate([d_ref[...][None, :], jnp.zeros((1, HALF), F32)], axis=1), (SUB, N_IMG + HALF))
     dq = d8
     for j in range(1, ROWS):
         dq = jnp.where(r == j, pltpu.roll(d8, N_IMG + HALF - QB * j, axis=1), dq)
@@ -358,17 +383,18 @@
 
     for h in halos:
         h.wait()
-    lane = lax.broadcasted_iota(jnp.int32, (RB, LANES), 1)
+    lane = lax.broadcasted_iota(jnp.int32, (LANES, LANES), 1)
     low = lane < HALF
-    slot = lane >> 5
     t0s, t9s = [], []
-    for j in range(4):
-        rows = slice(RB * j, RB * (j + 1))
-        add_first = pltpu.roll(halo[1], (HALF - QTR * j) % LANES, axis=1)
-        add_last = pltpu.roll(halo[0], (QTR - QTR * j) % LANES, axis=1)
-        e = edge_ref[rows, :] + jnp.where(slot == 2, add_first, jnp.where(slot == 1, add_last, 0.0))
+    for j in range(5):
+        rows = slice(LANES * j, LANES * (j + 1))
+        add_first = pltpu.roll(halo[1], (HALF - HW * j) % LANES, axis=1)
+        add_last = pltpu.roll(halo[0], (HALF - HW - HW * j) % LANES, axis=1)
+        e = edge_ref[rows, :] + jnp.where(low, jnp.where(lane >= HALF - HW, add_last, 0.0), jnp.where(lane < HALF + HW, add_first, 0.0))
         t0s.append(jnp.where(low, tb_ref[0, rows, :].astype(F32), e).astype(BF))
         t9s.append(jnp.where(low, e, tb_ref[9, rows, :].astype(F32)).astype(BF))
+    lane = lax.broadcasted_iota(jnp.int32, (PB, LANES), 1)
+    low = lane < HALF
     to_rows(4 * LANES, QTR, jnp.concatenate(t0s, axis=0), jnp.concatenate(t9s, axis=0))
     columns(1)
     for cp in swaps[2:]:
@@ -438,45 +464,46 @@
     sample_spec = ('exam', 'rows', 'cols')
     vm = pl.BlockSpec(memory_space=pltpu.VMEM)
     hbm = pl.BlockSpec(memory_space=pltpu.HBM)
-    spread_scratch = ([VMEM((NG * CW, LANES), F32)] * T + [VMEM((LANES, LANES), F32)] * 4 + [VMEM((LANES * PS, LANES), F32)] * 2
-                      + [VMEM((LANES, 768), BF), VMEM((NB, LANES), jnp.int32), pltpu.SMEM((NB, LANES), jnp.int32), pltpu.SemaphoreType.DMA])
-    big = 28 * MIB
+    spread_scratch = ([VMEM((LANES, LANES), F32)] * 4 + [VMEM((LANES * PS, LANES), F32)] * 2
+                      + [VMEM((LANES, WIDE * 3), BF), VMEM((NB, LANES), jnp.int32), pltpu.SMEM((NB, LANES), jnp.int32), pltpu.SemaphoreType.DMA])
+    acc_shape = [jax.ShapeDtypeStruct((NG * CW, LANES), F32)] * T
+    big = 6 * MIB
 
     def local_fn(kspace, wts_y, wts_x, idx_y, idx_x, coil_maps, deapod):
         own, far, maps = pl.pallas_call(
             prep_kernel,
-            out_shape=[jax.ShapeDtypeStruct((24, NS), F32)] * 2 + [jax.ShapeDtypeStruct((4, QB, N_GRID), F32)],
+            out_shape=[jax.ShapeDtypeStruct((PAY * NB, LANES), F32)] * 2 + [jax.ShapeDtypeStruct((4, QB, N_GRID), F32)],
             in_specs=[hbm] * 6, out_specs=[vm] * 3, name='prep',
             scratch_shapes=[VMEM((2, SUB, NS), F32), VMEM((KW, NS), F32), VMEM((KW, NS), F32), VMEM((NB, LANES), jnp.int32), VMEM((NB, LANES), jnp.int32), VMEM((2, 4, QB, N_IMG), F32), pltpu.SemaphoreType.DMA((6,))],
             compiler_params=pltpu.CompilerParams(vmem_limit_bytes=SUB * MIB),
         )(*[pltpu.with_memory_space_constraint(v, pltpu.HBM) for v in (kspace, wts_y, wts_x, idx_y.reshape(NB, LANES), idx_x.reshape(NB, LANES), jnp.swapaxes(coil_maps, 2, 3))])
         far_in = lax.ppermute(far, 'cols', [(0, 1), (1, 0)])
-        half = pl.pallas_call(
-            own_kernel, out_shape=jax.ShapeDtypeStruct((11, CW, LANES), F32), in_specs=[vm], out_specs=vm,
+        half, *accs = pl.pallas_call(
+            own_kernel, out_shape=[jax.ShapeDtypeStruct((11, CW, LANES), F32)] + acc_shape, in_specs=[vm], out_specs=[vm] * (T + 1),
             scratch_shapes=spread_scratch, compiler_params=pltpu.CompilerParams(vmem_limit_bytes=big), name='spread_own',
             cost_estimate=pl.CostEstimate(flops=4 * 10 ** 9, bytes_accessed=2 * 10 ** 6, transcendentals=0),
         )(own)
-        tb, edge, pack = pl.pallas_call(
-            far_kernel,
-            out_shape=(jax.ShapeDtypeStruct((10, N_GRID, LANES), BF), jax.ShapeDtypeStruct((N_GRID, LANES), F32), jax.ShapeDtypeStruct((2, RB, LANES), F32)),
-            in_specs=[vm, vm], out_specs=(vm, vm, vm), scratch_shapes=[VMEM((N_GRID, LANES), F32)] + spread_scratch,
+        *accs, pack = pl.pallas_call(
+            far_kernel, out_shape=acc_shape + [jax.ShapeDtypeStruct((2, LANES, LANES), F32)],
+            in_specs=[vm] * (T + 2), out_specs=[vm] * (T + 1), scratch_shapes=[VMEM((N_GRID, LANES), F32)] + spread_scratch,
+            input_output_aliases={i + 2: i for i in range(T)},
             compiler_params=pltpu.CompilerParams(vmem_limit_bytes=big), name='spread_far',
             cost_estimate=pl.CostEstimate(flops=4 * 10 ** 9, bytes_accessed=4 * 10 ** 6, transcendentals=0),
-        )(far_in, half)
+        )(far_in, half, *accs)
         maps_x = lax.ppermute(maps, 'rows', [(i, (i + 2) % ROWS) for i in range(ROWS)])
         dma = pltpu.SemaphoreType.DMA
         half_bufs = [VMEM((2, 2, 2, n, LANES), BF) for _, n in GROUPS] + [VMEM((2, n, LANES), BF) for _, n in GROUPS]
         full_bufs = [VMEM((2, 2, 2, 2, n, LANES), BF) for _, n in GROUPS] + [VMEM((2, 2, n, LANES), BF) for _, n in GROUPS]
         return pl.pallas_call(
             image_kernel,
-            out_shape=jax.ShapeDtypeStruct((2, PB, QB), F32), in_specs=[vm] * 9, out_specs=vm,
-            scratch_shapes=[VMEM((4 * RB, 2 * N_GRID), BF), VMEM((2, RB, LANES), F32)] + half_bufs + full_bufs + [
+            out_shape=jax.ShapeDtypeStruct((2, PB, QB), F32), in_specs=[vm] * (T + 8), out_specs=vm,
+            scratch_shapes=[VMEM((10, N_GRID, LANES), BF), VMEM((N_GRID, LANES), F32), VMEM((4 * RB, 2 * N_GRID), BF), VMEM((2, LANES, LANES), F32)] + half_bufs + full_bufs + [
                 VMEM((2, 2, 2, N_IMG, LANES), F32), VMEM((2, N_IMG, LANES), F32),
                 VMEM((2, 2 * N_IMG, 2 * LANES), F32), VMEM((2 * N_IMG, LANES), F32), VMEM((3, PB + PB // 4, LANES), F32), VMEM((3, PB + PB // 4, LANES), F32),
                 dma((2,)), dma((2,)), dma((4,)), dma((4,)), dma((3,)), dma((3,)),
             ],
             compiler_params=pltpu.CompilerParams(vmem_limit_bytes=20 * MIB, collective_id=0, has_side_effects=True), name='image',
-        )(tb, edge, pack, maps, maps_x, deapod.reshape(1, N_IMG), col_dft(), row_dft(), unmix())
+        )(*accs, half, pack, maps, maps_x, deapod, col_dft(), row_dft(), unmix())
 
     return jax.shard_map(
         local_fn,

time: 41.9 us -> 40.1 us (0.957)
  Pallas kernels: 35.3 us -> 34.2 us
  local copies, waits for them, and re-layouts: 1.37 us -> 0.7 us
    pallas_call x3, Pallas kernels: 20.9 us -> 18.2 us  [the longest x1 9.68 us: local_fn(): pl.pallas_call(own_kernel, out_shape=[jax.ShapeDtypeStruct((11, CW, LANES...]
    pallas_call x1, Pallas kernels: 14.5 us -> 15.9 us  [local_fn(): pl.pallas_call(image_kernel, out_shape=jax.ShapeDtypeStruct((2, PB, QB),...]
    reshape x1 -> x0, local copies, waits for them, and re-layouts: 0.68 us -> none  [local_fn(): deapod.reshape(1, N_IMG)]
  transfers between devices with their start and end apart: 2 -> 2, of which waited for: 0 -> 1; matrix products, arithmetic and copies ran while one was open for 2% -> 0% of each run, Pallas kernels for 46% -> 42%
where the time goes in v6:
time: 40.1 us; the launch traced here: 39.9 us
  Pallas kernels  34.2 us (85%)
  starting transfers between devices  4.88 us (12%)
  local copies, waits for them, and re-layouts  0.7 us (2%)
    pallas_call x1, Pallas kernels, local_fn(): pl.pallas_call(image_kernel, out_shape=jax.ShapeDtypeStruct((2, PB, QB),...  15.9 us
    pallas_call x1, Pallas kernels, local_fn(): pl.pallas_call(own_kernel, out_shape=[jax.ShapeDtypeStruct((11, CW, LANES...  9.68 us
    pallas_call x1, Pallas kernels, local_fn(): pl.pallas_call(far_kernel, out_shape=acc_shape + [jax.ShapeDtypeStruct((2...  6.91 us
    ppermute x1, starting transfers between devices, local_fn(): lax.ppermute(maps, 'rows', [(i, (i + 2) % ROWS) for i in range(ROWS)])  3.36 us
    pallas_call x1, Pallas kernels, local_fn(): pl.pallas_call(prep_kernel, out_shape=[jax.ShapeDtypeStruct((PAY * NB, LA...  1.65 us
    ppermute x1, starting transfers between devices, local_fn(): far_in = lax.ppermute(far, 'cols', [(0, 1), (1, 0)])  1.52 us
  transfers between devices with their start and end apart: 2, of which 1 were waited for; matrix products, arithmetic and copies ran while one was open for 0% of the time, Pallas kernels for 42%

profile of v6, /device:TPU:0, one launch (start us, length us, event | category | flops | bytes accessed | tf_op | source)
XLA Modules:
  0.0 39.9 jit_solution(12727263298032785844)
XLA Ops:
  0.0 1.6 %prep.1 = (f32[672,128]{1,0:T(8,128)S(1)}, f32[672,128]{1,0:T(8,128)S(1)}, f32[4,80,640]{2,1,0:T(8,128)S(1)}) custom-call(f32[2,8,4096]{2,1,0:T(8,128)} %ks_hbm.1, f32[6,4096]{1,0:T(8,128)} %wy_hbm.1, f32[6,4096]{1,0:T(8,128)} %wx_hbm.1, s32[32,128]{1,0:T(8,128)} %bitcast.4, s32[32,128]{1,0:T(8,128)} %bitcast.5, f32[2,4,80,320]{3,2,1,0:T(8,128)} %bitcast.3), custom_call_target="tpu_custom_call" | custom-call | tf_op jit(solution)/shard_map/prep/pallas_call | solution.py:473
  1.7 3.4 %collective-permute-start.1 = (f32[4,80,640]{2,1,0:T(8,128)S(1)}, f32[4,80,640]{2,1,0:T(8,128)S(1)}, u32[]{:S(2)}, u32[]{:S(2)}) collective-permute-start(f32[4,80,640]{2,1,0:T(8,128)S(1)} %get-tuple-element.38.refs_8_), channel_id=1, source_target_pairs={{0,2},{1,3},{2,0},{3,1},{4,6},{5,7},{6,4},{7,5}} | collective-permute-start | bytes 2457608 | tf_op jit(solution)/shard_map/ppermute | solution.py:493
  5.0 1.5 %collective-permute-start = (f32[672,128]{1,0:T(8,128)S(1)}, f32[672,128]{1,0:T(8,128)S(1)}, u32[]{:S(2)}, u32[]{:S(2)}) collective-permute-start(f32[672,128]{1,0:T(8,128)S(1)} %get-tuple-element.22), channel_id=1, source_target_pairs={{0,4},{4,0},{1,5},{5,1},{2,6},{6,2},{3,7},{7,3}} | collective-permute-start | bytes 1032200 | tf_op jit(solution)/shard_map/ppermute | solution.py:480
  6.5 9.7 %spread_own.1 = (f32[11,336,128]{2,1,0:T(8,128)S(1)}, f32[7056,128]{1,0:T(8,128)S(1)}, f32[7056,128]{1,0:T(8,128)S(1)}, f32[7056,128]{1,0:T(8,128)S(1)}, f32[705...) custom-call(f32[672,128]{1,0:T(8,128)S(1)} %get-tuple-element.23.pay_ref), custom_call_target="tpu_custom_call" | custom-call | flops 4000000000 | bytes 2000000 | tf_op jit(solution)/shard_map/spread_own/pallas_call | solution.py:481
  16.2 0.0 collective-permute-done.pay_ref
  16.2 0.0 copy-start
  16.3 0.0 copy-start.1
  16.3 0.0 copy-start.2
  16.3 0.0 copy-start.3
  16.3 6.9 %spread_far.1 = (f32[7056,128]{1,0:T(8,128)S(1)}, f32[7056,128]{1,0:T(8,128)S(1)}, f32[7056,128]{1,0:T(8,128)S(1)}, f32[7056,128]{1,0:T(8,128)S(1)}, f32[7056,12...) custom-call(f32[672,128]{1,0:T(8,128)S(1)} %collective-permute-done., ...), custom_call_target="tpu_custom_call", output_to_operand_aliasing={{0}: (2, {}), {1}: (3, {}), {2}: (4, {}), {3}: (5, {}), {4}... | custom-call | flops 4000000000 | bytes 4000000 | tf_op jit(solution)/shard_map/spread_far/pallas_call | solution.py:486
  23.2 0.1 collective-permute-done.1.refs_9_
  23.3 0.0 copy-done
  23.3 0.0 copy-done.1
  23.3 0.0 copy-done.2
  23.3 0.0 copy-done.3
  23.3 15.9 %image.1 = f32[2,160,80]{2,1,0:T(8,128)S(1)} custom-call(f32[7056,128]{1,0:T(8,128)S(1)} %get-tuple-element.31.refs_0_, f32[7056,128]{1,0:T(8,128)S(1)} %get-tuple-element.32.refs_1_, f32[7056,128]{1,0:T(8,128)S(1)} %get-tuple-element.33.refs_2_, f32[7056,128]{1,0:T(8,128)S(1)} %get-tuple-element.34.refs_3_, f32[7056,128]{1,0:T(8,128)S(1)} %get-tuple-element.35.refs_4_, ...), custom_call_target="tpu_custom_call" | custom-call | tf_op jit(solution)/shard_map/image/pallas_call | solution.py:497
  39.2 0.7 %copy.24 = f32[2,160,80]{2,1,0:T(8,128)} copy(f32[2,160,80]{2,1,0:T(8,128)S(1)} %image.1) | data formatting | bytes 204800
Async XLA Ops:
  1.7 21.6 %collective-permute-start.1 = (f32[4,80,640]{2,1,0:T(8,128)S(1)}, f32[4,80,640]{2,1,0:T(8,128)S(1)}, u32[]{:S(2)}, u32[]{:S(2)}) collective-permute-start(f32[4,80,640]{2,1,0:T(8,128)S(1)} %get-tuple-element.38.refs_8_), channel_id=1, source_target_pairs={{0,2},{1,3},{2,0},{3,1},{4,6},{5,7},{6,4},{7,5}} | collective-permute-start | bytes 2457608 | tf_op jit(solution)/shard_map/ppermute | solution.py:493
  5.0 11.2 %collective-permute-start = (f32[672,128]{1,0:T(8,128)S(1)}, f32[672,128]{1,0:T(8,128)S(1)}, u32[]{:S(2)}, u32[]{:S(2)}) collective-permute-start(f32[672,128]{1,0:T(8,128)S(1)} %get-tuple-element.22), channel_id=1, source_target_pairs={{0,4},{4,0},{1,5},{5,1},{2,6},{6,2},{3,7},{7,3}} | collective-permute-start | bytes 1032200 | tf_op jit(solution)/shard_map/ppermute | solution.py:480
  16.2 7.0 %copy-start = (bf16[1280,640]{1,0:T(8,128)(2,1)S(1)}, bf16[1280,640]{1,0:T(8,128)(2,1)}, u32[]{:S(2)}) copy-start(bf16[1280,640]{1,0:T(8,128)(2,1)} %constant.6.clone.refs_11_) | copy-start | bytes 4915204
  16.3 7.0 %copy-start.1 = (bf16[2,640,640]{2,1,0:T(8,128)(2,1)S(1)}, bf16[2,640,640]{2,1,0:T(8,128)(2,1)}, u32[]{:S(2)}) copy-start(bf16[2,640,640]{2,1,0:T(8,128)(2,1)} %constant.7.clone.refs_12_) | copy-start | bytes 4915204
  16.3 7.0 %copy-start.2 = (bf16[256,256]{1,0:T(8,128)(2,1)S(1)}, bf16[256,256]{1,0:T(8,128)(2,1)}, u32[]{:S(2)}) copy-start(bf16[256,256]{1,0:T(8,128)(2,1)} %constant.8.clone.refs_13_) | copy-start | bytes 393220
  16.3 7.0 %copy-start.3 = (f32[320]{0:T(512)S(1)}, f32[320]{0:T(512)}, u32[]{:S(2)}) copy-start(f32[320]{0:T(512)} %refs_10_.1) | copy-start | bytes 3844

commit v7 on v6

--- a/solution.py
+++ b/solution.py
@@ -14,6 +14,8 @@
 VMEM = pltpu.VMEM
 LANES = 128
 MIB = 1 << 20
+GIGA = 4000 * MIB
+TILES = 10
 SUB, WIN, QTR, HALF, WIDE = 8, 16, 32, 64, 256
 N_GRID, N_IMG, N_COILS, KW = 640, 320, 8, 6
 ROWS, COLS = 4, 2
@@ -23,7 +25,7 @@
 NB = NS // LANES
 NG = 21
 CW = CB + WIN
-T = 6
+T = 7
 PS = 9
 PAY = 21
 CODE = 512
@@ -82,7 +84,7 @@
     return jnp.asarray(m, BF)
 
 
-def prep_kernel(ks_hbm, wy_hbm, wx_hbm, iy_hbm, ix_hbm, maps_hbm, own_ref, far_ref, sp_ref, ks_ref, wy_ref, wx_ref, iy_ref, ix_ref, maps_ref, sem):
+def prep_kernel(ks_hbm, wy_hbm, wx_hbm, iy_hbm, ix_hbm, maps_hbm, own_ref, far_ref, sp_ref, sq_ref, ks_ref, wy_ref, wx_ref, iy_ref, ix_ref, maps_ref, sem):
     k = lax.axis_index('cols')
     r = lax.axis_index('rows')
     loads = []
@@ -108,9 +110,10 @@
             ref[PAY * (b + 1) - 1:PAY * (b + 1), :] = code[b:b + 1, :]
     loads[5].wait()
     for c in range(4):
-        for i in range(2):
-            sp_ref[c, :, WIDE * i:WIDE * (i + 1)] = maps_ref[i, c, :, :WIDE]
-        sp_ref[c, :, 512:] = jnp.concatenate([maps_ref[i, c, :, WIDE:] for i in range(2)], axis=1)
+        for ref, q in ((sp_ref, slice(0, HALF)), (sq_ref, slice(HALF, QB))):
+            for i in range(2):
+                ref[c, :, WIDE * i:WIDE * (i + 1)] = maps_ref[i, c, q, :WIDE]
+            ref[c, :, 2 * WIDE:] = jnp.concatenate([maps_ref[i, c, q, WIDE:] for i in range(2)], axis=1)
 
 
 def split3(x):
@@ -192,8 +195,8 @@
 
     high = lax.broadcasted_iota(jnp.int32, (n, LANES), 1) >= HALF
     even = [total(2 * p) for p in range(11)]
-    tiles = [total(2 * p + 1) + jnp.where(high, even[p], even[p + 1]) for p in range(10)]
-    return tiles + [jnp.where(high, even[10], even[0])]
+    tiles = [total(2 * p + 1) + jnp.where(high, even[p], even[p + 1]) for p in range(TILES)]
+    return tiles + [jnp.where(high, even[TILES], even[0])]
 
 
 def own_kernel(pay_ref, out_ref, *refs):
@@ -236,11 +239,11 @@
     def copy(n, _):
         o = pl.multiple_of(n * QTR, SUB)
         gh_ref[pl.ds(pl.multiple_of(far0 + o, SUB), QTR), :] = ghost(SUB + o, QTR)
-        gh_ref[pl.ds(pl.multiple_of(own0 + o, SUB), QTR), :] = a_ref[10, pl.ds(pl.multiple_of(SUB + o, SUB), QTR), :]
+        gh_ref[pl.ds(pl.multiple_of(own0 + o, SUB), QTR), :] = a_ref[TILES, pl.ds(pl.multiple_of(SUB + o, SUB), QTR), :]
         return 0
 
     lax.fori_loop(0, CB // QTR, copy, 0)
-    for dst, add in ((own0, ghost(CW - SUB, SUB)), (own0 + CB - SUB, ghost(0, SUB)), (far0, a_ref[10, CW - SUB:, :]), (far0 + CB - SUB, a_ref[10, :SUB, :])):
+    for dst, add in ((own0, ghost(CW - SUB, SUB)), (own0 + CB - SUB, ghost(0, SUB)), (far0, a_ref[TILES, CW - SUB:, :]), (far0 + CB - SUB, a_ref[TILES, :SUB, :])):
         rows = pl.ds(pl.multiple_of(dst, SUB), SUB)
         gh_ref[rows, :] = gh_ref[rows, :] + add
 
@@ -255,8 +258,8 @@
 
 def image_kernel(*refs):
     accs = refs[:T]
-    (a_ref, pack_ref, so_ref, sx_ref, d_ref, ev_ref, eu_ref, pm_ref, out_ref,
-     tb_ref, edge_ref, g_ref, halo, sm1, sm2, sr1, sr2, hm1, hm2, hr1, hr2, s_main, s_rem, acc_m, acc_r, pieces, recvs,
+    (a_ref, pack_ref, so_ref, sx_ref, se_ref, d_ref, ev_ref, eu_ref, pm_ref, out_ref,
+     tb_ref, edge_ref, g_ref, halo, sm1, sm2, sr1, sr2, hm1, hm2, hr1, hr2, s_main, s_rem, acc_m, acc_r, sx_end, pieces, recvs, tails, recvs_t,
      halo_ss, halo_rs, swap_ss, swap_rs, red_ss, red_rs) = refs[T:]
     k = lax.axis_index('cols')
     r = lax.axis_index('rows')
@@ -276,7 +279,7 @@
 
     def put(v, tiles):
         rows = pl.ds(pl.multiple_of(v, WIN), WIN)
-        for p in range(10):
+        for p in range(TILES):
             tb_ref[p, rows, :] = tiles[p].astype(BF)
         edge_ref[rows, :] = jnp.where(high16, tiles[0], tiles[9])
 
@@ -285,7 +288,7 @@
         return 0
 
     def own_part(n, _):
-        put(own0 + WIN * n, [a_ref[p, pl.ds(pl.multiple_of(SUB + WIN * n, SUB), WIN), :] for p in range(10)])
+        put(own0 + WIN * n, [a_ref[p, pl.ds(pl.multiple_of(SUB + WIN * n, SUB), WIN), :] for p in range(TILES)])
         return 0
 
     last = CB // WIN - 1
@@ -306,8 +309,10 @@
         near_tiles = folded(accs, off, WIN)
         far_ends = folded(accs, side, SUB)
         order = (lambda v: [v, none]) if n == 0 else (lambda v: [none, v])
-        put(far0 + WIN * n, [near_tiles[p] + jnp.concatenate(order(a_ref[p, side:side + SUB, :]), axis=0) for p in range(10)])
-        put(own0 + WIN * n, [a_ref[p, off:off + WIN, :] + jnp.concatenate(order(far_ends[p]), axis=0) for p in range(10)])
+        put(far0 + WIN * n, [near_tiles[p] + jnp.concatenate(order(a_ref[p, side:side + SUB, :]), axis=0) for p in range(TILES)])
+        put(own0 + WIN * n, [a_ref[p, off:off + WIN, :] + jnp.concatenate(order(far_ends[p]), axis=0) for p in range(TILES)])
+
+    end_copy = remote(se_ref, sx_end, halo_ss, halo_rs, 2, {'rows': across})
 
     def to_rows(row0, n, t0, t1):
         a = jnp.concatenate([t0, t1], axis=1)
@@ -360,26 +365,13 @@
 
     for j, ref in enumerate((so_ref, sx_ref)):
         for cp in range(2):
-            s_main[j, 0, cp], s_main[j, 1, cp] = turn(jnp.concatenate([ref[2 * cp + core, :HALF, :], ref[2 * cp + 1 - core, :HALF, :]], axis=0))
-    tails = [[ref[c, HALF:, :] for c in range(4)] for ref in (so_ref, sx_ref)]
-    s_rem[0], s_rem[1] = turn(jnp.concatenate([jnp.where(x == j, tails[0][c], tails[1][c]) for j in range(2) for c in range(4)], axis=0))
+            s_main[j, 0, cp], s_main[j, 1, cp] = turn(jnp.concatenate([ref[2 * cp + core], ref[2 * cp + 1 - core]], axis=0))
     d8 = jnp.broadcast_to(jnp.concatenate([d_ref[...][None, :], jnp.zeros((1, HALF), F32)], axis=1), (SUB, N_IMG + HALF))
     dq = d8
     for j in range(1, ROWS):
         dq = jnp.where(r == j, pltpu.roll(d8, N_IMG + HALF - QB * j, axis=1), dq)
     dp = jnp.where(k == 0, d8, pltpu.roll(d8, N_IMG + HALF - PB, axis=1))[:, :2 * LANES]
     dd = jnp.concatenate([dp] * WIN, axis=0).T[:PB] * dq[:1, :LANES]
-
-    for cp in swaps:
-        cp.wait_recv()
-    n0 = 4 * GROUPS[0][1]
-
-    def block_of(grp, j):
-        return jnp.concatenate([hms[grp][(x + j) % 2, cp].reshape(4 * GROUPS[grp][1], LANES) for cp in range(2)], axis=1)
-
-    for j in range(2):
-        acc_m[j] = jnp.dot(eu_ref[x, :, :n0], block_of(0, j), preferred_element_type=F32)
-    acc_r[...] = jnp.dot(eu_ref[x, :, :n0], hrs[0][...].reshape(n0, LANES), preferred_element_type=F32)
 
     for h in halos:
         h.wait()
@@ -397,6 +389,18 @@
     low = lane < HALF
     to_rows(4 * LANES, QTR, jnp.concatenate(t0s, axis=0), jnp.concatenate(t9s, axis=0))
     columns(1)
+
+    for cp in swaps[:2]:
+        cp.wait_recv()
+    n0 = 4 * GROUPS[0][1]
+
+    def block_of(grp, j):
+        return jnp.concatenate([hms[grp][(x + j) % 2, cp].reshape(4 * GROUPS[grp][1], LANES) for cp in range(2)], axis=1)
+
+    for j in range(2):
+        acc_m[j] = jnp.dot(eu_ref[x, :, :n0], block_of(0, j), preferred_element_type=F32)
+    acc_r[...] = jnp.dot(eu_ref[x, :, :n0], hrs[0][...].reshape(n0, LANES), preferred_element_type=F32)
+
     for cp in swaps[2:]:
         cp.wait_recv()
 
@@ -407,20 +411,7 @@
 
     quarter = lax.broadcasted_iota(jnp.int32, (PB // 4, LANES), 1) >> 5
 
-    def rest(half):
-        i_re, i_im = rows_dft(half, acc_r, hrs[1][...].reshape(4 * GROUPS[1][1], LANES))
-        rows = pl.ds(pl.multiple_of(half * PB, SUB), PB)
-        s_re, s_im = s_rem[0, rows, :], s_rem[1, rows, :]
-
-        def fold(v):
-            v = v + pltpu.roll(v, LANES - QTR, axis=1)
-            return v + pltpu.roll(v, LANES - WIN, axis=1)
-
-        re, im = fold(s_re * i_re + s_im * i_im), fold(s_re * i_im - s_im * i_re)
-        return jnp.where(lane & (HALF - 1) < WIN, re, pltpu.roll(im, WIN, axis=1))
-
-    def piece(half, j, tail):
-        dp = (x + j) % 2
+    def piece(half, j):
         i_re, i_im = rows_dft(half, acc_m.at[j], block_of(1, j))
         rows = pl.ds(pl.multiple_of(half * PB, SUB), PB)
         re, im = None, None
@@ -430,25 +421,48 @@
             a = s_re * i_re[:, cols] + s_im * i_im[:, cols]
             b = s_re * i_im[:, cols] - s_im * i_re[:, cols]
             re, im = (a, b) if re is None else (re + a, im + b)
-        main = jnp.where(low, re + pltpu.roll(re, HALF, axis=1), im + pltpu.roll(im, HALF, axis=1))
-        y = jnp.where(dp == 0, tail, pltpu.roll(tail, HALF, axis=1))
-        out = y[:PB // 4]
-        for g in range(1, 4):
-            out = jnp.where(quarter == g, pltpu.roll(y[PB // 4 * g:PB // 4 * (g + 1)], QTR * g, axis=1), out)
-        return main, out
+        return jnp.where(low, re + pltpu.roll(re, HALF, axis=1), im + pltpu.roll(im, HALF, axis=1))
+
+    def rest(half):
+        i_re, i_im = rows_dft(half, acc_r, hrs[1][...].reshape(4 * GROUPS[1][1], LANES))
+        rows = pl.ds(pl.multiple_of(half * PB, SUB), PB)
+        s_re, s_im = s_rem[0, rows, :], s_rem[1, rows, :]
+
+        def fold(v):
+            v = v + pltpu.roll(v, LANES - QTR, axis=1)
+            return v + pltpu.roll(v, LANES - WIN, axis=1)
+
+        re, im = fold(s_re * i_re + s_im * i_im), fold(s_re * i_im - s_im * i_re)
+        both = jnp.where(lane & (HALF - 1) < WIN, re, pltpu.roll(im, WIN, axis=1))
+        outs = []
+        for dp in range(2):
+            out = None
+            for g in range(4):
+                v = both[PB // 4 * g:PB // 4 * (g + 1)]
+                if g + 2 * dp:
+                    v = pltpu.roll(v, (QTR * g + HALF * dp) % LANES, axis=1)
+                out = v if out is None else jnp.where(quarter == g, v, out)
+            outs.append(out)
+        return jnp.where(x == 0, outs[0], outs[1]), jnp.where(x == 0, outs[1], outs[0])
 
     sends = []
-    far_tail = rest(1 - k)
     for i, (half, j) in enumerate(((1 - k, 1), (1 - k, 0), (k, 1))):
-        if i == 2:
-            own_tail = rest(k)
-        pieces[i, :PB], pieces[i, PB:] = piece(half, j, own_tail if i == 2 else far_tail)
+        pieces[i] = piece(half, j)
         sends.append(remote(pieces.at[i], recvs.at[i], red_ss, red_rs, i, homes[i]))
-    main, rem = piece(k, 0, own_tail)
-    for i in (2, 1, 0):
+    end_copy.wait_recv()
+    s_rem[0], s_rem[1] = turn(jnp.concatenate([jnp.where(x == j, se_ref[c], sx_end[c]) for j in range(2) for c in range(4)], axis=0))
+    tails[1], tails[0] = rest(1 - k)
+    for i in range(2):
+        sends.append(remote(tails.at[i], recvs_t.at[i], red_ss, red_rs, 3 + i, homes[i]))
+    rem, tails[2] = rest(k)
+    sends.append(remote(tails.at[2], recvs_t.at[2], red_ss, red_rs, 5, homes[2]))
+    main = piece(k, 0)
+    for i in (1, 0, 2):
         sends[i].wait_recv()
-        main = main + recvs[i, :PB]
-        rem = rem + recvs[i, PB:]
+        main = main + recvs[i]
+    for i in (1, 0, 2):
+        sends[3 + i].wait_recv()
+        rem = rem + recvs_t[i]
     for o in range(2):
         m = pltpu.roll(main, HALF, axis=1) if o else main
         for j in range(4):
@@ -456,7 +470,7 @@
             tail = pltpu.roll(rem, (HALF - QTR * j - WIN * o) % LANES, axis=1)
             out_ref[o, rows, :] = (jnp.where(low[rows], m[rows], tail) * dd[rows])[:, :QB]
 
-    for cp in sends + swaps:
+    for cp in sends + swaps + [end_copy]:
         cp.wait_send()
 
 
@@ -470,10 +484,10 @@
     big = 6 * MIB
 
     def local_fn(kspace, wts_y, wts_x, idx_y, idx_x, coil_maps, deapod):
-        own, far, maps = pl.pallas_call(
+        own, far, maps, maps_end = pl.pallas_call(
             prep_kernel,
-            out_shape=[jax.ShapeDtypeStruct((PAY * NB, LANES), F32)] * 2 + [jax.ShapeDtypeStruct((4, QB, N_GRID), F32)],
-            in_specs=[hbm] * 6, out_specs=[vm] * 3, name='prep',
+            out_shape=[jax.ShapeDtypeStruct((PAY * NB, LANES), F32)] * 2 + [jax.ShapeDtypeStruct((4, n, N_GRID), F32) for n in (HALF, WIN)],
+            in_specs=[hbm] * 6, out_specs=[vm] * 4, name='prep',
             scratch_shapes=[VMEM((2, SUB, NS), F32), VMEM((KW, NS), F32), VMEM((KW, NS), F32), VMEM((NB, LANES), jnp.int32), VMEM((NB, LANES), jnp.int32), VMEM((2, 4, QB, N_IMG), F32), pltpu.SemaphoreType.DMA((6,))],
             compiler_params=pltpu.CompilerParams(vmem_limit_bytes=SUB * MIB),
         )(*[pltpu.with_memory_space_constraint(v, pltpu.HBM) for v in (kspace, wts_y, wts_x, idx_y.reshape(NB, LANES), idx_x.reshape(NB, LANES), jnp.swapaxes(coil_maps, 2, 3))])
@@ -481,14 +495,14 @@
         half, *accs = pl.pallas_call(
             own_kernel, out_shape=[jax.ShapeDtypeStruct((11, CW, LANES), F32)] + acc_shape, in_specs=[vm], out_specs=[vm] * (T + 1),
             scratch_shapes=spread_scratch, compiler_params=pltpu.CompilerParams(vmem_limit_bytes=big), name='spread_own',
-            cost_estimate=pl.CostEstimate(flops=4 * 10 ** 9, bytes_accessed=2 * 10 ** 6, transcendentals=0),
+            cost_estimate=pl.CostEstimate(flops=GIGA, bytes_accessed=4 * MIB, transcendentals=0),
         )(own)
         *accs, pack = pl.pallas_call(
             far_kernel, out_shape=acc_shape + [jax.ShapeDtypeStruct((2, LANES, LANES), F32)],
             in_specs=[vm] * (T + 2), out_specs=[vm] * (T + 1), scratch_shapes=[VMEM((N_GRID, LANES), F32)] + spread_scratch,
             input_output_aliases={i + 2: i for i in range(T)},
             compiler_params=pltpu.CompilerParams(vmem_limit_bytes=big), name='spread_far',
-            cost_estimate=pl.CostEstimate(flops=4 * 10 ** 9, bytes_accessed=4 * 10 ** 6, transcendentals=0),
+            cost_estimate=pl.CostEstimate(flops=GIGA, bytes_accessed=4 * MIB, transcendentals=0),
         )(far_in, half, *accs)
         maps_x = lax.ppermute(maps, 'rows', [(i, (i + 2) % ROWS) for i in range(ROWS)])
         dma = pltpu.SemaphoreType.DMA
@@ -496,14 +510,15 @@
         full_bufs = [VMEM((2, 2, 2, 2, n, LANES), BF) for _, n in GROUPS] + [VMEM((2, 2, n, LANES), BF) for _, n in GROUPS]
         return pl.pallas_call(
             image_kernel,
-            out_shape=jax.ShapeDtypeStruct((2, PB, QB), F32), in_specs=[vm] * (T + 8), out_specs=vm,
-            scratch_shapes=[VMEM((10, N_GRID, LANES), BF), VMEM((N_GRID, LANES), F32), VMEM((4 * RB, 2 * N_GRID), BF), VMEM((2, LANES, LANES), F32)] + half_bufs + full_bufs + [
+            out_shape=jax.ShapeDtypeStruct((2, PB, QB), F32), in_specs=[vm] * (T + 9), out_specs=vm,
+            scratch_shapes=[VMEM((TILES, N_GRID, LANES), BF), VMEM((N_GRID, LANES), F32), VMEM((4 * RB, 2 * N_GRID), BF), VMEM((2, LANES, LANES), F32)] + half_bufs + full_bufs + [
                 VMEM((2, 2, 2, N_IMG, LANES), F32), VMEM((2, N_IMG, LANES), F32),
-                VMEM((2, 2 * N_IMG, 2 * LANES), F32), VMEM((2 * N_IMG, LANES), F32), VMEM((3, PB + PB // 4, LANES), F32), VMEM((3, PB + PB // 4, LANES), F32),
-                dma((2,)), dma((2,)), dma((4,)), dma((4,)), dma((3,)), dma((3,)),
+                VMEM((2, 2 * N_IMG, 2 * LANES), F32), VMEM((2 * N_IMG, LANES), F32), VMEM((4, WIN, N_GRID), F32),
+                VMEM((3, PB, LANES), F32), VMEM((3, PB, LANES), F32), VMEM((3, PB // 4, LANES), F32), VMEM((3, PB // 4, LANES), F32),
+                dma((3,)), dma((3,)), dma((4,)), dma((4,)), dma((6,)), dma((6,)),
             ],
-            compiler_params=pltpu.CompilerParams(vmem_limit_bytes=20 * MIB, collective_id=0, has_side_effects=True), name='image',
-        )(*accs, half, pack, maps, maps_x, deapod, col_dft(), row_dft(), unmix())
+            compiler_params=pltpu.CompilerParams(vmem_limit_bytes=11 * MIB, collective_id=0, has_side_effects=True), name='image',
+        )(*accs, half, pack, maps, maps_x, maps_end, deapod, col_dft(), row_dft(), unmix())
 
     return jax.shard_map(
         local_fn,

time: 40.1 us -> 38.7 us (0.965)
  Pallas kernels: 34.2 us -> 32.8 us
    ppermute x1, starting transfers between devices: 3.36 us -> 1.49 us  [local_fn(): lax.ppermute(maps, 'rows', [(i, (i + 2) % ROWS) for i in range(ROWS)])]
    ppermute x1, starting transfers between devices: 1.52 us -> 3.39 us  [local_fn(): far_in = lax.ppermute(far, 'cols', [(0, 1), (1, 0)])]
    pallas_call x1, Pallas kernels: 15.9 us -> 14.3 us  [local_fn(): pl.pallas_call(image_kernel, out_shape=jax.ShapeDtypeStruct((2, PB, QB),...]
    pallas_call x1, Pallas kernels: 9.68 us -> 10.2 us  [local_fn(): pl.pallas_call(own_kernel, out_shape=[jax.ShapeDtypeStruct((11, CW, LANES...]
  transfers between devices with their start and end apart: 2 -> 2, of which waited for: 1 -> 0; matrix products, arithmetic and copies ran while one was open for 0% -> 0% of each run, Pallas kernels for 42% -> 44%
where the time goes in v7:
time: 38.7 us; the launch traced here: 38.5 us
  Pallas kernels  32.8 us (85%)
  starting transfers between devices  4.88 us (13%)
  local copies, waits for them, and re-layouts  0.7 us (2%)
    pallas_call x1, Pallas kernels, local_fn(): pl.pallas_call(image_kernel, out_shape=jax.ShapeDtypeStruct((2, PB, QB),...  14.3 us
    pallas_call x1, Pallas kernels, local_fn(): pl.pallas_call(own_kernel, out_shape=[jax.ShapeDtypeStruct((11, CW, LANES...  10.2 us
    pallas_call x1, Pallas kernels, local_fn(): pl.pallas_call(far_kernel, out_shape=acc_shape + [jax.ShapeDtypeStruct((2...  6.69 us
    ppermute x1, starting transfers between devices, local_fn(): far_in = lax.ppermute(far, 'cols', [(0, 1), (1, 0)])  3.39 us
    pallas_call x1, Pallas kernels, local_fn(): pl.pallas_call(prep_kernel, out_shape=[jax.ShapeDtypeStruct((PAY * NB, LA...  1.65 us
    ppermute x1, starting transfers between devices, local_fn(): lax.ppermute(maps, 'rows', [(i, (i + 2) % ROWS) for i in range(ROWS)])  1.49 us
  transfers between devices with their start and end apart: 2, of which 0 were waited for; matrix products, arithmetic and copies ran while one was open for 0% of the time, Pallas kernels for 44%

profile of v7, /device:TPU:0, one launch (start us, length us, event | category | flops | bytes accessed | tf_op | source)
XLA Modules:
  0.0 38.5 jit_solution(2061678040468137783)
XLA Ops:
  0.0 1.6 %prep.1 = (f32[672,128]{1,0:T(8,128)S(1)}, f32[672,128]{1,0:T(8,128)S(1)}, f32[4,64,640]{2,1,0:T(8,128)S(1)}, f32[4,16,640]{2,1,0:T(8,128)S(1)}) custom-call(f32[2,8,4096]{2,1,0:T(8,128)} %ks_hbm.1, f32[6,4096]{1,0:T(8,128)} %wy_hbm.1, f32[6,4096]{1,0:T(8,128)} %wx_hbm.1, s32[32,128]{1,0:T(8,128)} %bitcast.4, s32[32,128]{1,0:T(8,128)} %bitcast.5, ...), custom_call_target="tpu_custom_call" | custom-call | tf_op jit(solution)/shard_map/prep/pallas_call | solution.py:487
  1.7 3.4 %collective-permute-start = (f32[672,128]{1,0:T(8,128)S(1)}, f32[672,128]{1,0:T(8,128)S(1)}, u32[]{:S(2)}, u32[]{:S(2)}) collective-permute-start(f32[672,128]{1,0:T(8,128)S(1)} %get-tuple-element.25), channel_id=1, source_target_pairs={{0,4},{4,0},{1,5},{5,1},{2,6},{6,2},{3,7},{7,3}} | collective-permute-start | bytes 1032200 | tf_op jit(solution)/shard_map/ppermute | solution.py:494
  5.0 1.5 %collective-permute-start.1 = (f32[4,64,640]{2,1,0:T(8,128)S(1)}, f32[4,64,640]{2,1,0:T(8,128)S(1)}, u32[]{:S(2)}, u32[]{:S(2)}) collective-permute-start(f32[4,64,640]{2,1,0:T(8,128)S(1)} %get-tuple-element.43.refs_9_), channel_id=1, source_target_pairs={{0,2},{1,3},{2,0},{3,1},{4,6},{5,7},{6,4},{7,5}} | collective-permute-start | bytes 1966088 | tf_op jit(solution)/shard_map/ppermute | solution.py:507
  6.5 10.2 %spread_own.1 = (f32[11,336,128]{2,1,0:T(8,128)S(1)}, f32[7056,128]{1,0:T(8,128)S(1)}, f32[7056,128]{1,0:T(8,128)S(1)}, f32[7056,128]{1,0:T(8,128)S(1)}, f32[705...) custom-call(f32[672,128]{1,0:T(8,128)S(1)} %get-tuple-element.26.pay_ref), custom_call_target="tpu_custom_call" | custom-call | flops 4194304000 | bytes 4194304 | tf_op jit(solution)/shard_map/spread_own/pallas_call | solution.py:495
  16.7 0.0 collective-permute-done.pay_ref
  16.7 0.0 copy-start
  16.8 0.0 copy-start.1
  16.8 0.0 copy-start.2
  16.8 0.0 copy-start.3
  16.8 6.7 %spread_far.1 = (f32[7056,128]{1,0:T(8,128)S(1)}, f32[7056,128]{1,0:T(8,128)S(1)}, f32[7056,128]{1,0:T(8,128)S(1)}, f32[7056,128]{1,0:T(8,128)S(1)}, f32[7056,12...) custom-call(f32[672,128]{1,0:T(8,128)S(1)} %collective-permute-done., ...), custom_call_target="tpu_custom_call", output_to_operand_aliasing={{0}: (2, {}), {1}: (3, {}), {2}: (4, {}), {3}: (5, {}), {4}... | custom-call | flops 4194304000 | bytes 4194304 | tf_op jit(solution)/shard_map/spread_far/pallas_call | solution.py:500
  23.5 0.0 collective-permute-done.1.refs_10_
  23.5 0.0 copy-done
  23.5 0.0 copy-done.1
  23.5 0.0 copy-done.2
  23.5 0.0 copy-done.3
  23.5 14.3 %image.1 = f32[2,160,80]{2,1,0:T(8,128)S(1)} custom-call(f32[7056,128]{1,0:T(8,128)S(1)} %get-tuple-element.35.refs_0_, f32[7056,128]{1,0:T(8,128)S(1)} %get-tuple-element.36.refs_1_, f32[7056,128]{1,0:T(8,128)S(1)} %get-tuple-element.37.refs_2_, f32[7056,128]{1,0:T(8,128)S(1)} %get-tuple-element.38.refs_3_, f32[7056,128]{1,0:T(8,128)S(1)} %get-tuple-element.39.refs_4_, ...), custom_call_target="tpu_custom_call" | custom-call | tf_op jit(solution)/shard_map/image/pallas_call | solution.py:511
  37.8 0.7 %copy.26 = f32[2,160,80]{2,1,0:T(8,128)} copy(f32[2,160,80]{2,1,0:T(8,128)S(1)} %image.1) | data formatting | bytes 204800
Async XLA Ops:
  1.7 15.1 %collective-permute-start = (f32[672,128]{1,0:T(8,128)S(1)}, f32[672,128]{1,0:T(8,128)S(1)}, u32[]{:S(2)}, u32[]{:S(2)}) collective-permute-start(f32[672,128]{1,0:T(8,128)S(1)} %get-tuple-element.25), channel_id=1, source_target_pairs={{0,4},{4,0},{1,5},{5,1},{2,6},{6,2},{3,7},{7,3}} | collective-permute-start | bytes 1032200 | tf_op jit(solution)/shard_map/ppermute | solution.py:494
  5.0 18.4 %collective-permute-start.1 = (f32[4,64,640]{2,1,0:T(8,128)S(1)}, f32[4,64,640]{2,1,0:T(8,128)S(1)}, u32[]{:S(2)}, u32[]{:S(2)}) collective-permute-start(f32[4,64,640]{2,1,0:T(8,128)S(1)} %get-tuple-element.43.refs_9_), channel_id=1, source_target_pairs={{0,2},{1,3},{2,0},{3,1},{4,6},{5,7},{6,4},{7,5}} | collective-permute-start | bytes 1966088 | tf_op jit(solution)/shard_map/ppermute | solution.py:507
  16.7 6.8 %copy-start = (bf16[1280,640]{1,0:T(8,128)(2,1)S(1)}, bf16[1280,640]{1,0:T(8,128)(2,1)}, u32[]{:S(2)}) copy-start(bf16[1280,640]{1,0:T(8,128)(2,1)} %constant.6.clone.refs_13_) | copy-start | bytes 4915204
  16.8 6.8 %copy-start.1 = (bf16[2,640,640]{2,1,0:T(8,128)(2,1)S(1)}, bf16[2,640,640]{2,1,0:T(8,128)(2,1)}, u32[]{:S(2)}) copy-start(bf16[2,640,640]{2,1,0:T(8,128)(2,1)} %constant.7.clone.refs_14_) | copy-start | bytes 4915204
  16.8 6.8 %copy-start.2 = (bf16[256,256]{1,0:T(8,128)(2,1)S(1)}, bf16[256,256]{1,0:T(8,128)(2,1)}, u32[]{:S(2)}) copy-start(bf16[256,256]{1,0:T(8,128)(2,1)} %constant.8.clone.refs_15_) | copy-start | bytes 393220
  16.8 6.7 %copy-start.3 = (f32[320]{0:T(512)S(1)}, f32[320]{0:T(512)}, u32[]{:S(2)}) copy-start(f32[320]{0:T(512)} %refs_12_.1) | copy-start | bytes 3844

commit v8 on v7

--- a/solution.py
+++ b/solution.py
@@ -25,7 +25,7 @@
 NB = NS // LANES
 NG = 21
 CW = CB + WIN
-T = 7
+T = 6
 PS = 9
 PAY = 21
 CODE = 512
@@ -150,9 +150,10 @@
                     vs[k][pl.ds(SUB * PS * g + 2 * bp + c, SUB, stride=PS), :] = v[SUB * g:SUB * g + SUB, :]
 
     def add_tiles(blk, k):
+        row = base_ref.at[blk]
         for j in range(LANES):
             acc = accs[j % T]
-            b = base_ref[blk, j]
+            b = row[j]
             acc[pl.ds(b, SUB), :] = acc[pl.ds(b, SUB), :] + vs[k][PS * j:PS * j + SUB, :]
 
     code = jnp.concatenate([pay_ref[PAY * (b + 1) - 1:PAY * (b + 1), :] for b in range(NB)], axis=0).astype(jnp.int32)
@@ -267,7 +268,7 @@
     near = r + 1 - 2 * core
     across = (r + 2) % 4
     prev, nxt = (r + 3) % 4, (r + 1) % 4
-    homes = ({'rows': across, 'cols': 1 - k}, {'cols': 1 - k}, {'rows': across})
+    homes = ({'rows': across, 'cols': 1 - k}, {'rows': across}, {'cols': 1 - k})
 
     barrier = pltpu.get_barrier_semaphore()
     for dev in ({'rows': prev}, {'rows': nxt}) + homes:
@@ -359,20 +360,6 @@
 
     columns(0)
 
-    def turn(rows):
-        t = [rows[:, LANES * i:LANES * (i + 1)].T for i in range(5)]
-        return [jnp.concatenate([t[2 * i], t[2 * i + 1], t[4][HALF * i:HALF * (i + 1)]], axis=0) for i in range(2)]
-
-    for j, ref in enumerate((so_ref, sx_ref)):
-        for cp in range(2):
-            s_main[j, 0, cp], s_main[j, 1, cp] = turn(jnp.concatenate([ref[2 * cp + core], ref[2 * cp + 1 - core]], axis=0))
-    d8 = jnp.broadcast_to(jnp.concatenate([d_ref[...][None, :], jnp.zeros((1, HALF), F32)], axis=1), (SUB, N_IMG + HALF))
-    dq = d8
-    for j in range(1, ROWS):
-        dq = jnp.where(r == j, pltpu.roll(d8, N_IMG + HALF - QB * j, axis=1), dq)
-    dp = jnp.where(k == 0, d8, pltpu.roll(d8, N_IMG + HALF - PB, axis=1))[:, :2 * LANES]
-    dd = jnp.concatenate([dp] * WIN, axis=0).T[:PB] * dq[:1, :LANES]
-
     for h in halos:
         h.wait()
     lane = lax.broadcasted_iota(jnp.int32, (LANES, LANES), 1)
@@ -390,6 +377,11 @@
     to_rows(4 * LANES, QTR, jnp.concatenate(t0s, axis=0), jnp.concatenate(t9s, axis=0))
     columns(1)
 
+    def turn(rows):
+        t = [rows[:, LANES * i:LANES * (i + 1)].T for i in range(5)]
+        return [jnp.concatenate([t[2 * i], t[2 * i + 1], t[4][HALF * i:HALF * (i + 1)]], axis=0) for i in range(2)]
+
+
     for cp in swaps[:2]:
         cp.wait_recv()
     n0 = 4 * GROUPS[0][1]
@@ -397,8 +389,10 @@
     def block_of(grp, j):
         return jnp.concatenate([hms[grp][(x + j) % 2, cp].reshape(4 * GROUPS[grp][1], LANES) for cp in range(2)], axis=1)
 
-    for j in range(2):
+    for j, ref in ((1, sx_ref), (0, so_ref)):
         acc_m[j] = jnp.dot(eu_ref[x, :, :n0], block_of(0, j), preferred_element_type=F32)
+        for cp in range(2):
+            s_main[j, 0, cp], s_main[j, 1, cp] = turn(jnp.concatenate([ref[2 * cp + core], ref[2 * cp + 1 - core]], axis=0))
     acc_r[...] = jnp.dot(eu_ref[x, :, :n0], hrs[0][...].reshape(n0, LANES), preferred_element_type=F32)
 
     for cp in swaps[2:]:
@@ -446,21 +440,28 @@
         return jnp.where(x == 0, outs[0], outs[1]), jnp.where(x == 0, outs[1], outs[0])
 
     sends = []
-    for i, (half, j) in enumerate(((1 - k, 1), (1 - k, 0), (k, 1))):
+    for i, (half, j) in enumerate(((1 - k, 1), (k, 1), (1 - k, 0))):
         pieces[i] = piece(half, j)
         sends.append(remote(pieces.at[i], recvs.at[i], red_ss, red_rs, i, homes[i]))
     end_copy.wait_recv()
     s_rem[0], s_rem[1] = turn(jnp.concatenate([jnp.where(x == j, se_ref[c], sx_end[c]) for j in range(2) for c in range(4)], axis=0))
-    tails[1], tails[0] = rest(1 - k)
-    for i in range(2):
+    tails[2], tails[0] = rest(1 - k)
+    sends.append(remote(tails.at[0], recvs_t.at[0], red_ss, red_rs, 3, homes[0]))
+    rem, tails[1] = rest(k)
+    for i in (1, 2):
         sends.append(remote(tails.at[i], recvs_t.at[i], red_ss, red_rs, 3 + i, homes[i]))
-    rem, tails[2] = rest(k)
-    sends.append(remote(tails.at[2], recvs_t.at[2], red_ss, red_rs, 5, homes[2]))
     main = piece(k, 0)
-    for i in (1, 0, 2):
+    d8 = jnp.broadcast_to(jnp.concatenate([d_ref[...][None, :], jnp.zeros((1, HALF), F32)], axis=1), (SUB, N_IMG + HALF))
+    dq = d8
+    for j in range(1, ROWS):
+        dq = jnp.where(r == j, pltpu.roll(d8, N_IMG + HALF - QB * j, axis=1), dq)
+    dp = jnp.where(k == 0, d8, pltpu.roll(d8, N_IMG + HALF - PB, axis=1))[:, :2 * LANES]
+    dd = jnp.concatenate([dp] * WIN, axis=0).T[:PB] * dq[:1, :LANES]
+
+    for i in (2, 0, 1):
         sends[i].wait_recv()
         main = main + recvs[i]
-    for i in (1, 0, 2):
+    for i in (2, 0, 1):
         sends[3 + i].wait_recv()
         rem = rem + recvs_t[i]
     for o in range(2):

time: 38.7 us -> 38.2 us (0.987)
  Pallas kernels: 32.8 us -> 32.3 us
    pallas_call x1, Pallas kernels: 10.2 us -> 9.58 us  [local_fn(): pl.pallas_call(own_kernel, out_shape=[jax.ShapeDtypeStruct((11, CW, LANES...]
  transfers between devices with their start and end apart: 2 -> 2, of which waited for: 0 -> 0; matrix products, arithmetic and copies ran while one was open for 0% -> 0% of each run, Pallas kernels for 44% -> 43%
where the time goes in v8:
time: 38.2 us; the launch traced here: 38 us
  Pallas kernels  32.3 us (85%)
  starting transfers between devices  4.88 us (13%)
  local copies, waits for them, and re-layouts  0.7 us (2%)
    pallas_call x1, Pallas kernels, local_fn(): pl.pallas_call(image_kernel, out_shape=jax.ShapeDtypeStruct((2, PB, QB),...  14.3 us
    pallas_call x1, Pallas kernels, local_fn(): pl.pallas_call(own_kernel, out_shape=[jax.ShapeDtypeStruct((11, CW, LANES...  9.58 us
    pallas_call x1, Pallas kernels, local_fn(): pl.pallas_call(far_kernel, out_shape=acc_shape + [jax.ShapeDtypeStruct((2...  6.8 us
    ppermute x1, starting transfers between devices, local_fn(): far_in = lax.ppermute(far, 'cols', [(0, 1), (1, 0)])  3.39 us
    pallas_call x1, Pallas kernels, local_fn(): pl.pallas_call(prep_kernel, out_shape=[jax.ShapeDtypeStruct((PAY * NB, LA...  1.65 us
    ppermute x1, starting transfers between devices, local_fn(): lax.ppermute(maps, 'rows', [(i, (i + 2) % ROWS) for i in range(ROWS)])  1.49 us
  transfers between devices with their start and end apart: 2, of which 0 were waited for; matrix products, arithmetic and copies ran while one was open for 0% of the time, Pallas kernels for 43%

profile of v8, /device:TPU:0, one launch (start us, length us, event | category | flops | bytes accessed | tf_op | source)
XLA Modules:
  0.0 38.0 jit_solution(14359483338433314652)
XLA Ops:
  0.0 1.6 %prep.1 = (f32[672,128]{1,0:T(8,128)S(1)}, f32[672,128]{1,0:T(8,128)S(1)}, f32[4,64,640]{2,1,0:T(8,128)S(1)}, f32[4,16,640]{2,1,0:T(8,128)S(1)}) custom-call(f32[2,8,4096]{2,1,0:T(8,128)} %ks_hbm.1, f32[6,4096]{1,0:T(8,128)} %wy_hbm.1, f32[6,4096]{1,0:T(8,128)} %wx_hbm.1, s32[32,128]{1,0:T(8,128)} %bitcast.4, s32[32,128]{1,0:T(8,128)} %bitcast.5, ...), custom_call_target="tpu_custom_call" | custom-call | tf_op jit(solution)/shard_map/prep/pallas_call | solution.py:488
  1.7 3.4 %collective-permute-start = (f32[672,128]{1,0:T(8,128)S(1)}, f32[672,128]{1,0:T(8,128)S(1)}, u32[]{:S(2)}, u32[]{:S(2)}) collective-permute-start(f32[672,128]{1,0:T(8,128)S(1)} %get-tuple-element.23), channel_id=1, source_target_pairs={{0,4},{4,0},{1,5},{5,1},{2,6},{6,2},{3,7},{7,3}} | collective-permute-start | bytes 1032200 | tf_op jit(solution)/shard_map/ppermute | solution.py:495
  5.0 1.5 %collective-permute-start.1 = (f32[4,64,640]{2,1,0:T(8,128)S(1)}, f32[4,64,640]{2,1,0:T(8,128)S(1)}, u32[]{:S(2)}, u32[]{:S(2)}) collective-permute-start(f32[4,64,640]{2,1,0:T(8,128)S(1)} %get-tuple-element.39.refs_8_), channel_id=1, source_target_pairs={{0,2},{1,3},{2,0},{3,1},{4,6},{5,7},{6,4},{7,5}} | collective-permute-start | bytes 1966088 | tf_op jit(solution)/shard_map/ppermute | solution.py:508
  6.5 9.6 %spread_own.1 = (f32[11,336,128]{2,1,0:T(8,128)S(1)}, f32[7056,128]{1,0:T(8,128)S(1)}, f32[7056,128]{1,0:T(8,128)S(1)}, f32[7056,128]{1,0:T(8,128)S(1)}, f32[705...) custom-call(f32[672,128]{1,0:T(8,128)S(1)} %get-tuple-element.24.pay_ref), custom_call_target="tpu_custom_call" | custom-call | flops 4194304000 | bytes 4194304 | tf_op jit(solution)/shard_map/spread_own/pallas_call | solution.py:496
  16.1 0.0 collective-permute-done.pay_ref
  16.1 0.0 copy-start
  16.1 0.0 copy-start.1
  16.2 0.0 copy-start.2
  16.2 0.0 copy-start.3
  16.2 6.8 %spread_far.1 = (f32[7056,128]{1,0:T(8,128)S(1)}, f32[7056,128]{1,0:T(8,128)S(1)}, f32[7056,128]{1,0:T(8,128)S(1)}, f32[7056,128]{1,0:T(8,128)S(1)}, f32[7056,12...) custom-call(f32[672,128]{1,0:T(8,128)S(1)} %collective-permute-done., ...), custom_call_target="tpu_custom_call", output_to_operand_aliasing={{0}: (2, {}), {1}: (3, {}), {2}: (4, {}), {3}: (5, {}), {4}... | custom-call | flops 4194304000 | bytes 4194304 | tf_op jit(solution)/shard_map/spread_far/pallas_call | solution.py:501
  23.0 0.0 collective-permute-done.1.refs_9_
  23.0 0.0 copy-done
  23.0 0.0 copy-done.1
  23.0 0.0 copy-done.2
  23.0 0.0 copy-done.3
  23.0 14.3 %image.1 = f32[2,160,80]{2,1,0:T(8,128)S(1)} custom-call(f32[7056,128]{1,0:T(8,128)S(1)} %get-tuple-element.32.refs_0_, f32[7056,128]{1,0:T(8,128)S(1)} %get-tuple-element.33.refs_1_, f32[7056,128]{1,0:T(8,128)S(1)} %get-tuple-element.34.refs_2_, f32[7056,128]{1,0:T(8,128)S(1)} %get-tuple-element.35.refs_3_, f32[7056,128]{1,0:T(8,128)S(1)} %get-tuple-element.36.refs_4_, ...), custom_call_target="tpu_custom_call" | custom-call | tf_op jit(solution)/shard_map/image/pallas_call | solution.py:512
  37.3 0.7 %copy.24 = f32[2,160,80]{2,1,0:T(8,128)} copy(f32[2,160,80]{2,1,0:T(8,128)S(1)} %image.1) | data formatting | bytes 204800
Async XLA Ops:
  1.7 14.5 %collective-permute-start = (f32[672,128]{1,0:T(8,128)S(1)}, f32[672,128]{1,0:T(8,128)S(1)}, u32[]{:S(2)}, u32[]{:S(2)}) collective-permute-start(f32[672,128]{1,0:T(8,128)S(1)} %get-tuple-element.23), channel_id=1, source_target_pairs={{0,4},{4,0},{1,5},{5,1},{2,6},{6,2},{3,7},{7,3}} | collective-permute-start | bytes 1032200 | tf_op jit(solution)/shard_map/ppermute | solution.py:495
  5.0 17.9 %collective-permute-start.1 = (f32[4,64,640]{2,1,0:T(8,128)S(1)}, f32[4,64,640]{2,1,0:T(8,128)S(1)}, u32[]{:S(2)}, u32[]{:S(2)}) collective-permute-start(f32[4,64,640]{2,1,0:T(8,128)S(1)} %get-tuple-element.39.refs_8_), channel_id=1, source_target_pairs={{0,2},{1,3},{2,0},{3,1},{4,6},{5,7},{6,4},{7,5}} | collective-permute-start | bytes 1966088 | tf_op jit(solution)/shard_map/ppermute | solution.py:508
  16.1 6.9 %copy-start = (bf16[1280,640]{1,0:T(8,128)(2,1)S(1)}, bf16[1280,640]{1,0:T(8,128)(2,1)}, u32[]{:S(2)}) copy-start(bf16[1280,640]{1,0:T(8,128)(2,1)} %constant.6.clone.refs_12_) | copy-start | bytes 4915204
  16.1 6.9 %copy-start.1 = (bf16[2,640,640]{2,1,0:T(8,128)(2,1)S(1)}, bf16[2,640,640]{2,1,0:T(8,128)(2,1)}, u32[]{:S(2)}) copy-start(bf16[2,640,640]{2,1,0:T(8,128)(2,1)} %constant.7.clone.refs_13_) | copy-start | bytes 4915204
  16.2 6.9 %copy-start.2 = (bf16[256,256]{1,0:T(8,128)(2,1)S(1)}, bf16[256,256]{1,0:T(8,128)(2,1)}, u32[]{:S(2)}) copy-start(bf16[256,256]{1,0:T(8,128)(2,1)} %constant.8.clone.refs_14_) | copy-start | bytes 393220
  16.2 6.9 %copy-start.3 = (f32[320]{0:T(512)S(1)}, f32[320]{0:T(512)}, u32[]{:S(2)}) copy-start(f32[320]{0:T(512)} %refs_11_.1) | copy-start | bytes 3844

commit v9 on v8

--- a/solution.py
+++ b/solution.py
@@ -23,7 +23,8 @@
 PB = N_IMG // COLS
 NS = 4096
 NB = NS // LANES
-NG = 21
+STEP = 11
+NG = 15
 CW = CB + WIN
 T = 6
 PS = 9
@@ -157,7 +158,7 @@
             acc[pl.ds(b, SUB), :] = acc[pl.ds(b, SUB), :] + vs[k][PS * j:PS * j + SUB, :]
 
     code = jnp.concatenate([pay_ref[PAY * (b + 1) - 1:PAY * (b + 1), :] for b in range(NB)], axis=0).astype(jnp.int32)
-    int_ref[...] = (code // (CODE * SUB)) * CW + (code & (CODE - 1))
+    int_ref[...] = (((code // CODE - 5) * 187) >> STEP) * CW + (code & (CODE - 1))
     kk = lax.broadcasted_iota(jnp.int32, (LANES, WIDE * 3), 0)
     ll = lax.broadcasted_iota(jnp.int32, (LANES, WIDE * 3), 1)
     r_ref[...] = jnp.where((kk < HW) & ((kk & 7) == (ll >> 7)), 1.0, 0.0).astype(BF)
@@ -194,10 +195,19 @@
                 a[rows, :] = jnp.zeros((n, LANES), F32)
         return v
 
-    high = lax.broadcasted_iota(jnp.int32, (n, LANES), 1) >= HALF
-    even = [total(2 * p) for p in range(11)]
-    tiles = [total(2 * p + 1) + jnp.where(high, even[p], even[p + 1]) for p in range(TILES)]
-    return tiles + [jnp.where(high, even[TILES], even[0])]
+    row = lax.broadcasted_iota(jnp.int32, (n, LANES), 1) >> 3
+    tiles = [None] * TILES
+    for g in range(NG):
+        v = total(g)
+        if g == 0:
+            ghost = v
+        first = 5 + STEP * g
+        for p in range(TILES):
+            lo, hi = max(first, SUB + WIN * p), min(first + WIN, SUB + WIN * (p + 1))
+            if lo < hi:
+                part = jnp.where((row - lo & (WIN - 1)) < hi - lo, v, 0.0)
+                tiles[p] = part if tiles[p] is None else tiles[p] + part
+    return tiles + [jnp.where(row >= SUB, v, ghost)]
 
 
 def own_kernel(pay_ref, out_ref, *refs):

time: 38.2 us -> 37.1 us (0.971)
  Pallas kernels: 32.3 us -> 31.3 us
    pallas_call x1, Pallas kernels: 9.58 us -> 8.57 us  [local_fn(): pl.pallas_call(own_kernel, out_shape=[jax.ShapeDtypeStruct((11, CW, LANES...]
  transfers between devices with their start and end apart: 2 -> 2, of which waited for: 0 -> 0; matrix products, arithmetic and copies ran while one was open for 0% -> 0% of each run, Pallas kernels for 43% -> 42%
where the time goes in v9:
time: 37.1 us; the launch traced here: 37 us
  Pallas kernels  31.3 us (84%)
  starting transfers between devices  4.88 us (13%)
  local copies, waits for them, and re-layouts  0.7 us (2%)
    pallas_call x1, Pallas kernels, local_fn(): pl.pallas_call(image_kernel, out_shape=jax.ShapeDtypeStruct((2, PB, QB),...  14.2 us
    pallas_call x1, Pallas kernels, local_fn(): pl.pallas_call(own_kernel, out_shape=[jax.ShapeDtypeStruct((11, CW, LANES...  8.57 us
    pallas_call x1, Pallas kernels, local_fn(): pl.pallas_call(far_kernel, out_shape=acc_shape + [jax.ShapeDtypeStruct((2...  6.83 us
    ppermute x1, starting transfers between devices, local_fn(): far_in = lax.ppermute(far, 'cols', [(0, 1), (1, 0)])  3.39 us
    pallas_call x1, Pallas kernels, local_fn(): pl.pallas_call(prep_kernel, out_shape=[jax.ShapeDtypeStruct((PAY * NB, LA...  1.65 us
    ppermute x1, starting transfers between devices, local_fn(): lax.ppermute(maps, 'rows', [(i, (i + 2) % ROWS) for i in range(ROWS)])  1.49 us
  transfers between devices with their start and end apart: 2, of which 0 were waited for; matrix products, arithmetic and copies ran while one was open for 0% of the time, Pallas kernels for 42%

profile of v9, /device:TPU:0, one launch (start us, length us, event | category | flops | bytes accessed | tf_op | source)
XLA Modules:
  0.0 37.0 jit_solution(164324793018028861)
XLA Ops:
  0.0 1.6 %prep.1 = (f32[672,128]{1,0:T(8,128)S(1)}, f32[672,128]{1,0:T(8,128)S(1)}, f32[4,64,640]{2,1,0:T(8,128)S(1)}, f32[4,16,640]{2,1,0:T(8,128)S(1)}) custom-call(f32[2,8,4096]{2,1,0:T(8,128)} %ks_hbm.1, f32[6,4096]{1,0:T(8,128)} %wy_hbm.1, f32[6,4096]{1,0:T(8,128)} %wx_hbm.1, s32[32,128]{1,0:T(8,128)} %bitcast.4, s32[32,128]{1,0:T(8,128)} %bitcast.5, ...), custom_call_target="tpu_custom_call" | custom-call | tf_op jit(solution)/shard_map/prep/pallas_call | solution.py:498
  1.7 3.4 %collective-permute-start = (f32[672,128]{1,0:T(8,128)S(1)}, f32[672,128]{1,0:T(8,128)S(1)}, u32[]{:S(2)}, u32[]{:S(2)}) collective-permute-start(f32[672,128]{1,0:T(8,128)S(1)} %get-tuple-element.23), channel_id=1, source_target_pairs={{0,4},{4,0},{1,5},{5,1},{2,6},{6,2},{3,7},{7,3}} | collective-permute-start | bytes 1032200 | tf_op jit(solution)/shard_map/ppermute | solution.py:505
  5.0 1.5 %collective-permute-start.1 = (f32[4,64,640]{2,1,0:T(8,128)S(1)}, f32[4,64,640]{2,1,0:T(8,128)S(1)}, u32[]{:S(2)}, u32[]{:S(2)}) collective-permute-start(f32[4,64,640]{2,1,0:T(8,128)S(1)} %get-tuple-element.39.refs_8_), channel_id=1, source_target_pairs={{0,2},{1,3},{2,0},{3,1},{4,6},{5,7},{6,4},{7,5}} | collective-permute-start | bytes 1966088 | tf_op jit(solution)/shard_map/ppermute | solution.py:518
  6.5 8.6 %spread_own.1 = (f32[11,336,128]{2,1,0:T(8,128)S(1)}, f32[5040,128]{1,0:T(8,128)S(1)}, f32[5040,128]{1,0:T(8,128)S(1)}, f32[5040,128]{1,0:T(8,128)S(1)}, f32[504...) custom-call(f32[672,128]{1,0:T(8,128)S(1)} %get-tuple-element.24.pay_ref), custom_call_target="tpu_custom_call" | custom-call | flops 4194304000 | bytes 4194304 | tf_op jit(solution)/shard_map/spread_own/pallas_call | solution.py:506
  15.1 0.0 collective-permute-done.pay_ref
  15.1 0.0 copy-start
  15.1 0.0 copy-start.1
  15.2 0.0 copy-start.2
  15.2 0.0 copy-start.3
  15.2 6.8 %spread_far.1 = (f32[5040,128]{1,0:T(8,128)S(1)}, f32[5040,128]{1,0:T(8,128)S(1)}, f32[5040,128]{1,0:T(8,128)S(1)}, f32[5040,128]{1,0:T(8,128)S(1)}, f32[5040,12...) custom-call(f32[672,128]{1,0:T(8,128)S(1)} %collective-permute-done., ...), custom_call_target="tpu_custom_call", output_to_operand_aliasing={{0}: (2, {}), {1}: (3, {}), {2}: (4, {}), {3}: (5, {}), {4}... | custom-call | flops 4194304000 | bytes 4194304 | tf_op jit(solution)/shard_map/spread_far/pallas_call | solution.py:511
  22.0 0.0 collective-permute-done.1.refs_9_
  22.0 0.0 copy-done
  22.0 0.0 copy-done.1
  22.0 0.0 copy-done.2
  22.1 0.0 copy-done.3
  22.1 14.2 %image.1 = f32[2,160,80]{2,1,0:T(8,128)S(1)} custom-call(f32[5040,128]{1,0:T(8,128)S(1)} %get-tuple-element.32.refs_0_, f32[5040,128]{1,0:T(8,128)S(1)} %get-tuple-element.33.refs_1_, f32[5040,128]{1,0:T(8,128)S(1)} %get-tuple-element.34.refs_2_, f32[5040,128]{1,0:T(8,128)S(1)} %get-tuple-element.35.refs_3_, f32[5040,128]{1,0:T(8,128)S(1)} %get-tuple-element.36.refs_4_, ...), custom_call_target="tpu_custom_call" | custom-call | tf_op jit(solution)/shard_map/image/pallas_call | solution.py:522
  36.3 0.7 %copy.24 = f32[2,160,80]{2,1,0:T(8,128)} copy(f32[2,160,80]{2,1,0:T(8,128)S(1)} %image.1) | data formatting | bytes 204800
Async XLA Ops:
  1.7 13.5 %collective-permute-start = (f32[672,128]{1,0:T(8,128)S(1)}, f32[672,128]{1,0:T(8,128)S(1)}, u32[]{:S(2)}, u32[]{:S(2)}) collective-permute-start(f32[672,128]{1,0:T(8,128)S(1)} %get-tuple-element.23), channel_id=1, source_target_pairs={{0,4},{4,0},{1,5},{5,1},{2,6},{6,2},{3,7},{7,3}} | collective-permute-start | bytes 1032200 | tf_op jit(solution)/shard_map/ppermute | solution.py:505
  5.0 17.0 %collective-permute-start.1 = (f32[4,64,640]{2,1,0:T(8,128)S(1)}, f32[4,64,640]{2,1,0:T(8,128)S(1)}, u32[]{:S(2)}, u32[]{:S(2)}) collective-permute-start(f32[4,64,640]{2,1,0:T(8,128)S(1)} %get-tuple-element.39.refs_8_), channel_id=1, source_target_pairs={{0,2},{1,3},{2,0},{3,1},{4,6},{5,7},{6,4},{7,5}} | collective-permute-start | bytes 1966088 | tf_op jit(solution)/shard_map/ppermute | solution.py:518
  15.1 6.9 %copy-start = (bf16[1280,640]{1,0:T(8,128)(2,1)S(1)}, bf16[1280,640]{1,0:T(8,128)(2,1)}, u32[]{:S(2)}) copy-start(bf16[1280,640]{1,0:T(8,128)(2,1)} %constant.6.clone.refs_12_) | copy-start | bytes 4915204
  15.1 6.9 %copy-start.1 = (bf16[2,640,640]{2,1,0:T(8,128)(2,1)S(1)}, bf16[2,640,640]{2,1,0:T(8,128)(2,1)}, u32[]{:S(2)}) copy-start(bf16[2,640,640]{2,1,0:T(8,128)(2,1)} %constant.7.clone.refs_13_) | copy-start | bytes 4915204
  15.2 6.9 %copy-start.2 = (bf16[256,256]{1,0:T(8,128)(2,1)S(1)}, bf16[256,256]{1,0:T(8,128)(2,1)}, u32[]{:S(2)}) copy-start(bf16[256,256]{1,0:T(8,128)(2,1)} %constant.8.clone.refs_14_) | copy-start | bytes 393220
  15.2 6.9 %copy-start.3 = (f32[320]{0:T(512)S(1)}, f32[320]{0:T(512)}, u32[]{:S(2)}) copy-start(f32[320]{0:T(512)} %refs_11_.1) | copy-start | bytes 3844

commit v10 on v9

--- a/solution.py
+++ b/solution.py
@@ -26,7 +26,7 @@
 STEP = 11
 NG = 15
 CW = CB + WIN
-T = 6
+T = 7
 PS = 9
 PAY = 21
 CODE = 512
@@ -323,7 +323,6 @@
         put(far0 + WIN * n, [near_tiles[p] + jnp.concatenate(order(a_ref[p, side:side + SUB, :]), axis=0) for p in range(TILES)])
         put(own0 + WIN * n, [a_ref[p, off:off + WIN, :] + jnp.concatenate(order(far_ends[p]), axis=0) for p in range(TILES)])
 
-    end_copy = remote(se_ref, sx_end, halo_ss, halo_rs, 2, {'rows': across})
 
     def to_rows(row0, n, t0, t1):
         a = jnp.concatenate([t0, t1], axis=1)
@@ -369,6 +368,7 @@
         swaps.append(remote(srs[grp], hrs[grp].at[:, core], swap_ss, swap_rs, 2 * grp + 1, {'rows': near}))
 
     columns(0)
+    end_copy = remote(se_ref, sx_end, halo_ss, halo_rs, 2, {'rows': across})
 
     for h in halos:
         h.wait()

time: 37.1 us -> 36.3 us (0.978)
  Pallas kernels: 31.3 us -> 30.4 us
    pallas_call x1, Pallas kernels: 14.2 us -> 13.7 us  [local_fn(): pl.pallas_call(image_kernel, out_shape=jax.ShapeDtypeStruct((2, PB, QB),...]
where the time goes in v10:
time: 36.3 us; the launch traced here: 36.1 us
  Pallas kernels  30.4 us (84%)
  starting transfers between devices  4.88 us (13%)
  local copies, waits for them, and re-layouts  0.7 us (2%)
    pallas_call x1, Pallas kernels, local_fn(): pl.pallas_call(image_kernel, out_shape=jax.ShapeDtypeStruct((2, PB, QB),...  13.7 us
    pallas_call x1, Pallas kernels, local_fn(): pl.pallas_call(own_kernel, out_shape=[jax.ShapeDtypeStruct((11, CW, LANES...  8.56 us
    pallas_call x1, Pallas kernels, local_fn(): pl.pallas_call(far_kernel, out_shape=acc_shape + [jax.ShapeDtypeStruct((2...  6.47 us
    ppermute x1, starting transfers between devices, local_fn(): far_in = lax.ppermute(far, 'cols', [(0, 1), (1, 0)])  3.39 us
    pallas_call x1, Pallas kernels, local_fn(): pl.pallas_call(prep_kernel, out_shape=[jax.ShapeDtypeStruct((PAY * NB, LA...  1.65 us
    ppermute x1, starting transfers between devices, local_fn(): lax.ppermute(maps, 'rows', [(i, (i + 2) % ROWS) for i in range(ROWS)])  1.49 us
  transfers between devices with their start and end apart: 2, of which 0 were waited for; matrix products, arithmetic and copies ran while one was open for 0% of the time, Pallas kernels for 42%

profile of v10, /device:TPU:0, one launch (start us, length us, event | category | flops | bytes accessed | tf_op | source)
XLA Modules:
  0.0 36.1 jit_solution(18341183274483800883)
XLA Ops:
  0.0 1.6 %prep.1 = (f32[672,128]{1,0:T(8,128)S(1)}, f32[672,128]{1,0:T(8,128)S(1)}, f32[4,64,640]{2,1,0:T(8,128)S(1)}, f32[4,16,640]{2,1,0:T(8,128)S(1)}) custom-call(f32[2,8,4096]{2,1,0:T(8,128)} %ks_hbm.1, f32[6,4096]{1,0:T(8,128)} %wy_hbm.1, f32[6,4096]{1,0:T(8,128)} %wx_hbm.1, s32[32,128]{1,0:T(8,128)} %bitcast.4, s32[32,128]{1,0:T(8,128)} %bitcast.5, ...), custom_call_target="tpu_custom_call" | custom-call | tf_op jit(solution)/shard_map/prep/pallas_call | solution.py:498
  1.7 3.4 %collective-permute-start = (f32[672,128]{1,0:T(8,128)S(1)}, f32[672,128]{1,0:T(8,128)S(1)}, u32[]{:S(2)}, u32[]{:S(2)}) collective-permute-start(f32[672,128]{1,0:T(8,128)S(1)} %get-tuple-element.25), channel_id=1, source_target_pairs={{0,4},{4,0},{1,5},{5,1},{2,6},{6,2},{3,7},{7,3}} | collective-permute-start | bytes 1032200 | tf_op jit(solution)/shard_map/ppermute | solution.py:505
  5.0 1.5 %collective-permute-start.1 = (f32[4,64,640]{2,1,0:T(8,128)S(1)}, f32[4,64,640]{2,1,0:T(8,128)S(1)}, u32[]{:S(2)}, u32[]{:S(2)}) collective-permute-start(f32[4,64,640]{2,1,0:T(8,128)S(1)} %get-tuple-element.43.refs_9_), channel_id=1, source_target_pairs={{0,2},{1,3},{2,0},{3,1},{4,6},{5,7},{6,4},{7,5}} | collective-permute-start | bytes 1966088 | tf_op jit(solution)/shard_map/ppermute | solution.py:518
  6.5 8.6 %spread_own.1 = (f32[11,336,128]{2,1,0:T(8,128)S(1)}, f32[5040,128]{1,0:T(8,128)S(1)}, f32[5040,128]{1,0:T(8,128)S(1)}, f32[5040,128]{1,0:T(8,128)S(1)}, f32[504...) custom-call(f32[672,128]{1,0:T(8,128)S(1)} %get-tuple-element.26.pay_ref), custom_call_target="tpu_custom_call" | custom-call | flops 4194304000 | bytes 4194304 | tf_op jit(solution)/shard_map/spread_own/pallas_call | solution.py:506
  15.1 0.0 collective-permute-done.pay_ref
  15.1 0.0 copy-start
  15.1 0.0 copy-start.1
  15.1 0.0 copy-start.2
  15.2 0.0 copy-start.3
  15.2 6.5 %spread_far.1 = (f32[5040,128]{1,0:T(8,128)S(1)}, f32[5040,128]{1,0:T(8,128)S(1)}, f32[5040,128]{1,0:T(8,128)S(1)}, f32[5040,128]{1,0:T(8,128)S(1)}, f32[5040,12...) custom-call(f32[672,128]{1,0:T(8,128)S(1)} %collective-permute-done., ...), custom_call_target="tpu_custom_call", output_to_operand_aliasing={{0}: (2, {}), {1}: (3, {}), {2}: (4, {}), {3}: (5, {}), {4}... | custom-call | flops 4194304000 | bytes 4194304 | tf_op jit(solution)/shard_map/spread_far/pallas_call | solution.py:511
  21.6 0.0 collective-permute-done.1.refs_10_
  21.7 0.0 copy-done
  21.7 0.0 copy-done.1
  21.7 0.0 copy-done.2
  21.7 0.0 copy-done.3
  21.7 13.7 %image.1 = f32[2,160,80]{2,1,0:T(8,128)S(1)} custom-call(f32[5040,128]{1,0:T(8,128)S(1)} %get-tuple-element.35.refs_0_, f32[5040,128]{1,0:T(8,128)S(1)} %get-tuple-element.36.refs_1_, f32[5040,128]{1,0:T(8,128)S(1)} %get-tuple-element.37.refs_2_, f32[5040,128]{1,0:T(8,128)S(1)} %get-tuple-element.38.refs_3_, f32[5040,128]{1,0:T(8,128)S(1)} %get-tuple-element.39.refs_4_, ...), custom_call_target="tpu_custom_call" | custom-call | tf_op jit(solution)/shard_map/image/pallas_call | solution.py:522
  35.4 0.7 %copy.26 = f32[2,160,80]{2,1,0:T(8,128)} copy(f32[2,160,80]{2,1,0:T(8,128)S(1)} %image.1) | data formatting | bytes 204800
Async XLA Ops:
  1.7 13.4 %collective-permute-start = (f32[672,128]{1,0:T(8,128)S(1)}, f32[672,128]{1,0:T(8,128)S(1)}, u32[]{:S(2)}, u32[]{:S(2)}) collective-permute-start(f32[672,128]{1,0:T(8,128)S(1)} %get-tuple-element.25), channel_id=1, source_target_pairs={{0,4},{4,0},{1,5},{5,1},{2,6},{6,2},{3,7},{7,3}} | collective-permute-start | bytes 1032200 | tf_op jit(solution)/shard_map/ppermute | solution.py:505
  5.0 16.6 %collective-permute-start.1 = (f32[4,64,640]{2,1,0:T(8,128)S(1)}, f32[4,64,640]{2,1,0:T(8,128)S(1)}, u32[]{:S(2)}, u32[]{:S(2)}) collective-permute-start(f32[4,64,640]{2,1,0:T(8,128)S(1)} %get-tuple-element.43.refs_9_), channel_id=1, source_target_pairs={{0,2},{1,3},{2,0},{3,1},{4,6},{5,7},{6,4},{7,5}} | collective-permute-start | bytes 1966088 | tf_op jit(solution)/shard_map/ppermute | solution.py:518
  15.1 6.5 %copy-start = (bf16[1280,640]{1,0:T(8,128)(2,1)S(1)}, bf16[1280,640]{1,0:T(8,128)(2,1)}, u32[]{:S(2)}) copy-start(bf16[1280,640]{1,0:T(8,128)(2,1)} %constant.6.clone.refs_13_) | copy-start | bytes 4915204
  15.1 6.5 %copy-start.1 = (bf16[2,640,640]{2,1,0:T(8,128)(2,1)S(1)}, bf16[2,640,640]{2,1,0:T(8,128)(2,1)}, u32[]{:S(2)}) copy-start(bf16[2,640,640]{2,1,0:T(8,128)(2,1)} %constant.7.clone.refs_14_) | copy-start | bytes 4915204
  15.1 6.5 %copy-start.2 = (bf16[256,256]{1,0:T(8,128)(2,1)S(1)}, bf16[256,256]{1,0:T(8,128)(2,1)}, u32[]{:S(2)}) copy-start(bf16[256,256]{1,0:T(8,128)(2,1)} %constant.8.clone.refs_15_) | copy-start | bytes 393220
  15.2 6.5 %copy-start.3 = (f32[320]{0:T(512)S(1)}, f32[320]{0:T(512)}, u32[]{:S(2)}) copy-start(f32[320]{0:T(512)} %refs_12_.1) | copy-start | bytes 3844

commit v11 on v10

--- a/solution.py
+++ b/solution.py
@@ -56,7 +56,7 @@
                 out[:, l0:l0 + HALF] = e[:, :, t, q0:q0 + HALF].reshape(2 * N_GRID, HALF)
     for t in range(2):
         for d in range(4):
-            l0 = 4 * LANES + HALF * (d // 2) + WIN * (2 * t + d % 2)
+            l0 = 4 * LANES + HALF * t + WIN * d
             out[:, l0:l0 + WIN] = e[:, :, t, QB * d + HALF:QB * (d + 1)].reshape(2 * N_GRID, WIN)
     return jnp.asarray(out, BF)
 
@@ -270,7 +270,7 @@
 def image_kernel(*refs):
     accs = refs[:T]
     (a_ref, pack_ref, so_ref, sx_ref, se_ref, d_ref, ev_ref, eu_ref, pm_ref, out_ref,
-     tb_ref, edge_ref, g_ref, halo, sm1, sm2, sr1, sr2, hm1, hm2, hr1, hr2, s_main, s_rem, acc_m, acc_r, sx_end, pieces, recvs, tails, recvs_t,
+     tb_ref, edge_ref, g_ref, halo, sm1, sm2, sr1, sr2, hm1, hm2, hr1, hr2, s_main, s_rem, acc_m, acc_r, pieces, recvs, tails, recvs_t,
      halo_ss, halo_rs, swap_ss, swap_rs, red_ss, red_rs) = refs[T:]
     k = lax.axis_index('cols')
     r = lax.axis_index('rows')
@@ -335,7 +335,7 @@
         to_rows(QTR * m, LANES, tb_ref[2 * m + 1], tb_ref[2 * m + 2])
 
     sms, srs, hms, hrs = (sm1, sm2), (sr1, sr2), (hm1, hm2), (hr1, hr2)
-    swaps = []
+    swaps, trades = [], []
 
     def columns(grp):
         start, n = GROUPS[grp]
@@ -353,22 +353,18 @@
                 odd = pltpu.roll(hs[1][i], HALF, axis=1)
                 sms[grp][dp, cp, t] = jnp.where(far_even, hs[0][i], odd).astype(BF)
                 hms[grp][dp, cp, t, core] = jnp.where(own_even, hs[0][i], odd).astype(BF)
-        for t in range(2):
-            both = []
-            for h in range(2):
-                i = 2 * t + h
-                out = rems[i]
-                for c in range(4):
-                    if c != i:
-                        out = jnp.where(block == c, pltpu.roll(rems[c], (WIN * (c - i)) % LANES, axis=1), out)
-                both.append(out)
-            srs[grp][t] = jnp.where(core == 0, both[1], both[0]).astype(BF)
-            hrs[grp][t, core] = jnp.where(core == 0, both[0], both[1]).astype(BF)
-        swaps.append(remote(sms[grp], hms[grp].at[:, :, :, core], swap_ss, swap_rs, 2 * grp, {'rows': near}))
-        swaps.append(remote(srs[grp], hrs[grp].at[:, core], swap_ss, swap_rs, 2 * grp + 1, {'rows': near}))
+        for d in range(ROWS):
+            out = rems[d]
+            for c in range(4):
+                if c != d:
+                    out = jnp.where(block == c, pltpu.roll(rems[c], (WIN * (c - d)) % LANES, axis=1), out)
+            srs[grp][d] = out.astype(BF)
+        hrs[grp][r] = srs[grp][r]
+        swaps.append(remote(sms[grp], hms[grp].at[:, :, :, core], swap_ss, swap_rs, grp, {'rows': near}))
+        for i, dev in enumerate((across, 3 - r, near)):
+            trades.append(remote(srs[grp].at[dev], hrs[grp].at[r], swap_ss, swap_rs, 2 + 3 * grp + i, {'rows': dev}))
 
     columns(0)
-    end_copy = remote(se_ref, sx_end, halo_ss, halo_rs, 2, {'rows': across})
 
     for h in halos:
         h.wait()
@@ -392,7 +388,7 @@
         return [jnp.concatenate([t[2 * i], t[2 * i + 1], t[4][HALF * i:HALF * (i + 1)]], axis=0) for i in range(2)]
 
 
-    for cp in swaps[:2]:
+    for cp in swaps[:1]:
         cp.wait_recv()
     n0 = 4 * GROUPS[0][1]
 
@@ -403,9 +399,8 @@
         acc_m[j] = jnp.dot(eu_ref[x, :, :n0], block_of(0, j), preferred_element_type=F32)
         for cp in range(2):
             s_main[j, 0, cp], s_main[j, 1, cp] = turn(jnp.concatenate([ref[2 * cp + core], ref[2 * cp + 1 - core]], axis=0))
-    acc_r[...] = jnp.dot(eu_ref[x, :, :n0], hrs[0][...].reshape(n0, LANES), preferred_element_type=F32)
-
-    for cp in swaps[2:]:
+
+    for cp in swaps[1:]:
         cp.wait_recv()
 
     def rows_dft(half, acc, rhs):
@@ -428,38 +423,40 @@
         return jnp.where(low, re + pltpu.roll(re, HALF, axis=1), im + pltpu.roll(im, HALF, axis=1))
 
     def rest(half):
-        i_re, i_im = rows_dft(half, acc_r, hrs[1][...].reshape(4 * GROUPS[1][1], LANES))
+        parts = []
+        for o in range(2):
+            rows = pl.ds(pl.multiple_of(half * N_IMG + PB * o, WIN), PB)
+            parts.append(acc_r[0, rows, :] + pltpu.roll(acc_r[1, rows, :], HALF, axis=1))
+        i_re, i_im = parts
         rows = pl.ds(pl.multiple_of(half * PB, SUB), PB)
         s_re, s_im = s_rem[0, rows, :], s_rem[1, rows, :]
-
-        def fold(v):
-            v = v + pltpu.roll(v, LANES - QTR, axis=1)
-            return v + pltpu.roll(v, LANES - WIN, axis=1)
-
-        re, im = fold(s_re * i_re + s_im * i_im), fold(s_re * i_im - s_im * i_re)
-        both = jnp.where(lane & (HALF - 1) < WIN, re, pltpu.roll(im, WIN, axis=1))
-        outs = []
-        for dp in range(2):
-            out = None
-            for g in range(4):
-                v = both[PB // 4 * g:PB // 4 * (g + 1)]
-                if g + 2 * dp:
-                    v = pltpu.roll(v, (QTR * g + HALF * dp) % LANES, axis=1)
-                out = v if out is None else jnp.where(quarter == g, v, out)
-            outs.append(out)
-        return jnp.where(x == 0, outs[0], outs[1]), jnp.where(x == 0, outs[1], outs[0])
+        w = s_re * i_re + s_im * i_im + pltpu.roll(s_re * i_im - s_im * i_re, HALF, axis=1)
+        w = w + pltpu.roll(w, LANES - QTR, axis=1)
+        w = w + pltpu.roll(w, LANES - WIN, axis=1)
+        w = jnp.where(lane < WIN, w, pltpu.roll(w, LANES - HALF + WIN, axis=1))
+        out = w[:PB // 4]
+        for g in range(1, 4):
+            out = jnp.where(quarter == g, pltpu.roll(w[PB // 4 * g:PB // 4 * (g + 1)], QTR * g, axis=1), out)
+        return out
 
     sends = []
     for i, (half, j) in enumerate(((1 - k, 1), (k, 1), (1 - k, 0))):
         pieces[i] = piece(half, j)
         sends.append(remote(pieces.at[i], recvs.at[i], red_ss, red_rs, i, homes[i]))
-    end_copy.wait_recv()
-    s_rem[0], s_rem[1] = turn(jnp.concatenate([jnp.where(x == j, se_ref[c], sx_end[c]) for j in range(2) for c in range(4)], axis=0))
-    tails[2], tails[0] = rest(1 - k)
-    sends.append(remote(tails.at[0], recvs_t.at[0], red_ss, red_rs, 3, homes[0]))
-    rem, tails[1] = rest(k)
-    for i in (1, 2):
-        sends.append(remote(tails.at[i], recvs_t.at[i], red_ss, red_rs, 3 + i, homes[i]))
+    for cp in trades:
+        cp.wait_recv()
+    for t in range(2):
+        total = None
+        for grp in range(2):
+            kk = 2 * GROUPS[grp][1]
+            for c in range(2):
+                part = jnp.dot(eu_ref[c, :, n0 * grp + kk * t:n0 * grp + kk * (t + 1)], hrs[grp][2 * c:2 * c + 2].reshape(kk, LANES), preferred_element_type=F32)
+                total = part if total is None else total + part
+        acc_r[t] = total
+    s_rem[0], s_rem[1] = turn(jnp.concatenate([se_ref[c] for c in range(4)] + [jnp.zeros((HALF, N_GRID), F32)], axis=0))
+    tails[...] = rest(1 - k)
+    tail = remote(tails, recvs_t, red_ss, red_rs, 3, homes[2])
+    rem = rest(k)
     main = piece(k, 0)
     d8 = jnp.broadcast_to(jnp.concatenate([d_ref[...][None, :], jnp.zeros((1, HALF), F32)], axis=1), (SUB, N_IMG + HALF))
     dq = d8
@@ -471,17 +468,16 @@
     for i in (2, 0, 1):
         sends[i].wait_recv()
         main = main + recvs[i]
-    for i in (2, 0, 1):
-        sends[3 + i].wait_recv()
-        rem = rem + recvs_t[i]
+    tail.wait_recv()
+    rem = rem + recvs_t[...]
     for o in range(2):
         m = pltpu.roll(main, HALF, axis=1) if o else main
         for j in range(4):
             rows = slice(PB // 4 * j, PB // 4 * (j + 1))
-            tail = pltpu.roll(rem, (HALF - QTR * j - WIN * o) % LANES, axis=1)
-            out_ref[o, rows, :] = (jnp.where(low[rows], m[rows], tail) * dd[rows])[:, :QB]
-
-    for cp in sends + swaps + [end_copy]:
+            end = pltpu.roll(rem, (HALF - QTR * j - WIN * o) % LANES, axis=1)
+            out_ref[o, rows, :] = (jnp.where(low[rows], m[rows], end) * dd[rows])[:, :QB]
+
+    for cp in sends + swaps + trades + [tail]:
         cp.wait_send()
 
 
@@ -517,16 +513,16 @@
         )(far_in, half, *accs)
         maps_x = lax.ppermute(maps, 'rows', [(i, (i + 2) % ROWS) for i in range(ROWS)])
         dma = pltpu.SemaphoreType.DMA
-        half_bufs = [VMEM((2, 2, 2, n, LANES), BF) for _, n in GROUPS] + [VMEM((2, n, LANES), BF) for _, n in GROUPS]
-        full_bufs = [VMEM((2, 2, 2, 2, n, LANES), BF) for _, n in GROUPS] + [VMEM((2, 2, n, LANES), BF) for _, n in GROUPS]
+        half_bufs = [VMEM((2, 2, 2, n, LANES), BF) for _, n in GROUPS] + [VMEM((ROWS, n, LANES), BF) for _, n in GROUPS]
+        full_bufs = [VMEM((2, 2, 2, 2, n, LANES), BF) for _, n in GROUPS] + [VMEM((ROWS, n, LANES), BF) for _, n in GROUPS]
         return pl.pallas_call(
             image_kernel,
             out_shape=jax.ShapeDtypeStruct((2, PB, QB), F32), in_specs=[vm] * (T + 9), out_specs=vm,
             scratch_shapes=[VMEM((TILES, N_GRID, LANES), BF), VMEM((N_GRID, LANES), F32), VMEM((4 * RB, 2 * N_GRID), BF), VMEM((2, LANES, LANES), F32)] + half_bufs + full_bufs + [
                 VMEM((2, 2, 2, N_IMG, LANES), F32), VMEM((2, N_IMG, LANES), F32),
-                VMEM((2, 2 * N_IMG, 2 * LANES), F32), VMEM((2 * N_IMG, LANES), F32), VMEM((4, WIN, N_GRID), F32),
-                VMEM((3, PB, LANES), F32), VMEM((3, PB, LANES), F32), VMEM((3, PB // 4, LANES), F32), VMEM((3, PB // 4, LANES), F32),
-                dma((3,)), dma((3,)), dma((4,)), dma((4,)), dma((6,)), dma((6,)),
+                VMEM((2, 2 * N_IMG, 2 * LANES), F32), VMEM((2, 2 * N_IMG, LANES), F32),
+                VMEM((3, PB, LANES), F32), VMEM((3, PB, LANES), F32), VMEM((PB // 4, LANES), F32), VMEM((PB // 4, LANES), F32),
+                dma((2,)), dma((2,)), dma((8,)), dma((8,)), dma((4,)), dma((4,)),
             ],
             compiler_params=pltpu.CompilerParams(vmem_limit_bytes=11 * MIB, collective_id=0, has_side_effects=True), name='image',
         )(*accs, half, pack, maps, maps_x, maps_end, deapod, col_dft(), row_dft(), unmix())

time: 36.3 us -> 35.7 us (0.983)
  Pallas kernels: 30.4 us -> 29.9 us
    pallas_call x1, Pallas kernels: 13.7 us -> 13.1 us  [local_fn(): pl.pallas_call(image_kernel, out_shape=jax.ShapeDtypeStruct((2, PB, QB),...]
where the time goes in v11:
time: 35.7 us; the launch traced here: 35.5 us
  Pallas kernels  29.9 us (84%)
  starting transfers between devices  4.88 us (14%)
  local copies, waits for them, and re-layouts  0.7 us (2%)
    pallas_call x1, Pallas kernels, local_fn(): pl.pallas_call(image_kernel, out_shape=jax.ShapeDtypeStruct((2, PB, QB),...  13.1 us
    pallas_call x1, Pallas kernels, local_fn(): pl.pallas_call(own_kernel, out_shape=[jax.ShapeDtypeStruct((11, CW, LANES...  8.57 us
    pallas_call x1, Pallas kernels, local_fn(): pl.pallas_call(far_kernel, out_shape=acc_shape + [jax.ShapeDtypeStruct((2...  6.5 us
    ppermute x1, starting transfers between devices, local_fn(): far_in = lax.ppermute(far, 'cols', [(0, 1), (1, 0)])  3.39 us
    pallas_call x1, Pallas kernels, local_fn(): pl.pallas_call(prep_kernel, out_shape=[jax.ShapeDtypeStruct((PAY * NB, LA...  1.65 us
    ppermute x1, starting transfers between devices, local_fn(): lax.ppermute(maps, 'rows', [(i, (i + 2) % ROWS) for i in range(ROWS)])  1.49 us
  transfers between devices with their start and end apart: 2, of which 0 were waited for; matrix products, arithmetic and copies ran while one was open for 0% of the time, Pallas kernels for 42%

profile of v11, /device:TPU:0, one launch (start us, length us, event | category | flops | bytes accessed | tf_op | source)
XLA Modules:
  0.0 35.5 jit_solution(13081023295055010328)
XLA Ops:
  0.0 1.6 %prep.1 = (f32[672,128]{1,0:T(8,128)S(1)}, f32[672,128]{1,0:T(8,128)S(1)}, f32[4,64,640]{2,1,0:T(8,128)S(1)}, f32[4,16,640]{2,1,0:T(8,128)S(1)}) custom-call(f32[2,8,4096]{2,1,0:T(8,128)} %ks_hbm.1, f32[6,4096]{1,0:T(8,128)} %wy_hbm.1, f32[6,4096]{1,0:T(8,128)} %wx_hbm.1, s32[32,128]{1,0:T(8,128)} %bitcast.4, s32[32,128]{1,0:T(8,128)} %bitcast.5, ...), custom_call_target="tpu_custom_call" | custom-call | tf_op jit(solution)/shard_map/prep/pallas_call | solution.py:494
  1.7 3.4 %collective-permute-start = (f32[672,128]{1,0:T(8,128)S(1)}, f32[672,128]{1,0:T(8,128)S(1)}, u32[]{:S(2)}, u32[]{:S(2)}) collective-permute-start(f32[672,128]{1,0:T(8,128)S(1)} %get-tuple-element.25), channel_id=1, source_target_pairs={{0,4},{4,0},{1,5},{5,1},{2,6},{6,2},{3,7},{7,3}} | collective-permute-start | bytes 1032200 | tf_op jit(solution)/shard_map/ppermute | solution.py:501
  5.0 1.5 %collective-permute-start.1 = (f32[4,64,640]{2,1,0:T(8,128)S(1)}, f32[4,64,640]{2,1,0:T(8,128)S(1)}, u32[]{:S(2)}, u32[]{:S(2)}) collective-permute-start(f32[4,64,640]{2,1,0:T(8,128)S(1)} %get-tuple-element.43.refs_9_), channel_id=1, source_target_pairs={{0,2},{1,3},{2,0},{3,1},{4,6},{5,7},{6,4},{7,5}} | collective-permute-start | bytes 1966088 | tf_op jit(solution)/shard_map/ppermute | solution.py:514
  6.5 8.6 %spread_own.1 = (f32[11,336,128]{2,1,0:T(8,128)S(1)}, f32[5040,128]{1,0:T(8,128)S(1)}, f32[5040,128]{1,0:T(8,128)S(1)}, f32[5040,128]{1,0:T(8,128)S(1)}, f32[504...) custom-call(f32[672,128]{1,0:T(8,128)S(1)} %get-tuple-element.26.pay_ref), custom_call_target="tpu_custom_call" | custom-call | flops 4194304000 | bytes 4194304 | tf_op jit(solution)/shard_map/spread_own/pallas_call | solution.py:502
  15.1 0.0 collective-permute-done.pay_ref
  15.1 0.0 copy-start
  15.1 0.0 copy-start.1
  15.2 0.0 copy-start.2
  15.2 0.0 copy-start.3
  15.2 6.5 %spread_far.1 = (f32[5040,128]{1,0:T(8,128)S(1)}, f32[5040,128]{1,0:T(8,128)S(1)}, f32[5040,128]{1,0:T(8,128)S(1)}, f32[5040,128]{1,0:T(8,128)S(1)}, f32[5040,12...) custom-call(f32[672,128]{1,0:T(8,128)S(1)} %collective-permute-done., ...), custom_call_target="tpu_custom_call", output_to_operand_aliasing={{0}: (2, {}), {1}: (3, {}), {2}: (4, {}), {3}: (5, {}), {4}... | custom-call | flops 4194304000 | bytes 4194304 | tf_op jit(solution)/shard_map/spread_far/pallas_call | solution.py:507
  21.7 0.0 collective-permute-done.1.refs_10_
  21.7 0.0 copy-done
  21.7 0.0 copy-done.1
  21.7 0.0 copy-done.2
  21.7 0.0 copy-done.3
  21.7 13.1 %image.1 = f32[2,160,80]{2,1,0:T(8,128)S(1)} custom-call(f32[5040,128]{1,0:T(8,128)S(1)} %get-tuple-element.35.refs_0_, f32[5040,128]{1,0:T(8,128)S(1)} %get-tuple-element.36.refs_1_, f32[5040,128]{1,0:T(8,128)S(1)} %get-tuple-element.37.refs_2_, f32[5040,128]{1,0:T(8,128)S(1)} %get-tuple-element.38.refs_3_, f32[5040,128]{1,0:T(8,128)S(1)} %get-tuple-element.39.refs_4_, ...), custom_call_target="tpu_custom_call" | custom-call | tf_op jit(solution)/shard_map/image/pallas_call | solution.py:518
  34.9 0.7 %copy.26 = f32[2,160,80]{2,1,0:T(8,128)} copy(f32[2,160,80]{2,1,0:T(8,128)S(1)} %image.1) | data formatting | bytes 204800
Async XLA Ops:
  1.7 13.5 %collective-permute-start = (f32[672,128]{1,0:T(8,128)S(1)}, f32[672,128]{1,0:T(8,128)S(1)}, u32[]{:S(2)}, u32[]{:S(2)}) collective-permute-start(f32[672,128]{1,0:T(8,128)S(1)} %get-tuple-element.25), channel_id=1, source_target_pairs={{0,4},{4,0},{1,5},{5,1},{2,6},{6,2},{3,7},{7,3}} | collective-permute-start | bytes 1032200 | tf_op jit(solution)/shard_map/ppermute | solution.py:501
  5.0 16.6 %collective-permute-start.1 = (f32[4,64,640]{2,1,0:T(8,128)S(1)}, f32[4,64,640]{2,1,0:T(8,128)S(1)}, u32[]{:S(2)}, u32[]{:S(2)}) collective-permute-start(f32[4,64,640]{2,1,0:T(8,128)S(1)} %get-tuple-element.43.refs_9_), channel_id=1, source_target_pairs={{0,2},{1,3},{2,0},{3,1},{4,6},{5,7},{6,4},{7,5}} | collective-permute-start | bytes 1966088 | tf_op jit(solution)/shard_map/ppermute | solution.py:514
  15.1 6.6 %copy-start = (bf16[1280,640]{1,0:T(8,128)(2,1)S(1)}, bf16[1280,640]{1,0:T(8,128)(2,1)}, u32[]{:S(2)}) copy-start(bf16[1280,640]{1,0:T(8,128)(2,1)} %constant.6.clone.refs_13_) | copy-start | bytes 4915204
  15.1 6.6 %copy-start.1 = (bf16[2,640,640]{2,1,0:T(8,128)(2,1)S(1)}, bf16[2,640,640]{2,1,0:T(8,128)(2,1)}, u32[]{:S(2)}) copy-start(bf16[2,640,640]{2,1,0:T(8,128)(2,1)} %constant.7.clone.refs_14_) | copy-start | bytes 4915204
  15.2 6.6 %copy-start.2 = (bf16[256,256]{1,0:T(8,128)(2,1)S(1)}, bf16[256,256]{1,0:T(8,128)(2,1)}, u32[]{:S(2)}) copy-start(bf16[256,256]{1,0:T(8,128)(2,1)} %constant.8.clone.refs_15_) | copy-start | bytes 393220
  15.2 6.6 %copy-start.3 = (f32[320]{0:T(512)S(1)}, f32[320]{0:T(512)}, u32[]{:S(2)}) copy-start(f32[320]{0:T(512)} %refs_12_.1) | copy-start | bytes 3844

commit v12 on v11

--- a/solution.py
+++ b/solution.py
@@ -439,10 +439,15 @@
             out = jnp.where(quarter == g, pltpu.roll(w[PB // 4 * g:PB // 4 * (g + 1)], QTR * g, axis=1), out)
         return out
 
-    sends = []
-    for i, (half, j) in enumerate(((1 - k, 1), (k, 1), (1 - k, 0))):
-        pieces[i] = piece(half, j)
-        sends.append(remote(pieces.at[i], recvs.at[i], red_ss, red_rs, i, homes[i]))
+    first, other = pl.ds(0, HALF), pl.ds(HALF, PB - HALF)
+    pieces[0] = piece(1 - k, 1)
+    joined = remote(pieces.at[0, first], recvs.at[0, first], red_ss, red_rs, 0, homes[1])
+    sends = [remote(pieces.at[0, other], recvs.at[0, other], red_ss, red_rs, 1, homes[0])]
+    pieces[1] = piece(k, 1)
+    sends.append(remote(pieces.at[1], recvs.at[1], red_ss, red_rs, 2, homes[1]))
+    across_y = piece(1 - k, 0)
+    pieces[2, HALF:] = across_y[HALF:]
+    sends.append(remote(pieces.at[2, other], recvs.at[2, other], red_ss, red_rs, 4, homes[2]))
     for cp in trades:
         cp.wait_recv()
     for t in range(2):
@@ -457,6 +462,9 @@
     tails[...] = rest(1 - k)
     tail = remote(tails, recvs_t, red_ss, red_rs, 3, homes[2])
     rem = rest(k)
+    joined.wait_recv()
+    pieces[2, :HALF] = across_y[:HALF] + recvs[0, :HALF]
+    sends.append(remote(pieces.at[2, first], recvs.at[2, first], red_ss, red_rs, 5, homes[2]))
     main = piece(k, 0)
     d8 = jnp.broadcast_to(jnp.concatenate([d_ref[...][None, :], jnp.zeros((1, HALF), F32)], axis=1), (SUB, N_IMG + HALF))
     dq = d8
@@ -465,9 +473,10 @@
     dp = jnp.where(k == 0, d8, pltpu.roll(d8, N_IMG + HALF - PB, axis=1))[:, :2 * LANES]
     dd = jnp.concatenate([dp] * WIN, axis=0).T[:PB] * dq[:1, :LANES]
 
-    for i in (2, 0, 1):
-        sends[i].wait_recv()
-        main = main + recvs[i]
+    for cp in sends:
+        cp.wait_recv()
+    main = main + recvs[1] + recvs[2]
+    main = jnp.concatenate([main[:HALF], main[HALF:] + recvs[0, HALF:]], axis=0)
     tail.wait_recv()
     rem = rem + recvs_t[...]
     for o in range(2):
@@ -477,7 +486,7 @@
             end = pltpu.roll(rem, (HALF - QTR * j - WIN * o) % LANES, axis=1)
             out_ref[o, rows, :] = (jnp.where(low[rows], m[rows], end) * dd[rows])[:, :QB]
 
-    for cp in sends + swaps + trades + [tail]:
+    for cp in sends + swaps + trades + [tail, joined]:
         cp.wait_send()
 
 
@@ -522,7 +531,7 @@
                 VMEM((2, 2, 2, N_IMG, LANES), F32), VMEM((2, N_IMG, LANES), F32),
                 VMEM((2, 2 * N_IMG, 2 * LANES), F32), VMEM((2, 2 * N_IMG, LANES), F32),
                 VMEM((3, PB, LANES), F32), VMEM((3, PB, LANES), F32), VMEM((PB // 4, LANES), F32), VMEM((PB // 4, LANES), F32),
-                dma((2,)), dma((2,)), dma((8,)), dma((8,)), dma((4,)), dma((4,)),
+                dma((2,)), dma((2,)), dma((8,)), dma((8,)), dma((6,)), dma((6,)),
             ],
             compiler_params=pltpu.CompilerParams(vmem_limit_bytes=11 * MIB, collective_id=0, has_side_effects=True), name='image',
         )(*accs, half, pack, maps, maps_x, maps_end, deapod, col_dft(), row_dft(), unmix())

time: 35.7 us -> 35.9 us (level)
  no operation moved by 1% of the time
where the time goes in v12:
time: 35.9 us; the launch traced here: 35.7 us
  Pallas kernels  30 us (84%)
  starting transfers between devices  4.88 us (14%)
  local copies, waits for them, and re-layouts  0.7 us (2%)
    pallas_call x1, Pallas kernels, local_fn(): pl.pallas_call(image_kernel, out_shape=jax.ShapeDtypeStruct((2, PB, QB),...  13.3 us
    pallas_call x1, Pallas kernels, local_fn(): pl.pallas_call(own_kernel, out_shape=[jax.ShapeDtypeStruct((11, CW, LANES...  8.56 us
    pallas_call x1, Pallas kernels, local_fn(): pl.pallas_call(far_kernel, out_shape=acc_shape + [jax.ShapeDtypeStruct((2...  6.5 us
    ppermute x1, starting transfers between devices, local_fn(): far_in = lax.ppermute(far, 'cols', [(0, 1), (1, 0)])  3.39 us
    pallas_call x1, Pallas kernels, local_fn(): pl.pallas_call(prep_kernel, out_shape=[jax.ShapeDtypeStruct((PAY * NB, LA...  1.65 us
    ppermute x1, starting transfers between devices, local_fn(): lax.ppermute(maps, 'rows', [(i, (i + 2) % ROWS) for i in range(ROWS)])  1.49 us
  transfers between devices with their start and end apart: 2, of which 0 were waited for; matrix products, arithmetic and copies ran while one was open for 0% of the time, Pallas kernels for 42%

profile of v12, /device:TPU:0, one launch (start us, length us, event | category | flops | bytes accessed | tf_op | source)
XLA Modules:
  0.0 35.7 jit_solution(14897524156494279370)
XLA Ops:
  0.0 1.6 %prep.1 = (f32[672,128]{1,0:T(8,128)S(1)}, f32[672,128]{1,0:T(8,128)S(1)}, f32[4,64,640]{2,1,0:T(8,128)S(1)}, f32[4,16,640]{2,1,0:T(8,128)S(1)}) custom-call(f32[2,8,4096]{2,1,0:T(8,128)} %ks_hbm.1, f32[6,4096]{1,0:T(8,128)} %wy_hbm.1, f32[6,4096]{1,0:T(8,128)} %wx_hbm.1, s32[32,128]{1,0:T(8,128)} %bitcast.4, s32[32,128]{1,0:T(8,128)} %bitcast.5, ...), custom_call_target="tpu_custom_call" | custom-call | tf_op jit(solution)/shard_map/prep/pallas_call | solution.py:503
  1.7 3.4 %collective-permute-start = (f32[672,128]{1,0:T(8,128)S(1)}, f32[672,128]{1,0:T(8,128)S(1)}, u32[]{:S(2)}, u32[]{:S(2)}) collective-permute-start(f32[672,128]{1,0:T(8,128)S(1)} %get-tuple-element.25), channel_id=1, source_target_pairs={{0,4},{4,0},{1,5},{5,1},{2,6},{6,2},{3,7},{7,3}} | collective-permute-start | bytes 1032200 | tf_op jit(solution)/shard_map/ppermute | solution.py:510
  5.0 1.5 %collective-permute-start.1 = (f32[4,64,640]{2,1,0:T(8,128)S(1)}, f32[4,64,640]{2,1,0:T(8,128)S(1)}, u32[]{:S(2)}, u32[]{:S(2)}) collective-permute-start(f32[4,64,640]{2,1,0:T(8,128)S(1)} %get-tuple-element.43.refs_9_), channel_id=1, source_target_pairs={{0,2},{1,3},{2,0},{3,1},{4,6},{5,7},{6,4},{7,5}} | collective-permute-start | bytes 1966088 | tf_op jit(solution)/shard_map/ppermute | solution.py:523
  6.5 8.6 %spread_own.1 = (f32[11,336,128]{2,1,0:T(8,128)S(1)}, f32[5040,128]{1,0:T(8,128)S(1)}, f32[5040,128]{1,0:T(8,128)S(1)}, f32[5040,128]{1,0:T(8,128)S(1)}, f32[504...) custom-call(f32[672,128]{1,0:T(8,128)S(1)} %get-tuple-element.26.pay_ref), custom_call_target="tpu_custom_call" | custom-call | flops 4194304000 | bytes 4194304 | tf_op jit(solution)/shard_map/spread_own/pallas_call | solution.py:511
  15.1 0.0 collective-permute-done.pay_ref
  15.1 0.0 copy-start
  15.1 0.0 copy-start.1
  15.1 0.0 copy-start.2
  15.2 0.0 copy-start.3
  15.2 6.5 %spread_far.1 = (f32[5040,128]{1,0:T(8,128)S(1)}, f32[5040,128]{1,0:T(8,128)S(1)}, f32[5040,128]{1,0:T(8,128)S(1)}, f32[5040,128]{1,0:T(8,128)S(1)}, f32[5040,12...) custom-call(f32[672,128]{1,0:T(8,128)S(1)} %collective-permute-done., ...), custom_call_target="tpu_custom_call", output_to_operand_aliasing={{0}: (2, {}), {1}: (3, {}), {2}: (4, {}), {3}: (5, {}), {4}... | custom-call | flops 4194304000 | bytes 4194304 | tf_op jit(solution)/shard_map/spread_far/pallas_call | solution.py:516
  21.7 0.0 collective-permute-done.1.refs_10_
  21.7 0.0 copy-done
  21.7 0.0 copy-done.1
  21.7 0.0 copy-done.2
  21.7 0.0 copy-done.3
  21.7 13.3 %image.1 = f32[2,160,80]{2,1,0:T(8,128)S(1)} custom-call(f32[5040,128]{1,0:T(8,128)S(1)} %get-tuple-element.35.refs_0_, f32[5040,128]{1,0:T(8,128)S(1)} %get-tuple-element.36.refs_1_, f32[5040,128]{1,0:T(8,128)S(1)} %get-tuple-element.37.refs_2_, f32[5040,128]{1,0:T(8,128)S(1)} %get-tuple-element.38.refs_3_, f32[5040,128]{1,0:T(8,128)S(1)} %get-tuple-element.39.refs_4_, ...), custom_call_target="tpu_custom_call" | custom-call | tf_op jit(solution)/shard_map/image/pallas_call | solution.py:527
  35.0 0.7 %copy.26 = f32[2,160,80]{2,1,0:T(8,128)} copy(f32[2,160,80]{2,1,0:T(8,128)S(1)} %image.1) | data formatting | bytes 204800
Async XLA Ops:
  1.7 13.5 %collective-permute-start = (f32[672,128]{1,0:T(8,128)S(1)}, f32[672,128]{1,0:T(8,128)S(1)}, u32[]{:S(2)}, u32[]{:S(2)}) collective-permute-start(f32[672,128]{1,0:T(8,128)S(1)} %get-tuple-element.25), channel_id=1, source_target_pairs={{0,4},{4,0},{1,5},{5,1},{2,6},{6,2},{3,7},{7,3}} | collective-permute-start | bytes 1032200 | tf_op jit(solution)/shard_map/ppermute | solution.py:510
  5.0 16.6 %collective-permute-start.1 = (f32[4,64,640]{2,1,0:T(8,128)S(1)}, f32[4,64,640]{2,1,0:T(8,128)S(1)}, u32[]{:S(2)}, u32[]{:S(2)}) collective-permute-start(f32[4,64,640]{2,1,0:T(8,128)S(1)} %get-tuple-element.43.refs_9_), channel_id=1, source_target_pairs={{0,2},{1,3},{2,0},{3,1},{4,6},{5,7},{6,4},{7,5}} | collective-permute-start | bytes 1966088 | tf_op jit(solution)/shard_map/ppermute | solution.py:523
  15.1 6.6 %copy-start = (bf16[1280,640]{1,0:T(8,128)(2,1)S(1)}, bf16[1280,640]{1,0:T(8,128)(2,1)}, u32[]{:S(2)}) copy-start(bf16[1280,640]{1,0:T(8,128)(2,1)} %constant.6.clone.refs_13_) | copy-start | bytes 4915204
  15.1 6.6 %copy-start.1 = (bf16[2,640,640]{2,1,0:T(8,128)(2,1)S(1)}, bf16[2,640,640]{2,1,0:T(8,128)(2,1)}, u32[]{:S(2)}) copy-start(bf16[2,640,640]{2,1,0:T(8,128)(2,1)} %constant.7.clone.refs_14_) | copy-start | bytes 4915204
  15.1 6.6 %copy-start.2 = (bf16[256,256]{1,0:T(8,128)(2,1)S(1)}, bf16[256,256]{1,0:T(8,128)(2,1)}, u32[]{:S(2)}) copy-start(bf16[256,256]{1,0:T(8,128)(2,1)} %constant.8.clone.refs_15_) | copy-start | bytes 393220
  15.2 6.6 %copy-start.3 = (f32[320]{0:T(512)S(1)}, f32[320]{0:T(512)}, u32[]{:S(2)}) copy-start(f32[320]{0:T(512)} %refs_12_.1) | copy-start | bytes 3844

commit v13 on v12

--- a/solution.py
+++ b/solution.py
@@ -366,6 +366,17 @@
 
     columns(0)
 
+    def turn(rows):
+        t = [rows[:, LANES * i:LANES * (i + 1)].T for i in range(5)]
+        return [jnp.concatenate([t[2 * i], t[2 * i + 1], t[4][HALF * i:HALF * (i + 1)]], axis=0) for i in range(2)]
+
+
+    def turn_main(j, ref):
+        for cp in range(2):
+            s_main[j, 0, cp], s_main[j, 1, cp] = turn(jnp.concatenate([ref[2 * cp + core], ref[2 * cp + 1 - core]], axis=0))
+
+    s_rem[0], s_rem[1] = turn(jnp.concatenate([se_ref[c] for c in range(4)] + [jnp.zeros((HALF, N_GRID), F32)], axis=0))
+
     for h in halos:
         h.wait()
     lane = lax.broadcasted_iota(jnp.int32, (LANES, LANES), 1)
@@ -383,11 +394,6 @@
     to_rows(4 * LANES, QTR, jnp.concatenate(t0s, axis=0), jnp.concatenate(t9s, axis=0))
     columns(1)
 
-    def turn(rows):
-        t = [rows[:, LANES * i:LANES * (i + 1)].T for i in range(5)]
-        return [jnp.concatenate([t[2 * i], t[2 * i + 1], t[4][HALF * i:HALF * (i + 1)]], axis=0) for i in range(2)]
-
-
     for cp in swaps[:1]:
         cp.wait_recv()
     n0 = 4 * GROUPS[0][1]
@@ -395,10 +401,14 @@
     def block_of(grp, j):
         return jnp.concatenate([hms[grp][(x + j) % 2, cp].reshape(4 * GROUPS[grp][1], LANES) for cp in range(2)], axis=1)
 
-    for j, ref in ((1, sx_ref), (0, so_ref)):
+    def ends_of(grp, c):
+        v = hrs[grp][2 * c:2 * c + 2].reshape(2 * GROUPS[grp][1], LANES)
+        return jnp.concatenate([v, pltpu.roll(v.astype(F32), HALF, axis=1).astype(BF)], axis=0)
+
+    for j in (1, 0):
         acc_m[j] = jnp.dot(eu_ref[x, :, :n0], block_of(0, j), preferred_element_type=F32)
-        for cp in range(2):
-            s_main[j, 0, cp], s_main[j, 1, cp] = turn(jnp.concatenate([ref[2 * cp + core], ref[2 * cp + 1 - core]], axis=0))
+    turn_main(1, sx_ref)
+    turn_main(0, so_ref)
 
     for cp in swaps[1:]:
         cp.wait_recv()
@@ -423,11 +433,7 @@
         return jnp.where(low, re + pltpu.roll(re, HALF, axis=1), im + pltpu.roll(im, HALF, axis=1))
 
     def rest(half):
-        parts = []
-        for o in range(2):
-            rows = pl.ds(pl.multiple_of(half * N_IMG + PB * o, WIN), PB)
-            parts.append(acc_r[0, rows, :] + pltpu.roll(acc_r[1, rows, :], HALF, axis=1))
-        i_re, i_im = parts
+        i_re, i_im = (acc_r[pl.ds(pl.multiple_of(half * N_IMG + PB * o, WIN), PB), :] for o in range(2))
         rows = pl.ds(pl.multiple_of(half * PB, SUB), PB)
         s_re, s_im = s_rem[0, rows, :], s_rem[1, rows, :]
         w = s_re * i_re + s_im * i_im + pltpu.roll(s_re * i_im - s_im * i_re, HALF, axis=1)
@@ -448,17 +454,12 @@
     across_y = piece(1 - k, 0)
     pieces[2, HALF:] = across_y[HALF:]
     sends.append(remote(pieces.at[2, other], recvs.at[2, other], red_ss, red_rs, 4, homes[2]))
-    for cp in trades:
+    for cp in trades[:3]:
         cp.wait_recv()
-    for t in range(2):
-        total = None
-        for grp in range(2):
-            kk = 2 * GROUPS[grp][1]
-            for c in range(2):
-                part = jnp.dot(eu_ref[c, :, n0 * grp + kk * t:n0 * grp + kk * (t + 1)], hrs[grp][2 * c:2 * c + 2].reshape(kk, LANES), preferred_element_type=F32)
-                total = part if total is None else total + part
-        acc_r[t] = total
-    s_rem[0], s_rem[1] = turn(jnp.concatenate([se_ref[c] for c in range(4)] + [jnp.zeros((HALF, N_GRID), F32)], axis=0))
+    acc_r[...] = sum(jnp.dot(eu_ref[c, :, :n0], ends_of(0, c), preferred_element_type=F32) for c in range(2))
+    for cp in trades[3:]:
+        cp.wait_recv()
+    acc_r[...] += jnp.dot(jnp.concatenate([eu_ref[c, :, n0:] for c in range(2)], axis=1), jnp.concatenate([ends_of(1, c) for c in range(2)], axis=0), preferred_element_type=F32)
     tails[...] = rest(1 - k)
     tail = remote(tails, recvs_t, red_ss, red_rs, 3, homes[2])
     rem = rest(k)
@@ -529,7 +530,7 @@
             out_shape=jax.ShapeDtypeStruct((2, PB, QB), F32), in_specs=[vm] * (T + 9), out_specs=vm,
             scratch_shapes=[VMEM((TILES, N_GRID, LANES), BF), VMEM((N_GRID, LANES), F32), VMEM((4 * RB, 2 * N_GRID), BF), VMEM((2, LANES, LANES), F32)] + half_bufs + full_bufs + [
                 VMEM((2, 2, 2, N_IMG, LANES), F32), VMEM((2, N_IMG, LANES), F32),
-                VMEM((2, 2 * N_IMG, 2 * LANES), F32), VMEM((2, 2 * N_IMG, LANES), F32),
+                VMEM((2, 2 * N_IMG, 2 * LANES), F32), VMEM((2 * N_IMG, LANES), F32),
                 VMEM((3, PB, LANES), F32), VMEM((3, PB, LANES), F32), VMEM((PB // 4, LANES), F32), VMEM((PB // 4, LANES), F32),
                 dma((2,)), dma((2,)), dma((8,)), dma((8,)), dma((6,)), dma((6,)),
             ],

time: 35.9 us -> 35.9 us (level)
  no operation moved by 1% of the time
where the time goes in v13:
time: 35.9 us; the launch traced here: 35.7 us
  Pallas kernels  30 us (84%)
  starting transfers between devices  4.88 us (14%)
  local copies, waits for them, and re-layouts  0.7 us (2%)
    pallas_call x1, Pallas kernels, local_fn(): pl.pallas_call(image_kernel, out_shape=jax.ShapeDtypeStruct((2, PB, QB),...  13.3 us
    pallas_call x1, Pallas kernels, local_fn(): pl.pallas_call(own_kernel, out_shape=[jax.ShapeDtypeStruct((11, CW, LANES...  8.53 us
    pallas_call x1, Pallas kernels, local_fn(): pl.pallas_call(far_kernel, out_shape=acc_shape + [jax.ShapeDtypeStruct((2...  6.5 us
    ppermute x1, starting transfers between devices, local_fn(): far_in = lax.ppermute(far, 'cols', [(0, 1), (1, 0)])  3.39 us
    pallas_call x1, Pallas kernels, local_fn(): pl.pallas_call(prep_kernel, out_shape=[jax.ShapeDtypeStruct((PAY * NB, LA...  1.65 us
    ppermute x1, starting transfers between devices, local_fn(): lax.ppermute(maps, 'rows', [(i, (i + 2) % ROWS) for i in range(ROWS)])  1.49 us
  transfers between devices with their start and end apart: 2, of which 0 were waited for; matrix products, arithmetic and copies ran while one was open for 0% of the time, Pallas kernels for 42%

profile of v13, /device:TPU:0, one launch (start us, length us, event | category | flops | bytes accessed | tf_op | source)
XLA Modules:
  0.0 35.7 jit_solution(1802236951858600828)
XLA Ops:
  0.0 1.6 %prep.1 = (f32[672,128]{1,0:T(8,128)S(1)}, f32[672,128]{1,0:T(8,128)S(1)}, f32[4,64,640]{2,1,0:T(8,128)S(1)}, f32[4,16,640]{2,1,0:T(8,128)S(1)}) custom-call(f32[2,8,4096]{2,1,0:T(8,128)} %ks_hbm.1, f32[6,4096]{1,0:T(8,128)} %wy_hbm.1, f32[6,4096]{1,0:T(8,128)} %wx_hbm.1, s32[32,128]{1,0:T(8,128)} %bitcast.4, s32[32,128]{1,0:T(8,128)} %bitcast.5, ...), custom_call_target="tpu_custom_call" | custom-call | tf_op jit(solution)/shard_map/prep/pallas_call | solution.py:504
  1.7 3.4 %collective-permute-start = (f32[672,128]{1,0:T(8,128)S(1)}, f32[672,128]{1,0:T(8,128)S(1)}, u32[]{:S(2)}, u32[]{:S(2)}) collective-permute-start(f32[672,128]{1,0:T(8,128)S(1)} %get-tuple-element.25), channel_id=1, source_target_pairs={{0,4},{4,0},{1,5},{5,1},{2,6},{6,2},{3,7},{7,3}} | collective-permute-start | bytes 1032200 | tf_op jit(solution)/shard_map/ppermute | solution.py:511
  5.0 1.5 %collective-permute-start.1 = (f32[4,64,640]{2,1,0:T(8,128)S(1)}, f32[4,64,640]{2,1,0:T(8,128)S(1)}, u32[]{:S(2)}, u32[]{:S(2)}) collective-permute-start(f32[4,64,640]{2,1,0:T(8,128)S(1)} %get-tuple-element.43.refs_9_), channel_id=1, source_target_pairs={{0,2},{1,3},{2,0},{3,1},{4,6},{5,7},{6,4},{7,5}} | collective-permute-start | bytes 1966088 | tf_op jit(solution)/shard_map/ppermute | solution.py:524
  6.5 8.5 %spread_own.1 = (f32[11,336,128]{2,1,0:T(8,128)S(1)}, f32[5040,128]{1,0:T(8,128)S(1)}, f32[5040,128]{1,0:T(8,128)S(1)}, f32[5040,128]{1,0:T(8,128)S(1)}, f32[504...) custom-call(f32[672,128]{1,0:T(8,128)S(1)} %get-tuple-element.26.pay_ref), custom_call_target="tpu_custom_call" | custom-call | flops 4194304000 | bytes 4194304 | tf_op jit(solution)/shard_map/spread_own/pallas_call | solution.py:512
  15.1 0.0 collective-permute-done.pay_ref
  15.1 0.0 copy-start
  15.1 0.0 copy-start.1
  15.1 0.0 copy-start.2
  15.1 0.0 copy-start.3
  15.1 6.5 %spread_far.1 = (f32[5040,128]{1,0:T(8,128)S(1)}, f32[5040,128]{1,0:T(8,128)S(1)}, f32[5040,128]{1,0:T(8,128)S(1)}, f32[5040,128]{1,0:T(8,128)S(1)}, f32[5040,12...) custom-call(f32[672,128]{1,0:T(8,128)S(1)} %collective-permute-done., ...), custom_call_target="tpu_custom_call", output_to_operand_aliasing={{0}: (2, {}), {1}: (3, {}), {2}: (4, {}), {3}: (5, {}), {4}... | custom-call | flops 4194304000 | bytes 4194304 | tf_op jit(solution)/shard_map/spread_far/pallas_call | solution.py:517
  21.6 0.0 collective-permute-done.1.refs_10_
  21.7 0.0 copy-done
  21.7 0.0 copy-done.1
  21.7 0.0 copy-done.2
  21.7 0.0 copy-done.3
  21.7 13.3 %image.1 = f32[2,160,80]{2,1,0:T(8,128)S(1)} custom-call(f32[5040,128]{1,0:T(8,128)S(1)} %get-tuple-element.35.refs_0_, f32[5040,128]{1,0:T(8,128)S(1)} %get-tuple-element.36.refs_1_, f32[5040,128]{1,0:T(8,128)S(1)} %get-tuple-element.37.refs_2_, f32[5040,128]{1,0:T(8,128)S(1)} %get-tuple-element.38.refs_3_, f32[5040,128]{1,0:T(8,128)S(1)} %get-tuple-element.39.refs_4_, ...), custom_call_target="tpu_custom_call" | custom-call | tf_op jit(solution)/shard_map/image/pallas_call | solution.py:528
  35.0 0.7 %copy.26 = f32[2,160,80]{2,1,0:T(8,128)} copy(f32[2,160,80]{2,1,0:T(8,128)S(1)} %image.1) | data formatting | bytes 204800
Async XLA Ops:
  1.7 13.4 %collective-permute-start = (f32[672,128]{1,0:T(8,128)S(1)}, f32[672,128]{1,0:T(8,128)S(1)}, u32[]{:S(2)}, u32[]{:S(2)}) collective-permute-start(f32[672,128]{1,0:T(8,128)S(1)} %get-tuple-element.25), channel_id=1, source_target_pairs={{0,4},{4,0},{1,5},{5,1},{2,6},{6,2},{3,7},{7,3}} | collective-permute-start | bytes 1032200 | tf_op jit(solution)/shard_map/ppermute | solution.py:511
  5.0 16.6 %collective-permute-start.1 = (f32[4,64,640]{2,1,0:T(8,128)S(1)}, f32[4,64,640]{2,1,0:T(8,128)S(1)}, u32[]{:S(2)}, u32[]{:S(2)}) collective-permute-start(f32[4,64,640]{2,1,0:T(8,128)S(1)} %get-tuple-element.43.refs_9_), channel_id=1, source_target_pairs={{0,2},{1,3},{2,0},{3,1},{4,6},{5,7},{6,4},{7,5}} | collective-permute-start | bytes 1966088 | tf_op jit(solution)/shard_map/ppermute | solution.py:524
  15.1 6.6 %copy-start = (bf16[1280,640]{1,0:T(8,128)(2,1)S(1)}, bf16[1280,640]{1,0:T(8,128)(2,1)}, u32[]{:S(2)}) copy-start(bf16[1280,640]{1,0:T(8,128)(2,1)} %constant.6.clone.refs_13_) | copy-start | bytes 4915204
  15.1 6.6 %copy-start.1 = (bf16[2,640,640]{2,1,0:T(8,128)(2,1)S(1)}, bf16[2,640,640]{2,1,0:T(8,128)(2,1)}, u32[]{:S(2)}) copy-start(bf16[2,640,640]{2,1,0:T(8,128)(2,1)} %constant.7.clone.refs_14_) | copy-start | bytes 4915204
  15.1 6.6 %copy-start.2 = (bf16[256,256]{1,0:T(8,128)(2,1)S(1)}, bf16[256,256]{1,0:T(8,128)(2,1)}, u32[]{:S(2)}) copy-start(bf16[256,256]{1,0:T(8,128)(2,1)} %constant.8.clone.refs_15_) | copy-start | bytes 393220
  15.1 6.6 %copy-start.3 = (f32[320]{0:T(512)S(1)}, f32[320]{0:T(512)}, u32[]{:S(2)}) copy-start(f32[320]{0:T(512)} %refs_12_.1) | copy-start | bytes 3844

commit v14 on v11

--- a/solution.py
+++ b/solution.py
@@ -30,6 +30,7 @@
 PS = 9
 PAY = 21
 CODE = 512
+MAPS = 240
 HW = 24
 ORDER = tuple(range(1, 9)) + (0, 9)
 GROUPS = ((0, 128), (128, 32))
@@ -85,14 +86,24 @@
     return jnp.asarray(m, BF)
 
 
-def prep_kernel(ks_hbm, wy_hbm, wx_hbm, iy_hbm, ix_hbm, maps_hbm, own_ref, far_ref, sp_ref, sq_ref, ks_ref, wy_ref, wx_ref, iy_ref, ix_ref, maps_ref, sem):
+def prep_kernel(ks_hbm, wy_hbm, wx_hbm, iy_hbm, ix_hbm, maps_hbm, own_ref, far_ref, sp_ref, sq_ref, sm_ref, ks_ref, wy_ref, wx_ref, iy_ref, ix_ref, maps_ref, sem):
     k = lax.axis_index('cols')
     r = lax.axis_index('rows')
     loads = []
-    for src, dst in ((iy_hbm, iy_ref), (ix_hbm, ix_ref), (wx_hbm, wx_ref), (wy_hbm, wy_ref), (ks_hbm, ks_ref), (maps_hbm, maps_ref)):
+    for src, dst in ((iy_hbm, iy_ref), (ix_hbm, ix_ref), (wx_hbm, wx_ref), (wy_hbm, wy_ref), (ks_hbm, ks_ref), (maps_hbm.at[:, :, :, WIDE:], maps_ref)):
         cp = pltpu.make_async_copy(src, dst, sem.at[len(loads)])
         cp.start()
         loads.append(cp)
+    parts = []
+    for c in range(4):
+        n = min(HALF, MAPS - HALF * c)
+        parts += [(sp_ref.at[pl.ds(HALF * c, n)], c, pl.ds(0, n)), (sq_ref.at[c], c, pl.ds(HALF, WIN))]
+    parts.append((sm_ref, 3, pl.ds(HALF - WIN, WIN)))
+    for ref, c, q in parts:
+        for i in range(2):
+            cp = pltpu.make_async_copy(maps_hbm.at[i, c, q, pl.ds(0, WIDE)], ref.at[:, pl.ds(WIDE * i, WIDE)], sem.at[len(loads)])
+            cp.start()
+            loads.append(cp)
     loads[0].wait()
     loads[1].wait()
     iy = iy_ref[...]
@@ -111,10 +122,14 @@
             ref[PAY * (b + 1) - 1:PAY * (b + 1), :] = code[b:b + 1, :]
     loads[5].wait()
     for c in range(4):
-        for ref, q in ((sp_ref, slice(0, HALF)), (sq_ref, slice(HALF, QB))):
-            for i in range(2):
-                ref[c, :, WIDE * i:WIDE * (i + 1)] = maps_ref[i, c, q, :WIDE]
-            ref[c, :, 2 * WIDE:] = jnp.concatenate([maps_ref[i, c, q, WIDE:] for i in range(2)], axis=1)
+        end = jnp.concatenate([maps_ref[i, c] for i in range(2)], axis=1)
+        n = min(HALF, MAPS - HALF * c)
+        sp_ref[HALF * c:HALF * c + n, 2 * WIDE:] = end[:n]
+        sq_ref[c, :, 2 * WIDE:] = end[HALF:]
+        if n < HALF:
+            sm_ref[:, 2 * WIDE:] = end[n:HALF]
+    for cp in loads[KW:]:
+        cp.wait()
 
 
 def split3(x):
@@ -269,8 +284,8 @@
 
 def image_kernel(*refs):
     accs = refs[:T]
-    (a_ref, pack_ref, so_ref, sx_ref, se_ref, d_ref, ev_ref, eu_ref, pm_ref, out_ref,
-     tb_ref, edge_ref, g_ref, halo, sm1, sm2, sr1, sr2, hm1, hm2, hr1, hr2, s_main, s_rem, acc_m, acc_r, pieces, recvs, tails, recvs_t,
+    (a_ref, pack_ref, so_ref, sx_ref, sm_ref, se_ref, d_ref, ev_ref, eu_ref, pm_ref, out_ref,
+     tb_ref, edge_ref, g_ref, halo, sm1, sm2, sr1, sr2, hm1, hm2, hr1, hr2, s_main, s_rem, acc_m, acc_r, sx_mid, pieces, recvs, tails, recvs_t,
      halo_ss, halo_rs, swap_ss, swap_rs, red_ss, red_rs) = refs[T:]
     k = lax.axis_index('cols')
     r = lax.axis_index('rows')
@@ -333,6 +348,8 @@
 
     for m in range(4):
         to_rows(QTR * m, LANES, tb_ref[2 * m + 1], tb_ref[2 * m + 2])
+
+    mid = remote(sm_ref, sx_mid, halo_ss, halo_rs, 2, {'rows': across})
 
     sms, srs, hms, hrs = (sm1, sm2), (sr1, sr2), (hm1, hm2), (hr1, hr2)
     swaps, trades = [], []
@@ -395,10 +412,12 @@
     def block_of(grp, j):
         return jnp.concatenate([hms[grp][(x + j) % 2, cp].reshape(4 * GROUPS[grp][1], LANES) for cp in range(2)], axis=1)
 
-    for j, ref in ((1, sx_ref), (0, so_ref)):
+    mid.wait_recv()
+    for j, ref, end in ((1, sx_ref, sx_mid), (0, so_ref, sm_ref)):
+        c = [ref[HALF * i:HALF * (i + 1), :] for i in range(3)] + [jnp.concatenate([ref[3 * HALF:, :], end[...]], axis=0)]
         acc_m[j] = jnp.dot(eu_ref[x, :, :n0], block_of(0, j), preferred_element_type=F32)
         for cp in range(2):
-            s_main[j, 0, cp], s_main[j, 1, cp] = turn(jnp.concatenate([ref[2 * cp + core], ref[2 * cp + 1 - core]], axis=0))
+            s_main[j, 0, cp], s_main[j, 1, cp] = turn(jnp.concatenate([jnp.where(core == 0, c[2 * cp], c[2 * cp + 1]), jnp.where(core == 0, c[2 * cp + 1], c[2 * cp])], axis=0))
 
     for cp in swaps[1:]:
         cp.wait_recv()
@@ -477,7 +496,7 @@
             end = pltpu.roll(rem, (HALF - QTR * j - WIN * o) % LANES, axis=1)
             out_ref[o, rows, :] = (jnp.where(low[rows], m[rows], end) * dd[rows])[:, :QB]
 
-    for cp in sends + swaps + trades + [tail]:
+    for cp in sends + swaps + trades + [mid, tail]:
         cp.wait_send()
 
 
@@ -491,11 +510,11 @@
     big = 6 * MIB
 
     def local_fn(kspace, wts_y, wts_x, idx_y, idx_x, coil_maps, deapod):
-        own, far, maps, maps_end = pl.pallas_call(
+        own, far, maps, maps_end, maps_mid = pl.pallas_call(
             prep_kernel,
-            out_shape=[jax.ShapeDtypeStruct((PAY * NB, LANES), F32)] * 2 + [jax.ShapeDtypeStruct((4, n, N_GRID), F32) for n in (HALF, WIN)],
-            in_specs=[hbm] * 6, out_specs=[vm] * 4, name='prep',
-            scratch_shapes=[VMEM((2, SUB, NS), F32), VMEM((KW, NS), F32), VMEM((KW, NS), F32), VMEM((NB, LANES), jnp.int32), VMEM((NB, LANES), jnp.int32), VMEM((2, 4, QB, N_IMG), F32), pltpu.SemaphoreType.DMA((6,))],
+            out_shape=[jax.ShapeDtypeStruct((PAY * NB, LANES), F32)] * 2 + [jax.ShapeDtypeStruct(d, F32) for d in ((MAPS, N_GRID), (4, WIN, N_GRID), (WIN, N_GRID))],
+            in_specs=[hbm] * 6, out_specs=[vm] * 5, name='prep',
+            scratch_shapes=[VMEM((2, SUB, NS), F32), VMEM((KW, NS), F32), VMEM((KW, NS), F32), VMEM((NB, LANES), jnp.int32), VMEM((NB, LANES), jnp.int32), VMEM((2, 4, QB, HALF), F32), pltpu.SemaphoreType.DMA((24,))],
             compiler_params=pltpu.CompilerParams(vmem_limit_bytes=SUB * MIB),
         )(*[pltpu.with_memory_space_constraint(v, pltpu.HBM) for v in (kspace, wts_y, wts_x, idx_y.reshape(NB, LANES), idx_x.reshape(NB, LANES), jnp.swapaxes(coil_maps, 2, 3))])
         far_in = lax.ppermute(far, 'cols', [(0, 1), (1, 0)])
@@ -517,15 +536,15 @@
         full_bufs = [VMEM((2, 2, 2, 2, n, LANES), BF) for _, n in GROUPS] + [VMEM((ROWS, n, LANES), BF) for _, n in GROUPS]
         return pl.pallas_call(
             image_kernel,
-            out_shape=jax.ShapeDtypeStruct((2, PB, QB), F32), in_specs=[vm] * (T + 9), out_specs=vm,
+            out_shape=jax.ShapeDtypeStruct((2, PB, QB), F32), in_specs=[vm] * (T + TILES), out_specs=vm,
             scratch_shapes=[VMEM((TILES, N_GRID, LANES), BF), VMEM((N_GRID, LANES), F32), VMEM((4 * RB, 2 * N_GRID), BF), VMEM((2, LANES, LANES), F32)] + half_bufs + full_bufs + [
                 VMEM((2, 2, 2, N_IMG, LANES), F32), VMEM((2, N_IMG, LANES), F32),
-                VMEM((2, 2 * N_IMG, 2 * LANES), F32), VMEM((2, 2 * N_IMG, LANES), F32),
+                VMEM((2, 2 * N_IMG, 2 * LANES), F32), VMEM((2, 2 * N_IMG, LANES), F32), VMEM((WIN, N_GRID), F32),
                 VMEM((3, PB, LANES), F32), VMEM((3, PB, LANES), F32), VMEM((PB // 4, LANES), F32), VMEM((PB // 4, LANES), F32),
-                dma((2,)), dma((2,)), dma((8,)), dma((8,)), dma((4,)), dma((4,)),
+                dma((3,)), dma((3,)), dma((8,)), dma((8,)), dma((4,)), dma((4,)),
             ],
             compiler_params=pltpu.CompilerParams(vmem_limit_bytes=11 * MIB, collective_id=0, has_side_effects=True), name='image',
-        )(*accs, half, pack, maps, maps_x, maps_end, deapod, col_dft(), row_dft(), unmix())
+        )(*accs, half, pack, maps, maps_x, maps_mid, maps_end, deapod, col_dft(), row_dft(), unmix())
 
     return jax.shard_map(
         local_fn,

time: 35.7 us -> 35.6 us (level)
  no operation moved by 1% of the time
where the time goes in v14:
time: 35.6 us; the launch traced here: 35.4 us
  Pallas kernels  29.7 us (83%)
  starting transfers between devices  4.88 us (14%)
  local copies, waits for them, and re-layouts  0.7 us (2%)
    pallas_call x1, Pallas kernels, local_fn(): pl.pallas_call(image_kernel, out_shape=jax.ShapeDtypeStruct((2, PB, QB),...  13.1 us
    pallas_call x1, Pallas kernels, local_fn(): pl.pallas_call(own_kernel, out_shape=[jax.ShapeDtypeStruct((11, CW, LANES...  8.54 us
    pallas_call x1, Pallas kernels, local_fn(): pl.pallas_call(far_kernel, out_shape=acc_shape + [jax.ShapeDtypeStruct((2...  6.46 us
    ppermute x1, starting transfers between devices, local_fn(): far_in = lax.ppermute(far, 'cols', [(0, 1), (1, 0)])  3.39 us
    pallas_call x1, Pallas kernels, local_fn(): pl.pallas_call(prep_kernel, out_shape=[jax.ShapeDtypeStruct((PAY * NB, LA...  1.56 us
    ppermute x1, starting transfers between devices, local_fn(): lax.ppermute(maps, 'rows', [(i, (i + 2) % ROWS) for i in range(ROWS)])  1.49 us
  transfers between devices with their start and end apart: 2, of which 0 were waited for; matrix products, arithmetic and copies ran while one was open for 0% of the time, Pallas kernels for 42%

profile of v14, /device:TPU:0, one launch (start us, length us, event | category | flops | bytes accessed | tf_op | source)
XLA Modules:
  0.0 35.4 jit_solution(9793332070497078286)
XLA Ops:
  0.0 1.6 %prep.1 = (f32[672,128]{1,0:T(8,128)S(1)}, f32[672,128]{1,0:T(8,128)S(1)}, f32[240,640]{1,0:T(8,128)S(1)}, f32[4,16,640]{2,1,0:T(8,128)S(1)}, f32[16,640]{1,0:T(8,128)S(1)}) custom-call(f32[2,8,4096]{2,1,0:T(8,128)} %ks_hbm.1, f32[6,4096]{1,0:T(8,128)} %wy_hbm.1, f32[6,4096]{1,0:T(8,128)} %wx_hbm.1, s32[32,128]{1,0:T(8,128)} %bitcast.4, s32[32,128]{1,0:T(8,128)} %bitcast.5, ...), custom_call_target="tpu_custom_call" | custom-call | tf_op jit(solution)/shard_map/prep/pallas_call | solution.py:513
  1.6 3.4 %collective-permute-start = (f32[672,128]{1,0:T(8,128)S(1)}, f32[672,128]{1,0:T(8,128)S(1)}, u32[]{:S(2)}, u32[]{:S(2)}) collective-permute-start(f32[672,128]{1,0:T(8,128)S(1)} %get-tuple-element.26), channel_id=1, source_target_pairs={{0,4},{4,0},{1,5},{5,1},{2,6},{6,2},{3,7},{7,3}} | collective-permute-start | bytes 1032200 | tf_op jit(solution)/shard_map/ppermute | solution.py:520
  5.0 1.5 %collective-permute-start.1 = (f32[240,640]{1,0:T(8,128)S(1)}, f32[240,640]{1,0:T(8,128)S(1)}, u32[]{:S(2)}, u32[]{:S(2)}) collective-permute-start(f32[240,640]{1,0:T(8,128)S(1)} %get-tuple-element.44.refs_9_), channel_id=1, source_target_pairs={{0,2},{1,3},{2,0},{3,1},{4,6},{5,7},{6,4},{7,5}} | collective-permute-start | bytes 1843208 | tf_op jit(solution)/shard_map/ppermute | solution.py:533
  6.5 8.5 %spread_own.1 = (f32[11,336,128]{2,1,0:T(8,128)S(1)}, f32[5040,128]{1,0:T(8,128)S(1)}, f32[5040,128]{1,0:T(8,128)S(1)}, f32[5040,128]{1,0:T(8,128)S(1)}, f32[504...) custom-call(f32[672,128]{1,0:T(8,128)S(1)} %get-tuple-element.27.pay_ref), custom_call_target="tpu_custom_call" | custom-call | flops 4194304000 | bytes 4194304 | tf_op jit(solution)/shard_map/spread_own/pallas_call | solution.py:521
  15.0 0.0 collective-permute-done.pay_ref
  15.0 0.0 copy-start
  15.0 0.0 copy-start.1
  15.0 0.0 copy-start.2
  15.1 0.0 copy-start.3
  15.1 6.5 %spread_far.1 = (f32[5040,128]{1,0:T(8,128)S(1)}, f32[5040,128]{1,0:T(8,128)S(1)}, f32[5040,128]{1,0:T(8,128)S(1)}, f32[5040,128]{1,0:T(8,128)S(1)}, f32[5040,12...) custom-call(f32[672,128]{1,0:T(8,128)S(1)} %collective-permute-done., ...), custom_call_target="tpu_custom_call", output_to_operand_aliasing={{0}: (2, {}), {1}: (3, {}), {2}: (4, {}), {3}: (5, {}), {4}... | custom-call | flops 4194304000 | bytes 4194304 | tf_op jit(solution)/shard_map/spread_far/pallas_call | solution.py:526
  21.5 0.0 collective-permute-done.1.refs_10_
  21.5 0.0 copy-done
  21.6 0.0 copy-done.1
  21.6 0.0 copy-done.2
  21.6 0.0 copy-done.3
  21.6 13.1 %image.1 = f32[2,160,80]{2,1,0:T(8,128)S(1)} custom-call(f32[5040,128]{1,0:T(8,128)S(1)} %get-tuple-element.36.refs_0_, f32[5040,128]{1,0:T(8,128)S(1)} %get-tuple-element.37.refs_1_, f32[5040,128]{1,0:T(8,128)S(1)} %get-tuple-element.38.refs_2_, f32[5040,128]{1,0:T(8,128)S(1)} %get-tuple-element.39.refs_3_, f32[5040,128]{1,0:T(8,128)S(1)} %get-tuple-element.40.refs_4_, ...), custom_call_target="tpu_custom_call" | custom-call | tf_op jit(solution)/shard_map/image/pallas_call | solution.py:537
  34.7 0.7 %copy.26 = f32[2,160,80]{2,1,0:T(8,128)} copy(f32[2,160,80]{2,1,0:T(8,128)S(1)} %image.1) | data formatting | bytes 204800
Async XLA Ops:
  1.6 13.4 %collective-permute-start = (f32[672,128]{1,0:T(8,128)S(1)}, f32[672,128]{1,0:T(8,128)S(1)}, u32[]{:S(2)}, u32[]{:S(2)}) collective-permute-start(f32[672,128]{1,0:T(8,128)S(1)} %get-tuple-element.26), channel_id=1, source_target_pairs={{0,4},{4,0},{1,5},{5,1},{2,6},{6,2},{3,7},{7,3}} | collective-permute-start | bytes 1032200 | tf_op jit(solution)/shard_map/ppermute | solution.py:520
  5.0 16.6 %collective-permute-start.1 = (f32[240,640]{1,0:T(8,128)S(1)}, f32[240,640]{1,0:T(8,128)S(1)}, u32[]{:S(2)}, u32[]{:S(2)}) collective-permute-start(f32[240,640]{1,0:T(8,128)S(1)} %get-tuple-element.44.refs_9_), channel_id=1, source_target_pairs={{0,2},{1,3},{2,0},{3,1},{4,6},{5,7},{6,4},{7,5}} | collective-permute-start | bytes 1843208 | tf_op jit(solution)/shard_map/ppermute | solution.py:533
  15.0 6.5 %copy-start = (bf16[1280,640]{1,0:T(8,128)(2,1)S(1)}, bf16[1280,640]{1,0:T(8,128)(2,1)}, u32[]{:S(2)}) copy-start(bf16[1280,640]{1,0:T(8,128)(2,1)} %constant.6.clone.refs_14_) | copy-start | bytes 4915204
  15.0 6.5 %copy-start.1 = (bf16[2,640,640]{2,1,0:T(8,128)(2,1)S(1)}, bf16[2,640,640]{2,1,0:T(8,128)(2,1)}, u32[]{:S(2)}) copy-start(bf16[2,640,640]{2,1,0:T(8,128)(2,1)} %constant.7.clone.refs_15_) | copy-start | bytes 4915204
  15.0 6.5 %copy-start.2 = (bf16[256,256]{1,0:T(8,128)(2,1)S(1)}, bf16[256,256]{1,0:T(8,128)(2,1)}, u32[]{:S(2)}) copy-start(bf16[256,256]{1,0:T(8,128)(2,1)} %constant.8.clone.refs_16_) | copy-start | bytes 393220
  15.1 6.5 %copy-start.3 = (f32[320]{0:T(512)S(1)}, f32[320]{0:T(512)}, u32[]{:S(2)}) copy-start(f32[320]{0:T(512)} %refs_13_.1) | copy-start | bytes 3844

commit v15 on v14

--- a/solution.py
+++ b/solution.py
@@ -86,7 +86,7 @@
     return jnp.asarray(m, BF)
 
 
-def prep_kernel(ks_hbm, wy_hbm, wx_hbm, iy_hbm, ix_hbm, maps_hbm, own_ref, far_ref, sp_ref, sq_ref, sm_ref, ks_ref, wy_ref, wx_ref, iy_ref, ix_ref, maps_ref, sem):
+def prep_kernel(ks_hbm, wy_hbm, wx_hbm, iy_hbm, ix_hbm, maps_hbm, own_ref, far_ref, sp_ref, sq_ref, sm_ref, r_ref, ks_ref, wy_ref, wx_ref, iy_ref, ix_ref, maps_ref, sem):
     k = lax.axis_index('cols')
     r = lax.axis_index('rows')
     loads = []
@@ -104,6 +104,9 @@
             cp = pltpu.make_async_copy(maps_hbm.at[i, c, q, pl.ds(0, WIDE)], ref.at[:, pl.ds(WIDE * i, WIDE)], sem.at[len(loads)])
             cp.start()
             loads.append(cp)
+    kk = lax.broadcasted_iota(jnp.int32, (LANES, WIDE * 3), 0)
+    ll = lax.broadcasted_iota(jnp.int32, (LANES, WIDE * 3), 1)
+    r_ref[...] = jnp.where((kk < HW) & ((kk & 7) == (ll >> 7)), 1.0, 0.0).astype(BF)
     loads[0].wait()
     loads[1].wait()
     iy = iy_ref[...]
@@ -139,7 +142,7 @@
     return hi, mid, r - mid
 
 
-def accumulate(pay_ref, accs, us, xs, vs, r_ref, int_ref, base_ref, sem):
+def accumulate(pay_ref, r_ref, accs, us, xs, vs, int_ref, base_ref, sem):
     row_i = lax.broadcasted_iota(jnp.int32, (WIN, LANES), 0)
 
     def make_u(blk, k):
@@ -174,11 +177,10 @@
 
     code = jnp.concatenate([pay_ref[PAY * (b + 1) - 1:PAY * (b + 1), :] for b in range(NB)], axis=0).astype(jnp.int32)
     int_ref[...] = (((code // CODE - 5) * 187) >> STEP) * CW + (code & (CODE - 1))
-    kk = lax.broadcasted_iota(jnp.int32, (LANES, WIDE * 3), 0)
-    ll = lax.broadcasted_iota(jnp.int32, (LANES, WIDE * 3), 1)
-    r_ref[...] = jnp.where((kk < HW) & ((kk & 7) == (ll >> 7)), 1.0, 0.0).astype(BF)
     for v in vs:
-        v[...] = jnp.zeros_like(v)
+        for g in range(WIN):
+            for c in range(KW, SUB):
+                v[pl.ds(SUB * PS * g + c, SUB, stride=PS), :] = jnp.zeros((SUB, LANES), F32)
     load = pltpu.make_async_copy(int_ref, base_ref, sem)
     load.start()
     make_u(0, 0)
@@ -225,7 +227,7 @@
     return tiles + [jnp.where(row >= SUB, v, ghost)]
 
 
-def own_kernel(pay_ref, out_ref, *refs):
+def own_kernel(pay_ref, r_ref, out_ref, *refs):
     accs, scr = refs[:T], refs[T:]
 
     def clear(n, _):
@@ -234,7 +236,7 @@
         return 0
 
     lax.fori_loop(0, NG, clear, 0)
-    accumulate(pay_ref, accs, scr[:2], scr[2:4], scr[4:6], *scr[6:])
+    accumulate(pay_ref, r_ref, accs, scr[:2], scr[2:4], scr[4:6], *scr[6:])
 
     def fold(q, _):
         off = pl.multiple_of(q * WIN, WIN)
@@ -245,9 +247,9 @@
     lax.fori_loop(0, CW // WIN, fold, 0)
 
 
-def far_kernel(pay_ref, a_ref, *refs):
+def far_kernel(pay_ref, r_ref, a_ref, *refs):
     accs, pack_ref, gh_ref, scr = refs[T:2 * T], refs[2 * T], refs[2 * T + 1], refs[2 * T + 2:]
-    accumulate(pay_ref, accs, scr[:2], scr[2:4], scr[4:6], *scr[6:])
+    accumulate(pay_ref, r_ref, accs, scr[:2], scr[2:4], scr[4:6], *scr[6:])
     own0 = lax.axis_index('cols') * CB
     far0 = CB - own0
 
@@ -505,31 +507,31 @@
     vm = pl.BlockSpec(memory_space=pltpu.VMEM)
     hbm = pl.BlockSpec(memory_space=pltpu.HBM)
     spread_scratch = ([VMEM((LANES, LANES), F32)] * 4 + [VMEM((LANES * PS, LANES), F32)] * 2
-                      + [VMEM((LANES, WIDE * 3), BF), VMEM((NB, LANES), jnp.int32), pltpu.SMEM((NB, LANES), jnp.int32), pltpu.SemaphoreType.DMA])
+                      + [VMEM((NB, LANES), jnp.int32), pltpu.SMEM((NB, LANES), jnp.int32), pltpu.SemaphoreType.DMA])
     acc_shape = [jax.ShapeDtypeStruct((NG * CW, LANES), F32)] * T
     big = 6 * MIB
 
     def local_fn(kspace, wts_y, wts_x, idx_y, idx_x, coil_maps, deapod):
-        own, far, maps, maps_end, maps_mid = pl.pallas_call(
+        own, far, maps, maps_end, maps_mid, spread_mat = pl.pallas_call(
             prep_kernel,
-            out_shape=[jax.ShapeDtypeStruct((PAY * NB, LANES), F32)] * 2 + [jax.ShapeDtypeStruct(d, F32) for d in ((MAPS, N_GRID), (4, WIN, N_GRID), (WIN, N_GRID))],
-            in_specs=[hbm] * 6, out_specs=[vm] * 5, name='prep',
+            out_shape=[jax.ShapeDtypeStruct((PAY * NB, LANES), F32)] * 2 + [jax.ShapeDtypeStruct(d, F32) for d in ((MAPS, N_GRID), (4, WIN, N_GRID), (WIN, N_GRID))] + [jax.ShapeDtypeStruct((LANES, WIDE * 3), BF)],
+            in_specs=[hbm] * 6, out_specs=[vm] * 6, name='prep',
             scratch_shapes=[VMEM((2, SUB, NS), F32), VMEM((KW, NS), F32), VMEM((KW, NS), F32), VMEM((NB, LANES), jnp.int32), VMEM((NB, LANES), jnp.int32), VMEM((2, 4, QB, HALF), F32), pltpu.SemaphoreType.DMA((24,))],
             compiler_params=pltpu.CompilerParams(vmem_limit_bytes=SUB * MIB),
         )(*[pltpu.with_memory_space_constraint(v, pltpu.HBM) for v in (kspace, wts_y, wts_x, idx_y.reshape(NB, LANES), idx_x.reshape(NB, LANES), jnp.swapaxes(coil_maps, 2, 3))])
         far_in = lax.ppermute(far, 'cols', [(0, 1), (1, 0)])
         half, *accs = pl.pallas_call(
-            own_kernel, out_shape=[jax.ShapeDtypeStruct((11, CW, LANES), F32)] + acc_shape, in_specs=[vm], out_specs=[vm] * (T + 1),
+            own_kernel, out_shape=[jax.ShapeDtypeStruct((11, CW, LANES), F32)] + acc_shape, in_specs=[vm] * 2, out_specs=[vm] * (T + 1),
             scratch_shapes=spread_scratch, compiler_params=pltpu.CompilerParams(vmem_limit_bytes=big), name='spread_own',
             cost_estimate=pl.CostEstimate(flops=GIGA, bytes_accessed=4 * MIB, transcendentals=0),
-        )(own)
+        )(own, spread_mat)
         *accs, pack = pl.pallas_call(
             far_kernel, out_shape=acc_shape + [jax.ShapeDtypeStruct((2, LANES, LANES), F32)],
-            in_specs=[vm] * (T + 2), out_specs=[vm] * (T + 1), scratch_shapes=[VMEM((N_GRID, LANES), F32)] + spread_scratch,
-            input_output_aliases={i + 2: i for i in range(T)},
+            in_specs=[vm] * (T + 3), out_specs=[vm] * (T + 1), scratch_shapes=[VMEM((N_GRID, LANES), F32)] + spread_scratch,
+            input_output_aliases={i + 3: i for i in range(T)},
             compiler_params=pltpu.CompilerParams(vmem_limit_bytes=big), name='spread_far',
             cost_estimate=pl.CostEstimate(flops=GIGA, bytes_accessed=4 * MIB, transcendentals=0),
-        )(far_in, half, *accs)
+        )(far_in, spread_mat, half, *accs)
         maps_x = lax.ppermute(maps, 'rows', [(i, (i + 2) % ROWS) for i in range(ROWS)])
         dma = pltpu.SemaphoreType.DMA
         half_bufs = [VMEM((2, 2, 2, n, LANES), BF) for _, n in GROUPS] + [VMEM((ROWS, n, LANES), BF) for _, n in GROUPS]

time: 35.6 us -> 35.8 us (level)
  transfers between devices with their start and end apart: 2 -> 2, of which waited for: 0 -> 0; matrix products, arithmetic and copies ran while one was open for 0% -> 0% of each run, Pallas kernels for 42% -> 43%
where the time goes in v15:
time: 35.8 us; the launch traced here: 35.6 us
  Pallas kernels  29.9 us (84%)
  starting transfers between devices  4.88 us (14%)
  local copies, waits for them, and re-layouts  0.7 us (2%)
    pallas_call x1, Pallas kernels, local_fn(): pl.pallas_call(image_kernel, out_shape=jax.ShapeDtypeStruct((2, PB, QB),...  13.1 us
    pallas_call x1, Pallas kernels, local_fn(): pl.pallas_call(own_kernel, out_shape=[jax.ShapeDtypeStruct((11, CW, LANES...  8.64 us
    pallas_call x1, Pallas kernels, local_fn(): pl.pallas_call(far_kernel, out_shape=acc_shape + [jax.ShapeDtypeStruct((2...  6.54 us
    ppermute x1, starting transfers between devices, local_fn(): far_in = lax.ppermute(far, 'cols', [(0, 1), (1, 0)])  3.39 us
    pallas_call x1, Pallas kernels, local_fn(): pl.pallas_call(prep_kernel, out_shape=[jax.ShapeDtypeStruct((PAY * NB, LA...  1.56 us
    ppermute x1, starting transfers between devices, local_fn(): lax.ppermute(maps, 'rows', [(i, (i + 2) % ROWS) for i in range(ROWS)])  1.49 us
  transfers between devices with their start and end apart: 2, of which 0 were waited for; matrix products, arithmetic and copies ran while one was open for 0% of the time, Pallas kernels for 43%

profile of v15, /device:TPU:0, one launch (start us, length us, event | category | flops | bytes accessed | tf_op | source)
XLA Modules:
  0.0 35.6 jit_solution(3319874157226591954)
XLA Ops:
  0.0 1.6 %prep.1 = (f32[672,128]{1,0:T(8,128)S(1)}, f32[672,128]{1,0:T(8,128)S(1)}, f32[240,640]{1,0:T(8,128)S(1)}, f32[4,16,640]{2,1,0:T(8,128)S(1)}, f32[16,640]{1,0:T(8,128)S(1)}, /*index=5*/bf16[128,768]{1,0:T(8,128)(2,1)S(1)}) custom-call(f32[2,8,4096]{2,1,0:T(8,128)} %ks_hbm.1, f32[6,4096]{1,0:T(8,128)} %wy_hbm.1, f32[6,4096]{1,0:T(8,128)} %wx_hbm.1, ...), custom_call_target="tpu_custom_call" | custom-call | tf_op jit(solution)/shard_map/prep/pallas_call | solution.py:515
  1.6 3.4 %collective-permute-start = (f32[672,128]{1,0:T(8,128)S(1)}, f32[672,128]{1,0:T(8,128)S(1)}, u32[]{:S(2)}, u32[]{:S(2)}) collective-permute-start(f32[672,128]{1,0:T(8,128)S(1)} %get-tuple-element.27), channel_id=1, source_target_pairs={{0,4},{4,0},{1,5},{5,1},{2,6},{6,2},{3,7},{7,3}} | collective-permute-start | bytes 1032200 | tf_op jit(solution)/shard_map/ppermute | solution.py:522
  5.0 1.5 %collective-permute-start.1 = (f32[240,640]{1,0:T(8,128)S(1)}, f32[240,640]{1,0:T(8,128)S(1)}, u32[]{:S(2)}, u32[]{:S(2)}) collective-permute-start(f32[240,640]{1,0:T(8,128)S(1)} %get-tuple-element.46.refs_9_), channel_id=1, source_target_pairs={{0,2},{1,3},{2,0},{3,1},{4,6},{5,7},{6,4},{7,5}} | collective-permute-start | bytes 1843208 | tf_op jit(solution)/shard_map/ppermute | solution.py:535
  6.5 8.6 %spread_own.1 = (f32[11,336,128]{2,1,0:T(8,128)S(1)}, f32[5040,128]{1,0:T(8,128)S(1)}, f32[5040,128]{1,0:T(8,128)S(1)}, f32[5040,128]{1,0:T(8,128)S(1)}, f32[504...) custom-call(f32[672,128]{1,0:T(8,128)S(1)} %get-tuple-element.29.pay_ref, ...), custom_call_target="tpu_custom_call" | custom-call | flops 4194304000 | bytes 4194304 | tf_op jit(solution)/shard_map/spread_own/pallas_call | solution.py:523
  15.1 0.0 collective-permute-done.pay_ref
  15.1 0.0 copy-start
  15.1 0.0 copy-start.1
  15.1 0.0 copy-start.2
  15.1 0.0 copy-start.3
  15.2 6.5 %spread_far.1 = (f32[5040,128]{1,0:T(8,128)S(1)}, f32[5040,128]{1,0:T(8,128)S(1)}, f32[5040,128]{1,0:T(8,128)S(1)}, f32[5040,128]{1,0:T(8,128)S(1)}, f32[5040,12...) custom-call(f32[672,128]{1,0:T(8,128)S(1)} %collective-permute-done., ...), custom_call_target="tpu_custom_call", output_to_operand_aliasing={{0}: (3, {}), {1}: (4, {}), {2}: (5, {}), {3}: (6, {}), {4}... | custom-call | flops 4194304000 | bytes 4194304 | tf_op jit(solution)/shard_map/spread_far/pallas_call | solution.py:528
  21.7 0.0 collective-permute-done.1.refs_10_
  21.7 0.0 copy-done
  21.7 0.0 copy-done.1
  21.7 0.0 copy-done.2
  21.7 0.0 copy-done.3
  21.8 13.1 %image.1 = f32[2,160,80]{2,1,0:T(8,128)S(1)} custom-call(f32[5040,128]{1,0:T(8,128)S(1)} %get-tuple-element.38.refs_0_, f32[5040,128]{1,0:T(8,128)S(1)} %get-tuple-element.39.refs_1_, f32[5040,128]{1,0:T(8,128)S(1)} %get-tuple-element.40.refs_2_, f32[5040,128]{1,0:T(8,128)S(1)} %get-tuple-element.41.refs_3_, f32[5040,128]{1,0:T(8,128)S(1)} %get-tuple-element.42.refs_4_, ...), custom_call_target="tpu_custom_call" | custom-call | tf_op jit(solution)/shard_map/image/pallas_call | solution.py:539
  34.9 0.7 %copy.26 = f32[2,160,80]{2,1,0:T(8,128)} copy(f32[2,160,80]{2,1,0:T(8,128)S(1)} %image.1) | data formatting | bytes 204800
Async XLA Ops:
  1.6 13.5 %collective-permute-start = (f32[672,128]{1,0:T(8,128)S(1)}, f32[672,128]{1,0:T(8,128)S(1)}, u32[]{:S(2)}, u32[]{:S(2)}) collective-permute-start(f32[672,128]{1,0:T(8,128)S(1)} %get-tuple-element.27), channel_id=1, source_target_pairs={{0,4},{4,0},{1,5},{5,1},{2,6},{6,2},{3,7},{7,3}} | collective-permute-start | bytes 1032200 | tf_op jit(solution)/shard_map/ppermute | solution.py:522
  5.0 16.7 %collective-permute-start.1 = (f32[240,640]{1,0:T(8,128)S(1)}, f32[240,640]{1,0:T(8,128)S(1)}, u32[]{:S(2)}, u32[]{:S(2)}) collective-permute-start(f32[240,640]{1,0:T(8,128)S(1)} %get-tuple-element.46.refs_9_), channel_id=1, source_target_pairs={{0,2},{1,3},{2,0},{3,1},{4,6},{5,7},{6,4},{7,5}} | collective-permute-start | bytes 1843208 | tf_op jit(solution)/shard_map/ppermute | solution.py:535
  15.1 6.6 %copy-start = (bf16[1280,640]{1,0:T(8,128)(2,1)S(1)}, bf16[1280,640]{1,0:T(8,128)(2,1)}, u32[]{:S(2)}) copy-start(bf16[1280,640]{1,0:T(8,128)(2,1)} %constant.6.clone.refs_14_) | copy-start | bytes 4915204
  15.1 6.6 %copy-start.1 = (bf16[2,640,640]{2,1,0:T(8,128)(2,1)S(1)}, bf16[2,640,640]{2,1,0:T(8,128)(2,1)}, u32[]{:S(2)}) copy-start(bf16[2,640,640]{2,1,0:T(8,128)(2,1)} %constant.7.clone.refs_15_) | copy-start | bytes 4915204
  15.1 6.6 %copy-start.2 = (bf16[256,256]{1,0:T(8,128)(2,1)S(1)}, bf16[256,256]{1,0:T(8,128)(2,1)}, u32[]{:S(2)}) copy-start(bf16[256,256]{1,0:T(8,128)(2,1)} %constant.8.clone.refs_16_) | copy-start | bytes 393220
  15.1 6.6 %copy-start.3 = (f32[320]{0:T(512)S(1)}, f32[320]{0:T(512)}, u32[]{:S(2)}) copy-start(f32[320]{0:T(512)} %refs_13_.1) | copy-start | bytes 3844

commit v16 on v14

--- a/solution.py
+++ b/solution.py
@@ -458,10 +458,15 @@
             out = jnp.where(quarter == g, pltpu.roll(w[PB // 4 * g:PB // 4 * (g + 1)], QTR * g, axis=1), out)
         return out
 
-    sends = []
-    for i, (half, j) in enumerate(((1 - k, 1), (k, 1), (1 - k, 0))):
-        pieces[i] = piece(half, j)
-        sends.append(remote(pieces.at[i], recvs.at[i], red_ss, red_rs, i, homes[i]))
+    first, other = pl.ds(0, (QTR + WIN)), pl.ds((QTR + WIN), PB - (QTR + WIN))
+    pieces[0] = piece(1 - k, 1)
+    joined = remote(pieces.at[0, first], recvs.at[0, first], red_ss, red_rs, 0, homes[1])
+    sends = [remote(pieces.at[0, other], recvs.at[0, other], red_ss, red_rs, 1, homes[0])]
+    pieces[1] = piece(k, 1)
+    sends.append(remote(pieces.at[1], recvs.at[1], red_ss, red_rs, 2, homes[1]))
+    across_y = piece(1 - k, 0)
+    pieces[2, (QTR + WIN):] = across_y[(QTR + WIN):]
+    sends.append(remote(pieces.at[2, other], recvs.at[2, other], red_ss, red_rs, 4, homes[2]))
     for cp in trades:
         cp.wait_recv()
     for t in range(2):
@@ -476,6 +481,9 @@
     tails[...] = rest(1 - k)
     tail = remote(tails, recvs_t, red_ss, red_rs, 3, homes[2])
     rem = rest(k)
+    joined.wait_recv()
+    pieces[2, :(QTR + WIN)] = across_y[:(QTR + WIN)] + recvs[0, :(QTR + WIN)]
+    sends.append(remote(pieces.at[2, first], recvs.at[2, first], red_ss, red_rs, 5, homes[2]))
     main = piece(k, 0)
     d8 = jnp.broadcast_to(jnp.concatenate([d_ref[...][None, :], jnp.zeros((1, HALF), F32)], axis=1), (SUB, N_IMG + HALF))
     dq = d8
@@ -484,9 +492,10 @@
     dp = jnp.where(k == 0, d8, pltpu.roll(d8, N_IMG + HALF - PB, axis=1))[:, :2 * LANES]
     dd = jnp.concatenate([dp] * WIN, axis=0).T[:PB] * dq[:1, :LANES]
 
-    for i in (2, 0, 1):
-        sends[i].wait_recv()
-        main = main + recvs[i]
+    for cp in sends:
+        cp.wait_recv()
+    main = main + recvs[1] + recvs[2]
+    main = jnp.concatenate([main[:(QTR + WIN)], main[(QTR + WIN):] + recvs[0, (QTR + WIN):]], axis=0)
     tail.wait_recv()
     rem = rem + recvs_t[...]
     for o in range(2):
@@ -496,7 +505,7 @@
             end = pltpu.roll(rem, (HALF - QTR * j - WIN * o) % LANES, axis=1)
             out_ref[o, rows, :] = (jnp.where(low[rows], m[rows], end) * dd[rows])[:, :QB]
 
-    for cp in sends + swaps + trades + [mid, tail]:
+    for cp in sends + swaps + trades + [mid, tail, joined]:
         cp.wait_send()
 
 
@@ -541,7 +550,7 @@
                 VMEM((2, 2, 2, N_IMG, LANES), F32), VMEM((2, N_IMG, LANES), F32),
                 VMEM((2, 2 * N_IMG, 2 * LANES), F32), VMEM((2, 2 * N_IMG, LANES), F32), VMEM((WIN, N_GRID), F32),
                 VMEM((3, PB, LANES), F32), VMEM((3, PB, LANES), F32), VMEM((PB // 4, LANES), F32), VMEM((PB // 4, LANES), F32),
-                dma((3,)), dma((3,)), dma((8,)), dma((8,)), dma((4,)), dma((4,)),
+                dma((3,)), dma((3,)), dma((8,)), dma((8,)), dma((6,)), dma((6,)),
             ],
             compiler_params=pltpu.CompilerParams(vmem_limit_bytes=11 * MIB, collective_id=0, has_side_effects=True), name='image',
         )(*accs, half, pack, maps, maps_x, maps_mid, maps_end, deapod, col_dft(), row_dft(), unmix())

time: 35.6 us -> 35.3 us (level)
    pallas_call x1, Pallas kernels: 13.1 us -> 12.8 us  [local_fn(): pl.pallas_call(image_kernel, out_shape=jax.ShapeDtypeStruct((2, PB, QB),...]
  transfers between devices with their start and end apart: 2 -> 2, of which waited for: 0 -> 0; matrix products, arithmetic and copies ran while one was open for 0% -> 0% of each run, Pallas kernels for 42% -> 43%
where the time goes in v16:
time: 35.3 us; the launch traced here: 35 us
  Pallas kernels  29.4 us (83%)
  starting transfers between devices  4.88 us (14%)
  local copies, waits for them, and re-layouts  0.7 us (2%)
    pallas_call x1, Pallas kernels, local_fn(): pl.pallas_call(image_kernel, out_shape=jax.ShapeDtypeStruct((2, PB, QB),...  12.8 us
    pallas_call x1, Pallas kernels, local_fn(): pl.pallas_call(own_kernel, out_shape=[jax.ShapeDtypeStruct((11, CW, LANES...  8.54 us
    pallas_call x1, Pallas kernels, local_fn(): pl.pallas_call(far_kernel, out_shape=acc_shape + [jax.ShapeDtypeStruct((2...  6.48 us
    ppermute x1, starting transfers between devices, local_fn(): far_in = lax.ppermute(far, 'cols', [(0, 1), (1, 0)])  3.39 us
    pallas_call x1, Pallas kernels, local_fn(): pl.pallas_call(prep_kernel, out_shape=[jax.ShapeDtypeStruct((PAY * NB, LA...  1.56 us
    ppermute x1, starting transfers between devices, local_fn(): lax.ppermute(maps, 'rows', [(i, (i + 2) % ROWS) for i in range(ROWS)])  1.49 us
  transfers between devices with their start and end apart: 2, of which 0 were waited for; matrix products, arithmetic and copies ran while one was open for 0% of the time, Pallas kernels for 43%

profile of v16, /device:TPU:0, one launch (start us, length us, event | category | flops | bytes accessed | tf_op | source)
XLA Modules:
  0.0 35.0 jit_solution(2636440963187016366)
XLA Ops:
  0.0 1.6 %prep.1 = (f32[672,128]{1,0:T(8,128)S(1)}, f32[672,128]{1,0:T(8,128)S(1)}, f32[240,640]{1,0:T(8,128)S(1)}, f32[4,16,640]{2,1,0:T(8,128)S(1)}, f32[16,640]{1,0:T(8,128)S(1)}) custom-call(f32[2,8,4096]{2,1,0:T(8,128)} %ks_hbm.1, f32[6,4096]{1,0:T(8,128)} %wy_hbm.1, f32[6,4096]{1,0:T(8,128)} %wx_hbm.1, s32[32,128]{1,0:T(8,128)} %bitcast.4, s32[32,128]{1,0:T(8,128)} %bitcast.5, ...), custom_call_target="tpu_custom_call" | custom-call | tf_op jit(solution)/shard_map/prep/pallas_call | solution.py:522
  1.6 3.4 %collective-permute-start = (f32[672,128]{1,0:T(8,128)S(1)}, f32[672,128]{1,0:T(8,128)S(1)}, u32[]{:S(2)}, u32[]{:S(2)}) collective-permute-start(f32[672,128]{1,0:T(8,128)S(1)} %get-tuple-element.26), channel_id=1, source_target_pairs={{0,4},{4,0},{1,5},{5,1},{2,6},{6,2},{3,7},{7,3}} | collective-permute-start | bytes 1032200 | tf_op jit(solution)/shard_map/ppermute | solution.py:529
  5.0 1.5 %collective-permute-start.1 = (f32[240,640]{1,0:T(8,128)S(1)}, f32[240,640]{1,0:T(8,128)S(1)}, u32[]{:S(2)}, u32[]{:S(2)}) collective-permute-start(f32[240,640]{1,0:T(8,128)S(1)} %get-tuple-element.44.refs_9_), channel_id=1, source_target_pairs={{0,2},{1,3},{2,0},{3,1},{4,6},{5,7},{6,4},{7,5}} | collective-permute-start | bytes 1843208 | tf_op jit(solution)/shard_map/ppermute | solution.py:542
  6.5 8.5 %spread_own.1 = (f32[11,336,128]{2,1,0:T(8,128)S(1)}, f32[5040,128]{1,0:T(8,128)S(1)}, f32[5040,128]{1,0:T(8,128)S(1)}, f32[5040,128]{1,0:T(8,128)S(1)}, f32[504...) custom-call(f32[672,128]{1,0:T(8,128)S(1)} %get-tuple-element.27.pay_ref), custom_call_target="tpu_custom_call" | custom-call | flops 4194304000 | bytes 4194304 | tf_op jit(solution)/shard_map/spread_own/pallas_call | solution.py:530
  15.0 0.0 collective-permute-done.pay_ref
  15.0 0.0 copy-start
  15.0 0.0 copy-start.1
  15.0 0.0 copy-start.2
  15.0 0.0 copy-start.3
  15.1 6.5 %spread_far.1 = (f32[5040,128]{1,0:T(8,128)S(1)}, f32[5040,128]{1,0:T(8,128)S(1)}, f32[5040,128]{1,0:T(8,128)S(1)}, f32[5040,128]{1,0:T(8,128)S(1)}, f32[5040,12...) custom-call(f32[672,128]{1,0:T(8,128)S(1)} %collective-permute-done., ...), custom_call_target="tpu_custom_call", output_to_operand_aliasing={{0}: (2, {}), {1}: (3, {}), {2}: (4, {}), {3}: (5, {}), {4}... | custom-call | flops 4194304000 | bytes 4194304 | tf_op jit(solution)/shard_map/spread_far/pallas_call | solution.py:535
  21.5 0.0 collective-permute-done.1.refs_10_
  21.6 0.0 copy-done
  21.6 0.0 copy-done.1
  21.6 0.0 copy-done.2
  21.6 0.0 copy-done.3
  21.6 12.8 %image.1 = f32[2,160,80]{2,1,0:T(8,128)S(1)} custom-call(f32[5040,128]{1,0:T(8,128)S(1)} %get-tuple-element.36.refs_0_, f32[5040,128]{1,0:T(8,128)S(1)} %get-tuple-element.37.refs_1_, f32[5040,128]{1,0:T(8,128)S(1)} %get-tuple-element.38.refs_2_, f32[5040,128]{1,0:T(8,128)S(1)} %get-tuple-element.39.refs_3_, f32[5040,128]{1,0:T(8,128)S(1)} %get-tuple-element.40.refs_4_, ...), custom_call_target="tpu_custom_call" | custom-call | tf_op jit(solution)/shard_map/image/pallas_call | solution.py:546
  34.4 0.7 %copy.26 = f32[2,160,80]{2,1,0:T(8,128)} copy(f32[2,160,80]{2,1,0:T(8,128)S(1)} %image.1) | data formatting | bytes 204800
Async XLA Ops:
  1.6 13.4 %collective-permute-start = (f32[672,128]{1,0:T(8,128)S(1)}, f32[672,128]{1,0:T(8,128)S(1)}, u32[]{:S(2)}, u32[]{:S(2)}) collective-permute-start(f32[672,128]{1,0:T(8,128)S(1)} %get-tuple-element.26), channel_id=1, source_target_pairs={{0,4},{4,0},{1,5},{5,1},{2,6},{6,2},{3,7},{7,3}} | collective-permute-start | bytes 1032200 | tf_op jit(solution)/shard_map/ppermute | solution.py:529
  5.0 16.6 %collective-permute-start.1 = (f32[240,640]{1,0:T(8,128)S(1)}, f32[240,640]{1,0:T(8,128)S(1)}, u32[]{:S(2)}, u32[]{:S(2)}) collective-permute-start(f32[240,640]{1,0:T(8,128)S(1)} %get-tuple-element.44.refs_9_), channel_id=1, source_target_pairs={{0,2},{1,3},{2,0},{3,1},{4,6},{5,7},{6,4},{7,5}} | collective-permute-start | bytes 1843208 | tf_op jit(solution)/shard_map/ppermute | solution.py:542
  15.0 6.6 %copy-start = (bf16[1280,640]{1,0:T(8,128)(2,1)S(1)}, bf16[1280,640]{1,0:T(8,128)(2,1)}, u32[]{:S(2)}) copy-start(bf16[1280,640]{1,0:T(8,128)(2,1)} %constant.6.clone.refs_14_) | copy-start | bytes 4915204
  15.0 6.5 %copy-start.1 = (bf16[2,640,640]{2,1,0:T(8,128)(2,1)S(1)}, bf16[2,640,640]{2,1,0:T(8,128)(2,1)}, u32[]{:S(2)}) copy-start(bf16[2,640,640]{2,1,0:T(8,128)(2,1)} %constant.7.clone.refs_15_) | copy-start | bytes 4915204
  15.0 6.5 %copy-start.2 = (bf16[256,256]{1,0:T(8,128)(2,1)S(1)}, bf16[256,256]{1,0:T(8,128)(2,1)}, u32[]{:S(2)}) copy-start(bf16[256,256]{1,0:T(8,128)(2,1)} %constant.8.clone.refs_16_) | copy-start | bytes 393220
  15.0 6.5 %copy-start.3 = (f32[320]{0:T(512)S(1)}, f32[320]{0:T(512)}, u32[]{:S(2)}) copy-start(f32[320]{0:T(512)} %refs_13_.1) | copy-start | bytes 3844

commit v17 on v16

--- a/solution.py
+++ b/solution.py
@@ -30,6 +30,8 @@
 PS = 9
 PAY = 21
 CODE = 512
+JOIN = 56
+CG = 4
 MAPS = 240
 HW = 24
 ORDER = tuple(range(1, 9)) + (0, 9)
@@ -56,7 +58,7 @@
                 l0 = LANES * (2 * dp + t) + HALF * h
                 out[:, l0:l0 + HALF] = e[:, :, t, q0:q0 + HALF].reshape(2 * N_GRID, HALF)
     for t in range(2):
-        for d in range(4):
+        for d in range(CG):
             l0 = 4 * LANES + HALF * t + WIN * d
             out[:, l0:l0 + WIN] = e[:, :, t, QB * d + HALF:QB * (d + 1)].reshape(2 * N_GRID, WIN)
     return jnp.asarray(out, BF)
@@ -95,7 +97,7 @@
         cp.start()
         loads.append(cp)
     parts = []
-    for c in range(4):
+    for c in range(CG):
         n = min(HALF, MAPS - HALF * c)
         parts += [(sp_ref.at[pl.ds(HALF * c, n)], c, pl.ds(0, n)), (sq_ref.at[c], c, pl.ds(HALF, WIN))]
     parts.append((sm_ref, 3, pl.ds(HALF - WIN, WIN)))
@@ -121,7 +123,7 @@
             ref[PAY * (b + 1) - KW - 1:PAY * (b + 1) - 1, :] = wy_ref[:, cols]
             ref[PAY * (b + 1) - 1:PAY * (b + 1), :] = code[b:b + 1, :]
     loads[5].wait()
-    for c in range(4):
+    for c in range(CG):
         end = jnp.concatenate([maps_ref[i, c] for i in range(2)], axis=1)
         n = min(HALF, MAPS - HALF * c)
         sp_ref[HALF * c:HALF * c + n, 2 * WIDE:] = end[:n]
@@ -346,7 +348,7 @@
             i, c = ch // 4, ch % 4
             g_ref[row0 + n * c:row0 + n * c + QTR, N_GRID * i:N_GRID * (i + 1)] = g[QTR * ch:QTR * (ch + 1), :]
 
-    for m in range(4):
+    for m in range(CG):
         to_rows(QTR * m, LANES, tb_ref[2 * m + 1], tb_ref[2 * m + 2])
 
     mid = remote(sm_ref, sx_mid, halo_ss, halo_rs, 2, {'rows': across})
@@ -361,18 +363,18 @@
         own_even, far_even = side == core, side != core
         block = (lane & (HALF - 1)) >> 4
         h = jnp.dot(g_ref[4 * start:4 * (start + n), :], ev_ref[...], preferred_element_type=F32)
-        hc = [h[n * c:n * (c + 1)] for c in range(4)]
+        hc = [h[n * c:n * (c + 1)] for c in range(CG)]
         rems = [v[:, 4 * LANES:] for v in hc]
         for cp in range(2):
-            hs = [[v[:, LANES * i:LANES * (i + 1)] for i in range(4)] for v in hc[2 * cp:2 * cp + 2]]
-            for i in range(4):
+            hs = [[v[:, LANES * i:LANES * (i + 1)] for i in range(CG)] for v in hc[2 * cp:2 * cp + 2]]
+            for i in range(CG):
                 dp, t = i // 2, i % 2
                 odd = pltpu.roll(hs[1][i], HALF, axis=1)
                 sms[grp][dp, cp, t] = jnp.where(far_even, hs[0][i], odd).astype(BF)
                 hms[grp][dp, cp, t, core] = jnp.where(own_even, hs[0][i], odd).astype(BF)
         for d in range(ROWS):
             out = rems[d]
-            for c in range(4):
+            for c in range(CG):
                 if c != d:
                     out = jnp.where(block == c, pltpu.roll(rems[c], (WIN * (c - d)) % LANES, axis=1), out)
             srs[grp][d] = out.astype(BF)
@@ -458,14 +460,14 @@
             out = jnp.where(quarter == g, pltpu.roll(w[PB // 4 * g:PB // 4 * (g + 1)], QTR * g, axis=1), out)
         return out
 
-    first, other = pl.ds(0, (QTR + WIN)), pl.ds((QTR + WIN), PB - (QTR + WIN))
+    first, other = pl.ds(0, JOIN), pl.ds(JOIN, PB - JOIN)
     pieces[0] = piece(1 - k, 1)
     joined = remote(pieces.at[0, first], recvs.at[0, first], red_ss, red_rs, 0, homes[1])
     sends = [remote(pieces.at[0, other], recvs.at[0, other], red_ss, red_rs, 1, homes[0])]
     pieces[1] = piece(k, 1)
     sends.append(remote(pieces.at[1], recvs.at[1], red_ss, red_rs, 2, homes[1]))
     across_y = piece(1 - k, 0)
-    pieces[2, (QTR + WIN):] = across_y[(QTR + WIN):]
+    pieces[2, JOIN:] = across_y[JOIN:]
     sends.append(remote(pieces.at[2, other], recvs.at[2, other], red_ss, red_rs, 4, homes[2]))
     for cp in trades:
         cp.wait_recv()
@@ -477,12 +479,12 @@
                 part = jnp.dot(eu_ref[c, :, n0 * grp + kk * t:n0 * grp + kk * (t + 1)], hrs[grp][2 * c:2 * c + 2].reshape(kk, LANES), preferred_element_type=F32)
                 total = part if total is None else total + part
         acc_r[t] = total
-    s_rem[0], s_rem[1] = turn(jnp.concatenate([se_ref[c] for c in range(4)] + [jnp.zeros((HALF, N_GRID), F32)], axis=0))
+    s_rem[0], s_rem[1] = turn(jnp.concatenate([se_ref[c] for c in range(CG)] + [jnp.zeros((HALF, N_GRID), F32)], axis=0))
     tails[...] = rest(1 - k)
     tail = remote(tails, recvs_t, red_ss, red_rs, 3, homes[2])
     rem = rest(k)
     joined.wait_recv()
-    pieces[2, :(QTR + WIN)] = across_y[:(QTR + WIN)] + recvs[0, :(QTR + WIN)]
+    pieces[2, :JOIN] = across_y[:JOIN] + recvs[0, :JOIN]
     sends.append(remote(pieces.at[2, first], recvs.at[2, first], red_ss, red_rs, 5, homes[2]))
     main = piece(k, 0)
     d8 = jnp.broadcast_to(jnp.concatenate([d_ref[...][None, :], jnp.zeros((1, HALF), F32)], axis=1), (SUB, N_IMG + HALF))
@@ -495,12 +497,12 @@
     for cp in sends:
         cp.wait_recv()
     main = main + recvs[1] + recvs[2]
-    main = jnp.concatenate([main[:(QTR + WIN)], main[(QTR + WIN):] + recvs[0, (QTR + WIN):]], axis=0)
+    main = jnp.concatenate([main[:JOIN], main[JOIN:] + recvs[0, JOIN:]], axis=0)
     tail.wait_recv()
     rem = rem + recvs_t[...]
     for o in range(2):
         m = pltpu.roll(main, HALF, axis=1) if o else main
-        for j in range(4):
+        for j in range(CG):
             rows = slice(PB // 4 * j, PB // 4 * (j + 1))
             end = pltpu.roll(rem, (HALF - QTR * j - WIN * o) % LANES, axis=1)
             out_ref[o, rows, :] = (jnp.where(low[rows], m[rows], end) * dd[rows])[:, :QB]

time: 35.3 us -> 35.2 us (level)
  no operation moved by 1% of the time
where the time goes in v17:
time: 35.2 us; the launch traced here: 35 us
  Pallas kernels  29.3 us (83%)
  starting transfers between devices  4.88 us (14%)
  local copies, waits for them, and re-layouts  0.7 us (2%)
    pallas_call x1, Pallas kernels, local_fn(): pl.pallas_call(image_kernel, out_shape=jax.ShapeDtypeStruct((2, PB, QB),...  12.7 us
    pallas_call x1, Pallas kernels, local_fn(): pl.pallas_call(own_kernel, out_shape=[jax.ShapeDtypeStruct((11, CW, LANES...  8.56 us
    pallas_call x1, Pallas kernels, local_fn(): pl.pallas_call(far_kernel, out_shape=acc_shape + [jax.ShapeDtypeStruct((2...  6.49 us
    ppermute x1, starting transfers between devices, local_fn(): far_in = lax.ppermute(far, 'cols', [(0, 1), (1, 0)])  3.39 us
    pallas_call x1, Pallas kernels, local_fn(): pl.pallas_call(prep_kernel, out_shape=[jax.ShapeDtypeStruct((PAY * NB, LA...  1.56 us
    ppermute x1, starting transfers between devices, local_fn(): lax.ppermute(maps, 'rows', [(i, (i + 2) % ROWS) for i in range(ROWS)])  1.49 us
  transfers between devices with their start and end apart: 2, of which 0 were waited for; matrix products, arithmetic and copies ran while one was open for 0% of the time, Pallas kernels for 43%

profile of v17, /device:TPU:0, one launch (start us, length us, event | category | flops | bytes accessed | tf_op | source)
XLA Modules:
  0.0 35.0 jit_solution(4375100560961761415)
XLA Ops:
  0.0 1.6 %prep.1 = (f32[672,128]{1,0:T(8,128)S(1)}, f32[672,128]{1,0:T(8,128)S(1)}, f32[240,640]{1,0:T(8,128)S(1)}, f32[4,16,640]{2,1,0:T(8,128)S(1)}, f32[16,640]{1,0:T(8,128)S(1)}) custom-call(f32[2,8,4096]{2,1,0:T(8,128)} %ks_hbm.1, f32[6,4096]{1,0:T(8,128)} %wy_hbm.1, f32[6,4096]{1,0:T(8,128)} %wx_hbm.1, s32[32,128]{1,0:T(8,128)} %bitcast.4, s32[32,128]{1,0:T(8,128)} %bitcast.5, ...), custom_call_target="tpu_custom_call" | custom-call | tf_op jit(solution)/shard_map/prep/pallas_call | solution.py:524
  1.6 3.4 %collective-permute-start = (f32[672,128]{1,0:T(8,128)S(1)}, f32[672,128]{1,0:T(8,128)S(1)}, u32[]{:S(2)}, u32[]{:S(2)}) collective-permute-start(f32[672,128]{1,0:T(8,128)S(1)} %get-tuple-element.26), channel_id=1, source_target_pairs={{0,4},{4,0},{1,5},{5,1},{2,6},{6,2},{3,7},{7,3}} | collective-permute-start | bytes 1032200 | tf_op jit(solution)/shard_map/ppermute | solution.py:531
  5.0 1.5 %collective-permute-start.1 = (f32[240,640]{1,0:T(8,128)S(1)}, f32[240,640]{1,0:T(8,128)S(1)}, u32[]{:S(2)}, u32[]{:S(2)}) collective-permute-start(f32[240,640]{1,0:T(8,128)S(1)} %get-tuple-element.44.refs_9_), channel_id=1, source_target_pairs={{0,2},{1,3},{2,0},{3,1},{4,6},{5,7},{6,4},{7,5}} | collective-permute-start | bytes 1843208 | tf_op jit(solution)/shard_map/ppermute | solution.py:544
  6.5 8.6 %spread_own.1 = (f32[11,336,128]{2,1,0:T(8,128)S(1)}, f32[5040,128]{1,0:T(8,128)S(1)}, f32[5040,128]{1,0:T(8,128)S(1)}, f32[5040,128]{1,0:T(8,128)S(1)}, f32[504...) custom-call(f32[672,128]{1,0:T(8,128)S(1)} %get-tuple-element.27.pay_ref), custom_call_target="tpu_custom_call" | custom-call | flops 4194304000 | bytes 4194304 | tf_op jit(solution)/shard_map/spread_own/pallas_call | solution.py:532
  15.0 0.0 collective-permute-done.pay_ref
  15.0 0.0 copy-start
  15.0 0.0 copy-start.1
  15.1 0.0 copy-start.2
  15.1 0.0 copy-start.3
  15.1 6.5 %spread_far.1 = (f32[5040,128]{1,0:T(8,128)S(1)}, f32[5040,128]{1,0:T(8,128)S(1)}, f32[5040,128]{1,0:T(8,128)S(1)}, f32[5040,128]{1,0:T(8,128)S(1)}, f32[5040,12...) custom-call(f32[672,128]{1,0:T(8,128)S(1)} %collective-permute-done., ...), custom_call_target="tpu_custom_call", output_to_operand_aliasing={{0}: (2, {}), {1}: (3, {}), {2}: (4, {}), {3}: (5, {}), {4}... | custom-call | flops 4194304000 | bytes 4194304 | tf_op jit(solution)/shard_map/spread_far/pallas_call | solution.py:537
  21.6 0.0 collective-permute-done.1.refs_10_
  21.6 0.0 copy-done
  21.6 0.0 copy-done.1
  21.6 0.0 copy-done.2
  21.6 0.0 copy-done.3
  21.6 12.7 %image.1 = f32[2,160,80]{2,1,0:T(8,128)S(1)} custom-call(f32[5040,128]{1,0:T(8,128)S(1)} %get-tuple-element.36.refs_0_, f32[5040,128]{1,0:T(8,128)S(1)} %get-tuple-element.37.refs_1_, f32[5040,128]{1,0:T(8,128)S(1)} %get-tuple-element.38.refs_2_, f32[5040,128]{1,0:T(8,128)S(1)} %get-tuple-element.39.refs_3_, f32[5040,128]{1,0:T(8,128)S(1)} %get-tuple-element.40.refs_4_, ...), custom_call_target="tpu_custom_call" | custom-call | tf_op jit(solution)/shard_map/image/pallas_call | solution.py:548
  34.4 0.7 %copy.26 = f32[2,160,80]{2,1,0:T(8,128)} copy(f32[2,160,80]{2,1,0:T(8,128)S(1)} %image.1) | data formatting | bytes 204800
Async XLA Ops:
  1.6 13.5 %collective-permute-start = (f32[672,128]{1,0:T(8,128)S(1)}, f32[672,128]{1,0:T(8,128)S(1)}, u32[]{:S(2)}, u32[]{:S(2)}) collective-permute-start(f32[672,128]{1,0:T(8,128)S(1)} %get-tuple-element.26), channel_id=1, source_target_pairs={{0,4},{4,0},{1,5},{5,1},{2,6},{6,2},{3,7},{7,3}} | collective-permute-start | bytes 1032200 | tf_op jit(solution)/shard_map/ppermute | solution.py:531
  5.0 16.6 %collective-permute-start.1 = (f32[240,640]{1,0:T(8,128)S(1)}, f32[240,640]{1,0:T(8,128)S(1)}, u32[]{:S(2)}, u32[]{:S(2)}) collective-permute-start(f32[240,640]{1,0:T(8,128)S(1)} %get-tuple-element.44.refs_9_), channel_id=1, source_target_pairs={{0,2},{1,3},{2,0},{3,1},{4,6},{5,7},{6,4},{7,5}} | collective-permute-start | bytes 1843208 | tf_op jit(solution)/shard_map/ppermute | solution.py:544
  15.0 6.6 %copy-start = (bf16[1280,640]{1,0:T(8,128)(2,1)S(1)}, bf16[1280,640]{1,0:T(8,128)(2,1)}, u32[]{:S(2)}) copy-start(bf16[1280,640]{1,0:T(8,128)(2,1)} %constant.6.clone.refs_14_) | copy-start | bytes 4915204
  15.0 6.6 %copy-start.1 = (bf16[2,640,640]{2,1,0:T(8,128)(2,1)S(1)}, bf16[2,640,640]{2,1,0:T(8,128)(2,1)}, u32[]{:S(2)}) copy-start(bf16[2,640,640]{2,1,0:T(8,128)(2,1)} %constant.7.clone.refs_15_) | copy-start | bytes 4915204
  15.1 6.6 %copy-start.2 = (bf16[256,256]{1,0:T(8,128)(2,1)S(1)}, bf16[256,256]{1,0:T(8,128)(2,1)}, u32[]{:S(2)}) copy-start(bf16[256,256]{1,0:T(8,128)(2,1)} %constant.8.clone.refs_16_) | copy-start | bytes 393220
  15.1 6.6 %copy-start.3 = (f32[320]{0:T(512)S(1)}, f32[320]{0:T(512)}, u32[]{:S(2)}) copy-start(f32[320]{0:T(512)} %refs_13_.1) | copy-start | bytes 3844

commit v18 on v17

--- a/solution.py
+++ b/solution.py
@@ -464,11 +464,11 @@
     pieces[0] = piece(1 - k, 1)
     joined = remote(pieces.at[0, first], recvs.at[0, first], red_ss, red_rs, 0, homes[1])
     sends = [remote(pieces.at[0, other], recvs.at[0, other], red_ss, red_rs, 1, homes[0])]
-    pieces[1] = piece(k, 1)
-    sends.append(remote(pieces.at[1], recvs.at[1], red_ss, red_rs, 2, homes[1]))
     across_y = piece(1 - k, 0)
     pieces[2, JOIN:] = across_y[JOIN:]
     sends.append(remote(pieces.at[2, other], recvs.at[2, other], red_ss, red_rs, 4, homes[2]))
+    pieces[1] = piece(k, 1)
+    sends.append(remote(pieces.at[1], recvs.at[1], red_ss, red_rs, 2, homes[1]))
     for cp in trades:
         cp.wait_recv()
     for t in range(2):

time: 35.2 us -> 35.2 us (level)
  no operation moved by 1% of the time
where the time goes in v18:
time: 35.2 us; the launch traced here: 35 us
  Pallas kernels  29.3 us (83%)
  starting transfers between devices  4.88 us (14%)
  local copies, waits for them, and re-layouts  0.7 us (2%)
    pallas_call x1, Pallas kernels, local_fn(): pl.pallas_call(image_kernel, out_shape=jax.ShapeDtypeStruct((2, PB, QB),...  12.7 us
    pallas_call x1, Pallas kernels, local_fn(): pl.pallas_call(own_kernel, out_shape=[jax.ShapeDtypeStruct((11, CW, LANES...  8.54 us
    pallas_call x1, Pallas kernels, local_fn(): pl.pallas_call(far_kernel, out_shape=acc_shape + [jax.ShapeDtypeStruct((2...  6.49 us
    ppermute x1, starting transfers between devices, local_fn(): far_in = lax.ppermute(far, 'cols', [(0, 1), (1, 0)])  3.39 us
    pallas_call x1, Pallas kernels, local_fn(): pl.pallas_call(prep_kernel, out_shape=[jax.ShapeDtypeStruct((PAY * NB, LA...  1.56 us
    ppermute x1, starting transfers between devices, local_fn(): lax.ppermute(maps, 'rows', [(i, (i + 2) % ROWS) for i in range(ROWS)])  1.49 us
  transfers between devices with their start and end apart: 2, of which 0 were waited for; matrix products, arithmetic and copies ran while one was open for 0% of the time, Pallas kernels for 43%

profile of v18, /device:TPU:0, one launch (start us, length us, event | category | flops | bytes accessed | tf_op | source)
XLA Modules:
  0.0 35.0 jit_solution(2862499063465648229)
XLA Ops:
  0.0 1.6 %prep.1 = (f32[672,128]{1,0:T(8,128)S(1)}, f32[672,128]{1,0:T(8,128)S(1)}, f32[240,640]{1,0:T(8,128)S(1)}, f32[4,16,640]{2,1,0:T(8,128)S(1)}, f32[16,640]{1,0:T(8,128)S(1)}) custom-call(f32[2,8,4096]{2,1,0:T(8,128)} %ks_hbm.1, f32[6,4096]{1,0:T(8,128)} %wy_hbm.1, f32[6,4096]{1,0:T(8,128)} %wx_hbm.1, s32[32,128]{1,0:T(8,128)} %bitcast.4, s32[32,128]{1,0:T(8,128)} %bitcast.5, ...), custom_call_target="tpu_custom_call" | custom-call | tf_op jit(solution)/shard_map/prep/pallas_call | solution.py:524
  1.6 3.4 %collective-permute-start = (f32[672,128]{1,0:T(8,128)S(1)}, f32[672,128]{1,0:T(8,128)S(1)}, u32[]{:S(2)}, u32[]{:S(2)}) collective-permute-start(f32[672,128]{1,0:T(8,128)S(1)} %get-tuple-element.26), channel_id=1, source_target_pairs={{0,4},{4,0},{1,5},{5,1},{2,6},{6,2},{3,7},{7,3}} | collective-permute-start | bytes 1032200 | tf_op jit(solution)/shard_map/ppermute | solution.py:531
  5.0 1.5 %collective-permute-start.1 = (f32[240,640]{1,0:T(8,128)S(1)}, f32[240,640]{1,0:T(8,128)S(1)}, u32[]{:S(2)}, u32[]{:S(2)}) collective-permute-start(f32[240,640]{1,0:T(8,128)S(1)} %get-tuple-element.44.refs_9_), channel_id=1, source_target_pairs={{0,2},{1,3},{2,0},{3,1},{4,6},{5,7},{6,4},{7,5}} | collective-permute-start | bytes 1843208 | tf_op jit(solution)/shard_map/ppermute | solution.py:544
  6.5 8.5 %spread_own.1 = (f32[11,336,128]{2,1,0:T(8,128)S(1)}, f32[5040,128]{1,0:T(8,128)S(1)}, f32[5040,128]{1,0:T(8,128)S(1)}, f32[5040,128]{1,0:T(8,128)S(1)}, f32[504...) custom-call(f32[672,128]{1,0:T(8,128)S(1)} %get-tuple-element.27.pay_ref), custom_call_target="tpu_custom_call" | custom-call | flops 4194304000 | bytes 4194304 | tf_op jit(solution)/shard_map/spread_own/pallas_call | solution.py:532
  15.0 0.0 collective-permute-done.pay_ref
  15.0 0.0 copy-start
  15.0 0.0 copy-start.1
  15.0 0.0 copy-start.2
  15.0 0.0 copy-start.3
  15.1 6.5 %spread_far.1 = (f32[5040,128]{1,0:T(8,128)S(1)}, f32[5040,128]{1,0:T(8,128)S(1)}, f32[5040,128]{1,0:T(8,128)S(1)}, f32[5040,128]{1,0:T(8,128)S(1)}, f32[5040,12...) custom-call(f32[672,128]{1,0:T(8,128)S(1)} %collective-permute-done., ...), custom_call_target="tpu_custom_call", output_to_operand_aliasing={{0}: (2, {}), {1}: (3, {}), {2}: (4, {}), {3}: (5, {}), {4}... | custom-call | flops 4194304000 | bytes 4194304 | tf_op jit(solution)/shard_map/spread_far/pallas_call | solution.py:537
  21.6 0.0 collective-permute-done.1.refs_10_
  21.6 0.0 copy-done
  21.6 0.0 copy-done.1
  21.6 0.0 copy-done.2
  21.6 0.0 copy-done.3
  21.6 12.7 %image.1 = f32[2,160,80]{2,1,0:T(8,128)S(1)} custom-call(f32[5040,128]{1,0:T(8,128)S(1)} %get-tuple-element.36.refs_0_, f32[5040,128]{1,0:T(8,128)S(1)} %get-tuple-element.37.refs_1_, f32[5040,128]{1,0:T(8,128)S(1)} %get-tuple-element.38.refs_2_, f32[5040,128]{1,0:T(8,128)S(1)} %get-tuple-element.39.refs_3_, f32[5040,128]{1,0:T(8,128)S(1)} %get-tuple-element.40.refs_4_, ...), custom_call_target="tpu_custom_call" | custom-call | tf_op jit(solution)/shard_map/image/pallas_call | solution.py:548
  34.3 0.7 %copy.26 = f32[2,160,80]{2,1,0:T(8,128)} copy(f32[2,160,80]{2,1,0:T(8,128)S(1)} %image.1) | data formatting | bytes 204800
Async XLA Ops:
  1.6 13.4 %collective-permute-start = (f32[672,128]{1,0:T(8,128)S(1)}, f32[672,128]{1,0:T(8,128)S(1)}, u32[]{:S(2)}, u32[]{:S(2)}) collective-permute-start(f32[672,128]{1,0:T(8,128)S(1)} %get-tuple-element.26), channel_id=1, source_target_pairs={{0,4},{4,0},{1,5},{5,1},{2,6},{6,2},{3,7},{7,3}} | collective-permute-start | bytes 1032200 | tf_op jit(solution)/shard_map/ppermute | solution.py:531
  5.0 16.6 %collective-permute-start.1 = (f32[240,640]{1,0:T(8,128)S(1)}, f32[240,640]{1,0:T(8,128)S(1)}, u32[]{:S(2)}, u32[]{:S(2)}) collective-permute-start(f32[240,640]{1,0:T(8,128)S(1)} %get-tuple-element.44.refs_9_), channel_id=1, source_target_pairs={{0,2},{1,3},{2,0},{3,1},{4,6},{5,7},{6,4},{7,5}} | collective-permute-start | bytes 1843208 | tf_op jit(solution)/shard_map/ppermute | solution.py:544
  15.0 6.6 %copy-start = (bf16[1280,640]{1,0:T(8,128)(2,1)S(1)}, bf16[1280,640]{1,0:T(8,128)(2,1)}, u32[]{:S(2)}) copy-start(bf16[1280,640]{1,0:T(8,128)(2,1)} %constant.6.clone.refs_14_) | copy-start | bytes 4915204
  15.0 6.6 %copy-start.1 = (bf16[2,640,640]{2,1,0:T(8,128)(2,1)S(1)}, bf16[2,640,640]{2,1,0:T(8,128)(2,1)}, u32[]{:S(2)}) copy-start(bf16[2,640,640]{2,1,0:T(8,128)(2,1)} %constant.7.clone.refs_15_) | copy-start | bytes 4915204
  15.0 6.6 %copy-start.2 = (bf16[256,256]{1,0:T(8,128)(2,1)S(1)}, bf16[256,256]{1,0:T(8,128)(2,1)}, u32[]{:S(2)}) copy-start(bf16[256,256]{1,0:T(8,128)(2,1)} %constant.8.clone.refs_16_) | copy-start | bytes 393220
  15.0 6.5 %copy-start.3 = (f32[320]{0:T(512)S(1)}, f32[320]{0:T(512)}, u32[]{:S(2)}) copy-start(f32[320]{0:T(512)} %refs_13_.1) | copy-start | bytes 3844

commit v19 on v18

--- a/solution.py
+++ b/solution.py
@@ -30,7 +30,7 @@
 PS = 9
 PAY = 21
 CODE = 512
-JOIN = 56
+JOIN = 64
 CG = 4
 MAPS = 240
 HW = 24

time: 35.2 us -> 35.3 us (level)
  no operation moved by 1% of the time
where the time goes in v19:
time: 35.3 us; the launch traced here: 35.1 us
  Pallas kernels  29.4 us (83%)
  starting transfers between devices  4.88 us (14%)
  local copies, waits for them, and re-layouts  0.7 us (2%)
    pallas_call x1, Pallas kernels, local_fn(): pl.pallas_call(image_kernel, out_shape=jax.ShapeDtypeStruct((2, PB, QB),...  12.8 us
    pallas_call x1, Pallas kernels, local_fn(): pl.pallas_call(own_kernel, out_shape=[jax.ShapeDtypeStruct((11, CW, LANES...  8.55 us
    pallas_call x1, Pallas kernels, local_fn(): pl.pallas_call(far_kernel, out_shape=acc_shape + [jax.ShapeDtypeStruct((2...  6.47 us
    ppermute x1, starting transfers between devices, local_fn(): far_in = lax.ppermute(far, 'cols', [(0, 1), (1, 0)])  3.39 us
    pallas_call x1, Pallas kernels, local_fn(): pl.pallas_call(prep_kernel, out_shape=[jax.ShapeDtypeStruct((PAY * NB, LA...  1.56 us
    ppermute x1, starting transfers between devices, local_fn(): lax.ppermute(maps, 'rows', [(i, (i + 2) % ROWS) for i in range(ROWS)])  1.49 us
  transfers between devices with their start and end apart: 2, of which 0 were waited for; matrix products, arithmetic and copies ran while one was open for 0% of the time, Pallas kernels for 43%

profile of v19, /device:TPU:0, one launch (start us, length us, event | category | flops | bytes accessed | tf_op | source)
XLA Modules:
  0.0 35.1 jit_solution(14114138105410411539)
XLA Ops:
  0.0 1.6 %prep.1 = (f32[672,128]{1,0:T(8,128)S(1)}, f32[672,128]{1,0:T(8,128)S(1)}, f32[240,640]{1,0:T(8,128)S(1)}, f32[4,16,640]{2,1,0:T(8,128)S(1)}, f32[16,640]{1,0:T(8,128)S(1)}) custom-call(f32[2,8,4096]{2,1,0:T(8,128)} %ks_hbm.1, f32[6,4096]{1,0:T(8,128)} %wy_hbm.1, f32[6,4096]{1,0:T(8,128)} %wx_hbm.1, s32[32,128]{1,0:T(8,128)} %bitcast.4, s32[32,128]{1,0:T(8,128)} %bitcast.5, ...), custom_call_target="tpu_custom_call" | custom-call | tf_op jit(solution)/shard_map/prep/pallas_call | solution.py:524
  1.6 3.4 %collective-permute-start = (f32[672,128]{1,0:T(8,128)S(1)}, f32[672,128]{1,0:T(8,128)S(1)}, u32[]{:S(2)}, u32[]{:S(2)}) collective-permute-start(f32[672,128]{1,0:T(8,128)S(1)} %get-tuple-element.26), channel_id=1, source_target_pairs={{0,4},{4,0},{1,5},{5,1},{2,6},{6,2},{3,7},{7,3}} | collective-permute-start | bytes 1032200 | tf_op jit(solution)/shard_map/ppermute | solution.py:531
  5.0 1.5 %collective-permute-start.1 = (f32[240,640]{1,0:T(8,128)S(1)}, f32[240,640]{1,0:T(8,128)S(1)}, u32[]{:S(2)}, u32[]{:S(2)}) collective-permute-start(f32[240,640]{1,0:T(8,128)S(1)} %get-tuple-element.44.refs_9_), channel_id=1, source_target_pairs={{0,2},{1,3},{2,0},{3,1},{4,6},{5,7},{6,4},{7,5}} | collective-permute-start | bytes 1843208 | tf_op jit(solution)/shard_map/ppermute | solution.py:544
  6.5 8.6 %spread_own.1 = (f32[11,336,128]{2,1,0:T(8,128)S(1)}, f32[5040,128]{1,0:T(8,128)S(1)}, f32[5040,128]{1,0:T(8,128)S(1)}, f32[5040,128]{1,0:T(8,128)S(1)}, f32[504...) custom-call(f32[672,128]{1,0:T(8,128)S(1)} %get-tuple-element.27.pay_ref), custom_call_target="tpu_custom_call" | custom-call | flops 4194304000 | bytes 4194304 | tf_op jit(solution)/shard_map/spread_own/pallas_call | solution.py:532
  15.0 0.0 collective-permute-done.pay_ref
  15.0 0.0 copy-start
  15.0 0.0 copy-start.1
  15.0 0.0 copy-start.2
  15.1 0.0 copy-start.3
  15.1 6.5 %spread_far.1 = (f32[5040,128]{1,0:T(8,128)S(1)}, f32[5040,128]{1,0:T(8,128)S(1)}, f32[5040,128]{1,0:T(8,128)S(1)}, f32[5040,128]{1,0:T(8,128)S(1)}, f32[5040,12...) custom-call(f32[672,128]{1,0:T(8,128)S(1)} %collective-permute-done., ...), custom_call_target="tpu_custom_call", output_to_operand_aliasing={{0}: (2, {}), {1}: (3, {}), {2}: (4, {}), {3}: (5, {}), {4}... | custom-call | flops 4194304000 | bytes 4194304 | tf_op jit(solution)/shard_map/spread_far/pallas_call | solution.py:537
  21.6 0.0 collective-permute-done.1.refs_10_
  21.6 0.0 copy-done
  21.6 0.0 copy-done.1
  21.6 0.0 copy-done.2
  21.6 0.0 copy-done.3
  21.6 12.8 %image.1 = f32[2,160,80]{2,1,0:T(8,128)S(1)} custom-call(f32[5040,128]{1,0:T(8,128)S(1)} %get-tuple-element.36.refs_0_, f32[5040,128]{1,0:T(8,128)S(1)} %get-tuple-element.37.refs_1_, f32[5040,128]{1,0:T(8,128)S(1)} %get-tuple-element.38.refs_2_, f32[5040,128]{1,0:T(8,128)S(1)} %get-tuple-element.39.refs_3_, f32[5040,128]{1,0:T(8,128)S(1)} %get-tuple-element.40.refs_4_, ...), custom_call_target="tpu_custom_call" | custom-call | tf_op jit(solution)/shard_map/image/pallas_call | solution.py:548
  34.5 0.7 %copy.26 = f32[2,160,80]{2,1,0:T(8,128)} copy(f32[2,160,80]{2,1,0:T(8,128)S(1)} %image.1) | data formatting | bytes 204800
Async XLA Ops:
  1.6 13.4 %collective-permute-start = (f32[672,128]{1,0:T(8,128)S(1)}, f32[672,128]{1,0:T(8,128)S(1)}, u32[]{:S(2)}, u32[]{:S(2)}) collective-permute-start(f32[672,128]{1,0:T(8,128)S(1)} %get-tuple-element.26), channel_id=1, source_target_pairs={{0,4},{4,0},{1,5},{5,1},{2,6},{6,2},{3,7},{7,3}} | collective-permute-start | bytes 1032200 | tf_op jit(solution)/shard_map/ppermute | solution.py:531
  5.0 16.6 %collective-permute-start.1 = (f32[240,640]{1,0:T(8,128)S(1)}, f32[240,640]{1,0:T(8,128)S(1)}, u32[]{:S(2)}, u32[]{:S(2)}) collective-permute-start(f32[240,640]{1,0:T(8,128)S(1)} %get-tuple-element.44.refs_9_), channel_id=1, source_target_pairs={{0,2},{1,3},{2,0},{3,1},{4,6},{5,7},{6,4},{7,5}} | collective-permute-start | bytes 1843208 | tf_op jit(solution)/shard_map/ppermute | solution.py:544
  15.0 6.5 %copy-start = (bf16[1280,640]{1,0:T(8,128)(2,1)S(1)}, bf16[1280,640]{1,0:T(8,128)(2,1)}, u32[]{:S(2)}) copy-start(bf16[1280,640]{1,0:T(8,128)(2,1)} %constant.6.clone.refs_14_) | copy-start | bytes 4915204
  15.0 6.5 %copy-start.1 = (bf16[2,640,640]{2,1,0:T(8,128)(2,1)S(1)}, bf16[2,640,640]{2,1,0:T(8,128)(2,1)}, u32[]{:S(2)}) copy-start(bf16[2,640,640]{2,1,0:T(8,128)(2,1)} %constant.7.clone.refs_15_) | copy-start | bytes 4915204
  15.0 6.5 %copy-start.2 = (bf16[256,256]{1,0:T(8,128)(2,1)S(1)}, bf16[256,256]{1,0:T(8,128)(2,1)}, u32[]{:S(2)}) copy-start(bf16[256,256]{1,0:T(8,128)(2,1)} %constant.8.clone.refs_16_) | copy-start | bytes 393220
  15.1 6.5 %copy-start.3 = (f32[320]{0:T(512)S(1)}, f32[320]{0:T(512)}, u32[]{:S(2)}) copy-start(f32[320]{0:T(512)} %refs_13_.1) | copy-start | bytes 3844
